TPU v7x, 1024 devices: a whole 4x8x16 slice. The times are simulated.
1024 devices in a mesh: lat: 128 (over z, x, core), lon: 8 (over y).
Axes of the slice: x: 4, y: 8, z: 16, core: 2. Of those that a mesh axis runs over, the one named last changes fastest.
Arguments:
- courant: float32 [2, 16, 2048, 1024], P(None, None, 'lat', 'lon'), may hold values from -0.45 to 0.45
- obs_matrix: float32 [128, 64, 128, 128], P('lat', 'lon'), may hold values from -0.5 to 0.5
- obs_weight: float32 [128, 64, 128], P('lat', 'lon'), may hold values from 0.5 to 4
- innovation: float32 [128, 64, 128], P('lat', 'lon'), may hold values from -6 to 6
- block_owner: int32 [128, 64, 1], P('lat', 'lon'), may hold values from 0 to 7; in each aligned block of 8 rows (0 to 7, 8 to 15, ..., all dimensions but the last counted through in order) at most 2 rows name the same one
- block_row: int32 [128, 64], P('lat', 'lon'), may hold values from 0 to 255
- block_count: int32 [128, 8], P('lat', 'lon'), may hold values from 1 to 8, as said below
Outputs:
- increment: float32 [16, 2048, 1024], P(None, 'lat', 'lon')
- residual: float32 [16, 2048, 1024], P(None, 'lat', 'lon')
Inputs may be any that keep to these rules, and one draw needn't show every extreme that they name: `block_owner`: among one device's 8 block slots no lon index is named more than 2 times, a bound that some block reaches. A device's first block_count slots are live, the rest are padding; some device has all 8 live.
All inputs are finite; a program needn't handle non-finite values.
Results may differ from a plain program's by a relative error of at most 0.0003.
Values sent between devices are 32-bit elements; how exact they have to be, the bound alone decides.
No kernel may reach another device: no remote copies, remote signals or barrier semaphores. Data moves between devices by JAX's collectives and lax.ppermute only.
A program may use at most 32 MiB of HBM per device.

v0:
```python
import jax
import jax.numpy as jnp
from jax import lax
from jax.sharding import Mesh
from jax.sharding import PartitionSpec as P

SLOT = 2
STEPS = 4
ITERS = 2
LAT = ("lat_0", "lat_1", "lat_2")
LAT_LON = ("lat_0", "lat_1", "lat_2", "lon")


def padded_2(cells, sides, width):
    for axis, dim in sides:
        count = lax.axis_size(axis)
        head = lax.slice_in_dim(cells, 0, width, axis=dim)
        tail = lax.slice_in_dim(cells, cells.shape[dim] - width, cells.shape[dim], axis=dim)
        cells = jnp.concatenate(
            [
                lax.ppermute(tail, axis, [(i, (i + 1) % count) for i in range(count)]),
                cells,
                lax.ppermute(head, axis, [((i + 1) % count, i) for i in range(count)]),
            ],
            axis=dim,
        )
    return cells


def sent_together(arrays, axis, split_dim, concat_dim, along):
    columns = [a.reshape(*a.shape[:along], -1) for a in arrays]
    both = jnp.concatenate(columns, axis=along)
    out, at, outs = (
        lax.all_to_all(both, axis, split_axis=split_dim, concat_axis=concat_dim, tiled=True),
        0,
        [],
    )
    for a, column in zip(arrays, columns):
        section = out[..., at : at + column.shape[along]]
        outs.append(section.reshape(*section.shape[:along], *a.shape[along:]))
        at += column.shape[along]
    return tuple(outs)


def one_axis_at_a_time(array, axes):
    for axis in axes:
        array = lax.psum(array, axis)
    return array


def window(array_in, row_start, col_start, row_span, col_span):
    rows_cut = lax.slice_in_dim(array_in, row_start, row_start + row_span, axis=array_in.ndim - 2)
    return lax.slice_in_dim(rows_cut, col_start, col_start + col_span, axis=array_in.ndim - 1)


def shards(courant, obs_matrix, obs_weight, innovation, block_owner, block_row, block_count):
    levels = courant.shape[1]
    lat_rows = courant.shape[2]
    lon_cells = courant.shape[3]
    capacity = block_row.shape[1]
    lon_count = lax.axis_size("lon")
    lat_index = lax.axis_index(LAT)
    lat_total = lax.axis_size(LAT)
    rate_parts = jnp.stack(
        [
            jnp.maximum(courant[0], 0.0),
            jnp.maximum(-courant[0], 0.0),
            jnp.maximum(courant[1], 0.0),
            jnp.maximum(-courant[1], 0.0),
        ]
    )

    def edge_mask(margin):
        global_rows = (
            jnp.arange(lat_rows + 2 * margin, dtype=jnp.int32) + lat_index * lat_rows - margin
        )
        inside = (global_rows >= 0) & (global_rows < lat_rows * lat_total)
        return jnp.where(inside, 1.0, 0.0).astype(jnp.float32)[:, None]

    deep_rates = padded_2(rate_parts, ((LAT, 2), ("lon", 3)), STEPS)
    deep_keep = 1.0 - deep_rates[0] - deep_rates[1] - deep_rates[2] - deep_rates[3]

    def model_tangent(grid_field):
        padded = padded_2(grid_field, ((LAT, 1), ("lon", 2)), STEPS) * edge_mask(STEPS)
        for sweep in range(STEPS):
            margin = STEPS - sweep - 1
            offset = sweep + 1
            row_span = lat_rows + 2 * margin
            col_span = lon_cells + 2 * margin
            fresh_field = (
                window(deep_keep, offset, offset, row_span, col_span) * padded[:, 1:-1, 1:-1]
                + window(deep_rates[0], offset, offset, row_span, col_span) * padded[:, :-2, 1:-1]
                + window(deep_rates[1], offset, offset, row_span, col_span) * padded[:, 2:, 1:-1]
                + window(deep_rates[2], offset, offset, row_span, col_span) * padded[:, 1:-1, :-2]
                + window(deep_rates[3], offset, offset, row_span, col_span) * padded[:, 1:-1, 2:]
            )
            padded = fresh_field * edge_mask(margin)
        return padded

    def model_adjoint(grid_field):
        padded = padded_2(grid_field, ((LAT, 1), ("lon", 2)), STEPS) * edge_mask(STEPS)
        for sweep in range(STEPS):
            margin = STEPS - sweep - 1
            offset = sweep + 1
            row_span = lat_rows + 2 * margin
            col_span = lon_cells + 2 * margin
            fresh_field = (
                window(deep_keep, offset, offset, row_span, col_span) * padded[:, 1:-1, 1:-1]
                + window(deep_rates[0], offset + 1, offset, row_span, col_span)
                * padded[:, 2:, 1:-1]
                + window(deep_rates[1], offset - 1, offset, row_span, col_span)
                * padded[:, :-2, 1:-1]
                + window(deep_rates[2], offset, offset + 1, row_span, col_span)
                * padded[:, 1:-1, 2:]
                + window(deep_rates[3], offset, offset - 1, row_span, col_span)
                * padded[:, 1:-1, :-2]
            )
            padded = fresh_field * edge_mask(margin)
        return padded

    owner_lon = block_owner[0, :, 0]
    onehot = (owner_lon[:, None] == jnp.arange(lon_count, dtype=jnp.int32)[None, :]).astype(
        jnp.int32
    )
    before = jnp.cumsum(onehot, axis=0) - onehot
    target = owner_lon * SLOT + jnp.sum(before * onehot, axis=1)
    live_mask = jnp.arange(capacity, dtype=jnp.int32) < block_count[0, 0]
    weighted = jnp.where(live_mask[:, None], obs_weight[0], 0.0)
    requests = (
        jnp.full((lon_count * SLOT,), -1, jnp.int32)
        .at[target]
        .set(jnp.where(live_mask, block_row[0], -1))
    )
    asked_raw = lax.all_to_all(requests, "lon", split_axis=0, concat_axis=0, tiled=True)
    asked_rows = jnp.maximum(asked_raw, 0)

    def accumulate(block_terms):
        flat_out = (
            jnp.zeros((levels * lat_rows, lon_cells), jnp.float32).at[asked_rows].add(block_terms)
        )
        return flat_out.reshape(levels, lat_rows, lon_cells)

    def to_slots(block_data):
        return (
            jnp.zeros((lon_count * SLOT,) + block_data.shape[1:], jnp.float32)
            .at[target]
            .set(block_data)
        )

    matrices, weights_there, innov_there = sent_together(
        (to_slots(obs_matrix[0]), to_slots(weighted), to_slots(innovation[0])), "lon", 0, 0, 2
    )

    def observe_adjoint(grid_field):
        seen_rows = grid_field.reshape(levels * lat_rows, lon_cells)[asked_rows]
        predicted = jnp.einsum("bok,bk->bo", matrices, seen_rows, precision=lax.Precision.HIGHEST)
        return accumulate(
            jnp.einsum(
                "bok,bo->bk", matrices, weights_there * predicted, precision=lax.Precision.HIGHEST
            )
        )

    departure = accumulate(
        jnp.einsum(
            "bok,bo->bk", matrices, weights_there * innov_there, precision=lax.Precision.HIGHEST
        )
    )

    def hessian(vector):
        return vector + model_adjoint(observe_adjoint(model_tangent(vector)))

    right_side = model_adjoint(departure)
    increment = jnp.zeros_like(right_side)
    residual = right_side

    def two_products(vector, image_vec):
        return (
            one_axis_at_a_time(jnp.sum(vector * vector), LAT_LON),
            one_axis_at_a_time(jnp.sum(vector * image_vec), LAT_LON),
        )

    image_vec = hessian(residual)
    norm_now, product = two_products(residual, image_vec)
    step_size = norm_now / product
    direction = residual
    along = image_vec
    for sweep in range(ITERS):
        increment = increment + step_size * direction
        residual = residual - step_size * along
        if sweep + 1 < ITERS:
            image_vec = hessian(residual)
            norm_next, product = two_products(residual, image_vec)
            beta_ratio = norm_next / norm_now
            step_size = norm_next / (product - beta_ratio * norm_next / step_size)
            direction = residual + beta_ratio * direction
            along = image_vec + beta_ratio * along
            norm_now = norm_next
    return (increment, residual)


def solution(mesh):
    torus = Mesh(
        mesh.devices.reshape(16, 4, 2, mesh.shape["lon"]), ("lat_0", "lat_1", "lat_2", "lon")
    )
    placed = (
        P(None, None, LAT, "lon"),
        P(LAT, "lon", None, None),
        P(LAT, "lon", None),
        P(LAT, "lon", None),
        P(LAT, "lon", None),
        P(LAT, "lon"),
        P(LAT, "lon"),
    )
    return jax.shard_map(
        shards,
        mesh=torus,
        in_specs=placed,
        out_specs=(P(None, LAT, "lon"), P(None, LAT, "lon")),
        check_vma=False,
    )
```

profile of v0, /device:TPU:1, one launch (start us, length us, event | category | flops | bytes accessed | tf_op | source)
XLA Modules:
  0.0 336.6 jit_solution(7521507458015975667)
XLA Ops:
  5.5 7.6 %all-to-all-start = ((s32[8,2,1]{1,2,0:T(1,128)}), s32[8,2,1]{1,2,0:T(1,128)S(1)}, u32[]{:S(2)}, u32[]{:S(2)}) async-start(s32[8,2,1]{1,2,0:T(1,128)} %bitcast.10), calls=%async_computation | async-start | bytes 8192 | tf_op jit(solution)/shard_map/all_to_all | solution.py:134
  18.4 2.5 scatter_fusion
  20.9 2.2 pad_maximum_fusion
  23.2 1.6 copy.44
  24.8 6.8 %all-to-all-start.1 = ((f32[16,128,130]{1,2,0:T(8,128)}), f32[16,128,130]{1,2,0:T(8,128)S(1)}, u32[]{:S(2)}, u32[]{:S(2)}) async-start(f32[16,128,130]{1,2,0:T(8,128)} %copy.44), calls=%async_computation.1 | async-start | bytes 2228224 | tf_op jit(solution)/shard_map/all_to_all | solution.py:34
  31.7 4.5 %collective-permute-start = (f32[4,16,4,128]{3,2,1,0:T(4,128)S(1)}, f32[4,16,4,128]{3,2,1,0:T(4,128)S(1)}, u32[]{:S(2)}, u32[]{:S(2)}) collective-permute-start(f32[4,16,4,128]{3,2,1,0:T(4,128)S(1)} %get-tuple-element.34), channel_id=1, source_target_pairs={{0,8},{8,16},{16,24},{24,32},{32,40},{40,48},{48,56},{56,64},{64,7... | collective-permute-start | bytes 393224 | tf_op jit(solution)/shard_map/ppermute | solution.py:21
  36.2 9.6 %collective-permute-start.1 = (f32[4,16,4,128]{3,2,1,0:T(4,128)S(1)}, f32[4,16,4,128]{3,2,1,0:T(4,128)S(1)}, u32[]{:S(2)}, u32[]{:S(2)}) collective-permute-start(f32[4,16,4,128]{3,2,1,0:T(4,128)S(1)} %get-tuple-element.35), channel_id=1, source_target_pairs={{8,0},{16,8},{24,16},{32,24},{40,32},{48,40},{56,48},{64,56},{72,6... | collective-permute-start | bytes 393224 | tf_op jit(solution)/shard_map/ppermute | solution.py:23
  48.1 1.6 copy.37
  49.7 3.7 %collective-permute-start.2 = (f32[4,16,24,4]{2,1,3,0:T(8,128)S(1)}, f32[4,16,24,4]{2,1,3,0:T(8,128)}, u32[]{:S(2)}, u32[]{:S(2)}) collective-permute-start(f32[4,16,24,4]{2,1,3,0:T(8,128)S(1)} %copy.37), channel_id=1, source_target_pairs={{0,1},{1,2},{2,3},{3,4},{4,5},{5,6},{6,7},{7,0},{8,9},{9,10},{10,1... | collective-permute-start | bytes 73736 | tf_op jit(solution)/shard_map/ppermute | solution.py:21
  54.5 3.1 collective-permute-start.3
  62.0 2.1 pad_maximum_fusion.1
  64.2 1.7 fusion.8
  66.7 6.6 %collective-permute-start.4 = (f32[16,4,128]{2,1,0:T(4,128)S(1)}, f32[16,4,128]{2,1,0:T(4,128)S(1)}, u32[]{:S(2)}, u32[]{:S(2)}) collective-permute-start(f32[16,4,128]{2,1,0:T(4,128)S(1)} %get-tuple-element.60), channel_id=1, source_target_pairs={{0,8},{8,16},{16,24},{24,32},{32,40},{40,48},{48,56},{56,64},{64,7... | collective-permute-start | bytes 98312 | tf_op jit(solution)/shard_map/ppermute | solution.py:21
  73.3 8.2 %collective-permute-start.5 = (f32[16,4,128]{2,1,0:T(4,128)S(1)}, f32[16,4,128]{2,1,0:T(4,128)S(1)}, u32[]{:S(2)}, u32[]{:S(2)}) collective-permute-start(f32[16,4,128]{2,1,0:T(4,128)S(1)} %get-tuple-element.61), channel_id=1, source_target_pairs={{8,0},{16,8},{24,16},{32,24},{40,32},{48,40},{56,48},{64,56},{72,6... | collective-permute-start | bytes 98312 | tf_op jit(solution)/shard_map/ppermute | solution.py:23
  83.2 3.1 collective-permute-start.6
  86.2 3.4 %collective-permute-start.7 = (f32[16,24,4]{2,1,0:T(8,128)S(1)}, f32[16,24,4]{2,1,0:T(8,128)S(1)}, u32[]{:S(2)}, u32[]{:S(2)}) collective-permute-start(f32[16,24,4]{2,1,0:T(8,128)S(1)} %get-tuple-element.49), channel_id=1, source_target_pairs={{1,0},{2,1},{3,2},{4,3},{5,4},{6,5},{7,6},{0,7},{9,8},{10,9},{11,1... | collective-permute-start | bytes 18440 | tf_op jit(solution)/shard_map/ppermute | solution.py:23
  90.8 2.3 collective-permute-done.7
  96.7 1.9 collective-permute-start.8
  98.6 11.1 %collective-permute-start.9 = (f32[16,4,128]{2,1,0:T(4,128)S(1)}, f32[16,4,128]{2,1,0:T(4,128)S(1)}, u32[]{:S(2)}, u32[]{:S(2)}) collective-permute-start(f32[16,4,128]{2,1,0:T(4,128)S(1)} %get-tuple-element.59), channel_id=1, source_target_pairs={{8,0},{16,8},{24,16},{32,24},{40,32},{48,40},{56,48},{64,56},{72,6... | collective-permute-start | bytes 98312 | tf_op jit(solution)/shard_map/ppermute | solution.py:23
  110.7 3.9 %collective-permute-start.10 = (f32[16,24,4]{2,1,0:T(8,128)S(1)}, f32[16,24,4]{2,1,0:T(8,128)S(1)}, u32[]{:S(2)}, u32[]{:S(2)}) collective-permute-start(f32[16,24,4]{2,1,0:T(8,128)S(1)} %get-tuple-element.46), channel_id=1, source_target_pairs={{0,1},{1,2},{2,3},{3,4},{4,5},{5,6},{6,7},{7,0},{8,9},{9,10},{10,1... | collective-permute-start | bytes 18440 | tf_op jit(solution)/shard_map/ppermute | solution.py:21
  114.6 3.5 %collective-permute-start.11 = (f32[16,24,4]{2,1,0:T(8,128)S(1)}, f32[16,24,4]{2,1,0:T(8,128)S(1)}, u32[]{:S(2)}, u32[]{:S(2)}) collective-permute-start(f32[16,24,4]{2,1,0:T(8,128)S(1)} %get-tuple-element.47), channel_id=1, source_target_pairs={{1,0},{2,1},{3,2},{4,3},{5,4},{6,5},{7,6},{0,7},{9,8},{10,9},{11,1... | collective-permute-start | bytes 18440 | tf_op jit(solution)/shard_map/ppermute | solution.py:23
  119.1 2.3 collective-permute-done.11
  126.7 1.7 fusion.4
  129.2 1.9 collective-permute-start.12
  131.1 8.9 %collective-permute-start.13 = (f32[16,4,128]{2,1,0:T(4,128)S(1)}, f32[16,4,128]{2,1,0:T(4,128)S(1)}, u32[]{:S(2)}, u32[]{:S(2)}) collective-permute-start(f32[16,4,128]{2,1,0:T(4,128)S(1)} %get-tuple-element.57), channel_id=1, source_target_pairs={{8,0},{16,8},{24,16},{32,24},{40,32},{48,40},{56,48},{64,56},{72,6... | collective-permute-start | bytes 98312 | tf_op jit(solution)/shard_map/ppermute | solution.py:23
  141.0 4.3 %collective-permute-start.14 = (f32[16,24,4]{2,1,0:T(8,128)S(1)}, f32[16,24,4]{2,1,0:T(8,128)S(1)}, u32[]{:S(2)}, u32[]{:S(2)}) collective-permute-start(f32[16,24,4]{2,1,0:T(8,128)S(1)} %get-tuple-element.44), channel_id=1, source_target_pairs={{0,1},{1,2},{2,3},{3,4},{4,5},{5,6},{6,7},{7,0},{8,9},{9,10},{10,1... | collective-permute-start | bytes 18440 | tf_op jit(solution)/shard_map/ppermute | solution.py:21
  145.2 2.8 collective-permute-start.15
  149.2 2.7 collective-permute-done.15
  156.2 24.8 %all-reduce.1 = (f32[]{:T(128)}, f32[]{:T(128)}) all-reduce(f32[]{:T(128)} %get-tuple-element.7, f32[]{:T(128)} %get-tuple-element.6), channel_id=1, replica_groups=mesh['lat_0'=16,'lat_1'=4,'lat_2'=2,'lon'=8] {'lat_0'}, use_global_device_ids=true, to_apply=%region_8.9 | all-reduce | flops 2 | bytes 16 | tf_op jit(solution)/shard_map/psum | solution.py:47
  181.0 13.5 %all-reduce.5 = (f32[]{:T(128)}, f32[]{:T(128)}) all-reduce(f32[]{:T(128)} %get-tuple-element.10, f32[]{:T(128)} %get-tuple-element.11), channel_id=1, replica_groups=mesh['lat_0'=16,'lat_1'=4,'lat_2'=2,'lon'=8] {'lat_1'}, use_global_device_ids=true, to_apply=%region_9.10 | all-reduce | flops 2 | bytes 16 | tf_op jit(solution)/shard_map/psum | solution.py:47
  194.5 7.9 %all-reduce.7 = (f32[]{:T(128)}, f32[]{:T(128)}) all-reduce(f32[]{:T(128)} %get-tuple-element.18, f32[]{:T(128)} %get-tuple-element.19), channel_id=1, replica_groups=mesh['lat_0'=16,'lat_1'=4,'lat_2'=2,'lon'=8] {'lat_2'}, use_global_device_ids=true, to_apply=%region_10.11 | all-reduce | flops 2 | bytes 16 | tf_op jit(solution)/shard_map/psum | solution.py:47
  202.4 13.8 %all-reduce.3 = (f32[]{:T(128)}, f32[]{:T(128)}) all-reduce(f32[]{:T(128)} %get-tuple-element.22, f32[]{:T(128)} %get-tuple-element.23), channel_id=1, replica_groups=mesh['lat_0'=16,'lat_1'=4,'lat_2'=2,'lon'=8] {'lon'}, use_global_device_ids=true, to_apply=%region_11.12 | all-reduce | flops 2 | bytes 16 | tf_op jit(solution)/shard_map/psum | solution.py:47
  217.6 7.6 %collective-permute-start.16 = (f32[16,4,128]{2,1,0:T(4,128)S(1)}, f32[16,4,128]{2,1,0:T(4,128)S(1)}, u32[]{:S(2)}, u32[]{:S(2)}) collective-permute-start(f32[16,4,128]{2,1,0:T(4,128)S(1)} %get-tuple-element.54), channel_id=1, source_target_pairs={{0,8},{8,16},{16,24},{24,32},{32,40},{40,48},{48,56},{56,64},{64,7... | collective-permute-start | bytes 98312 | tf_op jit(solution)/shard_map/ppermute | solution.py:21
  225.3 1.9 collective-permute-start.17
  227.2 3.3 collective-permute-done.17
  230.7 1.9 collective-permute-start.18
  232.6 4.8 %collective-permute-start.19 = (f32[16,24,4]{2,1,0:T(8,128)S(1)}, f32[16,24,4]{2,1,0:T(8,128)S(1)}, u32[]{:S(2)}, u32[]{:S(2)}) collective-permute-start(f32[16,24,4]{2,1,0:T(8,128)S(1)} %get-tuple-element.43), channel_id=1, source_target_pairs={{1,0},{2,1},{3,2},{4,3},{5,4},{6,5},{7,6},{0,7},{9,8},{10,9},{11,1... | collective-permute-start | bytes 18440 | tf_op jit(solution)/shard_map/ppermute | solution.py:23
  246.7 1.7 fusion
  249.2 3.2 collective-permute-start.20
  252.3 3.5 %collective-permute-start.21 = (f32[16,4,128]{2,1,0:T(4,128)S(1)}, f32[16,4,128]{2,1,0:T(4,128)S(1)}, u32[]{:S(2)}, u32[]{:S(2)}) collective-permute-start(f32[16,4,128]{2,1,0:T(4,128)S(1)} %get-tuple-element.53), channel_id=1, source_target_pairs={{8,0},{16,8},{24,16},{32,24},{40,32},{48,40},{56,48},{64,56},{72,6... | collective-permute-start | bytes 98312 | tf_op jit(solution)/shard_map/ppermute | solution.py:23
  255.9 1.7 collective-permute-done.21
  257.7 1.9 collective-permute-start.22
  259.7 5.3 %collective-permute-start.23 = (f32[16,24,4]{2,1,0:T(8,128)S(1)}, f32[16,24,4]{2,1,0:T(8,128)S(1)}, u32[]{:S(2)}, u32[]{:S(2)}) collective-permute-start(f32[16,24,4]{2,1,0:T(8,128)S(1)} %get-tuple-element.41), channel_id=1, source_target_pairs={{1,0},{2,1},{3,2},{4,3},{5,4},{6,5},{7,6},{0,7},{9,8},{10,9},{11,1... | collective-permute-start | bytes 18440 | tf_op jit(solution)/shard_map/ppermute | solution.py:23
  266.1 1.5 collective-permute-done.23
  271.8 22.4 %all-reduce = (f32[]{:T(128)}, f32[]{:T(128)}) all-reduce(f32[]{:T(128)} %get-tuple-element.5, f32[]{:T(128)} %get-tuple-element.4), channel_id=1, replica_groups=mesh['lat_0'=16,'lat_1'=4,'lat_2'=2,'lon'=8] {'lat_0'}, use_global_device_ids=true, to_apply=%region_19.20 | all-reduce | flops 2 | bytes 16 | tf_op jit(solution)/shard_map/psum | solution.py:47
  294.2 14.8 %all-reduce.4 = (f32[]{:T(128)}, f32[]{:T(128)}) all-reduce(f32[]{:T(128)} %get-tuple-element.8, f32[]{:T(128)} %get-tuple-element.9), channel_id=1, replica_groups=mesh['lat_0'=16,'lat_1'=4,'lat_2'=2,'lon'=8] {'lat_1'}, use_global_device_ids=true, to_apply=%region_20.21 | all-reduce | flops 2 | bytes 16 | tf_op jit(solution)/shard_map/psum | solution.py:47
  309.0 7.5 %all-reduce.6 = (f32[]{:T(128)}, f32[]{:T(128)}) all-reduce(f32[]{:T(128)} %get-tuple-element.16, f32[]{:T(128)} %get-tuple-element.17), channel_id=1, replica_groups=mesh['lat_0'=16,'lat_1'=4,'lat_2'=2,'lon'=8] {'lat_2'}, use_global_device_ids=true, to_apply=%region_21.22 | all-reduce | flops 2 | bytes 16 | tf_op jit(solution)/shard_map/psum | solution.py:47
  316.4 14.8 %all-reduce.2 = (f32[]{:T(128)}, f32[]{:T(128)}) all-reduce(f32[]{:T(128)} %get-tuple-element.20, f32[]{:T(128)} %get-tuple-element.21), channel_id=1, replica_groups=mesh['lat_0'=16,'lat_1'=4,'lat_2'=2,'lon'=8] {'lon'}, use_global_device_ids=true, to_apply=%region_22.23 | all-reduce | flops 2 | bytes 16 | tf_op jit(solution)/shard_map/psum | solution.py:47
  (111 shorter events, 55.1 us)
Async XLA Ops:
  0.6 14.7 %copy-start = (f32[1,8,128]{2,1,0:T(8,128)S(1)}, f32[1,8,128]{2,1,0:T(8,128)}, u32[]{:S(2)}) copy-start(f32[1,8,128]{2,1,0:T(8,128)} %param.10) | copy-start | bytes 12292
  5.5 19.3 %all-to-all-start = ((s32[8,2,1]{1,2,0:T(1,128)}), s32[8,2,1]{1,2,0:T(1,128)S(1)}, u32[]{:S(2)}, u32[]{:S(2)}) async-start(s32[8,2,1]{1,2,0:T(1,128)} %bitcast.10), calls=%async_computation | async-start | bytes 8192 | tf_op jit(solution)/shard_map/all_to_all | solution.py:134
  13.9 4.5 %copy-start.2 = (f32[1,8,128,128]{3,2,1,0:T(8,128)S(1)}, f32[1,8,128,128]{3,2,1,0:T(8,128)}, u32[]{:S(2)}) copy-start(f32[1,8,128,128]{3,2,1,0:T(8,128)} %param.8) | copy-start | bytes 1572868
  24.8 6.8 %copy-start.3 = (f32[2,16,16,128]{3,2,1,0:T(8,128)S(1)}, f32[2,16,16,128]{3,2,1,0:T(8,128)}, u32[]{:S(2)}) copy-start(f32[2,16,16,128]{3,2,1,0:T(8,128)} %param.7) | copy-start | bytes 786436
  24.8 39.3 %all-to-all-start.1 = ((f32[16,128,130]{1,2,0:T(8,128)}), f32[16,128,130]{1,2,0:T(8,128)S(1)}, u32[]{:S(2)}, u32[]{:S(2)}) async-start(f32[16,128,130]{1,2,0:T(8,128)} %copy.44), calls=%async_computation.1 | async-start | bytes 2228224 | tf_op jit(solution)/shard_map/all_to_all | solution.py:34
  31.7 14.2 %collective-permute-start = (f32[4,16,4,128]{3,2,1,0:T(4,128)S(1)}, f32[4,16,4,128]{3,2,1,0:T(4,128)S(1)}, u32[]{:S(2)}, u32[]{:S(2)}) collective-permute-start(f32[4,16,4,128]{3,2,1,0:T(4,128)S(1)} %get-tuple-element.34), channel_id=1, source_target_pairs={{0,8},{8,16},{16,24},{24,32},{32,40},{40,48},{48,56},{56,64},{64,7... | collective-permute-start | bytes 393224 | tf_op jit(solution)/shard_map/ppermute | solution.py:21
  36.2 10.6 %collective-permute-start.1 = (f32[4,16,4,128]{3,2,1,0:T(4,128)S(1)}, f32[4,16,4,128]{3,2,1,0:T(4,128)S(1)}, u32[]{:S(2)}, u32[]{:S(2)}) collective-permute-start(f32[4,16,4,128]{3,2,1,0:T(4,128)S(1)} %get-tuple-element.35), channel_id=1, source_target_pairs={{8,0},{16,8},{24,16},{32,24},{40,32},{48,40},{56,48},{64,56},{72,6... | collective-permute-start | bytes 393224 | tf_op jit(solution)/shard_map/ppermute | solution.py:23
  49.7 9.0 %collective-permute-start.2 = (f32[4,16,24,4]{2,1,3,0:T(8,128)S(1)}, f32[4,16,24,4]{2,1,3,0:T(8,128)}, u32[]{:S(2)}, u32[]{:S(2)}) collective-permute-start(f32[4,16,24,4]{2,1,3,0:T(8,128)S(1)} %copy.37), channel_id=1, source_target_pairs={{0,1},{1,2},{2,3},{3,4},{4,5},{5,6},{6,7},{7,0},{8,9},{9,10},{10,1... | collective-permute-start | bytes 73736 | tf_op jit(solution)/shard_map/ppermute | solution.py:21
  54.5 6.2 %collective-permute-start.3 = (f32[4,16,24,4]{2,1,3,0:T(8,128)}, f32[4,16,24,4]{2,1,3,0:T(8,128)}, u32[]{:S(2)}, u32[]{:S(2)}) collective-permute-start(f32[4,16,24,4]{2,1,3,0:T(8,128)} %copy.38), channel_id=1, source_target_pairs={{1,0},{2,1},{3,2},{4,3},{5,4},{6,5},{7,6},{0,7},{9,8},{10,9},{11,1... | collective-permute-start | bytes 73736 | tf_op jit(solution)/shard_map/ppermute | solution.py:23
  66.7 16.3 %collective-permute-start.4 = (f32[16,4,128]{2,1,0:T(4,128)S(1)}, f32[16,4,128]{2,1,0:T(4,128)S(1)}, u32[]{:S(2)}, u32[]{:S(2)}) collective-permute-start(f32[16,4,128]{2,1,0:T(4,128)S(1)} %get-tuple-element.60), channel_id=1, source_target_pairs={{0,8},{8,16},{16,24},{24,32},{32,40},{40,48},{48,56},{56,64},{64,7... | collective-permute-start | bytes 98312 | tf_op jit(solution)/shard_map/ppermute | solution.py:21
  73.3 16.4 %copy-start.1 = (f32[4,16,24,136]{3,2,1,0:T(8,128)S(1)}, f32[4,16,24,136]{3,2,1,0:T(8,128)}, u32[]{:S(2)}) copy-start(f32[4,16,24,136]{3,2,1,0:T(8,128)} %pad_maximum_fusion.1) | copy-start | bytes 2506756
  73.3 9.7 %collective-permute-start.5 = (f32[16,4,128]{2,1,0:T(4,128)S(1)}, f32[16,4,128]{2,1,0:T(4,128)S(1)}, u32[]{:S(2)}, u32[]{:S(2)}) collective-permute-start(f32[16,4,128]{2,1,0:T(4,128)S(1)} %get-tuple-element.61), channel_id=1, source_target_pairs={{8,0},{16,8},{24,16},{32,24},{40,32},{48,40},{56,48},{64,56},{72,6... | collective-permute-start | bytes 98312 | tf_op jit(solution)/shard_map/ppermute | solution.py:23
  83.2 7.6 %collective-permute-start.6 = (f32[16,24,4]{2,1,0:T(8,128)S(1)}, f32[16,24,4]{2,1,0:T(8,128)S(1)}, u32[]{:S(2)}, u32[]{:S(2)}) collective-permute-start(f32[16,24,4]{2,1,0:T(8,128)S(1)} %get-tuple-element.48), channel_id=1, source_target_pairs={{0,1},{1,2},{2,3},{3,4},{4,5},{5,6},{6,7},{7,0},{8,9},{9,10},{10,1... | collective-permute-start | bytes 18440 | tf_op jit(solution)/shard_map/ppermute | solution.py:21
  86.2 6.8 %collective-permute-start.7 = (f32[16,24,4]{2,1,0:T(8,128)S(1)}, f32[16,24,4]{2,1,0:T(8,128)S(1)}, u32[]{:S(2)}, u32[]{:S(2)}) collective-permute-start(f32[16,24,4]{2,1,0:T(8,128)S(1)} %get-tuple-element.49), channel_id=1, source_target_pairs={{1,0},{2,1},{3,2},{4,3},{5,4},{6,5},{7,6},{0,7},{9,8},{10,9},{11,1... | collective-permute-start | bytes 18440 | tf_op jit(solution)/shard_map/ppermute | solution.py:23
  96.7 13.0 %collective-permute-start.8 = (f32[16,4,128]{2,1,0:T(4,128)S(1)}, f32[16,4,128]{2,1,0:T(4,128)S(1)}, u32[]{:S(2)}, u32[]{:S(2)}) collective-permute-start(f32[16,4,128]{2,1,0:T(4,128)S(1)} %get-tuple-element.58), channel_id=1, source_target_pairs={{0,8},{8,16},{16,24},{24,32},{32,40},{40,48},{48,56},{56,64},{64,7... | collective-permute-start | bytes 98312 | tf_op jit(solution)/shard_map/ppermute | solution.py:21
  98.6 11.9 %collective-permute-start.9 = (f32[16,4,128]{2,1,0:T(4,128)S(1)}, f32[16,4,128]{2,1,0:T(4,128)S(1)}, u32[]{:S(2)}, u32[]{:S(2)}) collective-permute-start(f32[16,4,128]{2,1,0:T(4,128)S(1)} %get-tuple-element.59), channel_id=1, source_target_pairs={{8,0},{16,8},{24,16},{32,24},{40,32},{48,40},{56,48},{64,56},{72,6... | collective-permute-start | bytes 98312 | tf_op jit(solution)/shard_map/ppermute | solution.py:23
  110.7 8.4 %collective-permute-start.10 = (f32[16,24,4]{2,1,0:T(8,128)S(1)}, f32[16,24,4]{2,1,0:T(8,128)S(1)}, u32[]{:S(2)}, u32[]{:S(2)}) collective-permute-start(f32[16,24,4]{2,1,0:T(8,128)S(1)} %get-tuple-element.46), channel_id=1, source_target_pairs={{0,1},{1,2},{2,3},{3,4},{4,5},{5,6},{6,7},{7,0},{8,9},{9,10},{10,1... | collective-permute-start | bytes 18440 | tf_op jit(solution)/shard_map/ppermute | solution.py:21
  114.6 6.7 %collective-permute-start.11 = (f32[16,24,4]{2,1,0:T(8,128)S(1)}, f32[16,24,4]{2,1,0:T(8,128)S(1)}, u32[]{:S(2)}, u32[]{:S(2)}) collective-permute-start(f32[16,24,4]{2,1,0:T(8,128)S(1)} %get-tuple-element.47), channel_id=1, source_target_pairs={{1,0},{2,1},{3,2},{4,3},{5,4},{6,5},{7,6},{0,7},{9,8},{10,9},{11,1... | collective-permute-start | bytes 18440 | tf_op jit(solution)/shard_map/ppermute | solution.py:23
  129.2 10.8 %collective-permute-start.12 = (f32[16,4,128]{2,1,0:T(4,128)S(1)}, f32[16,4,128]{2,1,0:T(4,128)S(1)}, u32[]{:S(2)}, u32[]{:S(2)}) collective-permute-start(f32[16,4,128]{2,1,0:T(4,128)S(1)} %get-tuple-element.56), channel_id=1, source_target_pairs={{0,8},{8,16},{16,24},{24,32},{32,40},{40,48},{48,56},{56,64},{64,7... | collective-permute-start | bytes 98312 | tf_op jit(solution)/shard_map/ppermute | solution.py:21
  131.1 9.7 %collective-permute-start.13 = (f32[16,4,128]{2,1,0:T(4,128)S(1)}, f32[16,4,128]{2,1,0:T(4,128)S(1)}, u32[]{:S(2)}, u32[]{:S(2)}) collective-permute-start(f32[16,4,128]{2,1,0:T(4,128)S(1)} %get-tuple-element.57), channel_id=1, source_target_pairs={{8,0},{16,8},{24,16},{32,24},{40,32},{48,40},{56,48},{64,56},{72,6... | collective-permute-start | bytes 98312 | tf_op jit(solution)/shard_map/ppermute | solution.py:23
  141.0 8.2 %collective-permute-start.14 = (f32[16,24,4]{2,1,0:T(8,128)S(1)}, f32[16,24,4]{2,1,0:T(8,128)S(1)}, u32[]{:S(2)}, u32[]{:S(2)}) collective-permute-start(f32[16,24,4]{2,1,0:T(8,128)S(1)} %get-tuple-element.44), channel_id=1, source_target_pairs={{0,1},{1,2},{2,3},{3,4},{4,5},{5,6},{6,7},{7,0},{8,9},{9,10},{10,1... | collective-permute-start | bytes 18440 | tf_op jit(solution)/shard_map/ppermute | solution.py:21
  145.2 6.7 %collective-permute-start.15 = (f32[16,24,4]{2,1,0:T(8,128)S(1)}, f32[16,24,4]{2,1,0:T(8,128)S(1)}, u32[]{:S(2)}, u32[]{:S(2)}) collective-permute-start(f32[16,24,4]{2,1,0:T(8,128)S(1)} %get-tuple-element.45), channel_id=1, source_target_pairs={{1,0},{2,1},{3,2},{4,3},{5,4},{6,5},{7,6},{0,7},{9,8},{10,9},{11,1... | collective-permute-start | bytes 18440 | tf_op jit(solution)/shard_map/ppermute | solution.py:23
  217.6 9.6 %collective-permute-start.16 = (f32[16,4,128]{2,1,0:T(4,128)S(1)}, f32[16,4,128]{2,1,0:T(4,128)S(1)}, u32[]{:S(2)}, u32[]{:S(2)}) collective-permute-start(f32[16,4,128]{2,1,0:T(4,128)S(1)} %get-tuple-element.54), channel_id=1, source_target_pairs={{0,8},{8,16},{16,24},{24,32},{32,40},{40,48},{48,56},{56,64},{64,7... | collective-permute-start | bytes 98312 | tf_op jit(solution)/shard_map/ppermute | solution.py:21
  225.3 5.2 %collective-permute-start.17 = (f32[16,4,128]{2,1,0:T(4,128)S(1)}, f32[16,4,128]{2,1,0:T(4,128)S(1)}, u32[]{:S(2)}, u32[]{:S(2)}) collective-permute-start(f32[16,4,128]{2,1,0:T(4,128)S(1)} %get-tuple-element.55), channel_id=1, source_target_pairs={{8,0},{16,8},{24,16},{32,24},{40,32},{48,40},{56,48},{64,56},{72,6... | collective-permute-start | bytes 98312 | tf_op jit(solution)/shard_map/ppermute | solution.py:23
  230.7 7.6 %collective-permute-start.18 = (f32[16,24,4]{2,1,0:T(8,128)S(1)}, f32[16,24,4]{2,1,0:T(8,128)S(1)}, u32[]{:S(2)}, u32[]{:S(2)}) collective-permute-start(f32[16,24,4]{2,1,0:T(8,128)S(1)} %get-tuple-element.42), channel_id=1, source_target_pairs={{0,1},{1,2},{2,3},{3,4},{4,5},{5,6},{6,7},{7,0},{8,9},{9,10},{10,1... | collective-permute-start | bytes 18440 | tf_op jit(solution)/shard_map/ppermute | solution.py:21
  232.6 7.2 %collective-permute-start.19 = (f32[16,24,4]{2,1,0:T(8,128)S(1)}, f32[16,24,4]{2,1,0:T(8,128)S(1)}, u32[]{:S(2)}, u32[]{:S(2)}) collective-permute-start(f32[16,24,4]{2,1,0:T(8,128)S(1)} %get-tuple-element.43), channel_id=1, source_target_pairs={{1,0},{2,1},{3,2},{4,3},{5,4},{6,5},{7,6},{0,7},{9,8},{10,9},{11,1... | collective-permute-start | bytes 18440 | tf_op jit(solution)/shard_map/ppermute | solution.py:23
  249.2 6.7 %collective-permute-start.20 = (f32[16,4,128]{2,1,0:T(4,128)S(1)}, f32[16,4,128]{2,1,0:T(4,128)S(1)}, u32[]{:S(2)}, u32[]{:S(2)}) collective-permute-start(f32[16,4,128]{2,1,0:T(4,128)S(1)} %get-tuple-element.52), channel_id=1, source_target_pairs={{0,8},{8,16},{16,24},{24,32},{32,40},{40,48},{48,56},{56,64},{64,7... | collective-permute-start | bytes 98312 | tf_op jit(solution)/shard_map/ppermute | solution.py:21
  252.3 5.2 %collective-permute-start.21 = (f32[16,4,128]{2,1,0:T(4,128)S(1)}, f32[16,4,128]{2,1,0:T(4,128)S(1)}, u32[]{:S(2)}, u32[]{:S(2)}) collective-permute-start(f32[16,4,128]{2,1,0:T(4,128)S(1)} %get-tuple-element.53), channel_id=1, source_target_pairs={{8,0},{16,8},{24,16},{32,24},{40,32},{48,40},{56,48},{64,56},{72,6... | collective-permute-start | bytes 98312 | tf_op jit(solution)/shard_map/ppermute | solution.py:23
  257.7 8.4 %collective-permute-start.22 = (f32[16,24,4]{2,1,0:T(8,128)S(1)}, f32[16,24,4]{2,1,0:T(8,128)S(1)}, u32[]{:S(2)}, u32[]{:S(2)}) collective-permute-start(f32[16,24,4]{2,1,0:T(8,128)S(1)} %get-tuple-element.40), channel_id=1, source_target_pairs={{0,1},{1,2},{2,3},{3,4},{4,5},{5,6},{6,7},{7,0},{8,9},{9,10},{10,1... | collective-permute-start | bytes 18440 | tf_op jit(solution)/shard_map/ppermute | solution.py:21
  259.7 7.9 %collective-permute-start.23 = (f32[16,24,4]{2,1,0:T(8,128)S(1)}, f32[16,24,4]{2,1,0:T(8,128)S(1)}, u32[]{:S(2)}, u32[]{:S(2)}) collective-permute-start(f32[16,24,4]{2,1,0:T(8,128)S(1)} %get-tuple-element.41), channel_id=1, source_target_pairs={{1,0},{2,1},{3,2},{4,3},{5,4},{6,5},{7,6},{0,7},{9,8},{10,9},{11,1... | collective-permute-start | bytes 18440 | tf_op jit(solution)/shard_map/ppermute | solution.py:23
where the time goes:
time: 341 us; the launch traced here: 337 us
  starting transfers between devices  125 us (37%)
  blocking collectives  119 us (35%)
  other arithmetic  31.8 us (9%)
  waiting for transfers between devices  24.4 us (7%)
  local copies, waits for them, and re-layouts  20.7 us (6%)
  between operations  7.93 us (2%)
  matrix products  7.18 us (2%)
    psum x8, blocking collectives, one_axis_at_a_time(): array = lax.psum(array, axis)  119 us
    ppermute x12, starting transfers between devices, padded_2(): lax.ppermute(head, axis, [((i + 1) % count, i) for i in range(count)])  66.2 us
    ppermute x12, starting transfers between devices, padded_2(): lax.ppermute(tail, axis, [(i, (i + 1) % count) for i in range(count)])  44.5 us
    ppermute x12, waiting for transfers between devices, padded_2(): lax.ppermute(head, axis, [((i + 1) % count, i) for i in range(count)])  18.4 us
    mul x10, other arithmetic, model_adjoint(): padded = fresh_field * edge_mask(margin)  9.16 us
    mul x8, other arithmetic, model_tangent(): padded = fresh_field * edge_mask(margin)  7.65 us
    all_to_all x1, starting transfers between devices, shards(): lax.all_to_all(requests, 'lon', split_axis=0, concat_axis=0, tiled=True)  7.64 us
  transfers between devices with their start and end apart: 26, of which 17 were waited for; matrix products, arithmetic and copies ran while one was open for 7% of the time, Pallas kernels for 0%

commit v1 on v0

v1 whole, which is shorter than its diff:
```python
import jax
import jax.numpy as jnp
from jax import lax
from jax.sharding import Mesh
from jax.sharding import PartitionSpec as P

SLOT = 2
STEPS = 4
HALO = 2 * STEPS
LAT = ("lat_0", "lat_1", "lat_2")
HIGHEST = lax.Precision.HIGHEST


def from_sides(cells, axis, dim, width, wrap):
    count = lax.axis_size(axis)
    head = lax.slice_in_dim(cells, 0, width, axis=dim)
    tail = lax.slice_in_dim(cells, cells.shape[dim] - width, cells.shape[dim], axis=dim)
    last = count if wrap else count - 1
    before = lax.ppermute(tail, axis, [(i, (i + 1) % count) for i in range(last)])
    after = lax.ppermute(head, axis, [((i + 1) % count, i) for i in range(last)])
    return jnp.concatenate([before, cells, after], axis=dim)


def exchanged(cells, lat_dim, width):
    cells = from_sides(cells, LAT, lat_dim, width, False)
    return from_sides(cells, "lon", lat_dim + 1, width, True)


def cut(a, width):
    return a[..., width:-width, width:-width] if width else a


def total(values):
    for axes in (("lat_1", "lon"), ("lat_0", "lat_2")):
        count = lax.axis_size(axes)
        spread = jnp.broadcast_to(values[None], (count,) + values.shape)
        values = jnp.sum(lax.all_to_all(spread, axes, split_axis=0, concat_axis=0, tiled=True), axis=0)
    return values


def shards(courant, obs_matrix, obs_weight, innovation, block_owner, block_row, block_count):
    levels, lat_rows, lon_cells = courant.shape[1:]
    capacity = block_row.shape[1]
    lon_count = lax.axis_size("lon")
    lat_index = lax.axis_index(LAT)
    lat_total = lax.axis_size(LAT)

    owner_lon = block_owner[0, :, 0]
    onehot = (owner_lon[:, None] == jnp.arange(lon_count, dtype=jnp.int32)[None, :]).astype(jnp.int32)
    before = jnp.cumsum(onehot, axis=0) - onehot
    target = owner_lon * SLOT + jnp.sum(before * onehot, axis=1)
    live = jnp.arange(capacity, dtype=jnp.int32) < block_count[0, 0]
    weighted = jnp.where(live[:, None], obs_weight[0], 0.0)
    matrix = obs_matrix[0]
    gram = jnp.einsum("bok,bol->bkl", weighted[:, :, None] * matrix, matrix, precision=HIGHEST)
    pulled = jnp.einsum("bok,bo->bk", matrix, weighted * innovation[0], precision=HIGHEST)
    named = jnp.broadcast_to(block_row[0].astype(jnp.float32)[:, None], (capacity, lon_cells))
    parcel = jnp.concatenate([gram, pulled[:, None], named[:, None]], axis=1)
    parcels = jnp.zeros((lon_count * SLOT,) + parcel.shape[1:], jnp.float32).at[target].set(parcel)
    arrived = lax.all_to_all(parcels, "lon", split_axis=0, concat_axis=0, tiled=True)
    gram, pulled, rows = arrived[:, :lon_cells], arrived[:, lon_cells], arrived[:, lon_cells + 1, 0].astype(jnp.int32)

    def spread(terms):
        flat = jnp.zeros((levels * lat_rows, lon_cells), jnp.float32).at[rows].add(terms)
        return flat.reshape(levels, lat_rows, lon_cells)

    def seen(field):
        return field.reshape(levels * lat_rows, lon_cells)[rows]

    def weigh(terms):
        return jnp.einsum("bkl,bl->bk", gram, terms, precision=HIGHEST)

    first = exchanged(jnp.concatenate([courant, spread(pulled)[None]], axis=0), 2, HALO)
    flow, departure = first[:2], first[2]
    rates = (jnp.maximum(flow[0], 0.0), jnp.maximum(-flow[0], 0.0), jnp.maximum(flow[1], 0.0), jnp.maximum(-flow[1], 0.0))
    keep = 1.0 - rates[0] - rates[1] - rates[2] - rates[3]

    def inside(field):
        margin = (field.shape[1] - lat_rows) // 2
        at = jnp.arange(field.shape[1], dtype=jnp.int32) + lat_index * lat_rows - margin
        return jnp.where(((at >= 0) & (at < lat_rows * lat_total))[:, None], field, 0.0)

    def adjoint(field, reach):
        for _ in range(STEPS):
            a, b, e, f = (cut(r, HALO - reach) * field for r in rates)
            field = (
                cut(keep, HALO - reach + 1) * field[:, 1:-1, 1:-1]
                + a[:, 2:, 1:-1] + b[:, :-2, 1:-1] + e[:, 1:-1, 2:] + f[:, 1:-1, :-2]
            )
            reach -= 1
        return field

    def tangent(field, reach):
        for _ in range(STEPS):
            reach -= 1
            a, b, e, f = (cut(r, HALO - reach) for r in rates)
            field = (
                cut(keep, HALO - reach) * field[:, 1:-1, 1:-1]
                + a * field[:, :-2, 1:-1] + b * field[:, 2:, 1:-1] + e * field[:, 1:-1, :-2] + f * field[:, 1:-1, 2:]
            )
        return field

    right_wide = inside(adjoint(departure, HALO))
    right = cut(right_wide, STEPS)
    seen_1 = seen(tangent(right_wide, STEPS))
    terms_1 = weigh(seen_1)
    image_wide = right_wide + inside(adjoint(exchanged(spread(terms_1), 1, HALO), HALO))
    image = cut(image_wide, STEPS)
    seen_2 = seen(tangent(image_wide, STEPS))
    terms_2 = weigh(seen_2)
    sums = total(jnp.stack([jnp.sum(right * right), jnp.sum(seen_1 * terms_1), jnp.sum(image * image), jnp.sum(seen_2 * terms_2)]))
    second = image + adjoint(exchanged(spread(terms_2), 1, STEPS), STEPS)

    bb, b_ab, ab_ab, ab_aab = sums[0], sums[0] + sums[1], sums[2], sums[2] + sums[3]
    step_0 = bb / b_ab
    norm_1 = bb - 2.0 * step_0 * b_ab + step_0 * step_0 * ab_ab
    beta = norm_1 / bb
    curve = b_ab - 2.0 * step_0 * ab_ab + step_0 * step_0 * ab_aab - beta * beta * b_ab
    step_1 = norm_1 / curve
    main = step_0 + step_1 * (1.0 + beta)
    cross = step_0 * step_1
    return main * right - cross * image, right - main * image + cross * second


def solution(mesh):
    torus = Mesh(
        mesh.devices.reshape(16, 4, 2, mesh.shape["lon"]), ("lat_0", "lat_1", "lat_2", "lon")
    )
    placed = (
        P(None, None, LAT, "lon"),
        P(LAT, "lon", None, None),
        P(LAT, "lon", None),
        P(LAT, "lon", None),
        P(LAT, "lon", None),
        P(LAT, "lon"),
        P(LAT, "lon"),
    )
    return jax.shard_map(
        shards,
        mesh=torus,
        in_specs=placed,
        out_specs=(P(None, LAT, "lon"), P(None, LAT, "lon")),
        check_vma=False,
    )
```

time: 341 us -> 211 us (0.62); the launches traced: 337 us -> 210 us
  blocking collectives: 119 us -> 46.2 us
  starting transfers between devices: 125 us -> 71.1 us
  other arithmetic: 31.8 us -> 37.5 us
  local copies, waits for them, and re-layouts: 20.7 us -> 15.5 us
    psum x8 -> x0, blocking collectives: 119 us -> none  [one_axis_at_a_time(): array = lax.psum(array, axis)]
    ppermute x24 -> x12, starting transfers between devices: 111 us -> 48 us  [the longest x6 28.2 us: from_sides(): lax.ppermute(tail, axis, [(i, (i + 1) % count) for i in range(last)])]
    all_to_all x0 -> x2, blocking collectives: none -> 46.2 us  [the longest x1 28 us: shards(): lax.all_to_all(parcels, 'lon', split_axis=0, concat_axis=0, tiled=True)]
    mul x26 -> x1, other arithmetic: 18.3 us -> 0.78 us  [shards(): weighted * innovation[0]]
    add x0 -> x15, other arithmetic: none -> 15.8 us  [the longest x8 8.66 us: adjoint(): cut(keep, HALO - reach + 1) * field[:, 1:-1, 1:-1] + a[:, 2:, 1:-1]]
    ppermute x24 -> x12, waiting for transfers between devices: 24.4 us -> 13.6 us  [the longest x6 10.5 us: from_sides(): lax.ppermute(head, axis, [((i + 1) % count, i) for i in range(last)])]
    all_to_all x2 -> x1, waiting for transfers between devices: 0.01 us -> 9.58 us  [total(): lax.all_to_all(spread, axes, split_axis=0, concat_axis=0, tiled=True)]
    all_to_all x2 -> x1, starting transfers between devices: 14.4 us -> 23.1 us  [total(): lax.all_to_all(spread, axes, split_axis=0, concat_axis=0, tiled=True)]
  transfers between devices with their start and end apart: 26 -> 13, of which waited for: 17 -> 8; matrix products, arithmetic and copies ran while one was open for 7% -> 5% of each run, Pallas kernels for 0% -> 0%
where the time goes in v1:
time: 211 us; the launch traced here: 210 us
  starting transfers between devices  71.1 us (34%)
  blocking collectives  46.2 us (22%)
  other arithmetic  37.5 us (18%)
  waiting for transfers between devices  23.2 us (11%)
  local copies, waits for them, and re-layouts  15.5 us (7%)
  matrix products  8.99 us (4%)
  between operations  7.97 us (4%)
    ppermute x6, starting transfers between devices, from_sides(): lax.ppermute(tail, axis, [(i, (i + 1) % count) for i in range(last)])  28.2 us
    all_to_all x1, blocking collectives, shards(): lax.all_to_all(parcels, 'lon', split_axis=0, concat_axis=0, tiled=True)  28 us
    all_to_all x1, starting transfers between devices, total(): lax.all_to_all(spread, axes, split_axis=0, concat_axis=0, tiled=True)  23.1 us
    ppermute x6, starting transfers between devices, from_sides(): lax.ppermute(head, axis, [((i + 1) % count, i) for i in range(last)])  19.8 us
    all_to_all x1, blocking collectives, total(): lax.all_to_all(spread, axes, split_axis=0, concat_axis=0, tiled=True)  18.2 us
    ppermute x6, waiting for transfers between devices, from_sides(): lax.ppermute(head, axis, [((i + 1) % count, i) for i in range(last)])  10.5 us
    all_to_all x1, waiting for transfers between devices, total(): lax.all_to_all(spread, axes, split_axis=0, concat_axis=0, tiled=True)  9.58 us
    add x8, other arithmetic, adjoint(): cut(keep, HALO - reach + 1) * field[:, 1:-1, 1:-1] + a[:, 2:, 1:-1]  8.66 us
  transfers between devices with their start and end apart: 13, of which 8 were waited for; matrix products, arithmetic and copies ran while one was open for 5% of the time, Pallas kernels for 0%

profile of v1, /device:TPU:1, one launch (start us, length us, event | category | flops | bytes accessed | tf_op | source)
XLA Modules:
  0.0 210.4 jit_solution(15373281891869555436)
XLA Ops:
  2.2 2.4 %fusion.4 = f32[8,128,128]{2,1,0:T(8,128)S(1)} fusion(f32[1,8,128,128]{3,2,1,0:T(8,128)} %param.8, f32[8,128]{1,0:T(8,128)S(1)} %get-tuple-element.5), kind=kOutput, calls=%fused_computation.12 | convolution fusion | flops 201457664 | bytes 1052672 | tf_op jit(solution)/shard_map/bok,bol->bkl/dot_general | solution.py:55
  5.6 0.8 scatter_fusion
  6.4 28.0 %all_to_all.17 = f32[16,130,128]{2,1,0:T(8,128)S(1)} all-to-all(f32[16,130,128]{2,1,0:T(8,128)S(1)} %scatter_fusion), channel_id=1, replica_groups=mesh['lat_0'=16,'lat_1'=4,'lat_2'=2,'lon'=8] {'lon'}, dimensions={0} | all-to-all | bytes 2129920 | tf_op jit(solution)/shard_map/all_to_all | solution.py:60
  36.2 13.7 %collective-permute-start = (f32[3,16,8,128]{3,2,1,0:T(8,128)S(1)}, f32[3,16,8,128]{3,2,1,0:T(8,128)S(1)}, u32[]{:S(2)}, u32[]{:S(2)}) collective-permute-start(f32[3,16,8,128]{3,2,1,0:T(8,128)S(1)} %get-tuple-element.35), channel_id=1, source_target_pairs={{0,8},{8,16},{16,24},{24,32},{32,40},{40,48},{48,56},{56,64},{64,7... | collective-permute-start | bytes 589832 | tf_op jit(solution)/shard_map/ppermute | solution.py:19
  49.9 1.9 collective-permute-start.1
  52.5 4.4 %collective-permute-done.1 = f32[3,16,8,128]{3,2,1,0:T(8,128)S(1)} collective-permute-done((f32[3,16,8,128]{3,2,1,0:T(8,128)S(1)}, f32[3,16,8,128]{3,2,1,0:T(8,128)S(1)}, u32[]{:S(2)}, u32[]{:S(2)}) %collective-permute-start.1) | collective-permute-done | bytes 196640 | tf_op jit(solution)/shard_map/ppermute | solution.py:20
  57.5 2.2 %collective-permute-start.2 = (f32[3,16,32,8]{2,3,1,0:T(8,128)S(1)}, f32[3,16,32,8]{2,3,1,0:T(8,128)S(1)}, u32[]{:S(2)}, u32[]{:S(2)}) collective-permute-start(f32[3,16,32,8]{2,3,1,0:T(8,128)S(1)} %copy.63), channel_id=1, source_target_pairs={{0,1},{1,2},{2,3},{3,4},{4,5},{5,6},{6,7},{7,0},{8,9},{9,10},{10,1... | collective-permute-start | bytes 147464 | tf_op jit(solution)/shard_map/ppermute | solution.py:19
  59.9 4.5 %collective-permute-start.3 = (f32[3,16,32,8]{2,3,1,0:T(8,128)S(1)}, f32[3,16,32,8]{2,3,1,0:T(8,128)S(1)}, u32[]{:S(2)}, u32[]{:S(2)}) collective-permute-start(f32[3,16,32,8]{2,3,1,0:T(8,128)S(1)} %copy.64), channel_id=1, source_target_pairs={{1,0},{2,1},{3,2},{4,3},{5,4},{6,5},{7,6},{0,7},{9,8},{10,9},{11,1... | collective-permute-start | bytes 147464 | tf_op jit(solution)/shard_map/ppermute | solution.py:20
  65.4 1.4 collective-permute-done.3
  70.0 1.7 fusion.111
  71.8 1.2 fusion.22
  73.1 1.2 fusion.18
  74.3 0.9 fusion.76
  75.3 1.0 fusion.71
  76.3 2.3 %fusion.109 = (f32[16,20,132]{2,1,0:T(8,128)}, f32[16,20,132]{2,1,0:T(8,128)S(1)}, f32[16,20,132]{2,1,0:T(8,128)}, f32[16,20,132]{2,1,0:T(8,128)}, f32[16,20,132]{2,1,0:T(8,128)}) fusion(f32[16,32,144]{2,1,0:T(8,128)S(1)} %get-tuple-element.6, f32[16,22,134]{2,1,0:T(8,128)S(1)} %fusion.71, f32[16,32,144]{2,1,0:T(8,128)S(1)} %get-tuple-element.8, ...), kind=kLoop, calls=%fused_computation.249 | loop fusion | flops 380160 | bytes 2534400 | tf_op jit(solution)/shard_map/slice | solution.py:30
  78.6 2.2 %fusion.108 = (f32[16,18,130]{2,1,0:T(8,128)}, f32[16,18,130]{2,1,0:T(8,128)S(1)}, f32[16,18,130]{2,1,0:T(8,128)}, f32[16,18,130]{2,1,0:T(8,128)}, f32[16,18,130]{2,1,0:T(8,128)}) fusion(f32[16,32,144]{2,1,0:T(8,128)S(1)} %get-tuple-element.6, f32[16,20,132]{2,1,0:T(8,128)S(1)} %get-tuple-element.21, f32[16,32,144]{2,1,0:T(8,128)S(1)} %get-tuple-element.8, ...), kind=kLoop, calls=%fused_computation.248 | loop fusion | flops 336960 | bytes 2246400 | tf_op jit(solution)/shard_map/slice | solution.py:30
  81.7 3.2 %fusion.2 = f32[16,1,128]{2,1,0:T(1,128)S(1)} fusion(f32[16,128,1]{1,2,0:T(1,128)S(1)} %bitcast.90, f32[16,130,128]{2,1,0:T(8,128)} %copy-done), kind=kOutput, calls=%fused_computation.9 | convolution fusion | flops 3145728 | bytes 1064960 | tf_op jit(solution)/shard_map/bkl,bl->bk/dot_general | solution.py:71
  85.6 4.5 %collective-permute-start.4 = (f32[16,8,128]{2,1,0:T(8,128)S(1)}, f32[16,8,128]{2,1,0:T(8,128)S(1)}, u32[]{:S(2)}, u32[]{:S(2)}) collective-permute-start(f32[16,8,128]{2,1,0:T(8,128)S(1)} %get-tuple-element.43), channel_id=1, source_target_pairs={{0,8},{8,16},{16,24},{24,32},{32,40},{40,48},{48,56},{56,64},{64,7... | collective-permute-start | bytes 196616 | tf_op jit(solution)/shard_map/ppermute | solution.py:19
  90.1 1.9 collective-permute-start.5
  92.7 2.9 %collective-permute-done.5 = f32[16,8,128]{2,1,0:T(8,128)S(1)} collective-permute-done((f32[16,8,128]{2,1,0:T(8,128)S(1)}, f32[16,8,128]{2,1,0:T(8,128)S(1)}, u32[]{:S(2)}, u32[]{:S(2)}) %collective-permute-start.5) | collective-permute-done | bytes 65568 | tf_op jit(solution)/shard_map/ppermute | solution.py:20
  95.8 1.9 collective-permute-start.6
  97.8 5.3 %collective-permute-start.7 = (f32[16,32,8]{2,1,0:T(8,128)S(1)}, f32[16,32,8]{2,1,0:T(8,128)S(1)}, u32[]{:S(2)}, u32[]{:S(2)}) collective-permute-start(f32[16,32,8]{2,1,0:T(8,128)S(1)} %get-tuple-element.38), channel_id=1, source_target_pairs={{1,0},{2,1},{3,2},{4,3},{5,4},{6,5},{7,6},{0,7},{9,8},{10,9},{11,1... | collective-permute-start | bytes 49160 | tf_op jit(solution)/shard_map/ppermute | solution.py:20
  103.7 1.8 collective-permute-done.6
  105.5 1.8 collective-permute-done.7
  107.5 1.2 fusion.14
  109.0 1.2 fusion.10
  110.5 1.2 fusion.6
  112.0 0.9 fusion.59
  113.0 2.2 %fusion.110 = (f32[16,22,134]{2,1,0:T(8,128)}, f32[16,22,134]{2,1,0:T(8,128)S(1)}, f32[16,22,134]{2,1,0:T(8,128)}, f32[16,22,134]{2,1,0:T(8,128)}, f32[16,22,134]{2,1,0:T(8,128)}) fusion(f32[16,32,144]{2,1,0:T(8,128)S(1)} %get-tuple-element.6, f32[16,24,136]{2,1,0:T(8,128)S(1)} %fusion.59, f32[16,32,144]{2,1,0:T(8,128)S(1)} %get-tuple-element.8, ...), kind=kLoop, calls=%fused_computation.250 | loop fusion | flops 424512 | bytes 2830080 | tf_op jit(solution)/shard_map/slice | solution.py:30
  115.8 1.0 fusion.49
  116.9 1.0 fusion.45
  118.9 3.0 %fusion = f32[16,1,128]{2,1,0:T(1,128)S(1)} fusion(f32[16,128,1]{1,2,0:T(1,128)S(1)} %bitcast.91, f32[16,130,128]{2,1,0:T(8,128)} %copy-done), kind=kOutput, calls=%fused_computation.7 | convolution fusion | flops 3145728 | bytes 1064960 | tf_op jit(solution)/shard_map/bkl,bl->bk/dot_general | solution.py:71
  123.9 3.7 %collective-permute-start.8 = (f32[16,4,128]{2,0,1:T(8,128)}, f32[16,4,128]{2,0,1:T(8,128)}, u32[]{:S(2)}, u32[]{:S(2)}) collective-permute-start(f32[16,4,128]{2,0,1:T(8,128)} %copy.69), channel_id=1, source_target_pairs={{0,8},{8,16},{16,24},{24,32},{32,40},{40,48},{48,56},{56,64},{64,7... | collective-permute-start | bytes 98312 | tf_op jit(solution)/shard_map/ppermute | solution.py:19
  128.2 1.9 collective-permute-start.9
  130.1 2.4 %pad_maximum_fusion.8 = f32[4]{0:T(128)S(1)} fusion(f32[1]{0:T(128)} %bitcast.35, f32[1]{0:T(128)} %bitcast.29, f32[1]{0:T(128)} %bitcast.27, f32[1]{0:T(128)} %bitcast.21), kind=kLoop, calls=%fused_computation.243 | loop fusion | flops 12 | bytes 32 | tf_op jit(solution)/shard_map/stack | solution.py:111
  132.6 18.2 %all_to_all.18 = f32[32,1,4]{2,1,0:T(1,128)S(1)} all-to-all(f32[32,1,4]{2,1,0:T(1,128)S(1)} %broadcast_in_dim.64), channel_id=1, replica_groups=mesh['lat_0'=16,'lat_1'=4,'lat_2'=2,'lon'=8] {'lat_1','lon'}, dimensions={0} | all-to-all | bytes 1024 | tf_op jit(solution)/shard_map/all_to_all | solution.py:37
  151.4 1.2 broadcast_in_dim.65
  152.6 23.1 %all-to-all-start.2 = ((f32[32,1,4]{2,1,0:T(1,128)}), f32[32,1,4]{2,1,0:T(1,128)S(1)}, u32[]{:S(2)}, u32[]{:S(2)}) async-start(f32[32,1,4]{2,1,0:T(1,128)} %broadcast_in_dim.65), calls=%async_computation.2 | async-start | bytes 32768 | tf_op jit(solution)/shard_map/all_to_all | solution.py:37
  175.7 0.9 slice.888
  177.0 0.9 slice.897
  177.9 9.6 %all-to-all-done.2 = f32[32,1,4]{2,1,0:T(1,128)S(1)} async-done(((f32[32,1,4]{2,1,0:T(1,128)}), f32[32,1,4]{2,1,0:T(1,128)S(1)}, u32[]{:S(2)}, u32[]{:S(2)}) %all-to-all-start.2) | async-done | bytes 544 | tf_op jit(solution)/shard_map/all_to_all | solution.py:37
  190.0 2.2 %collective-permute-start.10 = (f32[16,24,4]{2,1,0:T(8,128)}, f32[16,24,4]{2,1,0:T(8,128)}, u32[]{:S(2)}, u32[]{:S(2)}) collective-permute-start(f32[16,24,4]{2,1,0:T(8,128)} %get-tuple-element.39), channel_id=1, source_target_pairs={{0,1},{1,2},{2,3},{3,4},{4,5},{5,6},{6,7},{7,0},{8,9},{9,10},{10,1... | collective-permute-start | bytes 18440 | tf_op jit(solution)/shard_map/ppermute | solution.py:19
  192.3 4.2 %collective-permute-start.11 = (f32[16,24,4]{2,1,0:T(8,128)}, f32[16,24,4]{2,1,0:T(8,128)}, u32[]{:S(2)}, u32[]{:S(2)}) collective-permute-start(f32[16,24,4]{2,1,0:T(8,128)} %get-tuple-element.40), channel_id=1, source_target_pairs={{1,0},{2,1},{3,2},{4,3},{5,4},{6,5},{7,6},{0,7},{9,8},{10,9},{11,1... | collective-permute-start | bytes 18440 | tf_op jit(solution)/shard_map/ppermute | solution.py:20
  203.0 1.3 pad_maximum_fusion.4
  204.3 0.9 fusion.41
  205.7 0.9 fusion.37
  207.0 0.9 fusion.33
  207.9 2.4 %fusion.85 = (f32[16,16,128]{2,1,0:T(8,128)}, f32[16,16,128]{2,1,0:T(8,128)}) fusion(f32[16,18,130]{2,1,0:T(8,128)S(1)} %fusion.33, f32[16,18,130]{2,1,0:T(8,128)} %get-tuple-element.19, f32[16,18,130]{2,1,0:T(8,128)} %get-tuple-element.18, f32[16,18,130]{2,1,0:T(8,128)} %get-tuple-element.17, f32[16,18,130]{2,1,0:T(8,128)} %get-tuple-element.15, ...), kind=kLoop, calls=%fused_computation.193 | loop fusion | flops 557056 | bytes 1835016 | tf_op jit(solution)/shard_map/add | solution.py:122
  (149 shorter events, 22.8 us)
Async XLA Ops:
  0.6 3.9 %copy-start.1 = (f32[1,8,128,128]{3,2,1,0:T(8,128)S(1)}, f32[1,8,128,128]{3,2,1,0:T(8,128)}, u32[]{:S(2)}) copy-start(f32[1,8,128,128]{3,2,1,0:T(8,128)} %param.8) | copy-start | bytes 1572868
  0.6 4.4 %copy-start.39 = (s32[1,8]{1,0:T(1,128)S(1)}, s32[1,8]{1,0:T(1,128)}, u32[]{:S(2)}) copy-start(s32[1,8]{1,0:T(1,128)} %param.12) | copy-start | bytes 100
  0.7 4.4 %copy-start.37 = (s32[1,8,1]{1,2,0:T(1,128)S(1)}, s32[1,8,1]{1,2,0:T(1,128)}, u32[]{:S(2)}) copy-start(s32[1,8,1]{1,2,0:T(1,128)} %param.11) | copy-start | bytes 100
  6.4 29.7 %copy-start.26 = (f32[2,16,16,128]{3,2,1,0:T(8,128)S(1)}, f32[2,16,16,128]{3,2,1,0:T(8,128)}, u32[]{:S(2)}) copy-start(f32[2,16,16,128]{3,2,1,0:T(8,128)} %param.7) | copy-start | bytes 786436
  35.4 49.5 %copy-start.38 = (s32[16]{0:T(128)}, s32[16]{0:T(128)S(1)}, u32[]{:S(2)}) copy-start(s32[16]{0:T(128)S(1)} %fusion.106) | copy-start | bytes 196
  36.2 16.3 %collective-permute-start = (f32[3,16,8,128]{3,2,1,0:T(8,128)S(1)}, f32[3,16,8,128]{3,2,1,0:T(8,128)S(1)}, u32[]{:S(2)}, u32[]{:S(2)}) collective-permute-start(f32[3,16,8,128]{3,2,1,0:T(8,128)S(1)} %get-tuple-element.35), channel_id=1, source_target_pairs={{0,8},{8,16},{16,24},{24,32},{32,40},{40,48},{48,56},{56,64},{64,7... | collective-permute-start | bytes 589832 | tf_op jit(solution)/shard_map/ppermute | solution.py:19
  49.9 7.0 %collective-permute-start.1 = (f32[3,16,8,128]{3,2,1,0:T(8,128)S(1)}, f32[3,16,8,128]{3,2,1,0:T(8,128)S(1)}, u32[]{:S(2)}, u32[]{:S(2)}) collective-permute-start(f32[3,16,8,128]{3,2,1,0:T(8,128)S(1)} %get-tuple-element.36), channel_id=1, source_target_pairs={{8,0},{16,8},{24,16},{32,24},{40,32},{48,40},{56,48},{64,56},{72,6... | collective-permute-start | bytes 589832 | tf_op jit(solution)/shard_map/ppermute | solution.py:20
  57.5 7.6 %collective-permute-start.2 = (f32[3,16,32,8]{2,3,1,0:T(8,128)S(1)}, f32[3,16,32,8]{2,3,1,0:T(8,128)S(1)}, u32[]{:S(2)}, u32[]{:S(2)}) collective-permute-start(f32[3,16,32,8]{2,3,1,0:T(8,128)S(1)} %copy.63), channel_id=1, source_target_pairs={{0,1},{1,2},{2,3},{3,4},{4,5},{5,6},{6,7},{7,0},{8,9},{9,10},{10,1... | collective-permute-start | bytes 147464 | tf_op jit(solution)/shard_map/ppermute | solution.py:19
  59.9 6.9 %collective-permute-start.3 = (f32[3,16,32,8]{2,3,1,0:T(8,128)S(1)}, f32[3,16,32,8]{2,3,1,0:T(8,128)S(1)}, u32[]{:S(2)}, u32[]{:S(2)}) collective-permute-start(f32[3,16,32,8]{2,3,1,0:T(8,128)S(1)} %copy.64), channel_id=1, source_target_pairs={{1,0},{2,1},{3,2},{4,3},{5,4},{6,5},{7,6},{0,7},{9,8},{10,9},{11,1... | collective-permute-start | bytes 147464 | tf_op jit(solution)/shard_map/ppermute | solution.py:20
  68.5 4.5 %copy-start.10 = (f32[16,28,140]{2,1,0:T(8,128)}, f32[16,28,140]{2,1,0:T(8,128)S(1)}, u32[]{:S(2)}) copy-start(f32[16,28,140]{2,1,0:T(8,128)S(1)} %slice.755) | copy-start | bytes 752644
  68.7 5.6 %copy-start.18 = (f32[16,26,138]{2,1,0:T(8,128)}, f32[16,26,138]{2,1,0:T(8,128)S(1)}, u32[]{:S(2)}) copy-start(f32[16,26,138]{2,1,0:T(8,128)S(1)} %slice.768) | copy-start | bytes 688900
  68.9 4.1 %copy-start.12 = (f32[16,28,140]{2,1,0:T(8,128)}, f32[16,28,140]{2,1,0:T(8,128)S(1)}, u32[]{:S(2)}) copy-start(f32[16,28,140]{2,1,0:T(8,128)S(1)} %slice.758) | copy-start | bytes 752644
  69.2 5.2 %copy-start.20 = (f32[16,26,138]{2,1,0:T(8,128)}, f32[16,26,138]{2,1,0:T(8,128)S(1)}, u32[]{:S(2)}) copy-start(f32[16,26,138]{2,1,0:T(8,128)S(1)} %slice.771) | copy-start | bytes 688900
  69.4 3.6 %copy-start.14 = (f32[16,28,140]{2,1,0:T(8,128)}, f32[16,28,140]{2,1,0:T(8,128)S(1)}, u32[]{:S(2)}) copy-start(f32[16,28,140]{2,1,0:T(8,128)S(1)} %slice.761) | copy-start | bytes 752644
  69.6 4.7 %copy-start.22 = (f32[16,26,138]{2,1,0:T(8,128)}, f32[16,26,138]{2,1,0:T(8,128)S(1)}, u32[]{:S(2)}) copy-start(f32[16,26,138]{2,1,0:T(8,128)S(1)} %slice.774) | copy-start | bytes 688900
  69.8 3.2 %copy-start.16 = (f32[16,28,140]{2,1,0:T(8,128)}, f32[16,28,140]{2,1,0:T(8,128)S(1)}, u32[]{:S(2)}) copy-start(f32[16,28,140]{2,1,0:T(8,128)S(1)} %slice.764) | copy-start | bytes 752644
  70.0 4.3 %copy-start.24 = (f32[16,26,138]{2,1,0:T(8,128)}, f32[16,26,138]{2,1,0:T(8,128)S(1)}, u32[]{:S(2)}) copy-start(f32[16,26,138]{2,1,0:T(8,128)S(1)} %slice.777) | copy-start | bytes 688900
  71.8 1.3 copy-start.2
  71.8 1.3 copy-start.4
  71.8 1.3 copy-start.6
  71.8 1.3 copy-start.8
  85.6 7.1 %collective-permute-start.4 = (f32[16,8,128]{2,1,0:T(8,128)S(1)}, f32[16,8,128]{2,1,0:T(8,128)S(1)}, u32[]{:S(2)}, u32[]{:S(2)}) collective-permute-start(f32[16,8,128]{2,1,0:T(8,128)S(1)} %get-tuple-element.43), channel_id=1, source_target_pairs={{0,8},{8,16},{16,24},{24,32},{32,40},{40,48},{48,56},{56,64},{64,7... | collective-permute-start | bytes 196616 | tf_op jit(solution)/shard_map/ppermute | solution.py:19
  90.1 5.6 %collective-permute-start.5 = (f32[16,8,128]{2,1,0:T(8,128)S(1)}, f32[16,8,128]{2,1,0:T(8,128)S(1)}, u32[]{:S(2)}, u32[]{:S(2)}) collective-permute-start(f32[16,8,128]{2,1,0:T(8,128)S(1)} %get-tuple-element.44), channel_id=1, source_target_pairs={{8,0},{16,8},{24,16},{32,24},{40,32},{48,40},{56,48},{64,56},{72,6... | collective-permute-start | bytes 196616 | tf_op jit(solution)/shard_map/ppermute | solution.py:20
  95.8 9.6 %collective-permute-start.6 = (f32[16,32,8]{2,1,0:T(8,128)S(1)}, f32[16,32,8]{2,1,0:T(8,128)S(1)}, u32[]{:S(2)}, u32[]{:S(2)}) collective-permute-start(f32[16,32,8]{2,1,0:T(8,128)S(1)} %get-tuple-element.37), channel_id=1, source_target_pairs={{0,1},{1,2},{2,3},{3,4},{4,5},{5,6},{6,7},{7,0},{8,9},{9,10},{10,1... | collective-permute-start | bytes 49160 | tf_op jit(solution)/shard_map/ppermute | solution.py:19
  97.8 9.5 %collective-permute-start.7 = (f32[16,32,8]{2,1,0:T(8,128)S(1)}, f32[16,32,8]{2,1,0:T(8,128)S(1)}, u32[]{:S(2)}, u32[]{:S(2)}) collective-permute-start(f32[16,32,8]{2,1,0:T(8,128)S(1)} %get-tuple-element.38), channel_id=1, source_target_pairs={{1,0},{2,1},{3,2},{4,3},{5,4},{6,5},{7,6},{0,7},{9,8},{10,9},{11,1... | collective-permute-start | bytes 49160 | tf_op jit(solution)/shard_map/ppermute | solution.py:20
  107.5 1.2 copy-start.3
  107.5 1.2 copy-start.5
  107.5 1.3 copy-start.7
  107.5 1.5 copy-start.9
  109.0 1.2 copy-start.11
  109.0 1.2 copy-start.13
  109.0 1.4 copy-start.15
  109.0 1.5 copy-start.17
  110.5 1.2 copy-start.19
  110.5 1.2 copy-start.21
  110.5 1.4 copy-start.23
  110.5 1.5 copy-start.25
  123.9 63.7 %collective-permute-start.8 = (f32[16,4,128]{2,0,1:T(8,128)}, f32[16,4,128]{2,0,1:T(8,128)}, u32[]{:S(2)}, u32[]{:S(2)}) collective-permute-start(f32[16,4,128]{2,0,1:T(8,128)} %copy.69), channel_id=1, source_target_pairs={{0,8},{8,16},{16,24},{24,32},{32,40},{40,48},{48,56},{56,64},{64,7... | collective-permute-start | bytes 98312 | tf_op jit(solution)/shard_map/ppermute | solution.py:19
  128.2 60.1 %collective-permute-start.9 = (f32[16,4,128]{2,0,1:T(8,128)}, f32[16,4,128]{2,0,1:T(8,128)}, u32[]{:S(2)}, u32[]{:S(2)}) collective-permute-start(f32[16,4,128]{2,0,1:T(8,128)} %copy.70), channel_id=1, source_target_pairs={{8,0},{16,8},{24,16},{32,24},{40,32},{48,40},{56,48},{64,56},{72,6... | collective-permute-start | bytes 98312 | tf_op jit(solution)/shard_map/ppermute | solution.py:20
  152.6 34.9 %all-to-all-start.2 = ((f32[32,1,4]{2,1,0:T(1,128)}), f32[32,1,4]{2,1,0:T(1,128)S(1)}, u32[]{:S(2)}, u32[]{:S(2)}) async-start(f32[32,1,4]{2,1,0:T(1,128)} %broadcast_in_dim.65), calls=%async_computation.2 | async-start | bytes 32768 | tf_op jit(solution)/shard_map/all_to_all | solution.py:37
  177.0 27.3 %copy-start.35 = (f32[16,24,136]{2,1,0:T(8,128)S(1)}, f32[16,24,136]{2,1,0:T(8,128)}, u32[]{:S(2)}) copy-start(f32[16,24,136]{2,1,0:T(8,128)} %slice.888) | copy-start | bytes 626692
  177.9 26.4 %copy-start.36 = (f32[16,24,136]{2,1,0:T(8,128)S(1)}, f32[16,24,136]{2,1,0:T(8,128)}, u32[]{:S(2)}) copy-start(f32[16,24,136]{2,1,0:T(8,128)} %slice.897) | copy-start | bytes 626692
  190.0 12.9 %collective-permute-start.10 = (f32[16,24,4]{2,1,0:T(8,128)}, f32[16,24,4]{2,1,0:T(8,128)}, u32[]{:S(2)}, u32[]{:S(2)}) collective-permute-start(f32[16,24,4]{2,1,0:T(8,128)} %get-tuple-element.39), channel_id=1, source_target_pairs={{0,1},{1,2},{2,3},{3,4},{4,5},{5,6},{6,7},{7,0},{8,9},{9,10},{10,1... | collective-permute-start | bytes 18440 | tf_op jit(solution)/shard_map/ppermute | solution.py:19
  192.3 10.7 %collective-permute-start.11 = (f32[16,24,4]{2,1,0:T(8,128)}, f32[16,24,4]{2,1,0:T(8,128)}, u32[]{:S(2)}, u32[]{:S(2)}) collective-permute-start(f32[16,24,4]{2,1,0:T(8,128)} %get-tuple-element.40), channel_id=1, source_target_pairs={{1,0},{2,1},{3,2},{4,3},{5,4},{6,5},{7,6},{0,7},{9,8},{10,9},{11,1... | collective-permute-start | bytes 18440 | tf_op jit(solution)/shard_map/ppermute | solution.py:20
  204.3 1.2 copy-start.33
  204.3 1.3 copy-start.34
  205.7 1.2 copy-start.29
  205.7 1.3 copy-start.30
  (5 other events, 5.2 us)

commit v2 on v1

v2 whole, which is shorter than its diff:
```python
import functools

import jax
import jax.numpy as jnp
from jax import lax
from jax.experimental import pallas as pl
from jax.experimental.pallas import tpu as pltpu
from jax.sharding import Mesh
from jax.sharding import PartitionSpec as P

LAT = ("lat_0", "lat_1", "lat_2")
LEVELS = 16
ROWS = 16
LANES = 128
CAP = 8
SLOT = 2
STEPS = 4
HALO = 2 * STEPS
WIDE = ROWS + 2 * HALO
LON = 8
HALF = LANES // 2
OWN = LON * SLOT
NEAR = 3 * OWN
BULK = 2 * HALF + 8
LIST = 24
SMALL = LIST + 64
NOWHERE = -4096.0
HIGHEST = lax.Precision.HIGHEST
F32 = jnp.float32
VMEM = pl.BlockSpec(memory_space=pltpu.VMEM)
SMEM = pl.BlockSpec(memory_space=pltpu.SMEM)


def lanes(rows):
    return lax.broadcasted_iota(jnp.int32, (rows, LANES), 1)


def places(rows):
    return lax.broadcasted_iota(jnp.int32, (rows, LANES), 0)


def roll(x, shift):
    shift %= LANES
    return pltpu.roll(x, shift, axis=1) if shift else x


def call(body, outs, args, flops, scratch=()):
    outs = [jax.ShapeDtypeStruct(s, F32) for s in outs]
    return pl.pallas_call(
        body,
        out_shape=outs,
        in_specs=[SMEM if a.dtype == jnp.int32 else VMEM for a in args],
        out_specs=[VMEM] * len(outs),
        scratch_shapes=list(scratch),
        compiler_params=pltpu.CompilerParams(vmem_limit_bytes=24 << 20),
        cost_estimate=pl.CostEstimate(flops=flops, bytes_accessed=0, transcendentals=0),
        name=body.__name__ if hasattr(body, "__name__") else body.func.__name__,
    )(*args)


def prepare(owner, row, count, flow, matrix, weight, innovation, up, down, bulk):
    for i in range(HALO):
        for f in range(2):
            for h in range(2):
                at = (i * 2 + f) * LEVELS + h * 8
                start = f * LEVELS * ROWS + h * 8 * ROWS
                up[at : at + 8, :] = flow[pl.ds(start + ROWS - HALO + i, 8, stride=ROWS), :]
                down[at : at + 8, :] = flow[pl.ds(start + i, 8, stride=ROWS), :]
    base = HALO * 2 * LEVELS
    up[base : base + OWN, :] = jnp.zeros((OWN, LANES), F32)
    bulk[...] = jnp.zeros(bulk.shape, F32)
    owners = [owner[j] for j in range(CAP)]
    turns = [sum([(owners[i] == owners[j]).astype(jnp.int32) for i in range(j)], jnp.int32(0)) for j in range(CAP)]
    column = jnp.transpose(weight[...] * innovation[...])
    ln, rw = lanes(HALF), places(HALF)
    where_to = jnp.full((8, LANES), NOWHERE, F32)
    for j in range(CAP):
        live = j < count[0]
        total = jnp.zeros((8, LANES), F32)
        for k in range(LANES // 8):
            total += matrix[j, k * 8 : k * 8 + 8, :] * column[k * 8 : k * 8 + 8, j : j + 1]
        pulled = jnp.where(live, jnp.sum(total, axis=0, keepdims=True), 0.0)
        slot = owners[j] * SLOT + turns[j]
        up[pl.ds(base + slot, 1), :] = pulled
        place = jnp.where(live, (lax.rem(row[j], ROWS) + HALO) * LEVELS + lax.div(row[j], ROWS), int(NOWHERE)).astype(F32)
        where_to = jnp.where(lanes(8) == slot, place, where_to)
    up[base + OWN :, :] = where_to
    down[base:, :] = up[base:, :]
    for j in range(CAP):
        block = matrix[j]
        scaled = jnp.transpose(block) * jnp.where(j < count[0], weight[j : j + 1, :], 0.0)
        gram = jnp.dot(scaled, block, precision=HIGHEST, preferred_element_type=F32)
        top, low = gram[:HALF], gram[HALF:]
        packed = jnp.where((ln >= HALF) & (ln - HALF <= rw), roll(top, HALF), low)
        diagonal = jnp.sum(jnp.where(ln - HALF == rw, low, 0.0), axis=0, keepdims=True)
        at = owners[j] * BULK + turns[j] * HALF
        bulk[pl.ds(pl.multiple_of(at, 8), HALF), :] = packed
        bulk[pl.ds(owners[j] * BULK + 2 * HALF + turns[j], 1), :] = diagonal


def widen(where, flow, below, above, own, wide, small):
    base = HALO * 2 * LEVELS
    wide[:base, :] = below[:base, :]
    wide[(HALO + ROWS) * 2 * LEVELS :, :] = above[:base, :]
    for r in range(ROWS):
        for f in range(2):
            for h in range(2):
                at = ((HALO + r) * 2 + f) * LEVELS + h * 8
                wide[at : at + 8, :] = flow[pl.ds(f * LEVELS * ROWS + h * 8 * ROWS + r, 8, stride=ROWS), :]
    me = where[0]
    right = lax.rem(me + 1, LON) * SMALL + LIST
    left = lax.rem(me + LON - 1, LON) * SMALL + LIST
    ln = lanes(8)
    lists = [below, own, above]
    spots = []
    for n, ref in enumerate(lists):
        p = ref[base + OWN : base + OWN + 8, :] + float((n - 1) * ROWS * LEVELS)
        spots.append(jnp.where(ln < OWN, p, roll(p, OWN)))
    for d in range(LON):
        first = 2 * (d - 1) % OWN
        spot = jnp.full((8, LANES), NOWHERE, F32)
        for n, ref in enumerate(lists):
            at = d * SMALL + n * 6
            fit = min(6, OWN - first)
            small[at : at + fit, :] = ref[base + first : base + first + fit, :]
            if fit < 6:
                small[at + fit : at + 6, :] = ref[base : base + 6 - fit, :]
            spot = jnp.where((ln >= n * 6) & (ln < n * 6 + 6), roll(spots[n], n * 6 - first), spot)
        small[d * SMALL + 18 : d * SMALL + LIST, :] = spot[:6]
        small[d * SMALL + LIST : (d + 1) * SMALL, :] = jnp.zeros((64, LANES), F32)
    for f in range(2):
        for g in range(WIDE // 8):
            to_right = jnp.zeros((8, LANES), F32)
            to_left = jnp.zeros((8, LANES), F32)
            for k in range(8):
                at = ((g * 8 + k) * 2 + f) * LEVELS
                low, high = wide[at : at + 8, :], wide[at + 8 : at + 16, :]
                mine_low = (ln >= 16 * k) & (ln < 16 * k + 8)
                mine_high = (ln >= 16 * k + 8) & (ln < 16 * k + 16)
                to_right = jnp.where(mine_low, roll(low, 16 * k + 8), jnp.where(mine_high, roll(high, 16 * k + 16), to_right))
                to_left = jnp.where(mine_low, roll(low, 16 * k), jnp.where(mine_high, roll(high, 16 * k + 8), to_left))
            at = (f * 4 + g) * 8
            small[pl.ds(pl.multiple_of(right + at, 8), 8), :] = to_right
            small[pl.ds(pl.multiple_of(left + at, 8), 8), :] = to_left


def unpack(bulk, grams):
    ln, rw = lanes(HALF), places(HALF)
    upper, diagonal, first = ln - HALF > rw, ln - HALF == rw, ln < HALF
    for s in range(LON):
        both = bulk[s * BULK : s * BULK + 2 * HALF, :]
        turned = jnp.transpose(both)
        ct, et = turned[:HALF], turned[HALF:]
        ct_rolled, et_rolled = roll(ct, HALF), roll(et, HALF)
        for o in range(SLOT):
            q = both[o * HALF : (o + 1) * HALF]
            d = bulk[s * BULK + 2 * HALF + o : s * BULK + 2 * HALF + o + 1, :]
            e_first, e_last = (et, et_rolled) if o == 0 else (et_rolled, et)
            c_last = ct_rolled if o == 0 else ct
            top = jnp.where(first, jnp.where(ln <= rw, roll(q, HALF), e_first), c_last)
            low = jnp.where(first | upper, q, jnp.where(diagonal, d, e_last))
            at = (o * LON + s) * LANES
            grams[at : at + HALF, :] = top
            grams[at + HALF : at + LANES, :] = low


def split(x):
    high = x.astype(jnp.bfloat16)
    rest = x - high.astype(F32)
    middle = rest.astype(jnp.bfloat16)
    low = (rest - middle.astype(F32)).astype(jnp.bfloat16)
    return jnp.concatenate([high, middle, low], axis=1)


def chosen(one_hot, parts):
    out = jnp.dot(one_hot, parts, preferred_element_type=F32)
    return out[:, :LANES] + out[:, LANES : 2 * LANES] + out[:, 2 * LANES :]


def one_hot(index, at):
    return jnp.where(index == at, 1.0, 0.0).astype(jnp.bfloat16)


def padded(x, rows):
    return jnp.concatenate([x, jnp.zeros((rows - x.shape[0], LANES), F32)], axis=0)


def lay_out(spot, own, sides, field, strips, low, high):
    spot = spot.astype(jnp.int32)
    by_lane = [jnp.transpose(spot[i * LANES : (i + 1) * LANES].astype(F32))[:8].astype(jnp.int32) for i in range(2)]
    ln = lanes(LANES)
    own_strip = jnp.where(ln < 32, jnp.where(ln >= 8, roll(own, 8), 0.0), jnp.where(ln < 56, roll(own, 56), 0.0))
    left = (places(LANES) < NEAR) & (ln < 8)
    right = (places(LANES) >= NEAR) & (ln >= 56) & (ln < 64)
    side_strip = jnp.where(left, roll(sides, 8), jnp.where(right, roll(sides, 56), 0.0))
    pieces = []
    for i, strip in enumerate((own_strip, side_strip)):
        upper = (spot[i * LANES : (i + 1) * LANES] & 8) != 0
        pieces.append(split(jnp.where(upper, roll(strip, HALF), strip)))
    own_parts = split(own)
    p = jnp.broadcast_to(by_lane[0][:1], (LANES, LANES))
    for start in range(low * LEVELS, high * LEVELS, LANES):
        field[start : start + LANES, :] = chosen(one_hot(places(LANES) + start, p), own_parts)
    folded = [jnp.broadcast_to((((b >> 4) << 3) + (b & 7))[:1], (64, LANES)) for b in by_lane]
    for start in range(low * 8, high * 8, 64):
        at = places(64) + start
        strips[start : start + 64, :] = chosen(one_hot(at, folded[0]), pieces[0]) + chosen(one_hot(at, folded[1]), pieces[1])


def adjoint(rates, source, target, first, last, height):
    before = kept = None
    for r in range(first, last + 1):
        y = source[r * height : (r + 1) * height, :]
        lat, lon = rates(r)
        t = lat * y
        a = jnp.where(lat > 0.0, t, 0.0)
        b = a - t
        s = lon * y
        e = jnp.where(lon > 0.0, s, 0.0)
        f = e - s
        if r > first + 1:
            target[(r - 1) * height : r * height, :] = kept + a
        if r > first:
            kept = y - (a + b) - (e + f) + roll(e, -1) + roll(f, 1) + before
        before = b


def tangent(rates, source, target, first, last, height):
    for r in range(first + 1, last):
        x = source[r * height : (r + 1) * height, :]
        south = source[(r - 1) * height : r * height, :]
        north = source[(r + 1) * height : (r + 2) * height, :]
        lat, lon = rates(r)
        out = x + jnp.abs(lat) * (jnp.where(lat > 0.0, south, north) - x)
        target[r * height : (r + 1) * height, :] = out + jnp.abs(lon) * (jnp.where(lon > 0.0, roll(x, 1), roll(x, -1)) - x)


def merged(field, strips, r):
    ln = lanes(8)
    t = strips[r * 8 : (r + 1) * 8, :]
    low, high = field[r * LEVELS : r * LEVELS + 8, :], field[r * LEVELS + 8 : (r + 1) * LEVELS, :]
    low = jnp.where(ln < 8, roll(t, -8), jnp.where(ln >= 120, roll(t, 72), low))
    high = jnp.where(ln < 8, roll(t, -72), jnp.where(ln >= 120, roll(t, 8), high))
    return low, high


def wide_rates(wide):
    return lambda r: (wide[r * 2 * LEVELS : (r * 2 + 1) * LEVELS, :], wide[(r * 2 + 1) * LEVELS : (r + 1) * 2 * LEVELS, :])


def edge_rates(edge):
    return lambda r: (edge[r * 16 : r * 16 + 8, :], edge[r * 16 + 8 : (r + 1) * 16, :])


def hessian_half(where, spot, own, sides, wide, edge, grams, kept, terms, fields, strips, image):
    field, other = fields
    strip, other_strip = strips
    lay_out(spot, own, sides, field, strip, 0, WIDE)
    full, narrow = wide_rates(wide), edge_rates(edge)
    pair, strip_pair = (field, other), (strip, other_strip)
    for k in range(STEPS):
        adjoint(full, *pair, k, WIDE - 1 - k, LEVELS)
        adjoint(narrow, *strip_pair, k, WIDE - 1 - k, 8)
        pair, strip_pair = pair[::-1], strip_pair[::-1]
    for flag, start in ((where[1], STEPS), (where[2], HALO + ROWS)):
        for ref, height in ((pair[0], LEVELS), (strip_pair[0], 8)):
            block = ref[start * height : (start + STEPS) * height, :]
            ref[start * height : (start + STEPS) * height, :] = jnp.where(flag == 1, 0.0, block)
    square = jnp.zeros((8, LANES), F32)
    for r in range(ROWS):
        low, high = merged(pair[0], strip_pair[0], r + HALO)
        kept[r * LEVELS : r * LEVELS + 8, :] = low
        kept[r * LEVELS + 8 : (r + 1) * LEVELS, :] = high
        square += low * low + high * high
    for k in range(STEPS, 2 * STEPS):
        tangent(full, *pair, k, WIDE - 1 - k, LEVELS)
        tangent(narrow, *strip_pair, k, WIDE - 1 - k, 8)
        pair, strip_pair = pair[::-1], strip_pair[::-1]
    for r in range(ROWS):
        low, high = merged(pair[0], strip_pair[0], r + HALO)
        image[r * LEVELS : r * LEVELS + 8, :] = low
        image[r * LEVELS + 8 : (r + 1) * LEVELS, :] = high
    mine = spot[OWN : 2 * OWN].astype(jnp.int32) - HALO * LEVELS
    hit = jnp.concatenate([one_hot(lanes(OWN), mine), one_hot(lanes(OWN) + LANES, mine)], axis=1)
    seen = chosen(hit, split(image[...]))
    column = jnp.transpose(seen)
    for t in range(OWN):
        total = jnp.zeros((8, LANES), F32)
        for k in range(LANES // 8):
            at = t * LANES + k * 8
            total += grams[at : at + 8, :] * column[k * 8 : k * 8 + 8, t : t + 1]
        terms[t : t + 1, :] = jnp.sum(total, axis=0, keepdims=True)
    return jnp.sum(square, keepdims=True), jnp.sum(seen * terms[...], keepdims=True)


def first_half(where, small, wide, grams, edge, spots, kept, terms, sums, field, other, strip, other_strip, image):
    ln = lanes(8)
    me = where[0]
    from_left = lax.rem(me + LON - 1, LON) * SMALL + LIST
    from_right = lax.rem(me + 1, LON) * SMALL + LIST
    for f in range(2):
        for g in range(WIDE // 8):
            at = (f * 4 + g) * 8
            left = small[pl.ds(pl.multiple_of(from_left + at, 8), 8), :]
            right = small[pl.ds(pl.multiple_of(from_right + at, 8), 8), :]
            for k in range(8):
                r = g * 8 + k
                at = (r * 2 + f) * LEVELS
                low, high = wide[at : at + 8, :], wide[at + 8 : at + 16, :]
                a = jnp.where(ln < 8, roll(left, -16 * k), jnp.where(ln < 32, roll(low, 8), jnp.where(ln < 56, roll(low, 56), roll(right, 56 - 16 * k))))
                b = jnp.where(ln < 72, roll(left, 56 - 16 * k), jnp.where(ln < 96, roll(high, 72), jnp.where(ln < 120, roll(high, 120), roll(right, 112 - 16 * k))))
                edge[(r * 2 + f) * 8 : (r * 2 + f + 1) * 8, :] = jnp.where(ln < HALF, a, b)
    named = small[pl.ds(18, LON, stride=SMALL), :]

    def spot_of(n, k):
        return jnp.broadcast_to(named[:, n * 6 + k : n * 6 + k + 1], (LON, LANES))

    def row_of(n, k):
        return small[pl.ds(n * 6 + k, LON, stride=SMALL), :]

    order = [[(n, k + o) for n in range(3) for o in range(SLOT)] for k in (2, 0, 4)]
    nowhere = jnp.full((LANES - NEAR, LANES), NOWHERE, F32)
    spot = jnp.concatenate(
        [spot_of(*i) for i in order[0]] + [nowhere] + [spot_of(*i) for i in order[1] + order[2]] + [nowhere[: LANES - 2 * NEAR]], axis=0
    )
    spots[...] = spot
    own = padded(jnp.concatenate([row_of(*i) for i in order[0]], axis=0), LANES)
    sides = padded(jnp.concatenate([row_of(*i) for i in order[1] + order[2]], axis=0), LANES)
    square, product = hessian_half(where, spot, own, sides, wide, edge, grams, kept, terms, (field, other), (strip, other_strip), image)
    sums[...] = jnp.where(ln == 0, square, jnp.where(ln == 1, product, 0.0))


def second_half(where, spots, own, left, right, wide, edge, grams, before, kept, terms, sums, field, other, strip, other_strip, image):
    own = padded(own[...], LANES)
    sides = padded(jnp.concatenate([left[...], right[...]], axis=0), LANES)
    square, product = hessian_half(where, spots[...], own, sides, wide, edge, grams, kept, terms, (field, other), (strip, other_strip), image)
    ln = lanes(8)
    mine = before[...] + jnp.where(ln == 2, square, jnp.where(ln == 3, product, 0.0))
    sums[...] = jnp.concatenate([mine] * (sums.shape[0] // 8), axis=0)


def gathered(parts, sums):
    sums[...] = jnp.broadcast_to(jnp.sum(parts[...], axis=0, keepdims=True), sums.shape)


def finish(spots, own, left, right, wide, edge, parts, right_side, image, increment, residual, field, other, strip, other_strip):
    own = padded(own[...], LANES)
    sides = padded(jnp.concatenate([left[...], right[...]], axis=0), LANES)
    lay_out(spots[...], own, sides, field, strip, HALO - STEPS, HALO + ROWS + STEPS)
    full, narrow = wide_rates(wide), edge_rates(edge)
    pair, strip_pair = (field, other), (strip, other_strip)
    for k in range(STEPS, 2 * STEPS):
        adjoint(full, *pair, k, WIDE - 1 - k, LEVELS)
        adjoint(narrow, *strip_pair, k, WIDE - 1 - k, 8)
        pair, strip_pair = pair[::-1], strip_pair[::-1]
    total = jnp.sum(parts[...], axis=0, keepdims=True)
    m0, m1, m2, m3 = (jnp.sum(jnp.where(lanes(1) == i, total, 0.0), keepdims=True) for i in range(4))
    step_0 = m0 / (m0 + m1)
    rho = m1 / m0
    spread = m2 - rho * m1
    curve = (m3 - rho * m2) - rho * (m2 - rho * m1)
    gamma = step_0 * spread / m0
    step_1 = spread / (spread + curve - gamma * spread)
    on_b = step_0 * (1.0 + step_1 * (gamma + rho))
    on_k = -step_0 * step_1
    rest_b = step_0 * ((1.0 - step_1) * rho - step_1 * gamma)
    rest_k = -step_0 * ((1.0 - step_1) + step_1 * (rho + gamma))
    rest_kk = step_0 * step_1
    on_b, on_k, rest_b, rest_k, rest_kk = (jnp.broadcast_to(v, (8, LANES)) for v in (on_b, on_k, rest_b, rest_k, rest_kk))
    for r in range(ROWS):
        for h, second in enumerate(merged(pair[0], strip_pair[0], r + HALO)):
            at = r * LEVELS + h * 8
            b, first = right_side[at : at + 8, :], image[at : at + 8, :]
            to = pl.ds(h * 8 * ROWS + r, 8, stride=ROWS)
            increment[to, :] = on_b * b + on_k * first
            residual[to, :] = rest_b * b + rest_k * first + rest_kk * second


def shift(x, axis, step, wrap):
    count = lax.axis_size(axis)
    pairs = [(i, (i + step) % count) for i in range(count) if wrap or 0 <= i + step < count]
    return lax.ppermute(x, axis, pairs)


def beside(terms):
    own = jnp.concatenate([shift(terms, LAT, 1, False), terms, shift(terms, LAT, -1, False)], axis=0)
    return own, shift(own, "lon", 1, True), shift(own, "lon", -1, True)


def spread_out(sums, axes):
    return lax.all_to_all(sums[:, None, :], axes, split_axis=0, concat_axis=0, tiled=True)[:, 0, :]


def shards(courant, obs_matrix, obs_weight, innovation, block_owner, block_row, block_count):
    lat_index = lax.axis_index(LAT)
    lat_total = lax.axis_size(LAT)
    where = jnp.stack([lax.axis_index("lon"), (lat_index == 0).astype(jnp.int32), (lat_index == lat_total - 1).astype(jnp.int32)]).astype(jnp.int32)
    flow = courant.reshape(-1, LANES)
    message = HALO * 2 * LEVELS + OWN + 8
    up, down, bulk = call(
        prepare,
        [(message, LANES), (message, LANES), (LON * BULK, LANES)],
        (block_owner.reshape(-1), block_row.reshape(-1), block_count.reshape(-1), flow, obs_matrix[0], obs_weight[0], innovation[0]),
        4_000_000,
    )
    packed = lax.all_to_all(bulk.reshape(LON, BULK, LANES), "lon", split_axis=0, concat_axis=0, tiled=True)
    below, above = shift(up, LAT, 1, False), shift(down, LAT, -1, False)
    wide, small = call(
        widen, [(WIDE * 2 * LEVELS, LANES), (LON * SMALL, LANES)], (where, flow, below, above, up), 2_000_000
    )
    small = lax.all_to_all(small.reshape(LON, SMALL, LANES), "lon", split_axis=0, concat_axis=0, tiled=True)
    (grams,) = call(unpack, [(OWN * LANES, LANES)], (packed.reshape(LON * BULK, LANES),), 2_000_000)
    cells = (ROWS * LEVELS, LANES)
    work = [pltpu.VMEM((WIDE * LEVELS, LANES), F32)] * 2 + [pltpu.VMEM((WIDE * 8, LANES), F32)] * 2
    image = pltpu.VMEM(cells, F32)
    edge, spots, right_side, terms, sums = call(
        first_half,
        [(WIDE * 2 * 8, LANES), (2 * LANES, LANES), cells, (OWN, LANES), (8, LANES)],
        (where, small.reshape(LON * SMALL, LANES), wide, grams),
        4_000_000,
        work + [image],
    )
    plane = lax.axis_size(("lat_1", "lon"))
    towers = lax.axis_size(("lat_0", "lat_2"))
    kept, terms, sums = call(
        second_half,
        [cells, (OWN, LANES), (plane, LANES)],
        (where, spots, *beside(terms), wide, edge, grams, sums),
        4_000_000,
        work + [image],
    )
    (sums,) = call(gathered, [(towers, LANES)], (spread_out(sums, ("lat_1", "lon")),), 10_000)
    parts = spread_out(sums, ("lat_0", "lat_2"))
    increment, residual = call(
        finish, [cells, cells], (spots, *beside(terms), wide, edge, parts, right_side, kept), 2_000_000, work
    )
    shape = courant.shape[1:]
    return increment.reshape(shape), residual.reshape(shape)


def solution(mesh):
    torus = Mesh(
        mesh.devices.reshape(-1, 4, 2, mesh.shape["lon"]), ("lat_0", "lat_1", "lat_2", "lon")
    )
    placed = (
        P(None, None, LAT, "lon"),
        P(LAT, "lon", None, None),
        P(LAT, "lon", None),
        P(LAT, "lon", None),
        P(LAT, "lon", None),
        P(LAT, "lon"),
        P(LAT, "lon"),
    )
    return jax.shard_map(
        shards,
        mesh=torus,
        in_specs=placed,
        out_specs=(P(None, LAT, "lon"), P(None, LAT, "lon")),
        check_vma=False,
    )
```

time: 211 us -> 134 us (0.64)
  blocking collectives: 46.2 us -> 0 us
  other arithmetic: 37.5 us -> 0.08 us
  Pallas kernels: 0 us -> 14.2 us
  local copies, waits for them, and re-layouts: 15.5 us -> 2.69 us
  starting transfers between devices: 71.1 us -> 82.2 us
  waiting for transfers between devices: 23.2 us -> 32.9 us
  matrix products: 8.99 us -> 0 us
  between operations: 7.97 us -> 1.52 us
    all_to_all x2 -> x0, blocking collectives: 46.2 us -> none  [the longest x1 28 us: shards(): lax.all_to_all(parcels, 'lon', split_axis=0, concat_axis=0, tiled=True)]
    all_to_all x1 -> x4, starting transfers between devices: 23.1 us -> 45.5 us  [the longest x2 30.9 us: spread_out(): lax.all_to_all(sums[:, None, :], axes, split_axis=0, concat_axis=0, tiled...]
    add x15 -> x0, other arithmetic: 15.8 us -> none  [the longest x8 8.66 us: adjoint(): cut(keep, HALO - reach + 1) * field[:, 1:-1, 1:-1] + a[:, 2:, 1:-1]]
    pallas_call x0 -> x7, Pallas kernels: none -> 14.2 us  [call(): pl.pallas_call(body, out_shape=outs, in_specs=[SMEM if a.dtype == jnp.int...]
    all_to_all x1 -> x4, waiting for transfers between devices: 9.58 us -> 22.6 us  [the longest x2 12 us: spread_out(): lax.all_to_all(sums[:, None, :], axes, split_axis=0, concat_axis=0, tiled...]
    ppermute x12 -> x10, starting transfers between devices: 48 us -> 36.7 us  [shift(): return lax.ppermute(x, axis, pairs)]
    dot_general x4 -> x0, matrix products: 8.99 us -> none  [the longest x2 6.11 us: weigh(): return jnp.einsum('bkl,bl->bk', gram, terms, precision=HIGHEST)]
    slice x4 -> x0, other arithmetic: 8.36 us -> none  [cut(): return a[..., width:-width, width:-width] if width else a]
  transfers between devices with their start and end apart: 13 -> 14, of which waited for: 8 -> 7; matrix products, arithmetic and copies ran while one was open for 5% -> 0% of each run, Pallas kernels for 0% -> 2%
where the time goes in v2:
time: 134 us
  starting transfers between devices  82.2 us (61%)
  waiting for transfers between devices  32.9 us (25%)
  Pallas kernels  14.2 us (11%)
  local copies, waits for them, and re-layouts  2.69 us (2%)
  between operations  1.52 us (1%)
    ppermute x10, starting transfers between devices, shift(): return lax.ppermute(x, axis, pairs)  36.7 us
    all_to_all x2, starting transfers between devices, spread_out(): lax.all_to_all(sums[:, None, :], axes, split_axis=0, concat_axis=0, tiled...  30.9 us
    pallas_call x7, Pallas kernels, call(): pl.pallas_call(body, out_shape=outs, in_specs=[SMEM if a.dtype == jnp.int...  14.2 us
    all_to_all x2, waiting for transfers between devices, spread_out(): lax.all_to_all(sums[:, None, :], axes, split_axis=0, concat_axis=0, tiled...  12 us
    all_to_all x1, waiting for transfers between devices, shards(): lax.all_to_all(small.reshape(LON, SMALL, LANES), 'lon', split_axis=0, con...  10.6 us
    ppermute x10, waiting for transfers between devices, shift(): return lax.ppermute(x, axis, pairs)  10.3 us
    all_to_all x1, starting transfers between devices, shards(): lax.all_to_all(bulk.reshape(LON, BULK, LANES), 'lon', split_axis=0, conca...  7.77 us
    all_to_all x1, starting transfers between devices, shards(): lax.all_to_all(small.reshape(LON, SMALL, LANES), 'lon', split_axis=0, con...  6.83 us
  transfers between devices with their start and end apart: 14, of which 7 were waited for; matrix products, arithmetic and copies ran while one was open for 0% of the time, Pallas kernels for 2%

profile of v2, /device:TPU:1, one launch (start us, length us, event | category | flops | bytes accessed | tf_op | source)
XLA Modules:
  0.0 133.6 jit_solution(13362979922707625100)
XLA Ops:
  1.3 0.0 copy-start.4
  1.3 0.0 copy-start.3
  1.3 0.0 copy-start.5
  1.3 0.0 copy-start.6
  1.3 0.6 copy-done.4
  2.0 0.0 copy-done.3
  2.0 0.0 copy-done.5
  2.0 0.0 copy-done.6
  2.0 0.0 copy-start
  2.0 0.9 copy-done
  2.9 1.0 copy-done.2
  4.0 2.2 %prepare.1 = (f32[280,128]{1,0:T(8,128)S(1)}, f32[280,128]{1,0:T(8,128)S(1)}, f32[1088,128]{1,0:T(8,128)}) custom-call(s32[8]{0:T(128)S(1)} %bitcast.34, s32[8]{0:T(128)S(1)} %bitcast.35, s32[1]{0:T(128)} %bitcast.24.count, f32[512,128]{1,0:T(8,128)S(1)} %bitcast.27, f32[8,128,128]{2,1,0:T(8,128)S(1)} %bitcast.29, f32[8,128]{1,0:T(8,128)S(1)} %bitcast.32, ...), custom_call_target="tpu_custom_call" | custom-call | flops 4000000 | tf_op jit(solution)/shard_map/prepare/pallas_call | solution.py:49
  6.2 7.8 %all-to-all-start.1 = ((f32[8,136,128]{2,1,0:T(8,128)}), f32[8,136,128]{2,1,0:T(8,128)S(1)}, u32[]{:S(2)}, u32[]{:S(2)}) async-start(f32[8,136,128]{2,1,0:T(8,128)} %bitcast.12), calls=%async_computation.1 | async-start | bytes 1114112 | tf_op jit(solution)/shard_map/all_to_all | solution.py:406
  14.0 11.9 %collective-permute-start.1 = (f32[280,128]{1,0:T(8,128)S(1)}, f32[280,128]{1,0:T(8,128)S(1)}, u32[]{:S(2)}, u32[]{:S(2)}) collective-permute-start(f32[280,128]{1,0:T(8,128)S(1)} %get-tuple-element.18), channel_id=1, source_target_pairs={{8,0},{16,8},{24,16},{32,24},{40,32},{48,40},{56,48},{64,56},{72,6... | collective-permute-start | bytes 430088 | tf_op jit(solution)/shard_map/ppermute | solution.py:382
  25.9 1.9 %collective-permute-start = (f32[280,128]{1,0:T(8,128)S(1)}, f32[280,128]{1,0:T(8,128)S(1)}, u32[]{:S(2)}, u32[]{:S(2)}) collective-permute-start(f32[280,128]{1,0:T(8,128)S(1)} %get-tuple-element.17.own), channel_id=1, source_target_pairs={{0,8},{8,16},{16,24},{24,32},{32,40},{40,48},{48,56},{56,64},{64,7... | collective-permute-start | bytes 430088 | tf_op jit(solution)/shard_map/ppermute | solution.py:382
  27.9 0.1 pad_add_fusion.where
  27.9 0.0 collective-permute-done.1.above
  28.0 1.9 %collective-permute-done.below = f32[280,128]{1,0:T(8,128)S(1)} collective-permute-done((f32[280,128]{1,0:T(8,128)S(1)}, f32[280,128]{1,0:T(8,128)S(1)}, u32[]{:S(2)}, u32[]{:S(2)}) %collective-permute-start) | collective-permute-done | bytes 143392 | tf_op jit(solution)/shard_map/ppermute | solution.py:382
  29.9 0.0 copy-done.1
  29.9 1.7 %widen.1 = (f32[1024,128]{1,0:T(8,128)S(1)}, f32[704,128]{1,0:T(8,128)}) custom-call(s32[3]{0:T(128)S(1)} %pad_add_fusion.where, f32[512,128]{1,0:T(8,128)S(1)} %bitcast.28, f32[280,128]{1,0:T(8,128)S(1)} %collective-permute-done.below, f32[280,128]{1,0:T(8,128)S(1)} %collective-permute-done.1.above, f32[280,128]{1,0:T(8,128)S(1)} %get-tuple-element.17.own), custom_call_target="tpu_custom_call" | custom-call | flops 2000000 | tf_op jit(solution)/shard_map/widen/pallas_call | solution.py:49
  31.6 0.0 all-to-all-done.1
  31.6 6.8 %all-to-all-start = ((f32[8,88,128]{2,1,0:T(8,128)}), f32[8,88,128]{2,1,0:T(8,128)S(1)}, u32[]{:S(2)}, u32[]{:S(2)}) async-start(f32[8,88,128]{2,1,0:T(8,128)} %bitcast.10), calls=%async_computation | async-start | bytes 720896 | tf_op jit(solution)/shard_map/all_to_all | solution.py:411
  38.4 0.5 unpack.1.grams
  38.9 10.6 %all-to-all-done = f32[8,88,128]{2,1,0:T(8,128)S(1)} async-done(((f32[8,88,128]{2,1,0:T(8,128)}), f32[8,88,128]{2,1,0:T(8,128)S(1)}, u32[]{:S(2)}, u32[]{:S(2)}) %all-to-all-start) | async-done | bytes 360480 | tf_op jit(solution)/shard_map/all_to_all | solution.py:411
  49.5 3.8 %first_half.1 = (f32[512,128]{1,0:T(8,128)S(1)}, f32[256,128]{1,0:T(8,128)S(1)}, f32[256,128]{1,0:T(8,128)S(1)}, f32[16,128]{1,0:T(8,128)S(1)}, f32[8,128]{1,0:T(8,128)S(1)}) custom-call(s32[3]{0:T(128)S(1)} %pad_add_fusion.where, f32[704,128]{1,0:T(8,128)S(1)} %bitcast.26, f32[1024,128]{1,0:T(8,128)S(1)} %get-tuple-element.20.wide, f32[2048,128]{1,0:T(8,128)S(1)} %unpack.1.grams), custom_call_target="tpu_custom_call" | custom-call | flops 4000000 | tf_op jit(solution)/shard_map/first_half/pallas_call | solution.py:49
  53.3 5.1 %collective-permute-start.2 = (f32[16,128]{1,0:T(8,128)S(1)}, f32[16,128]{1,0:T(8,128)S(1)}, u32[]{:S(2)}, u32[]{:S(2)}) collective-permute-start(f32[16,128]{1,0:T(8,128)S(1)} %get-tuple-element.23), channel_id=1, source_target_pairs={{0,8},{8,16},{16,24},{24,32},{32,40},{40,48},{48,56},{56,64},{64,7... | collective-permute-start | bytes 24584 | tf_op jit(solution)/shard_map/ppermute | solution.py:382
  58.4 1.9 %collective-permute-start.3 = (f32[16,128]{1,0:T(8,128)S(1)}, f32[16,128]{1,0:T(8,128)S(1)}, u32[]{:S(2)}, u32[]{:S(2)}) collective-permute-start(f32[16,128]{1,0:T(8,128)S(1)} %get-tuple-element.23), channel_id=1, source_target_pairs={{8,0},{16,8},{24,16},{32,24},{40,32},{48,40},{56,48},{64,56},{72,6... | collective-permute-start | bytes 24584 | tf_op jit(solution)/shard_map/ppermute | solution.py:382
  60.4 0.0 collective-permute-done.2
  60.4 3.0 %collective-permute-done.3 = f32[16,128]{1,0:T(8,128)S(1)} collective-permute-done((f32[16,128]{1,0:T(8,128)S(1)}, f32[16,128]{1,0:T(8,128)S(1)}, u32[]{:S(2)}, u32[]{:S(2)}) %collective-permute-start.3) | collective-permute-done | bytes 8224 | tf_op jit(solution)/shard_map/ppermute | solution.py:382
  63.4 1.9 %collective-permute-start.5 = (f32[48,128]{1,0:T(8,128)S(1)}, f32[48,128]{1,0:T(8,128)S(1)}, u32[]{:S(2)}, u32[]{:S(2)}) collective-permute-start(f32[48,128]{1,0:T(8,128)S(1)} %constant_dynamic-update-slice_fusion.own), channel_id=1, source_target_pairs={{0,7},{1,0},{2,1},{3,2},{4,3},{5,4},{6,5},{7,6},{8,15},{9,8},{10,9... | collective-permute-start | bytes 73736 | tf_op jit(solution)/shard_map/ppermute | solution.py:382
  65.3 3.4 %collective-permute-start.4 = (f32[48,128]{1,0:T(8,128)S(1)}, f32[48,128]{1,0:T(8,128)S(1)}, u32[]{:S(2)}, u32[]{:S(2)}) collective-permute-start(f32[48,128]{1,0:T(8,128)S(1)} %constant_dynamic-update-slice_fusion.own), channel_id=1, source_target_pairs={{0,1},{1,2},{2,3},{3,4},{4,5},{5,6},{6,7},{7,0},{8,9},{9,10},{10,1... | collective-permute-start | bytes 73736 | tf_op jit(solution)/shard_map/ppermute | solution.py:382
  68.7 0.0 collective-permute-done.5.right
  68.7 2.4 %collective-permute-done.4.left = f32[48,128]{1,0:T(8,128)S(1)} collective-permute-done((f32[48,128]{1,0:T(8,128)S(1)}, f32[48,128]{1,0:T(8,128)S(1)}, u32[]{:S(2)}, u32[]{:S(2)}) %collective-permute-start.4) | collective-permute-done | bytes 24608 | tf_op jit(solution)/shard_map/ppermute | solution.py:382
  71.1 3.6 %second_half.1 = (f32[256,128]{1,0:T(8,128)S(1)}, f32[16,128]{1,0:T(8,128)S(1)}, f32[32,128]{1,0:T(8,128)}) custom-call(s32[3]{0:T(128)S(1)} %pad_add_fusion.where, f32[256,128]{1,0:T(8,128)S(1)} %get-tuple-element.22.spots, f32[48,128]{1,0:T(8,128)S(1)} %constant_dynamic-update-slice_fusion.own, f32[48,128]{1,0:T(8,128)S(1)} %collective-permute-done.4.left, ...), custom_call_target="tpu_custom_call" | custom-call | flops 4000000 | tf_op jit(solution)/shard_map/second_half/pallas_call | solution.py:49
  74.7 3.3 %collective-permute-start.6 = (f32[16,128]{1,0:T(8,128)S(1)}, f32[16,128]{1,0:T(8,128)S(1)}, u32[]{:S(2)}, u32[]{:S(2)}) collective-permute-start(f32[16,128]{1,0:T(8,128)S(1)} %get-tuple-element.26), channel_id=1, source_target_pairs={{0,8},{8,16},{16,24},{24,32},{32,40},{40,48},{48,56},{56,64},{64,7... | collective-permute-start | bytes 24584 | tf_op jit(solution)/shard_map/ppermute | solution.py:382
  78.0 1.9 %collective-permute-start.7 = (f32[16,128]{1,0:T(8,128)S(1)}, f32[16,128]{1,0:T(8,128)S(1)}, u32[]{:S(2)}, u32[]{:S(2)}) collective-permute-start(f32[16,128]{1,0:T(8,128)S(1)} %get-tuple-element.26), channel_id=1, source_target_pairs={{8,0},{16,8},{24,16},{32,24},{40,32},{48,40},{56,48},{64,56},{72,6... | collective-permute-start | bytes 24584 | tf_op jit(solution)/shard_map/ppermute | solution.py:382
  80.0 8.4 %all-to-all-start.2 = ((f32[32,1,128]{2,1,0:T(1,128)}), f32[32,1,128]{2,1,0:T(1,128)S(1)}, u32[]{:S(2)}, u32[]{:S(2)}) async-start(f32[32,1,128]{2,1,0:T(1,128)} %bitcast.15), calls=%async_computation.2 | async-start | bytes 32768 | tf_op jit(solution)/shard_map/all_to_all | solution.py:391
  88.4 0.0 collective-permute-done.6
  88.4 8.6 %all-to-all-done.2 = f32[32,1,128]{2,1,0:T(1,128)S(1)} async-done(((f32[32,1,128]{2,1,0:T(1,128)}), f32[32,1,128]{2,1,0:T(1,128)S(1)}, u32[]{:S(2)}, u32[]{:S(2)}) %all-to-all-start.2) | async-done | bytes 16416 | tf_op jit(solution)/shard_map/all_to_all | solution.py:391
  97.0 0.6 gathered.1
  97.6 22.5 %all-to-all-start.3 = ((f32[32,1,128]{2,1,0:T(1,128)}), f32[32,1,128]{2,1,0:T(1,128)S(1)}, u32[]{:S(2)}, u32[]{:S(2)}) async-start(f32[32,1,128]{2,1,0:T(1,128)} %bitcast.18), calls=%async_computation.3 | async-start | bytes 32768 | tf_op jit(solution)/shard_map/all_to_all | solution.py:391
  120.1 0.0 collective-permute-done.7
  120.1 2.2 %collective-permute-start.9 = (f32[48,128]{1,0:T(8,128)S(1)}, f32[48,128]{1,0:T(8,128)S(1)}, u32[]{:S(2)}, u32[]{:S(2)}) collective-permute-start(f32[48,128]{1,0:T(8,128)S(1)} %constant_dynamic-update-slice_fusion.3.own), channel_id=1, source_target_pairs={{0,7},{1,0},{2,1},{3,2},{4,3},{5,4},{6,5},{7,6},{8,15},{9,8},{10,9... | collective-permute-start | bytes 73736 | tf_op jit(solution)/shard_map/ppermute | solution.py:382
  122.3 3.1 %collective-permute-start.8 = (f32[48,128]{1,0:T(8,128)S(1)}, f32[48,128]{1,0:T(8,128)S(1)}, u32[]{:S(2)}, u32[]{:S(2)}) collective-permute-start(f32[48,128]{1,0:T(8,128)S(1)} %constant_dynamic-update-slice_fusion.3.own), channel_id=1, source_target_pairs={{0,1},{1,2},{2,3},{3,4},{4,5},{5,6},{6,7},{7,0},{8,9},{9,10},{10,1... | collective-permute-start | bytes 73736 | tf_op jit(solution)/shard_map/ppermute | solution.py:382
  125.4 0.0 collective-permute-done.9.right
  125.4 2.9 %collective-permute-done.8.left = f32[48,128]{1,0:T(8,128)S(1)} collective-permute-done((f32[48,128]{1,0:T(8,128)S(1)}, f32[48,128]{1,0:T(8,128)S(1)}, u32[]{:S(2)}, u32[]{:S(2)}) %collective-permute-start.8) | collective-permute-done | bytes 24608 | tf_op jit(solution)/shard_map/ppermute | solution.py:382
  128.3 3.5 %all-to-all-done.3 = f32[32,1,128]{2,1,0:T(1,128)S(1)} async-done(((f32[32,1,128]{2,1,0:T(1,128)}), f32[32,1,128]{2,1,0:T(1,128)S(1)}, u32[]{:S(2)}, u32[]{:S(2)}) %all-to-all-start.3) | async-done | bytes 16416 | tf_op jit(solution)/shard_map/all_to_all | solution.py:391
  131.8 1.7 %finish.1 = (f32[256,128]{1,0:T(8,128)}, f32[256,128]{1,0:T(8,128)}) custom-call(f32[256,128]{1,0:T(8,128)S(1)} %get-tuple-element.22.spots, f32[48,128]{1,0:T(8,128)S(1)} %constant_dynamic-update-slice_fusion.3.own, f32[48,128]{1,0:T(8,128)S(1)} %collective-permute-done.8.left, f32[48,128]{1,0:T(8,128)S(1)} %collective-permute-done.9.right, ...), custom_call_target="tpu_custom_call" | custom-call | flops 2000000 | tf_op jit(solution)/shard_map/finish/pallas_call | solution.py:49
  (8 shorter events, 0.0 us)
Async XLA Ops:
  1.3 0.7 copy-start.4
  1.3 0.7 copy-start.3
  1.3 0.7 copy-start.5
  1.3 0.7 copy-start.6
  2.0 1.0 copy-start
  2.9 1.0 copy-start.2
  6.2 23.7 %copy-start.1 = (f32[2,16,16,128]{3,2,1,0:T(8,128)S(1)}, f32[2,16,16,128]{3,2,1,0:T(8,128)}, u32[]{:S(2)}) copy-start(f32[2,16,16,128]{3,2,1,0:T(8,128)} %param.7) | copy-start | bytes 786436
  6.2 25.3 %all-to-all-start.1 = ((f32[8,136,128]{2,1,0:T(8,128)}), f32[8,136,128]{2,1,0:T(8,128)S(1)}, u32[]{:S(2)}, u32[]{:S(2)}) async-start(f32[8,136,128]{2,1,0:T(8,128)} %bitcast.12), calls=%async_computation.1 | async-start | bytes 1114112 | tf_op jit(solution)/shard_map/all_to_all | solution.py:406
  14.0 14.0 %collective-permute-start.1 = (f32[280,128]{1,0:T(8,128)S(1)}, f32[280,128]{1,0:T(8,128)S(1)}, u32[]{:S(2)}, u32[]{:S(2)}) collective-permute-start(f32[280,128]{1,0:T(8,128)S(1)} %get-tuple-element.18), channel_id=1, source_target_pairs={{8,0},{16,8},{24,16},{32,24},{40,32},{48,40},{56,48},{64,56},{72,6... | collective-permute-start | bytes 430088 | tf_op jit(solution)/shard_map/ppermute | solution.py:382
  25.9 4.0 %collective-permute-start = (f32[280,128]{1,0:T(8,128)S(1)}, f32[280,128]{1,0:T(8,128)S(1)}, u32[]{:S(2)}, u32[]{:S(2)}) collective-permute-start(f32[280,128]{1,0:T(8,128)S(1)} %get-tuple-element.17.own), channel_id=1, source_target_pairs={{0,8},{8,16},{16,24},{24,32},{32,40},{40,48},{48,56},{56,64},{64,7... | collective-permute-start | bytes 430088 | tf_op jit(solution)/shard_map/ppermute | solution.py:382
  31.6 17.9 %all-to-all-start = ((f32[8,88,128]{2,1,0:T(8,128)}), f32[8,88,128]{2,1,0:T(8,128)S(1)}, u32[]{:S(2)}, u32[]{:S(2)}) async-start(f32[8,88,128]{2,1,0:T(8,128)} %bitcast.10), calls=%async_computation | async-start | bytes 720896 | tf_op jit(solution)/shard_map/all_to_all | solution.py:411
  53.3 7.1 %collective-permute-start.2 = (f32[16,128]{1,0:T(8,128)S(1)}, f32[16,128]{1,0:T(8,128)S(1)}, u32[]{:S(2)}, u32[]{:S(2)}) collective-permute-start(f32[16,128]{1,0:T(8,128)S(1)} %get-tuple-element.23), channel_id=1, source_target_pairs={{0,8},{8,16},{16,24},{24,32},{32,40},{40,48},{48,56},{56,64},{64,7... | collective-permute-start | bytes 24584 | tf_op jit(solution)/shard_map/ppermute | solution.py:382
  58.4 5.0 %collective-permute-start.3 = (f32[16,128]{1,0:T(8,128)S(1)}, f32[16,128]{1,0:T(8,128)S(1)}, u32[]{:S(2)}, u32[]{:S(2)}) collective-permute-start(f32[16,128]{1,0:T(8,128)S(1)} %get-tuple-element.23), channel_id=1, source_target_pairs={{8,0},{16,8},{24,16},{32,24},{40,32},{48,40},{56,48},{64,56},{72,6... | collective-permute-start | bytes 24584 | tf_op jit(solution)/shard_map/ppermute | solution.py:382
  63.4 5.3 %collective-permute-start.5 = (f32[48,128]{1,0:T(8,128)S(1)}, f32[48,128]{1,0:T(8,128)S(1)}, u32[]{:S(2)}, u32[]{:S(2)}) collective-permute-start(f32[48,128]{1,0:T(8,128)S(1)} %constant_dynamic-update-slice_fusion.own), channel_id=1, source_target_pairs={{0,7},{1,0},{2,1},{3,2},{4,3},{5,4},{6,5},{7,6},{8,15},{9,8},{10,9... | collective-permute-start | bytes 73736 | tf_op jit(solution)/shard_map/ppermute | solution.py:382
  65.3 5.8 %collective-permute-start.4 = (f32[48,128]{1,0:T(8,128)S(1)}, f32[48,128]{1,0:T(8,128)S(1)}, u32[]{:S(2)}, u32[]{:S(2)}) collective-permute-start(f32[48,128]{1,0:T(8,128)S(1)} %constant_dynamic-update-slice_fusion.own), channel_id=1, source_target_pairs={{0,1},{1,2},{2,3},{3,4},{4,5},{5,6},{6,7},{7,0},{8,9},{9,10},{10,1... | collective-permute-start | bytes 73736 | tf_op jit(solution)/shard_map/ppermute | solution.py:382
  74.7 13.7 %collective-permute-start.6 = (f32[16,128]{1,0:T(8,128)S(1)}, f32[16,128]{1,0:T(8,128)S(1)}, u32[]{:S(2)}, u32[]{:S(2)}) collective-permute-start(f32[16,128]{1,0:T(8,128)S(1)} %get-tuple-element.26), channel_id=1, source_target_pairs={{0,8},{8,16},{16,24},{24,32},{32,40},{40,48},{48,56},{56,64},{64,7... | collective-permute-start | bytes 24584 | tf_op jit(solution)/shard_map/ppermute | solution.py:382
  78.0 42.0 %collective-permute-start.7 = (f32[16,128]{1,0:T(8,128)S(1)}, f32[16,128]{1,0:T(8,128)S(1)}, u32[]{:S(2)}, u32[]{:S(2)}) collective-permute-start(f32[16,128]{1,0:T(8,128)S(1)} %get-tuple-element.26), channel_id=1, source_target_pairs={{8,0},{16,8},{24,16},{32,24},{40,32},{48,40},{56,48},{64,56},{72,6... | collective-permute-start | bytes 24584 | tf_op jit(solution)/shard_map/ppermute | solution.py:382
  80.0 17.0 %all-to-all-start.2 = ((f32[32,1,128]{2,1,0:T(1,128)}), f32[32,1,128]{2,1,0:T(1,128)S(1)}, u32[]{:S(2)}, u32[]{:S(2)}) async-start(f32[32,1,128]{2,1,0:T(1,128)} %bitcast.15), calls=%async_computation.2 | async-start | bytes 32768 | tf_op jit(solution)/shard_map/all_to_all | solution.py:391
  97.6 34.2 %all-to-all-start.3 = ((f32[32,1,128]{2,1,0:T(1,128)}), f32[32,1,128]{2,1,0:T(1,128)S(1)}, u32[]{:S(2)}, u32[]{:S(2)}) async-start(f32[32,1,128]{2,1,0:T(1,128)} %bitcast.18), calls=%async_computation.3 | async-start | bytes 32768 | tf_op jit(solution)/shard_map/all_to_all | solution.py:391
  120.1 5.3 %collective-permute-start.9 = (f32[48,128]{1,0:T(8,128)S(1)}, f32[48,128]{1,0:T(8,128)S(1)}, u32[]{:S(2)}, u32[]{:S(2)}) collective-permute-start(f32[48,128]{1,0:T(8,128)S(1)} %constant_dynamic-update-slice_fusion.3.own), channel_id=1, source_target_pairs={{0,7},{1,0},{2,1},{3,2},{4,3},{5,4},{6,5},{7,6},{8,15},{9,8},{10,9... | collective-permute-start | bytes 73736 | tf_op jit(solution)/shard_map/ppermute | solution.py:382
  122.3 6.1 %collective-permute-start.8 = (f32[48,128]{1,0:T(8,128)S(1)}, f32[48,128]{1,0:T(8,128)S(1)}, u32[]{:S(2)}, u32[]{:S(2)}) collective-permute-start(f32[48,128]{1,0:T(8,128)S(1)} %constant_dynamic-update-slice_fusion.3.own), channel_id=1, source_target_pairs={{0,1},{1,2},{2,3},{3,4},{4,5},{5,6},{6,7},{7,0},{8,9},{9,10},{10,1... | collective-permute-start | bytes 73736 | tf_op jit(solution)/shard_map/ppermute | solution.py:382

commit v3 on v2

v3 whole, which is shorter than its diff:
```python
import jax
import jax.numpy as jnp
from jax import lax
from jax.experimental import pallas as pl
from jax.experimental.pallas import tpu as pltpu
from jax.sharding import Mesh
from jax.sharding import PartitionSpec as P

LAT = ("lat_0", "lat_1", "lat_2")
LEVELS = 16
ROWS = 16
LANES = 128
CAP = 8
SLOT = 2
STEPS = 4
HALO = 2 * STEPS
WIDE = ROWS + 2 * HALO
LON = 8
HALF = LANES // 2
OWN = LON * SLOT
NEAR = 3 * OWN
BULK = 2 * HALF + 8
LIST = 8
SMALL = LIST + 32
EDGES = HALO * 2 * LEVELS
OWNS = EDGES + HALO * 2 * 8
LEFTS = OWNS + OWN
RIGHTS = LEFTS + OWN
SPOTS = RIGHTS + OWN
MESSAGE = SPOTS + 8
NOWHERE = -4096.0
HIGHEST = lax.Precision.HIGHEST
F32 = jnp.float32
VMEM = pl.BlockSpec(memory_space=pltpu.VMEM)
SMEM = pl.BlockSpec(memory_space=pltpu.SMEM)


def lanes(rows):
    return lax.broadcasted_iota(jnp.int32, (rows, LANES), 1)


def places(rows):
    return lax.broadcasted_iota(jnp.int32, (rows, LANES), 0)


def roll(x, shift):
    shift %= LANES
    return pltpu.roll(x, shift, axis=1) if shift else x


def call(body, outs, args, flops, scratch=(), specs=None, room=24):
    return pl.pallas_call(
        body,
        out_shape=[jax.ShapeDtypeStruct(s, F32) for s in outs],
        in_specs=specs or [SMEM if a.dtype == jnp.int32 else VMEM for a in args],
        out_specs=[VMEM] * len(outs),
        scratch_shapes=list(scratch),
        compiler_params=pltpu.CompilerParams(vmem_limit_bytes=room << 20),
        cost_estimate=pl.CostEstimate(flops=flops, bytes_accessed=0, transcendentals=0),
        name=body.__name__,
    )(*args)


def turns_of(owners):
    return [sum([(o == owners[j]).astype(jnp.int32) for o in owners[:j]], jnp.int32(0)) for j in range(CAP)]


def packed_edges(pick, shift):
    ln = lanes(8)
    out = jnp.zeros((8, LANES), F32)
    for k in range(8):
        low, high = pick(k)
        out = jnp.where((ln >= 16 * k) & (ln < 16 * k + 8), roll(low, 16 * k + shift), out)
        out = jnp.where((ln >= 16 * k + 8) & (ln < 16 * k + 16), roll(high, 16 * k + 8 + shift), out)
    return out


def prepare(where, owner_at, row_at, count_at, flow_at, matrix_at, weight_at, innovation_at, small, owner, row, count, flow, matrix, weight, innovation, lists, sems):
    pairs = ((owner_at, owner), (row_at, row), (count_at, count), (flow_at, flow), (weight_at, weight), (innovation_at, innovation), (matrix_at, matrix))
    copies = [pltpu.make_async_copy(a, b, sems.at[i]) for i, (a, b) in enumerate(pairs)]
    for copy in copies:
        copy.start()
    copies[3].wait()
    me = where[0]
    to_right = lax.rem(me + 1, LON) * SMALL + LIST
    to_left = lax.rem(me + LON - 1, LON) * SMALL + LIST
    for f in range(2):
        for g in range(2):

            def pick(k, f=f, g=g):
                at = f * LEVELS * ROWS + g * 8 + k
                return flow[pl.ds(at, 8, stride=ROWS), :], flow[pl.ds(at + 8 * ROWS, 8, stride=ROWS), :]

            at = (f * 2 + g) * 8
            small[pl.ds(pl.multiple_of(to_right + at, 8), 8), :] = packed_edges(pick, 8)
            small[pl.ds(pl.multiple_of(to_left + at, 8), 8), :] = packed_edges(pick, 0)
    for i in (0, 1, 2, 4, 5, 6):
        copies[i].wait()
    owners = [owner[j] for j in range(CAP)]
    turns = turns_of(owners)
    lists[...] = jnp.zeros(lists.shape, F32)
    column = jnp.transpose(weight[...] * innovation[...])
    ln = lanes(8)
    named = jnp.full((8, LANES), NOWHERE, F32)
    for j in range(CAP):
        live = j < count[0]
        total = jnp.zeros((8, LANES), F32)
        for k in range(LANES // 8):
            total += matrix[j, k * 8 : k * 8 + 8, :] * column[k * 8 : k * 8 + 8, j : j + 1]
        slot = owners[j] * SLOT + turns[j]
        lists[pl.ds(slot, 1), :] = jnp.where(live, jnp.sum(total, axis=0, keepdims=True), 0.0)
        place = jnp.where(live, (lax.rem(row[j], ROWS) + HALO) * LEVELS + lax.div(row[j], ROWS), int(NOWHERE)).astype(F32)
        named = jnp.where(ln == slot, place, named)
    named = jnp.where(ln < OWN, named, roll(named, OWN))
    line = lanes(1)
    for d in range(LON):
        left, right = 2 * (d - 1) % OWN, 2 * (d + 1) % OWN
        small[d * SMALL : d * SMALL + 2, :] = lists[2 * d : 2 * d + 2, :]
        edge = jnp.where(line < 8, roll(lists[left : left + 1, :], 8), roll(lists[left + 1 : left + 2, :], 16))
        edge = jnp.where(line < 16, edge, jnp.where(line < 24, roll(lists[right : right + 1, :], 16), roll(lists[right + 1 : right + 2, :], 24)))
        small[d * SMALL + 2 : d * SMALL + 3, :] = edge
        small[d * SMALL + 3 : d * SMALL + 4, :] = roll(named, -left)[:1]


def weigh_blocks(owner, row, count, matrix, weight, bulk):
    bulk[...] = jnp.zeros(bulk.shape, F32)
    owners = [owner[j] for j in range(CAP)]
    turns = turns_of(owners)
    ln, rw = lanes(HALF), places(HALF)
    for j in range(CAP):
        block = matrix[j]
        scaled = jnp.transpose(block) * jnp.where(j < count[0], weight[j : j + 1, :], 0.0)
        gram = jnp.dot(scaled, block, precision=HIGHEST, preferred_element_type=F32)
        top, low = gram[:HALF], gram[HALF:]
        packed = jnp.where((ln >= HALF) & (ln - HALF <= rw), roll(top, HALF), low)
        diagonal = jnp.sum(jnp.where(ln - HALF == rw, low, 0.0), axis=0, keepdims=True)
        at = owners[j] * BULK + turns[j] * HALF
        bulk[pl.ds(pl.multiple_of(at, 8), HALF), :] = packed
        bulk[pl.ds(owners[j] * BULK + 2 * HALF + turns[j], 1), :] = diagonal


def arrange(where, flow, small, up, down):
    ln = lanes(8)
    me = where[0]
    from_left = lax.rem(me + LON - 1, LON) * SMALL + LIST
    from_right = lax.rem(me + 1, LON) * SMALL + LIST
    for f in range(2):
        for g, out in enumerate((down, up)):
            at = (f * 2 + g) * 8
            left = small[pl.ds(pl.multiple_of(from_left + at, 8), 8), :]
            right = small[pl.ds(pl.multiple_of(from_right + at, 8), 8), :]
            for k in range(8):
                at = f * LEVELS * ROWS + g * 8 + k
                low, high = flow[pl.ds(at, 8, stride=ROWS), :], flow[pl.ds(at + 8 * ROWS, 8, stride=ROWS), :]
                at = (k * 2 + f) * LEVELS
                out[at : at + 8, :] = low
                out[at + 8 : at + 16, :] = high
                a = jnp.where(ln < 8, roll(left, -16 * k), jnp.where(ln < 32, roll(low, 8), jnp.where(ln < 56, roll(low, 56), roll(right, 56 - 16 * k))))
                b = jnp.where(ln < 72, roll(left, 56 - 16 * k), jnp.where(ln < 96, roll(high, 72), jnp.where(ln < 120, roll(high, 120), roll(right, 112 - 16 * k))))
                at = EDGES + (k * 2 + f) * 8
                out[at : at + 8, :] = jnp.where(ln < HALF, a, b)
    edge = small[pl.ds(2, LON, stride=SMALL), :]
    named = small[pl.ds(3, LON, stride=SMALL), :]
    turned = jnp.transpose(named)
    spot = jnp.full((1, LANES), NOWHERE, F32)
    line = lanes(1)
    for i, k in enumerate((2, 3, 0, 1, 4, 5)):
        line_k = jnp.concatenate([turned[k : k + 1, :], jnp.zeros((1, LANES - LON), F32)], axis=1)
        spot = jnp.where((line >= 8 * i) & (line < 8 * i + 8), roll(line_k, 8 * i), spot)
    for o in range(SLOT):
        own = small[pl.ds(o, LON, stride=SMALL), :]
        left = jnp.where(ln < 8, roll(edge, -8 * o), 0.0)
        right = jnp.where((ln >= 56) & (ln < 64), roll(edge, 40 - 8 * o), 0.0)
        for out in (up, down):
            out[OWNS + o * LON : OWNS + (o + 1) * LON, :] = own
            out[LEFTS + o * LON : LEFTS + (o + 1) * LON, :] = left
            out[RIGHTS + o * LON : RIGHTS + (o + 1) * LON, :] = right
    for out in (up, down):
        out[SPOTS:, :] = jnp.broadcast_to(spot, (8, LANES))


def unpack(bulk, grams):
    ln, rw = lanes(HALF), places(HALF)
    upper, diagonal, first = ln - HALF > rw, ln - HALF == rw, ln < HALF
    for s in range(LON):
        both = bulk[s * BULK : s * BULK + 2 * HALF, :]
        turned = jnp.transpose(both)
        ct, et = turned[:HALF], turned[HALF:]
        ct_rolled, et_rolled = roll(ct, HALF), roll(et, HALF)
        for o in range(SLOT):
            q = both[o * HALF : (o + 1) * HALF]
            d = bulk[s * BULK + 2 * HALF + o : s * BULK + 2 * HALF + o + 1, :]
            e_first, e_last = (et, et_rolled) if o == 0 else (et_rolled, et)
            c_last = ct_rolled if o == 0 else ct
            top = jnp.where(first, jnp.where(ln <= rw, roll(q, HALF), e_first), c_last)
            low = jnp.where(first | upper, q, jnp.where(diagonal, d, e_last))
            at = (o * LON + s) * LANES
            grams[at : at + HALF, :] = top
            grams[at + HALF : at + LANES, :] = low


def split(x):
    high = x.astype(jnp.bfloat16)
    rest = x - high.astype(F32)
    middle = rest.astype(jnp.bfloat16)
    low = (rest - middle.astype(F32)).astype(jnp.bfloat16)
    return jnp.concatenate([high, middle, low], axis=1)


def chosen(one_hot, parts):
    out = jnp.dot(one_hot, parts, preferred_element_type=F32)
    return out[:, :LANES] + out[:, LANES : 2 * LANES] + out[:, 2 * LANES :]


def one_hot(index, at):
    return jnp.where(index == at, 1.0, 0.0).astype(jnp.bfloat16)


def padded(x, rows):
    return jnp.concatenate([x, jnp.zeros((rows - x.shape[0], LANES), F32)], axis=0)


def left_strips(x):
    return jnp.where(lanes(x.shape[0]) < 8, roll(x, 8), 0.0)


def right_strips(x):
    ln = lanes(x.shape[0])
    return jnp.where((ln >= 56) & (ln < 64), roll(x, 56), 0.0)


def lay_out(spots, by_lane, own, sides, field, strips, low, high):
    ln = lanes(LANES)
    own_strip = jnp.where(ln < 32, jnp.where(ln >= 8, roll(own, 8), 0.0), jnp.where(ln < 56, roll(own, 56), 0.0))
    pieces = []
    for i, strip in enumerate((own_strip, sides)):
        upper = (spots[i * LANES : (i + 1) * LANES, :].astype(jnp.int32) & 8) != 0
        pieces.append(split(jnp.where(upper, roll(strip, HALF), strip)))
    own_parts = split(own)
    lane_spots = [by_lane[i * 8 : i * 8 + 1, :].astype(jnp.int32) for i in range(2)]
    p = jnp.broadcast_to(lane_spots[0], (LANES, LANES))
    for start in range(low * LEVELS, high * LEVELS, LANES):
        field[start : start + LANES, :] = chosen(one_hot(places(LANES) + start, p), own_parts)
    folded = [jnp.broadcast_to(((b >> 4) << 3) + (b & 7), (64, LANES)) for b in lane_spots]
    for start in range(low * 8, high * 8, 64):
        at = places(64) + start
        strips[start : start + 64, :] = chosen(one_hot(at, folded[0]), pieces[0]) + chosen(one_hot(at, folded[1]), pieces[1])


def adjoint(rates, source, target, first, last, height):
    before = kept = None
    for r in range(first, last + 1):
        y = source[r * height : (r + 1) * height, :]
        lat, lon = rates(r)
        t = lat * y
        a = jnp.where(lat > 0.0, t, 0.0)
        b = a - t
        s = lon * y
        e = jnp.where(lon > 0.0, s, 0.0)
        f = e - s
        if r > first + 1:
            target[(r - 1) * height : r * height, :] = kept + a
        if r > first:
            kept = y - (a + b) - (e + f) + roll(e, -1) + roll(f, 1) + before
        before = b


def tangent(rates, source, target, first, last, height):
    for r in range(first + 1, last):
        x = source[r * height : (r + 1) * height, :]
        south = source[(r - 1) * height : r * height, :]
        north = source[(r + 1) * height : (r + 2) * height, :]
        lat, lon = rates(r)
        out = x + jnp.abs(lat) * (jnp.where(lat > 0.0, south, north) - x)
        target[r * height : (r + 1) * height, :] = out + jnp.abs(lon) * (jnp.where(lon > 0.0, roll(x, 1), roll(x, -1)) - x)


def merged(field, strips, r):
    ln = lanes(8)
    t = strips[r * 8 : (r + 1) * 8, :]
    low, high = field[r * LEVELS : r * LEVELS + 8, :], field[r * LEVELS + 8 : (r + 1) * LEVELS, :]
    low = jnp.where(ln < 8, roll(t, -8), jnp.where(ln >= 120, roll(t, 72), low))
    high = jnp.where(ln < 8, roll(t, -72), jnp.where(ln >= 120, roll(t, 8), high))
    return low, high


def rates_of(below, down, up, above, start, height):
    def rates(r):
        part, r = (below, down, up, above)[r // HALO], r % HALO
        at = start + r * 2 * height
        return part[at : at + height, :], part[at + height : at + 2 * height, :]

    return rates


def steps_back(messages, fields, strips, first):
    full, narrow = rates_of(*messages, 0, LEVELS), rates_of(*messages, EDGES, 8)
    for k in range(first, first + STEPS):
        adjoint(full, *fields, k, WIDE - 1 - k, LEVELS)
        adjoint(narrow, *strips, k, WIDE - 1 - k, 8)
        fields, strips = fields[::-1], strips[::-1]
    return fields, strips


def steps_on(messages, fields, strips, first):
    full, narrow = rates_of(*messages, 0, LEVELS), rates_of(*messages, EDGES, 8)
    for k in range(first, first + STEPS):
        tangent(full, *fields, k, WIDE - 1 - k, LEVELS)
        tangent(narrow, *strips, k, WIDE - 1 - k, 8)
        fields, strips = fields[::-1], strips[::-1]
    return fields, strips


def back_and_on(where, spots, by_lane, own, sides, messages, kept, fields, strips, image):
    lay_out(spots, by_lane, own, sides, fields[0], strips[0], 0, WIDE)
    fields, strips = steps_back(messages, fields, strips, 0)
    for flag, start in ((where[1], STEPS), (where[2], HALO + ROWS)):
        for ref, height in ((fields[0], LEVELS), (strips[0], 8)):
            block = ref[start * height : (start + STEPS) * height, :]
            ref[start * height : (start + STEPS) * height, :] = jnp.where(flag == 1, 0.0, block)
    square = jnp.zeros((8, LANES), F32)
    for r in range(ROWS):
        low, high = merged(fields[0], strips[0], r + HALO)
        kept[r * LEVELS : r * LEVELS + 8, :] = low
        kept[r * LEVELS + 8 : (r + 1) * LEVELS, :] = high
        square += low * low + high * high
    fields, strips = steps_on(messages, fields, strips, STEPS)
    for r in range(ROWS):
        low, high = merged(fields[0], strips[0], r + HALO)
        image[r * LEVELS : r * LEVELS + 8, :] = low
        image[r * LEVELS + 8 : (r + 1) * LEVELS, :] = high
    mine = spots[OWN : 2 * OWN, :].astype(jnp.int32) - HALO * LEVELS
    hit = jnp.concatenate([one_hot(lanes(OWN), mine), one_hot(lanes(OWN) + LANES, mine)], axis=1)
    return jnp.sum(square, keepdims=True), chosen(hit, split(image[...]))


def weigh(seen, grams):
    column = jnp.transpose(seen)
    out = []
    for t in range(OWN):
        total = jnp.zeros((8, LANES), F32)
        for k in range(LANES // 8):
            at = t * LANES + k * 8
            total += grams[at : at + 8, :] * column[k * 8 : k * 8 + 8, t : t + 1]
        out.append(jnp.sum(total, axis=0, keepdims=True))
    return jnp.concatenate(out, axis=0)


def in_lanes(first, values):
    ln = lanes(8)
    out = jnp.zeros((8, LANES), F32)
    for i, v in enumerate(values):
        out = jnp.where(ln == first + i, v, out)
    return out


def first_half(where, below, down, up, above, spots, by_lane, kept, seen, sums, field, other, strip, other_strip, image):
    ln = lanes(8)
    b, o, a = below[SPOTS:, :] - float(ROWS * LEVELS), up[SPOTS:, :], above[SPOTS:, :] + float(ROWS * LEVELS)
    tables = (((b, 0), (o, 0), (a, 0)), ((b, 16), (o, 16), (a, 16), (b, 32), (o, 32), (a, 32)))
    for i, table in enumerate(tables):
        spot = jnp.full((8, LANES), NOWHERE, F32)
        for n, (x, at) in enumerate(table):
            spot = jnp.where((ln >= OWN * n) & (ln < OWN * (n + 1)), roll(x, OWN * n - at), spot)
        by_lane[i * 8 : i * 8 + 8, :] = spot
        spots[i * LANES : (i + 1) * LANES, :] = jnp.transpose(jnp.broadcast_to(spot[:1], (LANES, LANES)))
    parts = (below, up, above)
    own = padded(jnp.concatenate([x[OWNS:LEFTS, :] for x in parts], axis=0), LANES)
    sides = padded(jnp.concatenate([x[LEFTS:RIGHTS, :] for x in parts] + [x[RIGHTS:SPOTS, :] for x in parts], axis=0), LANES)
    messages = (below, down, up, above)
    square, rows = back_and_on(where, spots, by_lane, own, sides, messages, kept, (field, other), (strip, other_strip), image)
    seen[...] = rows
    sums[...] = in_lanes(0, [square])


def first_terms(bulk, seen, before, grams, terms, sums):
    unpack(bulk, grams)
    rows = weigh(seen[...], grams)
    terms[...] = rows
    sums[...] = before[...] + in_lanes(1, [jnp.sum(seen[...] * rows, keepdims=True)])


def stepped(x, unit):
    row = places(OWN)
    for bit in range(4):
        x = jnp.where((row & (1 << bit)) != 0, roll(x, unit << bit), x)
    return x


def second_half(where, spots, by_lane, own, left, right, below, down, up, above, grams, before, kept, terms, parcels, field, other, strip, other_strip, image):
    own = padded(own[...], LANES)
    sides = padded(jnp.concatenate([left_strips(left[...]), right_strips(right[...])], axis=0), LANES)
    messages = (below, down, up, above)
    square, seen = back_and_on(where, spots, by_lane, own, sides, messages, kept, (field, other), (strip, other_strip), image)
    rows = weigh(seen, grams)
    terms[...] = rows
    sums = before[...] + in_lanes(2, [square, jnp.sum(seen * rows, keepdims=True)])
    parcels[...] = jnp.concatenate([sums] * (parcels.shape[0] // 8), axis=0)
    mine = (lanes(OWN) >> 3) == places(OWN)
    to_left = jnp.sum(jnp.where(mine, stepped(rows, 8), 0.0), axis=0, keepdims=True)
    to_right = jnp.sum(jnp.where(mine, stepped(roll(rows, 8), 8), 0.0), axis=0, keepdims=True)
    base = where[3] * LON
    parcels[pl.ds((base + lax.rem(where[0] + 1, LON)) * 2 + 1, 1), :] = to_right
    parcels[pl.ds((base + lax.rem(where[0] + LON - 1, LON)) * 2 + 1, 1), :] = to_left


def gathered(where, parts, terms, sums, message):
    count = parts.shape[0] // 2
    sums[...] = jnp.broadcast_to(jnp.sum(parts[pl.ds(0, count, stride=2), :], axis=0, keepdims=True), sums.shape)
    base = where[3] * LON
    message[:OWN, :] = terms[...]
    message[OWN : OWN + 1, :] = parts[pl.ds((base + lax.rem(where[0] + LON - 1, LON)) * 2 + 1, 1), :]
    message[OWN + 1 : OWN + 2, :] = parts[pl.ds((base + lax.rem(where[0] + 1, LON)) * 2 + 1, 1), :]
    message[OWN + 2 :, :] = jnp.zeros((6, LANES), F32)


def finish(spots, by_lane, south, mine, north, below, down, up, above, parts, right_side, image, increment, residual, field, other, strip, other_strip):
    lists = (south, mine, north)
    own = padded(jnp.concatenate([x[:OWN, :] for x in lists], axis=0), LANES)
    ln = lanes(OWN)
    rows = [stepped(jnp.broadcast_to(x[OWN : OWN + 1, :], (OWN, LANES)), -8) for x in lists]
    lefts = [jnp.where(ln < 8, x, 0.0) for x in rows]
    rows = [stepped(jnp.broadcast_to(x[OWN + 1 : OWN + 2, :], (OWN, LANES)), -8) for x in lists]
    rights = [right_strips(x) for x in rows]
    sides = padded(jnp.concatenate(lefts + rights, axis=0), LANES)
    lay_out(spots, by_lane, own, sides, field, strip, HALO - STEPS, HALO + ROWS + STEPS)
    fields, strips = steps_back((below, down, up, above), (field, other), (strip, other_strip), STEPS)
    total = jnp.sum(parts[...], axis=0, keepdims=True)
    m0, m1, m2, m3 = (jnp.sum(jnp.where(lanes(1) == i, total, 0.0), keepdims=True) for i in range(4))
    step_0 = m0 / (m0 + m1)
    rho = m1 / m0
    spread = m2 - rho * m1
    curve = (m3 - rho * m2) - rho * (m2 - rho * m1)
    gamma = step_0 * spread / m0
    step_1 = spread / (spread + curve - gamma * spread)
    on_b = step_0 * (1.0 + step_1 * (gamma + rho))
    on_k = -step_0 * step_1
    rest_b = step_0 * ((1.0 - step_1) * rho - step_1 * gamma)
    rest_k = -step_0 * ((1.0 - step_1) + step_1 * (rho + gamma))
    rest_kk = step_0 * step_1
    on_b, on_k, rest_b, rest_k, rest_kk = (jnp.broadcast_to(v, (8, LANES)) for v in (on_b, on_k, rest_b, rest_k, rest_kk))
    for r in range(ROWS):
        for h, second in enumerate(merged(fields[0], strips[0], r + HALO)):
            at = r * LEVELS + h * 8
            b, first = right_side[at : at + 8, :], image[at : at + 8, :]
            to = pl.ds(h * 8 * ROWS + r, 8, stride=ROWS)
            increment[to, :] = on_b * b + on_k * first
            residual[to, :] = rest_b * b + rest_k * first + rest_kk * second


def shift(x, axis, step, wrap):
    count = lax.axis_size(axis)
    pairs = [(i, (i + step) % count) for i in range(count) if wrap or 0 <= i + step < count]
    return lax.ppermute(x, axis, pairs)


def spread_out(x, axes):
    return lax.all_to_all(x, axes, split_axis=0, concat_axis=0, tiled=True)


def shards(courant, obs_matrix, obs_weight, innovation, block_owner, block_row, block_count):
    lat_index = lax.axis_index(LAT)
    lat_total = lax.axis_size(LAT)
    ends = [(lat_index == at).astype(jnp.int32) for at in (0, lat_total - 1)]
    where = jnp.stack([lax.axis_index("lon"), *ends, lax.axis_index("lat_1")]).astype(jnp.int32)
    flow = courant.reshape(-1, LANES)
    owner, row, count = block_owner.reshape(-1), block_row.reshape(-1), block_count.reshape(-1)
    matrix, weight = obs_matrix[0], obs_weight[0]
    wholes = (flow, matrix, weight, innovation[0])
    (small,) = call(
        prepare,
        [(LON * SMALL, LANES)],
        (where, owner, row, count, *wholes),
        1_000_000,
        [pltpu.SMEM((CAP,), jnp.int32), pltpu.SMEM((CAP,), jnp.int32), pltpu.SMEM((1,), jnp.int32)]
        + [pltpu.VMEM(x.shape, F32) for x in wholes]
        + [pltpu.VMEM((OWN, LANES), F32), pltpu.SemaphoreType.DMA((7,))],
        [SMEM] + [pl.BlockSpec(memory_space=pltpu.HBM)] * 7,
        62,
    )
    small = spread_out(small.reshape(LON, SMALL, LANES), "lon").reshape(LON * SMALL, LANES)
    (bulk,) = call(weigh_blocks, [(LON * BULK, LANES)], (owner, row, count, matrix, weight), 4_000_000)
    bulk = spread_out(bulk.reshape(LON, BULK, LANES), "lon").reshape(LON * BULK, LANES)
    up, down = call(arrange, [(MESSAGE, LANES)] * 2, (where, flow, small), 2_000_000)
    below, above = shift(up, LAT, 1, False), shift(down, LAT, -1, False)
    messages = (below, down, up, above)
    cells, listed = (ROWS * LEVELS, LANES), (OWN, LANES)
    work = [pltpu.VMEM((WIDE * LEVELS, LANES), F32)] * 2 + [pltpu.VMEM((WIDE * 8, LANES), F32)] * 2
    image = pltpu.VMEM(cells, F32)
    spots, by_lane, right_side, seen, sums = call(
        first_half, [(2 * LANES, LANES), (16, LANES), cells, listed, (8, LANES)], (where, *messages), 4_000_000, work + [image]
    )
    grams, terms, sums = call(first_terms, [(OWN * LANES, LANES), listed, (8, LANES)], (bulk, seen, sums), 2_000_000)
    own = jnp.concatenate([shift(terms, LAT, 1, False), terms, shift(terms, LAT, -1, False)], axis=0)
    sides = (shift(own, "lon", 1, True), shift(own, "lon", -1, True))
    plane = lax.axis_size(("lat_1", "lon"))
    towers = lax.axis_size(("lat_0", "lat_2"))
    kept, terms, parcels = call(
        second_half,
        [cells, listed, (plane * 2, LANES)],
        (where, spots, by_lane, own, *sides, *messages, grams, sums),
        4_000_000,
        work + [image],
    )
    parcels = spread_out(parcels.reshape(plane, 2, LANES), ("lat_1", "lon")).reshape(plane * 2, LANES)
    sums, mine = call(gathered, [(towers, LANES), (OWN + 8, LANES)], (where, parcels, terms), 10_000)
    south, north = shift(mine, LAT, 1, False), shift(mine, LAT, -1, False)
    parts = spread_out(sums.reshape(towers, 1, LANES), ("lat_0", "lat_2")).reshape(towers, LANES)
    increment, residual = call(
        finish, [cells, cells], (spots, by_lane, south, mine, north, *messages, parts, right_side, kept), 2_000_000, work
    )
    shape = courant.shape[1:]
    return increment.reshape(shape), residual.reshape(shape)


def solution(mesh):
    torus = Mesh(
        mesh.devices.reshape(-1, 4, 2, mesh.shape["lon"]), ("lat_0", "lat_1", "lat_2", "lon")
    )
    placed = (
        P(None, None, LAT, "lon"),
        P(LAT, "lon", None, None),
        P(LAT, "lon", None),
        P(LAT, "lon", None),
        P(LAT, "lon", None),
        P(LAT, "lon"),
        P(LAT, "lon"),
    )
    return jax.shard_map(
        shards,
        mesh=torus,
        in_specs=placed,
        out_specs=(P(None, LAT, "lon"), P(None, LAT, "lon")),
        check_vma=False,
    )
```

time: 134 us -> 120 us (0.90)
  blocking collectives: 0 us -> 16.7 us
  starting transfers between devices: 82.2 us -> 66.1 us
  waiting for transfers between devices: 32.9 us -> 16.9 us
  Pallas kernels: 14.2 us -> 16 us
  local copies, waits for them, and re-layouts: 2.69 us -> 1.31 us
    all_to_all x0 -> x1, blocking collectives: none -> 16.7 us  [spread_out(): return lax.all_to_all(x, axes, split_axis=0, concat_axis=0, tiled=True)]
    all_to_all x4 -> x3, starting transfers between devices: 45.5 us -> 31.9 us  [spread_out(): return lax.all_to_all(x, axes, split_axis=0, concat_axis=0, tiled=True)]
    all_to_all x4 -> x3, waiting for transfers between devices: 22.6 us -> 10.9 us  [spread_out(): return lax.all_to_all(x, axes, split_axis=0, concat_axis=0, tiled=True)]
    ppermute x10 -> x8, waiting for transfers between devices: 10.3 us -> 6.04 us  [shift(): return lax.ppermute(x, axis, pairs)]
    ppermute x10 -> x8, starting transfers between devices: 36.7 us -> 34.1 us  [shift(): return lax.ppermute(x, axis, pairs)]
    pallas_call x7 -> x8, Pallas kernels: 14.2 us -> 16 us  [call(): pl.pallas_call(body, out_shape=[jax.ShapeDtypeStruct(s, F32) for s in out...]
    unnamed x18 -> x14, local copies, waits for them, and re-layouts: 2.68 us -> 1.31 us
  transfers between devices with their start and end apart: 14 -> 11, of which waited for: 7 -> 6; matrix products, arithmetic and copies ran while one was open for 0% -> 0% of each run, Pallas kernels for 2% -> 5%
where the time goes in v3:
time: 120 us; the launch traced here: 119 us
  starting transfers between devices  66.1 us (55%)
  waiting for transfers between devices  16.9 us (14%)
  blocking collectives  16.7 us (14%)
  Pallas kernels  16 us (13%)
  between operations  1.5 us (1%)
  local copies, waits for them, and re-layouts  1.31 us (1%)
    ppermute x8, starting transfers between devices, shift(): return lax.ppermute(x, axis, pairs)  34.1 us
    all_to_all x3, starting transfers between devices, spread_out(): return lax.all_to_all(x, axes, split_axis=0, concat_axis=0, tiled=True)  31.9 us
    all_to_all x1, blocking collectives, spread_out(): return lax.all_to_all(x, axes, split_axis=0, concat_axis=0, tiled=True)  16.7 us
    pallas_call x8, Pallas kernels, call(): pl.pallas_call(body, out_shape=[jax.ShapeDtypeStruct(s, F32) for s in out...  16 us
    all_to_all x3, waiting for transfers between devices, spread_out(): return lax.all_to_all(x, axes, split_axis=0, concat_axis=0, tiled=True)  10.9 us
    ppermute x8, waiting for transfers between devices, shift(): return lax.ppermute(x, axis, pairs)  6.04 us
  transfers between devices with their start and end apart: 11, of which 6 were waited for; matrix products, arithmetic and copies ran while one was open for 0% of the time, Pallas kernels for 5%

profile of v3, /device:TPU:1, one launch (start us, length us, event | category | flops | bytes accessed | tf_op | source)
XLA Modules:
  0.0 119.1 jit_solution(2030143817895184766)
XLA Ops:
  1.3 0.7 pad_add_fusion.where
  1.9 0.0 copy-start
  1.9 3.2 %prepare.1 = f32[320,128]{1,0:T(8,128)} custom-call(s32[4]{0:T(128)} %pad_add_fusion.where, s32[8]{0:T(128)} %bitcast.36, s32[8]{0:T(128)} %bitcast.38, s32[1]{0:T(128)} %bitcast.23.count_at, f32[512,128]{1,0:T(8,128)} %bitcast.28, f32[8,128,128]{2,1,0:T(8,128)} %bitcast.26, f32[8,128]{1,0:T(8,128)} %bitcast.34, f32[8,128]{1,0:T(8,128)} %bitcast.41), custom_call_target="tpu_custom_call" | custom-call | flops 1000000 | tf_op jit(solution)/shard_map/prepare/pallas_call | solution.py:52
  5.1 0.0 copy-start.3
  5.1 7.6 %all-to-all-start = ((f32[8,40,128]{2,1,0:T(8,128)}), f32[8,40,128]{2,1,0:T(8,128)S(1)}, u32[]{:S(2)}, u32[]{:S(2)}) async-start(f32[8,40,128]{2,1,0:T(8,128)} %bitcast.40), calls=%async_computation | async-start | bytes 327680 | tf_op jit(solution)/shard_map/all_to_all | solution.py:458
  12.8 0.0 copy-start.4
  12.8 0.0 copy-start.5
  12.8 0.0 copy-done
  12.8 0.0 copy-done.3
  12.8 0.6 copy-done.4
  13.4 0.0 copy-done.5
  13.4 2.1 %weigh_blocks.1 = f32[1088,128]{1,0:T(8,128)} custom-call(s32[8]{0:T(128)S(1)} %bitcast.37, s32[8]{0:T(128)S(1)} %bitcast.39, s32[1]{0:T(128)} %bitcast.24.count, f32[8,128,128]{2,1,0:T(8,128)S(1)} %bitcast.27, f32[8,128]{1,0:T(8,128)S(1)} %bitcast.35), custom_call_target="tpu_custom_call" | custom-call | flops 4000000 | tf_op jit(solution)/shard_map/weigh_blocks/pallas_call | solution.py:52
  15.5 5.5 %all-to-all-done = f32[8,40,128]{2,1,0:T(8,128)S(1)} async-done(((f32[8,40,128]{2,1,0:T(8,128)}), f32[8,40,128]{2,1,0:T(8,128)S(1)}, u32[]{:S(2)}, u32[]{:S(2)}) %all-to-all-start) | async-done | bytes 163872 | tf_op jit(solution)/shard_map/all_to_all | solution.py:458
  21.0 0.0 copy-start.1
  21.1 3.7 %all-to-all-start.1 = ((f32[8,136,128]{2,1,0:T(8,128)}), f32[8,136,128]{2,1,0:T(8,128)S(1)}, u32[]{:S(2)}, u32[]{:S(2)}) async-start(f32[8,136,128]{2,1,0:T(8,128)} %bitcast.13), calls=%async_computation.1 | async-start | bytes 1114112 | tf_op jit(solution)/shard_map/all_to_all | solution.py:458
  24.7 0.0 copy-start.2
  24.7 0.0 copy-done.1
  24.7 0.6 copy-done.2
  25.4 0.9 arrange.1
  26.3 5.5 %collective-permute-start = (f32[440,128]{1,0:T(8,128)S(1)}, f32[440,128]{1,0:T(8,128)S(1)}, u32[]{:S(2)}, u32[]{:S(2)}) collective-permute-start(f32[440,128]{1,0:T(8,128)S(1)} %get-tuple-element.19.up), channel_id=1, source_target_pairs={{0,8},{8,16},{16,24},{24,32},{32,40},{40,48},{48,56},{56,64},{64,7... | collective-permute-start | bytes 675848 | tf_op jit(solution)/shard_map/ppermute | solution.py:454
  31.8 9.5 %collective-permute-start.1 = (f32[440,128]{1,0:T(8,128)S(1)}, f32[440,128]{1,0:T(8,128)S(1)}, u32[]{:S(2)}, u32[]{:S(2)}) collective-permute-start(f32[440,128]{1,0:T(8,128)S(1)} %get-tuple-element.20.down), channel_id=1, source_target_pairs={{8,0},{16,8},{24,16},{32,24},{40,32},{48,40},{56,48},{64,56},{72,6... | collective-permute-start | bytes 675848 | tf_op jit(solution)/shard_map/ppermute | solution.py:454
  41.3 0.0 collective-permute-done.below
  41.3 1.1 collective-permute-done.1.above
  42.4 2.5 %first_half.1 = (f32[256,128]{1,0:T(8,128)S(1)}, f32[16,128]{1,0:T(8,128)S(1)}, f32[256,128]{1,0:T(8,128)S(1)}, f32[16,128]{1,0:T(8,128)S(1)}, f32[8,128]{1,0:T(8,128)S(1)}) custom-call(s32[4]{0:T(128)S(1)} %copy-done.2, f32[440,128]{1,0:T(8,128)S(1)} %collective-permute-done.below, f32[440,128]{1,0:T(8,128)S(1)} %get-tuple-element.20.down, ...), custom_call_target="tpu_custom_call" | custom-call | flops 4000000 | tf_op jit(solution)/shard_map/first_half/pallas_call | solution.py:52
  44.9 0.0 all-to-all-done.1
  44.9 1.0 first_terms.1
  45.9 1.9 %collective-permute-start.2 = (f32[16,128]{1,0:T(8,128)S(1)}, f32[16,128]{1,0:T(8,128)S(1)}, u32[]{:S(2)}, u32[]{:S(2)}) collective-permute-start(f32[16,128]{1,0:T(8,128)S(1)} %get-tuple-element.25), channel_id=1, source_target_pairs={{0,8},{8,16},{16,24},{24,32},{32,40},{40,48},{48,56},{56,64},{64,7... | collective-permute-start | bytes 24584 | tf_op jit(solution)/shard_map/ppermute | solution.py:454
  47.8 6.4 %collective-permute-start.3 = (f32[16,128]{1,0:T(8,128)S(1)}, f32[16,128]{1,0:T(8,128)S(1)}, u32[]{:S(2)}, u32[]{:S(2)}) collective-permute-start(f32[16,128]{1,0:T(8,128)S(1)} %get-tuple-element.25), channel_id=1, source_target_pairs={{8,0},{16,8},{24,16},{32,24},{40,32},{48,40},{56,48},{64,56},{72,6... | collective-permute-start | bytes 24584 | tf_op jit(solution)/shard_map/ppermute | solution.py:454
  54.2 0.0 collective-permute-done.2
  54.3 0.8 collective-permute-done.3
  55.1 2.5 %collective-permute-start.5 = (f32[48,128]{1,0:T(8,128)S(1)}, f32[48,128]{1,0:T(8,128)S(1)}, u32[]{:S(2)}, u32[]{:S(2)}) collective-permute-start(f32[48,128]{1,0:T(8,128)S(1)} %constant_dynamic-update-slice_fusion.own), channel_id=1, source_target_pairs={{0,7},{1,0},{2,1},{3,2},{4,3},{5,4},{6,5},{7,6},{8,15},{9,8},{10,9... | collective-permute-start | bytes 73736 | tf_op jit(solution)/shard_map/ppermute | solution.py:454
  57.6 2.7 %collective-permute-start.4 = (f32[48,128]{1,0:T(8,128)S(1)}, f32[48,128]{1,0:T(8,128)S(1)}, u32[]{:S(2)}, u32[]{:S(2)}) collective-permute-start(f32[48,128]{1,0:T(8,128)S(1)} %constant_dynamic-update-slice_fusion.own), channel_id=1, source_target_pairs={{0,1},{1,2},{2,3},{3,4},{4,5},{5,6},{6,7},{7,0},{8,9},{9,10},{10,1... | collective-permute-start | bytes 73736 | tf_op jit(solution)/shard_map/ppermute | solution.py:454
  60.3 0.0 collective-permute-done.5.right
  60.4 3.4 %collective-permute-done.4.left = f32[48,128]{1,0:T(8,128)S(1)} collective-permute-done((f32[48,128]{1,0:T(8,128)S(1)}, f32[48,128]{1,0:T(8,128)S(1)}, u32[]{:S(2)}, u32[]{:S(2)}) %collective-permute-start.4) | collective-permute-done | bytes 24608 | tf_op jit(solution)/shard_map/ppermute | solution.py:454
  63.7 3.3 %second_half.1 = (f32[256,128]{1,0:T(8,128)S(1)}, f32[16,128]{1,0:T(8,128)S(1)}, f32[64,128]{1,0:T(8,128)S(1)}) custom-call(s32[4]{0:T(128)S(1)} %copy-done.2, f32[256,128]{1,0:T(8,128)S(1)} %get-tuple-element.21.spots, f32[16,128]{1,0:T(8,128)S(1)} %get-tuple-element.22.by_lane, f32[48,128]{1,0:T(8,128)S(1)} %constant_dynamic-update-slice_fusion.own, ...), custom_call_target="tpu_custom_call" | custom-call | flops 4000000 | tf_op jit(solution)/shard_map/second_half/pallas_call | solution.py:52
  67.1 16.7 %all_to_all.20 = f32[32,2,128]{2,1,0:T(2,128)S(1)} all-to-all(f32[32,2,128]{2,1,0:T(2,128)S(1)} %bitcast.33), channel_id=1, replica_groups=mesh['lat_0'=16,'lat_1'=4,'lat_2'=2,'lon'=8] {'lat_1','lon'}, dimensions={0} | all-to-all | bytes 65536 | tf_op jit(solution)/shard_map/all_to_all | solution.py:458
  83.8 1.2 gathered.1
  84.9 20.6 %all-to-all-start.3 = ((f32[32,1,128]{2,1,0:T(1,128)}), f32[32,1,128]{2,1,0:T(1,128)S(1)}, u32[]{:S(2)}, u32[]{:S(2)}) async-start(f32[32,1,128]{2,1,0:T(1,128)} %bitcast.18), calls=%async_computation.3 | async-start | bytes 32768 | tf_op jit(solution)/shard_map/all_to_all | solution.py:458
  105.5 2.1 %collective-permute-start.7 = (f32[24,128]{1,0:T(8,128)S(1)}, f32[24,128]{1,0:T(8,128)S(1)}, u32[]{:S(2)}, u32[]{:S(2)}) collective-permute-start(f32[24,128]{1,0:T(8,128)S(1)} %get-tuple-element.30.mine), channel_id=1, source_target_pairs={{8,0},{16,8},{24,16},{32,24},{40,32},{48,40},{56,48},{64,56},{72,6... | collective-permute-start | bytes 36872 | tf_op jit(solution)/shard_map/ppermute | solution.py:454
  107.7 3.4 %collective-permute-start.6 = (f32[24,128]{1,0:T(8,128)S(1)}, f32[24,128]{1,0:T(8,128)S(1)}, u32[]{:S(2)}, u32[]{:S(2)}) collective-permute-start(f32[24,128]{1,0:T(8,128)S(1)} %get-tuple-element.30.mine), channel_id=1, source_target_pairs={{0,8},{8,16},{16,24},{24,32},{32,40},{40,48},{48,56},{56,64},{64,7... | collective-permute-start | bytes 36872 | tf_op jit(solution)/shard_map/ppermute | solution.py:454
  111.1 0.0 collective-permute-done.7.north
  111.1 0.8 collective-permute-done.6.south
  111.9 5.4 %all-to-all-done.3 = f32[32,1,128]{2,1,0:T(1,128)S(1)} async-done(((f32[32,1,128]{2,1,0:T(1,128)}), f32[32,1,128]{2,1,0:T(1,128)S(1)}, u32[]{:S(2)}, u32[]{:S(2)}) %all-to-all-start.3) | async-done | bytes 16416 | tf_op jit(solution)/shard_map/all_to_all | solution.py:458
  117.3 1.8 %finish.1 = (f32[256,128]{1,0:T(8,128)}, f32[256,128]{1,0:T(8,128)}) custom-call(f32[256,128]{1,0:T(8,128)S(1)} %get-tuple-element.21.spots, f32[16,128]{1,0:T(8,128)S(1)} %get-tuple-element.22.by_lane, f32[24,128]{1,0:T(8,128)S(1)} %collective-permute-done.6.south, f32[24,128]{1,0:T(8,128)S(1)} %get-tuple-element.30.mine, ...), custom_call_target="tpu_custom_call" | custom-call | flops 2000000 | tf_op jit(solution)/shard_map/finish/pallas_call | solution.py:52
  (3 shorter events, 0.0 us)
Async XLA Ops:
  1.9 10.8 %copy-start = (f32[1,8,128,128]{3,2,1,0:T(8,128)S(1)}, f32[1,8,128,128]{3,2,1,0:T(8,128)}, u32[]{:S(2)}) copy-start(f32[1,8,128,128]{3,2,1,0:T(8,128)} %param.8) | copy-start | bytes 1572868
  5.1 7.7 %copy-start.3 = (f32[1,8,128]{2,1,0:T(8,128)S(1)}, f32[1,8,128]{2,1,0:T(8,128)}, u32[]{:S(2)}) copy-start(f32[1,8,128]{2,1,0:T(8,128)} %param.9) | copy-start | bytes 12292
  5.1 15.9 %all-to-all-start = ((f32[8,40,128]{2,1,0:T(8,128)}), f32[8,40,128]{2,1,0:T(8,128)S(1)}, u32[]{:S(2)}, u32[]{:S(2)}) async-start(f32[8,40,128]{2,1,0:T(8,128)} %bitcast.40), calls=%async_computation | async-start | bytes 327680 | tf_op jit(solution)/shard_map/all_to_all | solution.py:458
  12.8 0.7 copy-start.4
  12.8 0.7 copy-start.5
  21.0 3.7 %copy-start.1 = (f32[2,16,16,128]{3,2,1,0:T(8,128)S(1)}, f32[2,16,16,128]{3,2,1,0:T(8,128)}, u32[]{:S(2)}) copy-start(f32[2,16,16,128]{3,2,1,0:T(8,128)} %param.7) | copy-start | bytes 786436
  21.1 23.8 %all-to-all-start.1 = ((f32[8,136,128]{2,1,0:T(8,128)}), f32[8,136,128]{2,1,0:T(8,128)S(1)}, u32[]{:S(2)}, u32[]{:S(2)}) async-start(f32[8,136,128]{2,1,0:T(8,128)} %bitcast.13), calls=%async_computation.1 | async-start | bytes 1114112 | tf_op jit(solution)/shard_map/all_to_all | solution.py:458
  24.7 0.7 copy-start.2
  26.3 15.0 %collective-permute-start = (f32[440,128]{1,0:T(8,128)S(1)}, f32[440,128]{1,0:T(8,128)S(1)}, u32[]{:S(2)}, u32[]{:S(2)}) collective-permute-start(f32[440,128]{1,0:T(8,128)S(1)} %get-tuple-element.19.up), channel_id=1, source_target_pairs={{0,8},{8,16},{16,24},{24,32},{32,40},{40,48},{48,56},{56,64},{64,7... | collective-permute-start | bytes 675848 | tf_op jit(solution)/shard_map/ppermute | solution.py:454
  31.8 10.6 %collective-permute-start.1 = (f32[440,128]{1,0:T(8,128)S(1)}, f32[440,128]{1,0:T(8,128)S(1)}, u32[]{:S(2)}, u32[]{:S(2)}) collective-permute-start(f32[440,128]{1,0:T(8,128)S(1)} %get-tuple-element.20.down), channel_id=1, source_target_pairs={{8,0},{16,8},{24,16},{32,24},{40,32},{48,40},{56,48},{64,56},{72,6... | collective-permute-start | bytes 675848 | tf_op jit(solution)/shard_map/ppermute | solution.py:454
  45.9 8.4 %collective-permute-start.2 = (f32[16,128]{1,0:T(8,128)S(1)}, f32[16,128]{1,0:T(8,128)S(1)}, u32[]{:S(2)}, u32[]{:S(2)}) collective-permute-start(f32[16,128]{1,0:T(8,128)S(1)} %get-tuple-element.25), channel_id=1, source_target_pairs={{0,8},{8,16},{16,24},{24,32},{32,40},{40,48},{48,56},{56,64},{64,7... | collective-permute-start | bytes 24584 | tf_op jit(solution)/shard_map/ppermute | solution.py:454
  47.8 7.2 %collective-permute-start.3 = (f32[16,128]{1,0:T(8,128)S(1)}, f32[16,128]{1,0:T(8,128)S(1)}, u32[]{:S(2)}, u32[]{:S(2)}) collective-permute-start(f32[16,128]{1,0:T(8,128)S(1)} %get-tuple-element.25), channel_id=1, source_target_pairs={{8,0},{16,8},{24,16},{32,24},{40,32},{48,40},{56,48},{64,56},{72,6... | collective-permute-start | bytes 24584 | tf_op jit(solution)/shard_map/ppermute | solution.py:454
  55.1 5.3 %collective-permute-start.5 = (f32[48,128]{1,0:T(8,128)S(1)}, f32[48,128]{1,0:T(8,128)S(1)}, u32[]{:S(2)}, u32[]{:S(2)}) collective-permute-start(f32[48,128]{1,0:T(8,128)S(1)} %constant_dynamic-update-slice_fusion.own), channel_id=1, source_target_pairs={{0,7},{1,0},{2,1},{3,2},{4,3},{5,4},{6,5},{7,6},{8,15},{9,8},{10,9... | collective-permute-start | bytes 73736 | tf_op jit(solution)/shard_map/ppermute | solution.py:454
  57.6 6.1 %collective-permute-start.4 = (f32[48,128]{1,0:T(8,128)S(1)}, f32[48,128]{1,0:T(8,128)S(1)}, u32[]{:S(2)}, u32[]{:S(2)}) collective-permute-start(f32[48,128]{1,0:T(8,128)S(1)} %constant_dynamic-update-slice_fusion.own), channel_id=1, source_target_pairs={{0,1},{1,2},{2,3},{3,4},{4,5},{5,6},{6,7},{7,0},{8,9},{9,10},{10,1... | collective-permute-start | bytes 73736 | tf_op jit(solution)/shard_map/ppermute | solution.py:454
  84.9 32.3 %all-to-all-start.3 = ((f32[32,1,128]{2,1,0:T(1,128)}), f32[32,1,128]{2,1,0:T(1,128)S(1)}, u32[]{:S(2)}, u32[]{:S(2)}) async-start(f32[32,1,128]{2,1,0:T(1,128)} %bitcast.18), calls=%async_computation.3 | async-start | bytes 32768 | tf_op jit(solution)/shard_map/all_to_all | solution.py:458
  105.5 5.6 %collective-permute-start.7 = (f32[24,128]{1,0:T(8,128)S(1)}, f32[24,128]{1,0:T(8,128)S(1)}, u32[]{:S(2)}, u32[]{:S(2)}) collective-permute-start(f32[24,128]{1,0:T(8,128)S(1)} %get-tuple-element.30.mine), channel_id=1, source_target_pairs={{8,0},{16,8},{24,16},{32,24},{40,32},{48,40},{56,48},{64,56},{72,6... | collective-permute-start | bytes 36872 | tf_op jit(solution)/shard_map/ppermute | solution.py:454
  107.7 4.2 %collective-permute-start.6 = (f32[24,128]{1,0:T(8,128)S(1)}, f32[24,128]{1,0:T(8,128)S(1)}, u32[]{:S(2)}, u32[]{:S(2)}) collective-permute-start(f32[24,128]{1,0:T(8,128)S(1)} %get-tuple-element.30.mine), channel_id=1, source_target_pairs={{0,8},{8,16},{16,24},{24,32},{32,40},{40,48},{48,56},{56,64},{64,7... | collective-permute-start | bytes 36872 | tf_op jit(solution)/shard_map/ppermute | solution.py:454

commit v4 on v3

v4 whole, which is shorter than its diff:
```python
import jax
import jax.numpy as jnp
from jax import lax
from jax.experimental import pallas as pl
from jax.experimental.pallas import tpu as pltpu
from jax.sharding import Mesh
from jax.sharding import PartitionSpec as P

LAT = ("lat_0", "lat_1", "lat_2")
LEVELS = 16
ROWS = 16
LANES = 128
CAP = 8
SLOT = 2
STEPS = 4
HALO = 2 * STEPS
WIDE = ROWS + 2 * HALO
LON = 8
HALF = LANES // 2
OWN = LON * SLOT
NEAR = 3 * OWN
BULK = 2 * HALF + 8
LIST = BULK + 8
PARCEL = LIST + 32
EDGE = HALO * 2 * LEVELS
STRIP = HALO * 2 * 8
LEFTS = STRIP + OWN
RIGHTS = LEFTS + OWN
SPOTS = RIGHTS + OWN
MESSAGE = SPOTS + 8
HERALD = OWN + 8
NOWHERE = -4096.0
HIGHEST = lax.Precision.HIGHEST
F32 = jnp.float32
VMEM = pl.BlockSpec(memory_space=pltpu.VMEM)
SMEM = pl.BlockSpec(memory_space=pltpu.SMEM)


def lanes(rows):
    return lax.broadcasted_iota(jnp.int32, (rows, LANES), 1)


def places(rows):
    return lax.broadcasted_iota(jnp.int32, (rows, LANES), 0)


def roll(x, shift):
    shift %= LANES
    return pltpu.roll(x, shift, axis=1) if shift else x


def call(body, outs, args, flops, scratch=(), specs=None, room=24):
    return pl.pallas_call(
        body,
        out_shape=[jax.ShapeDtypeStruct(s, F32) for s in outs],
        in_specs=specs or [SMEM if a.dtype == jnp.int32 else VMEM for a in args],
        out_specs=[VMEM] * len(outs),
        scratch_shapes=list(scratch),
        compiler_params=pltpu.CompilerParams(vmem_limit_bytes=room << 20),
        cost_estimate=pl.CostEstimate(flops=flops, bytes_accessed=0, transcendentals=0),
        name=body.__name__,
    )(*args)


def turns_of(owners):
    return [sum([(o == owners[j]).astype(jnp.int32) for o in owners[:j]], jnp.int32(0)) for j in range(CAP)]


def packed_edges(pick, shift):
    ln = lanes(8)
    out = jnp.zeros((8, LANES), F32)
    for k in range(8):
        low, high = pick(k)
        out = jnp.where((ln >= 16 * k) & (ln < 16 * k + 8), roll(low, 16 * k + shift), out)
        out = jnp.where((ln >= 16 * k + 8) & (ln < 16 * k + 16), roll(high, 16 * k + 8 + shift), out)
    return out


def weigh_blocks(owners, turns, count, matrix, weight, parcels):
    ln, rw = lanes(HALF), places(HALF)
    for j in range(CAP):
        block = matrix[j]
        scaled = jnp.transpose(block) * jnp.where(j < count[0], weight[j : j + 1, :], 0.0)
        gram = jnp.dot(scaled, block, precision=HIGHEST, preferred_element_type=F32)
        top, low = gram[:HALF], gram[HALF:]
        packed = jnp.where((ln >= HALF) & (ln - HALF <= rw), roll(top, HALF), low)
        diagonal = jnp.sum(jnp.where(ln - HALF == rw, low, 0.0), axis=0, keepdims=True)
        at = owners[j] * PARCEL + turns[j] * HALF
        parcels[pl.ds(pl.multiple_of(at, 8), HALF), :] = packed
        parcels[pl.ds(owners[j] * PARCEL + 2 * HALF + turns[j], 1), :] = diagonal


def prepare(owner_at, row_at, count_at, flow_at, matrix_at, weight_at, innovation_at, parcels, to_core, to_inter, owner, row, count, flow, matrix, weight, innovation, lists, sems):
    pairs = ((owner_at, owner), (row_at, row), (count_at, count), (flow_at, flow), (weight_at, weight), (innovation_at, innovation), (matrix_at, matrix))
    copies = [pltpu.make_async_copy(a, b, sems.at[i]) for i, (a, b) in enumerate(pairs)]
    for copy in copies:
        copy.start()
    for d in range(LON):
        parcels[d * PARCEL : d * PARCEL + BULK, :] = jnp.zeros((BULK, LANES), F32)
    lists[...] = jnp.zeros(lists.shape, F32)
    me = lax.axis_index("lon")
    even = lax.axis_index("lat_2") == 0
    to_right = lax.rem(me + 1, LON) * PARCEL + LIST
    to_left = lax.rem(me + LON - 1, LON) * PARCEL + LIST
    copies[3].wait()
    for f in range(2):
        for g in range(2):

            def pick(k, f=f, g=g):
                at = f * LEVELS * ROWS + g * 8 + k
                return flow[pl.ds(at, 8, stride=ROWS), :], flow[pl.ds(at + 8 * ROWS, 8, stride=ROWS), :]

            at = (f * 2 + g) * 8
            parcels[pl.ds(pl.multiple_of(to_right + at, 8), 8), :] = packed_edges(pick, 8)
            parcels[pl.ds(pl.multiple_of(to_left + at, 8), 8), :] = packed_edges(pick, 0)
        for i in range(HALO):
            for h in range(2):
                at = f * LEVELS * ROWS + h * 8 * ROWS + i
                up, down = flow[pl.ds(at + ROWS - HALO, 8, stride=ROWS), :], flow[pl.ds(at, 8, stride=ROWS), :]
                at = (i * 2 + f) * LEVELS + h * 8
                to_core[at : at + 8, :] = jnp.where(even, up, down)
                to_inter[at : at + 8, :] = jnp.where(even, down, up)
    for i in (0, 1, 2, 4, 5, 6):
        copies[i].wait()
    owners = [owner[j] for j in range(CAP)]
    turns = turns_of(owners)
    column = jnp.transpose(weight[...] * innovation[...])
    ln = lanes(8)
    named = jnp.full((8, LANES), NOWHERE, F32)
    for j in range(CAP):
        live = j < count[0]
        total = jnp.zeros((8, LANES), F32)
        for k in range(LANES // 8):
            total += matrix[j, k * 8 : k * 8 + 8, :] * column[k * 8 : k * 8 + 8, j : j + 1]
        slot = owners[j] * SLOT + turns[j]
        lists[pl.ds(slot, 1), :] = jnp.where(live, jnp.sum(total, axis=0, keepdims=True), 0.0)
        place = jnp.where(live, (lax.rem(row[j], ROWS) + HALO) * LEVELS + lax.div(row[j], ROWS), int(NOWHERE)).astype(F32)
        named = jnp.where(ln == slot, place, named)
    weigh_blocks(owners, turns, count, matrix, weight, parcels)
    named = jnp.where(ln < OWN, named, roll(named, OWN))
    line = lanes(1)
    for d in range(LON):
        left, right = 2 * (d - 1) % OWN, 2 * (d + 1) % OWN
        at = d * PARCEL + BULK
        parcels[at : at + 2, :] = lists[2 * d : 2 * d + 2, :]
        edge = jnp.where(line < 8, roll(lists[left : left + 1, :], 8), roll(lists[left + 1 : left + 2, :], 16))
        edge = jnp.where(line < 16, edge, jnp.where(line < 24, roll(lists[right : right + 1, :], 16), roll(lists[right + 1 : right + 2, :], 24)))
        parcels[at + 2 : at + 3, :] = edge
        parcels[at + 3 : at + 4, :] = roll(named, -left)[:1]


def arrange(flow, parcels, core, inter, wide, strips, to_core, to_inter):
    ln = lanes(8)
    me = lax.axis_index("lon")
    even = lax.axis_index("lat_2") == 0
    wide[:EDGE, :] = jnp.where(even, inter[...], core[...])
    wide[EDGE + ROWS * 2 * LEVELS :, :] = jnp.where(even, core[...], inter[...])
    from_left = lax.rem(me + LON - 1, LON) * PARCEL + LIST
    from_right = lax.rem(me + 1, LON) * PARCEL + LIST
    for f in range(2):
        for g in range(2):
            at = (f * 2 + g) * 8
            left = parcels[pl.ds(pl.multiple_of(from_left + at, 8), 8), :]
            right = parcels[pl.ds(pl.multiple_of(from_right + at, 8), 8), :]
            for k in range(8):
                at = f * LEVELS * ROWS + g * 8 + k
                low, high = flow[pl.ds(at, 8, stride=ROWS), :], flow[pl.ds(at + 8 * ROWS, 8, stride=ROWS), :]
                at = EDGE + ((g * 8 + k) * 2 + f) * LEVELS
                wide[at : at + 8, :] = low
                wide[at + 8 : at + 16, :] = high
                a = jnp.where(ln < 8, roll(left, -16 * k), jnp.where(ln < 32, roll(low, 8), jnp.where(ln < 56, roll(low, 56), roll(right, 56 - 16 * k))))
                b = jnp.where(ln < 72, roll(left, 56 - 16 * k), jnp.where(ln < 96, roll(high, 72), jnp.where(ln < 120, roll(high, 120), roll(right, 112 - 16 * k))))
                strip = jnp.where(ln < HALF, a, b)
                at = ((g * 8 + k) * 2 + f) * 8
                strips[at : at + 8, :] = strip
    lower, upper = strips[:STRIP, :], strips[STRIP:, :]
    to_core[:STRIP, :] = jnp.where(even, upper, lower)
    to_inter[:STRIP, :] = jnp.where(even, lower, upper)
    edge = parcels[pl.ds(BULK + 2, LON, stride=PARCEL), :]
    named = parcels[pl.ds(BULK + 3, LON, stride=PARCEL), :]
    turned = jnp.transpose(named)
    spot = jnp.full((1, LANES), NOWHERE, F32)
    line = lanes(1)
    for i, k in enumerate((2, 3, 0, 1, 4, 5)):
        line_k = jnp.concatenate([turned[k : k + 1, :], jnp.zeros((1, LANES - LON), F32)], axis=1)
        spot = jnp.where((line >= 8 * i) & (line < 8 * i + 8), roll(line_k, 8 * i), spot)
    for o in range(SLOT):
        own = parcels[pl.ds(BULK + o, LON, stride=PARCEL), :]
        left = jnp.where(ln < 8, roll(edge, -8 * o), 0.0)
        right = jnp.where((ln >= 56) & (ln < 64), roll(edge, 40 - 8 * o), 0.0)
        for out in (to_core, to_inter):
            out[STRIP + o * LON : STRIP + (o + 1) * LON, :] = own
            out[LEFTS + o * LON : LEFTS + (o + 1) * LON, :] = left
            out[RIGHTS + o * LON : RIGHTS + (o + 1) * LON, :] = right
    for out in (to_core, to_inter):
        out[SPOTS:, :] = jnp.broadcast_to(spot, (8, LANES))


def unpack(parcels, grams):
    ln, rw = lanes(HALF), places(HALF)
    upper, diagonal, first = ln - HALF > rw, ln - HALF == rw, ln < HALF
    for s in range(LON):
        both = parcels[s * PARCEL : s * PARCEL + 2 * HALF, :]
        turned = jnp.transpose(both)
        ct, et = turned[:HALF], turned[HALF:]
        ct_rolled, et_rolled = roll(ct, HALF), roll(et, HALF)
        for o in range(SLOT):
            q = both[o * HALF : (o + 1) * HALF]
            d = parcels[s * PARCEL + 2 * HALF + o : s * PARCEL + 2 * HALF + o + 1, :]
            e_first, e_last = (et, et_rolled) if o == 0 else (et_rolled, et)
            c_last = ct_rolled if o == 0 else ct
            top = jnp.where(first, jnp.where(ln <= rw, roll(q, HALF), e_first), c_last)
            low = jnp.where(first | upper, q, jnp.where(diagonal, d, e_last))
            at = (o * LON + s) * LANES
            grams[at : at + HALF, :] = top
            grams[at + HALF : at + LANES, :] = low


def split(x):
    high = x.astype(jnp.bfloat16)
    rest = x - high.astype(F32)
    middle = rest.astype(jnp.bfloat16)
    low = (rest - middle.astype(F32)).astype(jnp.bfloat16)
    return jnp.concatenate([high, middle, low], axis=1)


def chosen(one_hot, parts):
    out = jnp.dot(one_hot, parts, preferred_element_type=F32)
    return out[:, :LANES] + out[:, LANES : 2 * LANES] + out[:, 2 * LANES :]


def one_hot(index, at):
    return jnp.where(index == at, 1.0, 0.0).astype(jnp.bfloat16)


def padded(x, rows):
    return jnp.concatenate([x, jnp.zeros((rows - x.shape[0], LANES), F32)], axis=0)


def left_strips(x):
    return jnp.where(lanes(x.shape[0]) < 8, roll(x, 8), 0.0)


def right_strips(x):
    ln = lanes(x.shape[0])
    return jnp.where((ln >= 56) & (ln < 64), roll(x, 56), 0.0)


def lay_out(spots, by_lane, own, sides, field, strips, low, high):
    ln = lanes(LANES)
    own_strip = jnp.where(ln < 32, jnp.where(ln >= 8, roll(own, 8), 0.0), jnp.where(ln < 56, roll(own, 56), 0.0))
    pieces = []
    for i, strip in enumerate((own_strip, sides)):
        upper = (spots[i * LANES : (i + 1) * LANES, :].astype(jnp.int32) & 8) != 0
        pieces.append(split(jnp.where(upper, roll(strip, HALF), strip)))
    own_parts = split(own)
    lane_spots = [by_lane[i * 8 : i * 8 + 1, :].astype(jnp.int32) for i in range(2)]
    p = jnp.broadcast_to(lane_spots[0], (LANES, LANES))
    for start in range(low * LEVELS, high * LEVELS, LANES):
        field[start : start + LANES, :] = chosen(one_hot(places(LANES) + start, p), own_parts)
    folded = [jnp.broadcast_to(((b >> 4) << 3) + (b & 7), (64, LANES)) for b in lane_spots]
    for start in range(low * 8, high * 8, 64):
        at = places(64) + start
        strips[start : start + 64, :] = chosen(one_hot(at, folded[0]), pieces[0]) + chosen(one_hot(at, folded[1]), pieces[1])


def adjoint(rates, source, target, first, last, height):
    before = kept = None
    for r in range(first, last + 1):
        y = source[r * height : (r + 1) * height, :]
        lat, lon = rates(r)
        t = lat * y
        a = jnp.where(lat > 0.0, t, 0.0)
        b = a - t
        s = lon * y
        e = jnp.where(lon > 0.0, s, 0.0)
        f = e - s
        if r > first + 1:
            target[(r - 1) * height : r * height, :] = kept + a
        if r > first:
            kept = y - (a + b) - (e + f) + roll(e, -1) + roll(f, 1) + before
        before = b


def tangent(rates, source, target, first, last, height):
    for r in range(first + 1, last):
        x = source[r * height : (r + 1) * height, :]
        south = source[(r - 1) * height : r * height, :]
        north = source[(r + 1) * height : (r + 2) * height, :]
        lat, lon = rates(r)
        out = x + jnp.abs(lat) * (jnp.where(lat > 0.0, south, north) - x)
        target[r * height : (r + 1) * height, :] = out + jnp.abs(lon) * (jnp.where(lon > 0.0, roll(x, 1), roll(x, -1)) - x)


def merged(field, strips, r):
    ln = lanes(8)
    t = strips[r * 8 : (r + 1) * 8, :]
    low, high = field[r * LEVELS : r * LEVELS + 8, :], field[r * LEVELS + 8 : (r + 1) * LEVELS, :]
    low = jnp.where(ln < 8, roll(t, -8), jnp.where(ln >= 120, roll(t, 72), low))
    high = jnp.where(ln < 8, roll(t, -72), jnp.where(ln >= 120, roll(t, 8), high))
    return low, high


def steps_back(rates, fields, strips, first):
    full, narrow = rates
    for k in range(first, first + STEPS):
        adjoint(full, *fields, k, WIDE - 1 - k, LEVELS)
        adjoint(narrow, *strips, k, WIDE - 1 - k, 8)
        fields, strips = fields[::-1], strips[::-1]
    return fields, strips


def steps_on(rates, fields, strips, first):
    full, narrow = rates
    for k in range(first, first + STEPS):
        tangent(full, *fields, k, WIDE - 1 - k, LEVELS)
        tangent(narrow, *strips, k, WIDE - 1 - k, 8)
        fields, strips = fields[::-1], strips[::-1]
    return fields, strips


def rates_of(wide, mine, beside):
    def full(r):
        at = r * 2 * LEVELS
        return wide[at : at + LEVELS, :], wide[at + LEVELS : at + 2 * LEVELS, :]

    def narrow(r):
        ref, r = (mine, r - HALO) if HALO <= r < HALO + ROWS else (beside, r if r < HALO else r - ROWS)
        return ref[r * 16 : r * 16 + 8, :], ref[r * 16 + 8 : r * 16 + 16, :]

    return full, narrow


def back_and_on(spots, by_lane, own, sides, rates, kept, fields, strips, image):
    lay_out(spots, by_lane, own, sides, fields[0], strips[0], 0, WIDE)
    fields, strips = steps_back(rates, fields, strips, 0)
    lat, last = lax.axis_index(LAT), lax.axis_size(LAT) - 1
    for outside, start in ((lat == 0, STEPS), (lat == last, HALO + ROWS)):
        for ref, height in ((fields[0], LEVELS), (strips[0], 8)):
            block = ref[start * height : (start + STEPS) * height, :]
            ref[start * height : (start + STEPS) * height, :] = jnp.where(outside, 0.0, block)
    square = jnp.zeros((8, LANES), F32)
    for r in range(ROWS):
        low, high = merged(fields[0], strips[0], r + HALO)
        kept[r * LEVELS : r * LEVELS + 8, :] = low
        kept[r * LEVELS + 8 : (r + 1) * LEVELS, :] = high
        square += low * low + high * high
    fields, strips = steps_on(rates, fields, strips, STEPS)
    for r in range(ROWS):
        low, high = merged(fields[0], strips[0], r + HALO)
        image[r * LEVELS : r * LEVELS + 8, :] = low
        image[r * LEVELS + 8 : (r + 1) * LEVELS, :] = high
    mine = spots[OWN : 2 * OWN, :].astype(jnp.int32) - HALO * LEVELS
    hit = jnp.concatenate([one_hot(lanes(OWN), mine), one_hot(lanes(OWN) + LANES, mine)], axis=1)
    return jnp.sum(square, keepdims=True), chosen(hit, split(image[...]))


def weigh(seen, grams):
    column = jnp.transpose(seen)
    out = []
    for t in range(OWN):
        total = jnp.zeros((8, LANES), F32)
        for k in range(LANES // 8):
            at = t * LANES + k * 8
            total += grams[at : at + 8, :] * column[k * 8 : k * 8 + 8, t : t + 1]
        out.append(jnp.sum(total, axis=0, keepdims=True))
    return jnp.concatenate(out, axis=0)


def in_lanes(first, values):
    ln = lanes(8)
    out = jnp.zeros((8, LANES), F32)
    for i, v in enumerate(values):
        out = jnp.where(ln == first + i, v, out)
    return out


def first_half(wide, mine, core, own_message, inter, beside, spots, by_lane, kept, seen, sums, field, other, strip, other_strip, image):
    ln = lanes(8)
    even = lax.axis_index("lat_2") == 0
    beside[:STRIP, :] = jnp.where(even, inter[:STRIP, :], core[:STRIP, :])
    beside[STRIP:, :] = jnp.where(even, core[:STRIP, :], inter[:STRIP, :])
    step = jnp.where(even, float(ROWS * LEVELS), -float(ROWS * LEVELS))
    c, o, i = core[SPOTS:, :] + step, own_message[SPOTS:, :], inter[SPOTS:, :] - step
    tables = (((c, 0), (o, 0), (i, 0)), ((c, 16), (o, 16), (i, 16), (c, 32), (o, 32), (i, 32)))
    for t, table in enumerate(tables):
        spot = jnp.full((8, LANES), NOWHERE, F32)
        for n, (x, at) in enumerate(table):
            spot = jnp.where((ln >= OWN * n) & (ln < OWN * (n + 1)), roll(x, OWN * n - at), spot)
        by_lane[t * 8 : t * 8 + 8, :] = spot
        spots[t * LANES : (t + 1) * LANES, :] = jnp.transpose(jnp.broadcast_to(spot[:1], (LANES, LANES)))
    parts = (core, own_message, inter)
    own = padded(jnp.concatenate([x[STRIP:LEFTS, :] for x in parts], axis=0), LANES)
    sides = padded(jnp.concatenate([x[LEFTS:RIGHTS, :] for x in parts] + [x[RIGHTS:SPOTS, :] for x in parts], axis=0), LANES)
    square, rows = back_and_on(spots, by_lane, own, sides, rates_of(wide, mine, beside), kept, (field, other), (strip, other_strip), image)
    seen[...] = rows
    sums[...] = in_lanes(0, [square])


def stepped(x, unit):
    row = places(OWN)
    for bit in range(4):
        x = jnp.where((row & (1 << bit)) != 0, roll(x, unit << bit), x)
    return x


def herald(rows, message):
    mine = (lanes(OWN) >> 3) == places(OWN)
    message[:OWN, :] = rows
    message[OWN : OWN + 1, :] = jnp.sum(jnp.where(mine, stepped(rows, 8), 0.0), axis=0, keepdims=True)
    message[OWN + 1 : OWN + 2, :] = jnp.sum(jnp.where(mine, stepped(roll(rows, 8), 8), 0.0), axis=0, keepdims=True)
    message[OWN + 2 :, :] = jnp.zeros((HERALD - OWN - 2, LANES), F32)


def first_terms(parcels, seen, before, grams, message, sums):
    unpack(parcels, grams)
    rows = weigh(seen[...], grams)
    herald(rows, message)
    sums[...] = before[...] + in_lanes(1, [jnp.sum(seen[...] * rows, keepdims=True)])


def near(core, step):
    here = lax.axis_index("lat_2")
    return (here if core else 1 - here) * LON + lax.rem(lax.axis_index("lon") + LON + step, LON)


def address(mine, inter, parcels):
    parcels[...] = jnp.zeros(parcels.shape, F32)
    parcels[pl.ds(pl.multiple_of(near(False, 0) * OWN, OWN), OWN), :] = mine[:OWN, :]
    for step, row in ((1, OWN + 1), (-1, OWN)):
        parcels[pl.ds(near(True, step) * OWN, 1), :] = mine[row : row + 1, :]
        parcels[pl.ds(near(True, step) * OWN + 1, 1), :] = inter[row : row + 1, :]
        parcels[pl.ds(near(False, step) * OWN, 1), :] = mine[row : row + 1, :]


def side_strips(lefts, rights):
    ln = lanes(OWN)
    rows = [stepped(jnp.broadcast_to(x, (OWN, LANES)), -8) for x in lefts]
    out = [jnp.where(ln < 8, x, 0.0) for x in rows]
    rows = [stepped(jnp.broadcast_to(x, (OWN, LANES)), -8) for x in rights]
    return padded(jnp.concatenate(out + [right_strips(x) for x in rows], axis=0), LANES)


def second_half(spots, by_lane, mine, inter, parcels, wide, strips, beside, grams, before, kept, message, out, field, other, strip, other_strip, image):
    core = parcels[pl.ds(pl.multiple_of(near(False, 0) * OWN, OWN), OWN), :]
    own = padded(jnp.concatenate([core, mine[:OWN, :], inter[:OWN, :]], axis=0), LANES)
    edges = [
        [parcels[pl.ds(near(here, step) * OWN + row, 1), :] for here, row in ((False, 0), (True, 0), (True, 1))]
        for step in (-1, 1)
    ]
    square, seen = back_and_on(
        spots, by_lane, own, side_strips(*edges), rates_of(wide, strips, beside), kept, (field, other), (strip, other_strip), image
    )
    rows = weigh(seen, grams)
    herald(rows, message)
    sums = before[...] + in_lanes(2, [square, jnp.sum(seen * rows, keepdims=True)])
    out[...] = jnp.concatenate([sums] * (out.shape[0] // 8), axis=0)
    for step, row in ((1, OWN + 1), (-1, OWN)):
        out[pl.ds(in_plane(step) * 2 + 1, 1), :] = message[row : row + 1, :]


def in_plane(step):
    return lax.axis_index("lat_1") * LON + lax.rem(lax.axis_index("lon") + LON + step, LON)


def gathered(parts, mine, sums, message):
    count = parts.shape[0] // 2
    sums[...] = jnp.broadcast_to(jnp.sum(parts[pl.ds(0, count, stride=2), :], axis=0, keepdims=True), sums.shape)
    message[...] = mine[...]
    for i, step in enumerate((-1, 1)):
        message[OWN + i : OWN + i + 1, :] = parts[pl.ds(in_plane(step) * 2 + 1, 1), :]


def finish(spots, by_lane, core, mine, inter, wide, strips, beside, parts, right_side, image, increment, residual, field, other, strip, other_strip):
    lists = (core, mine, inter)
    own = padded(jnp.concatenate([x[:OWN, :] for x in lists], axis=0), LANES)
    sides = side_strips(*([x[OWN + i : OWN + i + 1, :] for x in lists] for i in range(2)))
    lay_out(spots, by_lane, own, sides, field, strip, HALO - STEPS, HALO + ROWS + STEPS)
    fields, narrow = steps_back(rates_of(wide, strips, beside), (field, other), (strip, other_strip), STEPS)
    total = jnp.sum(parts[...], axis=0, keepdims=True)
    m0, m1, m2, m3 = (jnp.sum(jnp.where(lanes(1) == i, total, 0.0), keepdims=True) for i in range(4))
    step_0 = m0 / (m0 + m1)
    rho = m1 / m0
    spread = m2 - rho * m1
    curve = (m3 - rho * m2) - rho * (m2 - rho * m1)
    gamma = step_0 * spread / m0
    step_1 = spread / (spread + curve - gamma * spread)
    on_b = step_0 * (1.0 + step_1 * (gamma + rho))
    on_k = -step_0 * step_1
    rest_b = step_0 * ((1.0 - step_1) * rho - step_1 * gamma)
    rest_k = -step_0 * ((1.0 - step_1) + step_1 * (rho + gamma))
    rest_kk = step_0 * step_1
    on_b, on_k, rest_b, rest_k, rest_kk = (jnp.broadcast_to(v, (8, LANES)) for v in (on_b, on_k, rest_b, rest_k, rest_kk))
    for r in range(ROWS):
        for h, second in enumerate(merged(fields[0], narrow[0], r + HALO)):
            at = r * LEVELS + h * 8
            b, first = right_side[at : at + 8, :], image[at : at + 8, :]
            to = pl.ds(h * 8 * ROWS + r, 8, stride=ROWS)
            increment[to, :] = on_b * b + on_k * first
            residual[to, :] = rest_b * b + rest_k * first + rest_kk * second


def to_core(x):
    return lax.ppermute(x, LAT, [(i, i ^ 1) for i in range(lax.axis_size(LAT))])


def to_inter(x):
    return lax.ppermute(x, LAT, [(i, ((i + 1) ^ 1) - 1) for i in range(1, lax.axis_size(LAT) - 1)])


def spread_out(x, axes):
    return lax.all_to_all(x, axes, split_axis=0, concat_axis=0, tiled=True)


def shards(courant, obs_matrix, obs_weight, innovation, block_owner, block_row, block_count):
    flow = courant.reshape(-1, LANES)
    owner, row, count = block_owner.reshape(-1), block_row.reshape(-1), block_count.reshape(-1)
    wholes = (flow, obs_matrix[0], obs_weight[0], innovation[0])
    parcels, for_core, for_inter = call(
        prepare,
        [(LON * PARCEL, LANES), (EDGE, LANES), (EDGE, LANES)],
        (owner, row, count, *wholes),
        4_000_000,
        [pltpu.SMEM((CAP,), jnp.int32), pltpu.SMEM((CAP,), jnp.int32), pltpu.SMEM((1,), jnp.int32)]
        + [pltpu.VMEM(x.shape, F32) for x in wholes]
        + [pltpu.VMEM((OWN, LANES), F32), pltpu.SemaphoreType.DMA((7,))],
        [pl.BlockSpec(memory_space=pltpu.HBM)] * 7,
        62,
    )
    parcels = spread_out(parcels.reshape(LON, PARCEL, LANES), "lon").reshape(LON * PARCEL, LANES)
    core, inter = to_core(for_core), to_inter(for_inter)
    wide, strips, for_core, for_inter = call(
        arrange,
        [(WIDE * 2 * LEVELS, LANES), (2 * STRIP, LANES), (MESSAGE, LANES), (MESSAGE, LANES)],
        (flow, parcels, core, inter),
        2_000_000,
    )
    core, inter = to_core(for_core), to_inter(for_inter)
    cells, listed = (ROWS * LEVELS, LANES), (OWN, LANES)
    work = [pltpu.VMEM((WIDE * LEVELS, LANES), F32)] * 2 + [pltpu.VMEM((WIDE * 8, LANES), F32)] * 2
    work_too = work + [pltpu.VMEM(cells, F32)]
    beside, spots, by_lane, right_side, seen, sums = call(
        first_half,
        [(2 * STRIP, LANES), (2 * LANES, LANES), (16, LANES), cells, listed, (8, LANES)],
        (wide, strips, core, for_core, inter),
        4_000_000,
        work_too,
    )
    rates = (wide, strips, beside)
    short = (HERALD, LANES)
    grams, mine, sums = call(first_terms, [(OWN * LANES, LANES), short, (8, LANES)], (parcels, seen, sums), 2_000_000)
    inter = to_inter(mine)
    ring = lax.axis_size(("lat_2", "lon"))
    (parcels,) = call(address, [(ring * OWN, LANES)], (mine, inter), 10_000)
    parcels = spread_out(parcels.reshape(ring, OWN, LANES), ("lat_2", "lon")).reshape(ring * OWN, LANES)
    plane, towers = lax.axis_size(("lat_1", "lon")), lax.axis_size(("lat_0", "lat_2"))
    image, mine, parcels = call(
        second_half, [cells, short, (plane * 2, LANES)], (spots, by_lane, mine, inter, parcels, *rates, grams, sums), 4_000_000, work_too
    )
    parcels = spread_out(parcels.reshape(plane, 2, LANES), ("lat_1", "lon")).reshape(plane * 2, LANES)
    sums, mine = call(gathered, [(towers, LANES), short], (parcels, mine), 10_000)
    core, inter = to_core(mine), to_inter(mine)
    parts = spread_out(sums.reshape(towers, 1, LANES), ("lat_0", "lat_2")).reshape(towers, LANES)
    increment, residual = call(
        finish, [cells, cells], (spots, by_lane, core, mine, inter, *rates, parts, right_side, image), 2_000_000, work
    )
    shape = courant.shape[1:]
    return increment.reshape(shape), residual.reshape(shape)


def solution(mesh):
    torus = Mesh(
        mesh.devices.reshape(-1, 4, 2, mesh.shape["lon"]), ("lat_0", "lat_1", "lat_2", "lon")
    )
    placed = (
        P(None, None, LAT, "lon"),
        P(LAT, "lon", None, None),
        P(LAT, "lon", None),
        P(LAT, "lon", None),
        P(LAT, "lon", None),
        P(LAT, "lon"),
        P(LAT, "lon"),
    )
    return jax.shard_map(
        shards,
        mesh=torus,
        in_specs=placed,
        out_specs=(P(None, LAT, "lon"), P(None, LAT, "lon")),
        check_vma=False,
    )
```

time: 120 us -> 117 us (0.975)
  blocking collectives: 16.7 us -> 26.9 us
  Pallas kernels: 16 us -> 11.7 us
  starting transfers between devices: 66.1 us -> 61.9 us
  waiting for transfers between devices: 16.9 us -> 14.9 us
  local copies, waits for them, and re-layouts: 1.31 us -> 0.02 us
    all_to_all x1 -> x2, blocking collectives: 16.7 us -> 26.9 us  [spread_out(): return lax.all_to_all(x, axes, split_axis=0, concat_axis=0, tiled=True)]
    all_to_all x3 -> x2, waiting for transfers between devices: 10.9 us -> 6.37 us  [spread_out(): return lax.all_to_all(x, axes, split_axis=0, concat_axis=0, tiled=True)]
    pallas_call x8, Pallas kernels: 16 us -> 11.7 us  [call(): pl.pallas_call(body, out_shape=[jax.ShapeDtypeStruct(s, F32) for s in out...]
    ppermute x8 -> x7, starting transfers between devices: 34.1 us -> 30.6 us  [the longest x3 16.1 us: to_core(): return lax.ppermute(x, LAT, [(i, i ^ 1) for i in range(lax.axis_size(LAT))])]
    ppermute x8 -> x7, waiting for transfers between devices: 6.04 us -> 8.57 us  [the longest x4 7.59 us: to_inter(): lax.ppermute(x, LAT, [(i, (i + 1 ^ 1) - 1) for i in range(1, lax.axis_siz...]
    unnamed x14 -> x6, local copies, waits for them, and re-layouts: 1.31 us -> 0.02 us
    all_to_all x3 -> x2, starting transfers between devices: 31.9 us -> 31.3 us  [spread_out(): return lax.all_to_all(x, axes, split_axis=0, concat_axis=0, tiled=True)]
  transfers between devices with their start and end apart: 11 -> 9, of which waited for: 6 -> 6; matrix products, arithmetic and copies ran while one was open for 0% -> 0% of each run, Pallas kernels for 5% -> 0%
where the time goes in v4:
time: 117 us
  starting transfers between devices  61.9 us (53%)
  blocking collectives  26.9 us (23%)
  waiting for transfers between devices  14.9 us (13%)
  Pallas kernels  11.7 us (10%)
  between operations  1.42 us (1%)
    all_to_all x2, starting transfers between devices, spread_out(): return lax.all_to_all(x, axes, split_axis=0, concat_axis=0, tiled=True)  31.3 us
    all_to_all x2, blocking collectives, spread_out(): return lax.all_to_all(x, axes, split_axis=0, concat_axis=0, tiled=True)  26.9 us
    ppermute x3, starting transfers between devices, to_core(): return lax.ppermute(x, LAT, [(i, i ^ 1) for i in range(lax.axis_size(LAT))])  16.1 us
    ppermute x4, starting transfers between devices, to_inter(): lax.ppermute(x, LAT, [(i, (i + 1 ^ 1) - 1) for i in range(1, lax.axis_siz...  14.5 us
    pallas_call x8, Pallas kernels, call(): pl.pallas_call(body, out_shape=[jax.ShapeDtypeStruct(s, F32) for s in out...  11.7 us
    ppermute x4, waiting for transfers between devices, to_inter(): lax.ppermute(x, LAT, [(i, (i + 1 ^ 1) - 1) for i in range(1, lax.axis_siz...  7.59 us
    all_to_all x2, waiting for transfers between devices, spread_out(): return lax.all_to_all(x, axes, split_axis=0, concat_axis=0, tiled=True)  6.37 us
  transfers between devices with their start and end apart: 9, of which 6 were waited for; matrix products, arithmetic and copies ran while one was open for 0% of the time, Pallas kernels for 0%

profile of v4, /device:TPU:1, one launch (start us, length us, event | category | flops | bytes accessed | tf_op | source)
XLA Modules:
  0.0 116.9 jit_solution(8920795911917951408)
XLA Ops:
  1.3 3.0 %prepare.1 = (f32[1408,128]{1,0:T(8,128)}, f32[256,128]{1,0:T(8,128)}, f32[256,128]{1,0:T(8,128)}) custom-call(s32[8]{0:T(128)} %bitcast.33, s32[8]{0:T(128)} %bitcast.34, s32[1]{0:T(128)} %bitcast.19.count_at, f32[512,128]{1,0:T(8,128)} %bitcast.22, f32[8,128,128]{2,1,0:T(8,128)} %bitcast.30, f32[8,128]{1,0:T(8,128)} %bitcast.31, f32[8,128]{1,0:T(8,128)} %bitcast.32), custom_call_target="tpu_custom_call" | custom-call | flops 4000000 | tf_op jit(solution)/shard_map/prepare/pallas_call | solution.py:53
  4.3 0.0 copy-start.2
  4.3 0.0 copy-start.1
  4.3 0.0 copy-start
  4.3 7.8 %all-to-all-start = ((f32[8,176,128]{2,1,0:T(8,128)}), f32[8,176,128]{2,1,0:T(8,128)S(1)}, u32[]{:S(2)}, u32[]{:S(2)}) async-start(f32[8,176,128]{2,1,0:T(8,128)} %bitcast.29), calls=%async_computation | async-start | bytes 1441792 | tf_op jit(solution)/shard_map/all_to_all | solution.py:512
  12.1 0.0 copy-done.2
  12.1 11.9 %collective-permute-start = (f32[256,128]{1,0:T(8,128)S(1)}, f32[256,128]{1,0:T(8,128)S(1)}, u32[]{:S(2)}, u32[]{:S(2)}) collective-permute-start(f32[256,128]{1,0:T(8,128)S(1)} %copy-done.2), channel_id=1, source_target_pairs={{0,8},{8,0},{16,24},{24,16},{32,40},{40,32},{48,56},{56,48},{64,72... | collective-permute-start | bytes 393224 | tf_op jit(solution)/shard_map/ppermute | solution.py:504
  24.1 0.0 copy-done.1
  24.1 1.9 %collective-permute-start.1 = (f32[256,128]{1,0:T(8,128)S(1)}, f32[256,128]{1,0:T(8,128)S(1)}, u32[]{:S(2)}, u32[]{:S(2)}) collective-permute-start(f32[256,128]{1,0:T(8,128)S(1)} %copy-done.1), channel_id=1, source_target_pairs={{8,16},{16,8},{24,32},{32,24},{40,48},{48,40},{56,64},{64,56},{72,... | collective-permute-start | bytes 393224 | tf_op jit(solution)/shard_map/ppermute | solution.py:508
  26.0 0.0 collective-permute-done.core
  26.0 4.6 %collective-permute-done.1.inter = f32[256,128]{1,0:T(8,128)S(1)} collective-permute-done((f32[256,128]{1,0:T(8,128)S(1)}, f32[256,128]{1,0:T(8,128)S(1)}, u32[]{:S(2)}, u32[]{:S(2)}) %collective-permute-start.1) | collective-permute-done | bytes 131104 | tf_op jit(solution)/shard_map/ppermute | solution.py:508
  30.6 0.0 all-to-all-done
  30.6 0.0 copy-done
  30.7 0.4 arrange.1
  31.0 7.1 %collective-permute-start.3 = (f32[184,128]{1,0:T(8,128)S(1)}, f32[184,128]{1,0:T(8,128)S(1)}, u32[]{:S(2)}, u32[]{:S(2)}) collective-permute-start(f32[184,128]{1,0:T(8,128)S(1)} %get-tuple-element.31), channel_id=1, source_target_pairs={{8,16},{16,8},{24,32},{32,24},{40,48},{48,40},{56,64},{64,56},{72,... | collective-permute-start | bytes 282632 | tf_op jit(solution)/shard_map/ppermute | solution.py:508
  38.2 2.3 %collective-permute-start.2 = (f32[184,128]{1,0:T(8,128)S(1)}, f32[184,128]{1,0:T(8,128)S(1)}, u32[]{:S(2)}, u32[]{:S(2)}) collective-permute-start(f32[184,128]{1,0:T(8,128)S(1)} %get-tuple-element.30.own_message), channel_id=1, source_target_pairs={{0,8},{8,0},{16,24},{24,16},{32,40},{40,32},{48,56},{56,48},{64,72... | collective-permute-start | bytes 282632 | tf_op jit(solution)/shard_map/ppermute | solution.py:504
  40.5 0.0 collective-permute-done.3.inter
  40.5 0.9 collective-permute-done.2.core
  41.4 1.9 %first_half.1 = (f32[256,128]{1,0:T(8,128)S(1)}, f32[256,128]{1,0:T(8,128)S(1)}, f32[16,128]{1,0:T(8,128)S(1)}, f32[256,128]{1,0:T(8,128)S(1)}, f32[16,128]{1,0:T(8,128)S(1)}, /*index=5*/f32[8,128]{1,0:T(8,128)S(1)}) custom-call(f32[1024,128]{1,0:T(8,128)S(1)} %get-tuple-element.28.wide, f32[256,128]{1,0:T(8,128)S(1)} %get-tuple-element.29.mine.strips, ...), custom_call_target="tpu_custom_call" | custom-call | flops 4000000 | tf_op jit(solution)/shard_map/first_half/pallas_call | solution.py:53
  43.3 1.2 %first_terms.1 = (f32[2048,128]{1,0:T(8,128)S(1)}, f32[24,128]{1,0:T(8,128)S(1)}, f32[8,128]{1,0:T(8,128)S(1)}) custom-call(f32[1408,128]{1,0:T(8,128)S(1)} %bitcast.21, f32[16,128]{1,0:T(8,128)S(1)} %get-tuple-element.34.seen, f32[8,128]{1,0:T(8,128)S(1)} %get-tuple-element.35.before), custom_call_target="tpu_custom_call" | custom-call | flops 2000000 | tf_op jit(solution)/shard_map/first_terms/pallas_call | solution.py:53
  44.5 3.1 %collective-permute-start.4 = (f32[24,128]{1,0:T(8,128)S(1)}, f32[24,128]{1,0:T(8,128)S(1)}, u32[]{:S(2)}, u32[]{:S(2)}) collective-permute-start(f32[24,128]{1,0:T(8,128)S(1)} %get-tuple-element.36.mine), channel_id=1, source_target_pairs={{8,16},{16,8},{24,32},{32,24},{40,48},{48,40},{56,64},{64,56},{72,... | collective-permute-start | bytes 36872 | tf_op jit(solution)/shard_map/ppermute | solution.py:508
  47.6 1.9 %collective-permute-done.4.inter = f32[24,128]{1,0:T(8,128)S(1)} collective-permute-done((f32[24,128]{1,0:T(8,128)S(1)}, f32[24,128]{1,0:T(8,128)S(1)}, u32[]{:S(2)}, u32[]{:S(2)}) %collective-permute-start.4) | collective-permute-done | bytes 12320 | tf_op jit(solution)/shard_map/ppermute | solution.py:508
  49.5 10.0 %all_to_all.20 = f32[16,16,128]{2,1,0:T(8,128)S(1)} all-to-all(f32[16,16,128]{2,1,0:T(8,128)S(1)} %bitcast.25), channel_id=1, replica_groups=mesh['lat_0'=16,'lat_1'=4,'lat_2'=2,'lon'=8] {'lat_2','lon'}, dimensions={0} | all-to-all | bytes 262144 | tf_op jit(solution)/shard_map/all_to_all | solution.py:512
  59.5 2.8 %second_half.1 = (f32[256,128]{1,0:T(8,128)S(1)}, f32[24,128]{1,0:T(8,128)S(1)}, f32[64,128]{1,0:T(8,128)S(1)}) custom-call(f32[256,128]{1,0:T(8,128)S(1)} %get-tuple-element.32.spots, f32[16,128]{1,0:T(8,128)S(1)} %get-tuple-element.33.by_lane, f32[24,128]{1,0:T(8,128)S(1)} %get-tuple-element.36.mine, f32[24,128]{1,0:T(8,128)S(1)} %collective-permute-done.4.inter, ...), custom_call_target="tpu_custom_call" | custom-call | flops 4000000 | tf_op jit(solution)/shard_map/second_half/pallas_call | solution.py:53
  62.3 16.9 %all_to_all.21 = f32[32,2,128]{2,1,0:T(2,128)S(1)} all-to-all(f32[32,2,128]{2,1,0:T(2,128)S(1)} %bitcast.28), channel_id=1, replica_groups=mesh['lat_0'=16,'lat_1'=4,'lat_2'=2,'lon'=8] {'lat_1','lon'}, dimensions={0} | all-to-all | bytes 65536 | tf_op jit(solution)/shard_map/all_to_all | solution.py:512
  79.2 0.6 gathered.1
  79.8 23.5 %all-to-all-start.3 = ((f32[32,1,128]{2,1,0:T(1,128)}), f32[32,1,128]{2,1,0:T(1,128)S(1)}, u32[]{:S(2)}, u32[]{:S(2)}) async-start(f32[32,1,128]{2,1,0:T(1,128)} %bitcast.14), calls=%async_computation.3 | async-start | bytes 32768 | tf_op jit(solution)/shard_map/all_to_all | solution.py:512
  103.3 2.3 %collective-permute-start.6 = (f32[24,128]{1,0:T(8,128)S(1)}, f32[24,128]{1,0:T(8,128)S(1)}, u32[]{:S(2)}, u32[]{:S(2)}) collective-permute-start(f32[24,128]{1,0:T(8,128)S(1)} %get-tuple-element.42.mine), channel_id=1, source_target_pairs={{8,16},{16,8},{24,32},{32,24},{40,48},{48,40},{56,64},{64,56},{72,... | collective-permute-start | bytes 36872 | tf_op jit(solution)/shard_map/ppermute | solution.py:508
  105.6 1.9 %collective-permute-start.5 = (f32[24,128]{1,0:T(8,128)S(1)}, f32[24,128]{1,0:T(8,128)S(1)}, u32[]{:S(2)}, u32[]{:S(2)}) collective-permute-start(f32[24,128]{1,0:T(8,128)S(1)} %get-tuple-element.42.mine), channel_id=1, source_target_pairs={{0,8},{8,0},{16,24},{24,16},{32,40},{40,32},{48,56},{56,48},{64,72... | collective-permute-start | bytes 36872 | tf_op jit(solution)/shard_map/ppermute | solution.py:504
  107.5 1.1 collective-permute-done.6.inter
  108.6 0.1 collective-permute-done.5.core
  108.7 6.4 %all-to-all-done.3 = f32[32,1,128]{2,1,0:T(1,128)S(1)} async-done(((f32[32,1,128]{2,1,0:T(1,128)}), f32[32,1,128]{2,1,0:T(1,128)S(1)}, u32[]{:S(2)}, u32[]{:S(2)}) %all-to-all-start.3) | async-done | bytes 16416 | tf_op jit(solution)/shard_map/all_to_all | solution.py:512
  115.0 1.8 %finish.1 = (f32[256,128]{1,0:T(8,128)}, f32[256,128]{1,0:T(8,128)}) custom-call(f32[256,128]{1,0:T(8,128)S(1)} %get-tuple-element.32.spots, f32[16,128]{1,0:T(8,128)S(1)} %get-tuple-element.33.by_lane, f32[24,128]{1,0:T(8,128)S(1)} %collective-permute-done.5.core, f32[24,128]{1,0:T(8,128)S(1)} %get-tuple-element.42.mine, ...), custom_call_target="tpu_custom_call" | custom-call | flops 2000000 | tf_op jit(solution)/shard_map/finish/pallas_call | solution.py:53
  (1 shorter events, 0.0 us)
Async XLA Ops:
  4.3 7.8 %copy-start.2 = (f32[256,128]{1,0:T(8,128)S(1)}, f32[256,128]{1,0:T(8,128)}, u32[]{:S(2)}) copy-start(f32[256,128]{1,0:T(8,128)} %get-tuple-element.26) | copy-start | bytes 393220
  4.3 19.8 %copy-start.1 = (f32[256,128]{1,0:T(8,128)S(1)}, f32[256,128]{1,0:T(8,128)}, u32[]{:S(2)}) copy-start(f32[256,128]{1,0:T(8,128)} %get-tuple-element.27) | copy-start | bytes 393220
  4.3 26.3 %copy-start = (f32[2,16,16,128]{3,2,1,0:T(8,128)S(1)}, f32[2,16,16,128]{3,2,1,0:T(8,128)}, u32[]{:S(2)}) copy-start(f32[2,16,16,128]{3,2,1,0:T(8,128)} %param.7) | copy-start | bytes 786436
  4.3 26.3 %all-to-all-start = ((f32[8,176,128]{2,1,0:T(8,128)}), f32[8,176,128]{2,1,0:T(8,128)S(1)}, u32[]{:S(2)}, u32[]{:S(2)}) async-start(f32[8,176,128]{2,1,0:T(8,128)} %bitcast.29), calls=%async_computation | async-start | bytes 1441792 | tf_op jit(solution)/shard_map/all_to_all | solution.py:512
  12.1 13.9 %collective-permute-start = (f32[256,128]{1,0:T(8,128)S(1)}, f32[256,128]{1,0:T(8,128)S(1)}, u32[]{:S(2)}, u32[]{:S(2)}) collective-permute-start(f32[256,128]{1,0:T(8,128)S(1)} %copy-done.2), channel_id=1, source_target_pairs={{0,8},{8,0},{16,24},{24,16},{32,40},{40,32},{48,56},{56,48},{64,72... | collective-permute-start | bytes 393224 | tf_op jit(solution)/shard_map/ppermute | solution.py:504
  24.1 6.6 %collective-permute-start.1 = (f32[256,128]{1,0:T(8,128)S(1)}, f32[256,128]{1,0:T(8,128)S(1)}, u32[]{:S(2)}, u32[]{:S(2)}) collective-permute-start(f32[256,128]{1,0:T(8,128)S(1)} %copy-done.1), channel_id=1, source_target_pairs={{8,16},{16,8},{24,32},{32,24},{40,48},{48,40},{56,64},{64,56},{72,... | collective-permute-start | bytes 393224 | tf_op jit(solution)/shard_map/ppermute | solution.py:508
  31.0 9.4 %collective-permute-start.3 = (f32[184,128]{1,0:T(8,128)S(1)}, f32[184,128]{1,0:T(8,128)S(1)}, u32[]{:S(2)}, u32[]{:S(2)}) collective-permute-start(f32[184,128]{1,0:T(8,128)S(1)} %get-tuple-element.31), channel_id=1, source_target_pairs={{8,16},{16,8},{24,32},{32,24},{40,48},{48,40},{56,64},{64,56},{72,... | collective-permute-start | bytes 282632 | tf_op jit(solution)/shard_map/ppermute | solution.py:508
  38.2 3.2 %collective-permute-start.2 = (f32[184,128]{1,0:T(8,128)S(1)}, f32[184,128]{1,0:T(8,128)S(1)}, u32[]{:S(2)}, u32[]{:S(2)}) collective-permute-start(f32[184,128]{1,0:T(8,128)S(1)} %get-tuple-element.30.own_message), channel_id=1, source_target_pairs={{0,8},{8,0},{16,24},{24,16},{32,40},{40,32},{48,56},{56,48},{64,72... | collective-permute-start | bytes 282632 | tf_op jit(solution)/shard_map/ppermute | solution.py:504
  44.5 5.0 %collective-permute-start.4 = (f32[24,128]{1,0:T(8,128)S(1)}, f32[24,128]{1,0:T(8,128)S(1)}, u32[]{:S(2)}, u32[]{:S(2)}) collective-permute-start(f32[24,128]{1,0:T(8,128)S(1)} %get-tuple-element.36.mine), channel_id=1, source_target_pairs={{8,16},{16,8},{24,32},{32,24},{40,48},{48,40},{56,64},{64,56},{72,... | collective-permute-start | bytes 36872 | tf_op jit(solution)/shard_map/ppermute | solution.py:508
  79.8 35.3 %all-to-all-start.3 = ((f32[32,1,128]{2,1,0:T(1,128)}), f32[32,1,128]{2,1,0:T(1,128)S(1)}, u32[]{:S(2)}, u32[]{:S(2)}) async-start(f32[32,1,128]{2,1,0:T(1,128)} %bitcast.14), calls=%async_computation.3 | async-start | bytes 32768 | tf_op jit(solution)/shard_map/all_to_all | solution.py:512
  103.3 5.3 %collective-permute-start.6 = (f32[24,128]{1,0:T(8,128)S(1)}, f32[24,128]{1,0:T(8,128)S(1)}, u32[]{:S(2)}, u32[]{:S(2)}) collective-permute-start(f32[24,128]{1,0:T(8,128)S(1)} %get-tuple-element.42.mine), channel_id=1, source_target_pairs={{8,16},{16,8},{24,32},{32,24},{40,48},{48,40},{56,64},{64,56},{72,... | collective-permute-start | bytes 36872 | tf_op jit(solution)/shard_map/ppermute | solution.py:508
  105.6 3.1 %collective-permute-start.5 = (f32[24,128]{1,0:T(8,128)S(1)}, f32[24,128]{1,0:T(8,128)S(1)}, u32[]{:S(2)}, u32[]{:S(2)}) collective-permute-start(f32[24,128]{1,0:T(8,128)S(1)} %get-tuple-element.42.mine), channel_id=1, source_target_pairs={{0,8},{8,0},{16,24},{24,16},{32,40},{40,32},{48,56},{56,48},{64,72... | collective-permute-start | bytes 36872 | tf_op jit(solution)/shard_map/ppermute | solution.py:504

commit v5 on v4

--- a/solution.py
+++ b/solution.py
@@ -19,8 +19,8 @@
 HALF = LANES // 2
 OWN = LON * SLOT
 NEAR = 3 * OWN
-BULK = 2 * HALF + 8
-LIST = BULK + 8
+BULK = 2 * HALF + 2
+LIST = BULK + 6
 PARCEL = LIST + 32
 EDGE = HALO * 2 * LEVELS
 STRIP = HALO * 2 * 8
@@ -96,7 +96,7 @@
     for copy in copies:
         copy.start()
     for d in range(LON):
-        parcels[d * PARCEL : d * PARCEL + BULK, :] = jnp.zeros((BULK, LANES), F32)
+        parcels[d * PARCEL : d * PARCEL + LIST, :] = jnp.zeros((LIST, LANES), F32)
     lists[...] = jnp.zeros(lists.shape, F32)
     me = lax.axis_index("lon")
     even = lax.axis_index("lat_2") == 0
@@ -412,25 +412,17 @@
     message[OWN + 2 :, :] = jnp.zeros((HERALD - OWN - 2, LANES), F32)
 
 
-def first_terms(parcels, seen, before, grams, message, sums):
-    unpack(parcels, grams)
+def first_terms(grams, seen, before, message, sums):
     rows = weigh(seen[...], grams)
     herald(rows, message)
     sums[...] = before[...] + in_lanes(1, [jnp.sum(seen[...] * rows, keepdims=True)])
 
 
-def near(core, step):
-    here = lax.axis_index("lat_2")
-    return (here if core else 1 - here) * LON + lax.rem(lax.axis_index("lon") + LON + step, LON)
-
-
-def address(mine, inter, parcels):
-    parcels[...] = jnp.zeros(parcels.shape, F32)
-    parcels[pl.ds(pl.multiple_of(near(False, 0) * OWN, OWN), OWN), :] = mine[:OWN, :]
-    for step, row in ((1, OWN + 1), (-1, OWN)):
-        parcels[pl.ds(near(True, step) * OWN, 1), :] = mine[row : row + 1, :]
-        parcels[pl.ds(near(True, step) * OWN + 1, 1), :] = inter[row : row + 1, :]
-        parcels[pl.ds(near(False, step) * OWN, 1), :] = mine[row : row + 1, :]
+def edges_of(core, mine, inter, out):
+    for i, x in enumerate((core, mine, inter)):
+        out[i : i + 1, :] = x[OWN : OWN + 1, :]
+        out[i + 3 : i + 4, :] = x[OWN + 1 : OWN + 2, :]
+    out[6:, :] = jnp.zeros((2, LANES), F32)
 
 
 def side_strips(lefts, rights):
@@ -441,15 +433,13 @@
     return padded(jnp.concatenate(out + [right_strips(x) for x in rows], axis=0), LANES)
 
 
-def second_half(spots, by_lane, mine, inter, parcels, wide, strips, beside, grams, before, kept, message, out, field, other, strip, other_strip, image):
-    core = parcels[pl.ds(pl.multiple_of(near(False, 0) * OWN, OWN), OWN), :]
-    own = padded(jnp.concatenate([core, mine[:OWN, :], inter[:OWN, :]], axis=0), LANES)
-    edges = [
-        [parcels[pl.ds(near(here, step) * OWN + row, 1), :] for here, row in ((False, 0), (True, 0), (True, 1))]
-        for step in (-1, 1)
-    ]
+def second_half(spots, by_lane, core, mine, inter, even, odd, wide, strips, beside, grams, before, kept, message, out, field, other, strip, other_strip, image):
+    own = padded(jnp.concatenate([x[:OWN, :] for x in (core, mine, inter)], axis=0), LANES)
+    here = lax.rem(lax.axis_index("lon"), 2) == 0
+    left, right = jnp.where(here, odd[...], even[...]), jnp.where(here, even[...], odd[...])
+    sides = side_strips([left[i : i + 1] for i in (3, 4, 5)], [right[i : i + 1] for i in (0, 1, 2)])
     square, seen = back_and_on(
-        spots, by_lane, own, side_strips(*edges), rates_of(wide, strips, beside), kept, (field, other), (strip, other_strip), image
+        spots, by_lane, own, sides, rates_of(wide, strips, beside), kept, (field, other), (strip, other_strip), image
     )
     rows = weigh(seen, grams)
     herald(rows, message)
@@ -471,12 +461,17 @@
         message[OWN + i : OWN + i + 1, :] = parts[pl.ds(in_plane(step) * 2 + 1, 1), :]
 
 
-def finish(spots, by_lane, core, mine, inter, wide, strips, beside, parts, right_side, image, increment, residual, field, other, strip, other_strip):
+def last_rows(spots, by_lane, core, mine, inter, wide, strips, beside, kept, field, other, strip, other_strip):
     lists = (core, mine, inter)
     own = padded(jnp.concatenate([x[:OWN, :] for x in lists], axis=0), LANES)
     sides = side_strips(*([x[OWN + i : OWN + i + 1, :] for x in lists] for i in range(2)))
     lay_out(spots, by_lane, own, sides, field, strip, HALO - STEPS, HALO + ROWS + STEPS)
     fields, narrow = steps_back(rates_of(wide, strips, beside), (field, other), (strip, other_strip), STEPS)
+    for r in range(ROWS):
+        kept[r * LEVELS : r * LEVELS + 8, :], kept[r * LEVELS + 8 : (r + 1) * LEVELS, :] = merged(fields[0], narrow[0], r + HALO)
+
+
+def finish(parts, right_side, image, second, increment, residual):
     total = jnp.sum(parts[...], axis=0, keepdims=True)
     m0, m1, m2, m3 = (jnp.sum(jnp.where(lanes(1) == i, total, 0.0), keepdims=True) for i in range(4))
     step_0 = m0 / (m0 + m1)
@@ -492,12 +487,12 @@
     rest_kk = step_0 * step_1
     on_b, on_k, rest_b, rest_k, rest_kk = (jnp.broadcast_to(v, (8, LANES)) for v in (on_b, on_k, rest_b, rest_k, rest_kk))
     for r in range(ROWS):
-        for h, second in enumerate(merged(fields[0], narrow[0], r + HALO)):
+        for h in range(2):
             at = r * LEVELS + h * 8
-            b, first = right_side[at : at + 8, :], image[at : at + 8, :]
+            b, k, kk = right_side[at : at + 8, :], image[at : at + 8, :], second[at : at + 8, :]
             to = pl.ds(h * 8 * ROWS + r, 8, stride=ROWS)
-            increment[to, :] = on_b * b + on_k * first
-            residual[to, :] = rest_b * b + rest_k * first + rest_kk * second
+            increment[to, :] = on_b * b + on_k * k
+            residual[to, :] = rest_b * b + rest_k * k + rest_kk * kk
 
 
 def to_core(x):
@@ -506,6 +501,14 @@
 
 def to_inter(x):
     return lax.ppermute(x, LAT, [(i, ((i + 1) ^ 1) - 1) for i in range(1, lax.axis_size(LAT) - 1)])
+
+
+def to_even(x):
+    return lax.ppermute(x, "lon", [(i, i ^ 1) for i in range(LON)])
+
+
+def to_odd(x):
+    return lax.ppermute(x, "lon", [(i, (((i + 1) % LON ^ 1) - 1) % LON) for i in range(LON)])
 
 
 def spread_out(x, axes):
@@ -536,6 +539,7 @@
         2_000_000,
     )
     core, inter = to_core(for_core), to_inter(for_inter)
+    (grams,) = call(unpack, [(OWN * LANES, LANES)], (parcels,), 4_000_000)
     cells, listed = (ROWS * LEVELS, LANES), (OWN, LANES)
     work = [pltpu.VMEM((WIDE * LEVELS, LANES), F32)] * 2 + [pltpu.VMEM((WIDE * 8, LANES), F32)] * 2
     work_too = work + [pltpu.VMEM(cells, F32)]
@@ -548,22 +552,20 @@
     )
     rates = (wide, strips, beside)
     short = (HERALD, LANES)
-    grams, mine, sums = call(first_terms, [(OWN * LANES, LANES), short, (8, LANES)], (parcels, seen, sums), 2_000_000)
-    inter = to_inter(mine)
-    ring = lax.axis_size(("lat_2", "lon"))
-    (parcels,) = call(address, [(ring * OWN, LANES)], (mine, inter), 10_000)
-    parcels = spread_out(parcels.reshape(ring, OWN, LANES), ("lat_2", "lon")).reshape(ring * OWN, LANES)
+    mine, sums = call(first_terms, [short, (8, LANES)], (grams, seen, sums), 2_000_000)
+    core, inter = to_core(mine), to_inter(mine)
+    (edges,) = call(edges_of, [(8, LANES)], (core, mine, inter), 10_000)
+    lists = (core, mine, inter, to_even(edges), to_odd(edges))
     plane, towers = lax.axis_size(("lat_1", "lon")), lax.axis_size(("lat_0", "lat_2"))
     image, mine, parcels = call(
-        second_half, [cells, short, (plane * 2, LANES)], (spots, by_lane, mine, inter, parcels, *rates, grams, sums), 4_000_000, work_too
+        second_half, [cells, short, (plane * 2, LANES)], (spots, by_lane, *lists, *rates, grams, sums), 4_000_000, work_too
     )
     parcels = spread_out(parcels.reshape(plane, 2, LANES), ("lat_1", "lon")).reshape(plane * 2, LANES)
     sums, mine = call(gathered, [(towers, LANES), short], (parcels, mine), 10_000)
     core, inter = to_core(mine), to_inter(mine)
     parts = spread_out(sums.reshape(towers, 1, LANES), ("lat_0", "lat_2")).reshape(towers, LANES)
-    increment, residual = call(
-        finish, [cells, cells], (spots, by_lane, core, mine, inter, *rates, parts, right_side, image), 2_000_000, work
-    )
+    (second,) = call(last_rows, [cells], (spots, by_lane, core, mine, inter, *rates), 4_000_000, work)
+    increment, residual = call(finish, [cells, cells], (parts, right_side, image, second), 100_000)
     shape = courant.shape[1:]
     return increment.reshape(shape), residual.reshape(shape)
 

time: 117 us -> 112 us (0.957)
  blocking collectives: 26.9 us -> 17.3 us
  starting transfers between devices: 61.9 us -> 66 us
    all_to_all x2 -> x1, blocking collectives: 26.9 us -> 17.3 us  [spread_out(): return lax.all_to_all(x, axes, split_axis=0, concat_axis=0, tiled=True)]
    ppermute x0 -> x2, starting transfers between devices: none -> 4.1 us  [the longest x1 2.19 us: to_even(): return lax.ppermute(x, 'lon', [(i, i ^ 1) for i in range(LON)])]
    ppermute x0 -> x2, waiting for transfers between devices: none -> 2.35 us  [the longest x1 1.43 us: to_odd(): lax.ppermute(x, 'lon', [(i, (((i + 1) % LON ^ 1) - 1) % LON) for i in ran...]
    ppermute x3 -> x4, starting transfers between devices: 16.1 us -> 18.4 us  [to_core(): return lax.ppermute(x, LAT, [(i, i ^ 1) for i in range(lax.axis_size(LAT))])]
    ppermute x4, waiting for transfers between devices: 7.59 us -> 5.89 us  [to_inter(): lax.ppermute(x, LAT, [(i, (i + 1 ^ 1) - 1) for i in range(1, lax.axis_siz...]
    all_to_all x2, starting transfers between devices: 31.3 us -> 30 us  [spread_out(): return lax.all_to_all(x, axes, split_axis=0, concat_axis=0, tiled=True)]
    all_to_all x2, waiting for transfers between devices: 6.37 us -> 5.17 us  [spread_out(): return lax.all_to_all(x, axes, split_axis=0, concat_axis=0, tiled=True)]
    pallas_call x8 -> x10, Pallas kernels: 11.7 us -> 12.1 us  [call(): pl.pallas_call(body, out_shape=[jax.ShapeDtypeStruct(s, F32) for s in out...]
  transfers between devices with their start and end apart: 9 -> 12, of which waited for: 6 -> 9; matrix products, arithmetic and copies ran while one was open for 0% -> 0% of each run, Pallas kernels for 0% -> 1%
where the time goes in v5:
time: 112 us
  starting transfers between devices  66 us (59%)
  blocking collectives  17.3 us (15%)
  waiting for transfers between devices  14.8 us (13%)
  Pallas kernels  12.1 us (11%)
  between operations  1.45 us (1%)
    all_to_all x2, starting transfers between devices, spread_out(): return lax.all_to_all(x, axes, split_axis=0, concat_axis=0, tiled=True)  30 us
    ppermute x4, starting transfers between devices, to_core(): return lax.ppermute(x, LAT, [(i, i ^ 1) for i in range(lax.axis_size(LAT))])  18.4 us
    all_to_all x1, blocking collectives, spread_out(): return lax.all_to_all(x, axes, split_axis=0, concat_axis=0, tiled=True)  17.3 us
    ppermute x4, starting transfers between devices, to_inter(): lax.ppermute(x, LAT, [(i, (i + 1 ^ 1) - 1) for i in range(1, lax.axis_siz...  13.5 us
    pallas_call x10, Pallas kernels, call(): pl.pallas_call(body, out_shape=[jax.ShapeDtypeStruct(s, F32) for s in out...  12.1 us
    ppermute x4, waiting for transfers between devices, to_inter(): lax.ppermute(x, LAT, [(i, (i + 1 ^ 1) - 1) for i in range(1, lax.axis_siz...  5.89 us
    all_to_all x2, waiting for transfers between devices, spread_out(): return lax.all_to_all(x, axes, split_axis=0, concat_axis=0, tiled=True)  5.17 us
  transfers between devices with their start and end apart: 12, of which 9 were waited for; matrix products, arithmetic and copies ran while one was open for 0% of the time, Pallas kernels for 1%

profile of v5, /device:TPU:1, one launch (start us, length us, event | category | flops | bytes accessed | tf_op | source)
XLA Modules:
  0.0 111.7 jit_solution(4831953178245361962)
XLA Ops:
  1.3 3.0 %prepare.1 = (f32[1344,128]{1,0:T(8,128)}, f32[256,128]{1,0:T(8,128)}, f32[256,128]{1,0:T(8,128)}) custom-call(s32[8]{0:T(128)} %bitcast.29, s32[8]{0:T(128)} %bitcast.30, s32[1]{0:T(128)} %bitcast.17.count_at, f32[512,128]{1,0:T(8,128)} %bitcast.20, f32[8,128,128]{2,1,0:T(8,128)} %bitcast.26, f32[8,128]{1,0:T(8,128)} %bitcast.27, f32[8,128]{1,0:T(8,128)} %bitcast.28), custom_call_target="tpu_custom_call" | custom-call | flops 4000000 | tf_op jit(solution)/shard_map/prepare/pallas_call | solution.py:53
  4.3 0.0 copy-start.2
  4.3 0.0 copy-start.1
  4.3 0.0 copy-start
  4.3 7.8 %all-to-all-start = ((f32[8,168,128]{2,1,0:T(8,128)}), f32[8,168,128]{2,1,0:T(8,128)S(1)}, u32[]{:S(2)}, u32[]{:S(2)}) async-start(f32[8,168,128]{2,1,0:T(8,128)} %bitcast.25), calls=%async_computation | async-start | bytes 1376256 | tf_op jit(solution)/shard_map/all_to_all | solution.py:515
  12.1 0.0 copy-done.2
  12.1 11.9 %collective-permute-start = (f32[256,128]{1,0:T(8,128)S(1)}, f32[256,128]{1,0:T(8,128)S(1)}, u32[]{:S(2)}, u32[]{:S(2)}) collective-permute-start(f32[256,128]{1,0:T(8,128)S(1)} %copy-done.2), channel_id=1, source_target_pairs={{0,8},{8,0},{16,24},{24,16},{32,40},{40,32},{48,56},{56,48},{64,72... | collective-permute-start | bytes 393224 | tf_op jit(solution)/shard_map/ppermute | solution.py:499
  24.0 0.0 copy-done.1
  24.0 1.9 %collective-permute-start.1 = (f32[256,128]{1,0:T(8,128)S(1)}, f32[256,128]{1,0:T(8,128)S(1)}, u32[]{:S(2)}, u32[]{:S(2)}) collective-permute-start(f32[256,128]{1,0:T(8,128)S(1)} %copy-done.1), channel_id=1, source_target_pairs={{8,16},{16,8},{24,32},{32,24},{40,48},{48,40},{56,64},{64,56},{72,... | collective-permute-start | bytes 393224 | tf_op jit(solution)/shard_map/ppermute | solution.py:503
  26.0 0.0 collective-permute-done.core
  26.0 4.6 %collective-permute-done.1.inter = f32[256,128]{1,0:T(8,128)S(1)} collective-permute-done((f32[256,128]{1,0:T(8,128)S(1)}, f32[256,128]{1,0:T(8,128)S(1)}, u32[]{:S(2)}, u32[]{:S(2)}) %collective-permute-start.1) | collective-permute-done | bytes 131104 | tf_op jit(solution)/shard_map/ppermute | solution.py:503
  30.6 0.0 all-to-all-done
  30.6 0.0 copy-done
  30.6 0.4 arrange.1
  31.0 6.4 %collective-permute-start.3 = (f32[184,128]{1,0:T(8,128)S(1)}, f32[184,128]{1,0:T(8,128)S(1)}, u32[]{:S(2)}, u32[]{:S(2)}) collective-permute-start(f32[184,128]{1,0:T(8,128)S(1)} %get-tuple-element.30), channel_id=1, source_target_pairs={{8,16},{16,8},{24,32},{32,24},{40,48},{48,40},{56,64},{64,56},{72,... | collective-permute-start | bytes 282632 | tf_op jit(solution)/shard_map/ppermute | solution.py:503
  37.4 2.6 %collective-permute-start.2 = (f32[184,128]{1,0:T(8,128)S(1)}, f32[184,128]{1,0:T(8,128)S(1)}, u32[]{:S(2)}, u32[]{:S(2)}) collective-permute-start(f32[184,128]{1,0:T(8,128)S(1)} %get-tuple-element.29.own_message), channel_id=1, source_target_pairs={{0,8},{8,0},{16,24},{24,16},{32,40},{40,32},{48,56},{56,48},{64,72... | collective-permute-start | bytes 282632 | tf_op jit(solution)/shard_map/ppermute | solution.py:499
  40.0 0.5 unpack.1.grams
  40.6 0.0 collective-permute-done.3.inter
  40.6 0.4 collective-permute-done.2.core
  41.0 1.9 %first_half.1 = (f32[256,128]{1,0:T(8,128)S(1)}, f32[256,128]{1,0:T(8,128)S(1)}, f32[16,128]{1,0:T(8,128)S(1)}, f32[256,128]{1,0:T(8,128)S(1)}, f32[16,128]{1,0:T(8,128)S(1)}, /*index=5*/f32[8,128]{1,0:T(8,128)S(1)}) custom-call(f32[1024,128]{1,0:T(8,128)S(1)} %get-tuple-element.27.wide, f32[256,128]{1,0:T(8,128)S(1)} %get-tuple-element.28.mine.strips, ...), custom_call_target="tpu_custom_call" | custom-call | flops 4000000 | tf_op jit(solution)/shard_map/first_half/pallas_call | solution.py:53
  42.8 0.9 first_terms.1
  43.7 2.8 %collective-permute-start.5 = (f32[24,128]{1,0:T(8,128)S(1)}, f32[24,128]{1,0:T(8,128)S(1)}, u32[]{:S(2)}, u32[]{:S(2)}) collective-permute-start(f32[24,128]{1,0:T(8,128)S(1)} %get-tuple-element.35.mine), channel_id=1, source_target_pairs={{8,16},{16,8},{24,32},{32,24},{40,48},{48,40},{56,64},{64,56},{72,... | collective-permute-start | bytes 36872 | tf_op jit(solution)/shard_map/ppermute | solution.py:503
  46.6 1.9 %collective-permute-start.4 = (f32[24,128]{1,0:T(8,128)S(1)}, f32[24,128]{1,0:T(8,128)S(1)}, u32[]{:S(2)}, u32[]{:S(2)}) collective-permute-start(f32[24,128]{1,0:T(8,128)S(1)} %get-tuple-element.35.mine), channel_id=1, source_target_pairs={{0,8},{8,0},{16,24},{24,16},{32,40},{40,32},{48,56},{56,48},{64,72... | collective-permute-start | bytes 36872 | tf_op jit(solution)/shard_map/ppermute | solution.py:499
  48.5 0.2 collective-permute-done.5.inter
  48.7 0.9 collective-permute-done.4.core
  49.6 1.9 %collective-permute-start.7 = (f32[8,128]{1,0:T(8,128)S(1)}, f32[8,128]{1,0:T(8,128)S(1)}, u32[]{:S(2)}, u32[]{:S(2)}) collective-permute-start(f32[8,128]{1,0:T(8,128)S(1)} %edges_of.1), channel_id=1, source_target_pairs={{0,7},{1,2},{2,1},{3,4},{4,3},{5,6},{6,5},{7,0},{8,15},{9,10},{10,... | collective-permute-start | bytes 12296 | tf_op jit(solution)/shard_map/ppermute | solution.py:511
  51.6 2.2 %collective-permute-start.6 = (f32[8,128]{1,0:T(8,128)S(1)}, f32[8,128]{1,0:T(8,128)S(1)}, u32[]{:S(2)}, u32[]{:S(2)}) collective-permute-start(f32[8,128]{1,0:T(8,128)S(1)} %edges_of.1), channel_id=1, source_target_pairs={{0,1},{1,0},{2,3},{3,2},{4,5},{5,4},{6,7},{7,6},{8,9},{9,8},{10,11... | collective-permute-start | bytes 12296 | tf_op jit(solution)/shard_map/ppermute | solution.py:507
  53.8 1.4 %collective-permute-done.7.odd = f32[8,128]{1,0:T(8,128)S(1)} collective-permute-done((f32[8,128]{1,0:T(8,128)S(1)}, f32[8,128]{1,0:T(8,128)S(1)}, u32[]{:S(2)}, u32[]{:S(2)}) %collective-permute-start.7) | collective-permute-done | bytes 4128 | tf_op jit(solution)/shard_map/ppermute | solution.py:511
  55.2 0.9 collective-permute-done.6.even
  56.1 2.7 %second_half.1 = (f32[256,128]{1,0:T(8,128)S(1)}, f32[24,128]{1,0:T(8,128)S(1)}, f32[64,128]{1,0:T(8,128)S(1)}) custom-call(f32[256,128]{1,0:T(8,128)S(1)} %get-tuple-element.31.spots, f32[16,128]{1,0:T(8,128)S(1)} %get-tuple-element.32.by_lane, f32[24,128]{1,0:T(8,128)S(1)} %collective-permute-done.4.core, f32[24,128]{1,0:T(8,128)S(1)} %get-tuple-element.35.mine, ...), custom_call_target="tpu_custom_call" | custom-call | flops 4000000 | tf_op jit(solution)/shard_map/second_half/pallas_call | solution.py:53
  58.8 17.3 %all_to_all.15 = f32[32,2,128]{2,1,0:T(2,128)S(1)} all-to-all(f32[32,2,128]{2,1,0:T(2,128)S(1)} %bitcast.24), channel_id=1, replica_groups=mesh['lat_0'=16,'lat_1'=4,'lat_2'=2,'lon'=8] {'lat_1','lon'}, dimensions={0} | all-to-all | bytes 65536 | tf_op jit(solution)/shard_map/all_to_all | solution.py:515
  76.2 0.6 gathered.1
  76.8 22.2 %all-to-all-start.2 = ((f32[32,1,128]{2,1,0:T(1,128)}), f32[32,1,128]{2,1,0:T(1,128)S(1)}, u32[]{:S(2)}, u32[]{:S(2)}) async-start(f32[32,1,128]{2,1,0:T(1,128)} %bitcast.12), calls=%async_computation.2 | async-start | bytes 32768 | tf_op jit(solution)/shard_map/all_to_all | solution.py:515
  99.0 2.4 %collective-permute-start.9 = (f32[24,128]{1,0:T(8,128)S(1)}, f32[24,128]{1,0:T(8,128)S(1)}, u32[]{:S(2)}, u32[]{:S(2)}) collective-permute-start(f32[24,128]{1,0:T(8,128)S(1)} %get-tuple-element.43.mine), channel_id=1, source_target_pairs={{8,16},{16,8},{24,32},{32,24},{40,48},{48,40},{56,64},{64,56},{72,... | collective-permute-start | bytes 36872 | tf_op jit(solution)/shard_map/ppermute | solution.py:503
  101.4 1.9 %collective-permute-start.8 = (f32[24,128]{1,0:T(8,128)S(1)}, f32[24,128]{1,0:T(8,128)S(1)}, u32[]{:S(2)}, u32[]{:S(2)}) collective-permute-start(f32[24,128]{1,0:T(8,128)S(1)} %get-tuple-element.43.mine), channel_id=1, source_target_pairs={{0,8},{8,0},{16,24},{24,16},{32,40},{40,32},{48,56},{56,48},{64,72... | collective-permute-start | bytes 36872 | tf_op jit(solution)/shard_map/ppermute | solution.py:499
  103.3 1.0 collective-permute-done.9.inter
  104.3 0.1 collective-permute-done.8.core
  104.5 1.1 %last_rows.1.second = f32[256,128]{1,0:T(8,128)S(1)} custom-call(f32[256,128]{1,0:T(8,128)S(1)} %get-tuple-element.31.spots, f32[16,128]{1,0:T(8,128)S(1)} %get-tuple-element.32.by_lane, f32[24,128]{1,0:T(8,128)S(1)} %collective-permute-done.8.core, f32[24,128]{1,0:T(8,128)S(1)} %get-tuple-element.43.mine, f32[24,128]{1,0:T(8,128)S(1)} %collective-permute-done.9.inter, ...), custom_call_target="tpu_custom_call" | custom-call | flops 4000000 | tf_op jit(solution)/shard_map/last_rows/pallas_call | solution.py:53
  105.6 5.2 %all-to-all-done.2 = f32[32,1,128]{2,1,0:T(1,128)S(1)} async-done(((f32[32,1,128]{2,1,0:T(1,128)}), f32[32,1,128]{2,1,0:T(1,128)S(1)}, u32[]{:S(2)}, u32[]{:S(2)}) %all-to-all-start.2) | async-done | bytes 16416 | tf_op jit(solution)/shard_map/all_to_all | solution.py:515
  110.8 1.0 finish.1
  (1 shorter events, 0.0 us)
Async XLA Ops:
  4.3 7.8 %copy-start.2 = (f32[256,128]{1,0:T(8,128)S(1)}, f32[256,128]{1,0:T(8,128)}, u32[]{:S(2)}) copy-start(f32[256,128]{1,0:T(8,128)} %get-tuple-element.25) | copy-start | bytes 393220
  4.3 19.8 %copy-start.1 = (f32[256,128]{1,0:T(8,128)S(1)}, f32[256,128]{1,0:T(8,128)}, u32[]{:S(2)}) copy-start(f32[256,128]{1,0:T(8,128)} %get-tuple-element.26) | copy-start | bytes 393220
  4.3 26.3 %copy-start = (f32[2,16,16,128]{3,2,1,0:T(8,128)S(1)}, f32[2,16,16,128]{3,2,1,0:T(8,128)}, u32[]{:S(2)}) copy-start(f32[2,16,16,128]{3,2,1,0:T(8,128)} %param.7) | copy-start | bytes 786436
  4.3 26.3 %all-to-all-start = ((f32[8,168,128]{2,1,0:T(8,128)}), f32[8,168,128]{2,1,0:T(8,128)S(1)}, u32[]{:S(2)}, u32[]{:S(2)}) async-start(f32[8,168,128]{2,1,0:T(8,128)} %bitcast.25), calls=%async_computation | async-start | bytes 1376256 | tf_op jit(solution)/shard_map/all_to_all | solution.py:515
  12.1 13.9 %collective-permute-start = (f32[256,128]{1,0:T(8,128)S(1)}, f32[256,128]{1,0:T(8,128)S(1)}, u32[]{:S(2)}, u32[]{:S(2)}) collective-permute-start(f32[256,128]{1,0:T(8,128)S(1)} %copy-done.2), channel_id=1, source_target_pairs={{0,8},{8,0},{16,24},{24,16},{32,40},{40,32},{48,56},{56,48},{64,72... | collective-permute-start | bytes 393224 | tf_op jit(solution)/shard_map/ppermute | solution.py:499
  24.0 6.6 %collective-permute-start.1 = (f32[256,128]{1,0:T(8,128)S(1)}, f32[256,128]{1,0:T(8,128)S(1)}, u32[]{:S(2)}, u32[]{:S(2)}) collective-permute-start(f32[256,128]{1,0:T(8,128)S(1)} %copy-done.1), channel_id=1, source_target_pairs={{8,16},{16,8},{24,32},{32,24},{40,48},{48,40},{56,64},{64,56},{72,... | collective-permute-start | bytes 393224 | tf_op jit(solution)/shard_map/ppermute | solution.py:503
  31.0 9.5 %collective-permute-start.3 = (f32[184,128]{1,0:T(8,128)S(1)}, f32[184,128]{1,0:T(8,128)S(1)}, u32[]{:S(2)}, u32[]{:S(2)}) collective-permute-start(f32[184,128]{1,0:T(8,128)S(1)} %get-tuple-element.30), channel_id=1, source_target_pairs={{8,16},{16,8},{24,32},{32,24},{40,48},{48,40},{56,64},{64,56},{72,... | collective-permute-start | bytes 282632 | tf_op jit(solution)/shard_map/ppermute | solution.py:503
  37.4 3.5 %collective-permute-start.2 = (f32[184,128]{1,0:T(8,128)S(1)}, f32[184,128]{1,0:T(8,128)S(1)}, u32[]{:S(2)}, u32[]{:S(2)}) collective-permute-start(f32[184,128]{1,0:T(8,128)S(1)} %get-tuple-element.29.own_message), channel_id=1, source_target_pairs={{0,8},{8,0},{16,24},{24,16},{32,40},{40,32},{48,56},{56,48},{64,72... | collective-permute-start | bytes 282632 | tf_op jit(solution)/shard_map/ppermute | solution.py:499
  43.7 5.0 %collective-permute-start.5 = (f32[24,128]{1,0:T(8,128)S(1)}, f32[24,128]{1,0:T(8,128)S(1)}, u32[]{:S(2)}, u32[]{:S(2)}) collective-permute-start(f32[24,128]{1,0:T(8,128)S(1)} %get-tuple-element.35.mine), channel_id=1, source_target_pairs={{8,16},{16,8},{24,32},{32,24},{40,48},{48,40},{56,64},{64,56},{72,... | collective-permute-start | bytes 36872 | tf_op jit(solution)/shard_map/ppermute | solution.py:503
  46.6 3.1 %collective-permute-start.4 = (f32[24,128]{1,0:T(8,128)S(1)}, f32[24,128]{1,0:T(8,128)S(1)}, u32[]{:S(2)}, u32[]{:S(2)}) collective-permute-start(f32[24,128]{1,0:T(8,128)S(1)} %get-tuple-element.35.mine), channel_id=1, source_target_pairs={{0,8},{8,0},{16,24},{24,16},{32,40},{40,32},{48,56},{56,48},{64,72... | collective-permute-start | bytes 36872 | tf_op jit(solution)/shard_map/ppermute | solution.py:499
  49.6 5.6 %collective-permute-start.7 = (f32[8,128]{1,0:T(8,128)S(1)}, f32[8,128]{1,0:T(8,128)S(1)}, u32[]{:S(2)}, u32[]{:S(2)}) collective-permute-start(f32[8,128]{1,0:T(8,128)S(1)} %edges_of.1), channel_id=1, source_target_pairs={{0,7},{1,2},{2,1},{3,4},{4,3},{5,6},{6,5},{7,0},{8,15},{9,10},{10,... | collective-permute-start | bytes 12296 | tf_op jit(solution)/shard_map/ppermute | solution.py:511
  51.6 4.6 %collective-permute-start.6 = (f32[8,128]{1,0:T(8,128)S(1)}, f32[8,128]{1,0:T(8,128)S(1)}, u32[]{:S(2)}, u32[]{:S(2)}) collective-permute-start(f32[8,128]{1,0:T(8,128)S(1)} %edges_of.1), channel_id=1, source_target_pairs={{0,1},{1,0},{2,3},{3,2},{4,5},{5,4},{6,7},{7,6},{8,9},{9,8},{10,11... | collective-permute-start | bytes 12296 | tf_op jit(solution)/shard_map/ppermute | solution.py:507
  76.8 34.0 %all-to-all-start.2 = ((f32[32,1,128]{2,1,0:T(1,128)}), f32[32,1,128]{2,1,0:T(1,128)S(1)}, u32[]{:S(2)}, u32[]{:S(2)}) async-start(f32[32,1,128]{2,1,0:T(1,128)} %bitcast.12), calls=%async_computation.2 | async-start | bytes 32768 | tf_op jit(solution)/shard_map/all_to_all | solution.py:515
  99.0 5.3 %collective-permute-start.9 = (f32[24,128]{1,0:T(8,128)S(1)}, f32[24,128]{1,0:T(8,128)S(1)}, u32[]{:S(2)}, u32[]{:S(2)}) collective-permute-start(f32[24,128]{1,0:T(8,128)S(1)} %get-tuple-element.43.mine), channel_id=1, source_target_pairs={{8,16},{16,8},{24,32},{32,24},{40,48},{48,40},{56,64},{64,56},{72,... | collective-permute-start | bytes 36872 | tf_op jit(solution)/shard_map/ppermute | solution.py:503
  101.4 3.1 %collective-permute-start.8 = (f32[24,128]{1,0:T(8,128)S(1)}, f32[24,128]{1,0:T(8,128)S(1)}, u32[]{:S(2)}, u32[]{:S(2)}) collective-permute-start(f32[24,128]{1,0:T(8,128)S(1)} %get-tuple-element.43.mine), channel_id=1, source_target_pairs={{0,8},{8,0},{16,24},{24,16},{32,40},{40,32},{48,56},{56,48},{64,72... | collective-permute-start | bytes 36872 | tf_op jit(solution)/shard_map/ppermute | solution.py:499

commit v6 on v5

--- a/solution.py
+++ b/solution.py
@@ -21,7 +21,7 @@
 NEAR = 3 * OWN
 BULK = 2 * HALF + 2
 LIST = BULK + 6
-PARCEL = LIST + 32
+PARCEL = LIST
 EDGE = HALO * 2 * LEVELS
 STRIP = HALO * 2 * 8
 LEFTS = STRIP + OWN
@@ -66,6 +66,10 @@
     return [sum([(o == owners[j]).astype(jnp.int32) for o in owners[:j]], jnp.int32(0)) for j in range(CAP)]
 
 
+def chunk(owner):
+    return (owner + LON // 2) % LON if isinstance(owner, int) else lax.rem(owner + LON // 2, LON)
+
+
 def packed_edges(pick, shift):
     ln = lanes(8)
     out = jnp.zeros((8, LANES), F32)
@@ -80,17 +84,17 @@
     ln, rw = lanes(HALF), places(HALF)
     for j in range(CAP):
         block = matrix[j]
-        scaled = jnp.transpose(block) * jnp.where(j < count[0], weight[j : j + 1, :], 0.0)
+        scaled = jnp.transpose(block) * jnp.where(j < count[0, 0], weight[j : j + 1, :], 0.0)
         gram = jnp.dot(scaled, block, precision=HIGHEST, preferred_element_type=F32)
         top, low = gram[:HALF], gram[HALF:]
         packed = jnp.where((ln >= HALF) & (ln - HALF <= rw), roll(top, HALF), low)
         diagonal = jnp.sum(jnp.where(ln - HALF == rw, low, 0.0), axis=0, keepdims=True)
-        at = owners[j] * PARCEL + turns[j] * HALF
+        at = chunk(owners[j]) * PARCEL + turns[j] * HALF
         parcels[pl.ds(pl.multiple_of(at, 8), HALF), :] = packed
-        parcels[pl.ds(owners[j] * PARCEL + 2 * HALF + turns[j], 1), :] = diagonal
-
-
-def prepare(owner_at, row_at, count_at, flow_at, matrix_at, weight_at, innovation_at, parcels, to_core, to_inter, owner, row, count, flow, matrix, weight, innovation, lists, sems):
+        parcels[pl.ds(chunk(owners[j]) * PARCEL + 2 * HALF + turns[j], 1), :] = diagonal
+
+
+def prepare(owner_at, row_at, count_at, flow_at, matrix_at, weight_at, innovation_at, parcels, to_core, to_inter, to_even, to_odd, owner, row, count, flow, matrix, weight, innovation, lists, sems):
     pairs = ((owner_at, owner), (row_at, row), (count_at, count), (flow_at, flow), (weight_at, weight), (innovation_at, innovation), (matrix_at, matrix))
     copies = [pltpu.make_async_copy(a, b, sems.at[i]) for i, (a, b) in enumerate(pairs)]
     for copy in copies:
@@ -98,10 +102,8 @@
     for d in range(LON):
         parcels[d * PARCEL : d * PARCEL + LIST, :] = jnp.zeros((LIST, LANES), F32)
     lists[...] = jnp.zeros(lists.shape, F32)
-    me = lax.axis_index("lon")
     even = lax.axis_index("lat_2") == 0
-    to_right = lax.rem(me + 1, LON) * PARCEL + LIST
-    to_left = lax.rem(me + LON - 1, LON) * PARCEL + LIST
+    here = lax.rem(lax.axis_index("lon"), 2) == 0
     copies[3].wait()
     for f in range(2):
         for g in range(2):
@@ -111,8 +113,9 @@
                 return flow[pl.ds(at, 8, stride=ROWS), :], flow[pl.ds(at + 8 * ROWS, 8, stride=ROWS), :]
 
             at = (f * 2 + g) * 8
-            parcels[pl.ds(pl.multiple_of(to_right + at, 8), 8), :] = packed_edges(pick, 8)
-            parcels[pl.ds(pl.multiple_of(to_left + at, 8), 8), :] = packed_edges(pick, 0)
+            to_right, to_left = packed_edges(pick, 8), packed_edges(pick, 0)
+            to_even[at : at + 8, :] = jnp.where(here, to_right, to_left)
+            to_odd[at : at + 8, :] = jnp.where(here, to_left, to_right)
         for i in range(HALO):
             for h in range(2):
                 at = f * LEVELS * ROWS + h * 8 * ROWS + i
@@ -128,7 +131,7 @@
     ln = lanes(8)
     named = jnp.full((8, LANES), NOWHERE, F32)
     for j in range(CAP):
-        live = j < count[0]
+        live = j < count[0, 0]
         total = jnp.zeros((8, LANES), F32)
         for k in range(LANES // 8):
             total += matrix[j, k * 8 : k * 8 + 8, :] * column[k * 8 : k * 8 + 8, j : j + 1]
@@ -141,7 +144,7 @@
     line = lanes(1)
     for d in range(LON):
         left, right = 2 * (d - 1) % OWN, 2 * (d + 1) % OWN
-        at = d * PARCEL + BULK
+        at = chunk(d) * PARCEL + BULK
         parcels[at : at + 2, :] = lists[2 * d : 2 * d + 2, :]
         edge = jnp.where(line < 8, roll(lists[left : left + 1, :], 8), roll(lists[left + 1 : left + 2, :], 16))
         edge = jnp.where(line < 16, edge, jnp.where(line < 24, roll(lists[right : right + 1, :], 16), roll(lists[right + 1 : right + 2, :], 24)))
@@ -149,19 +152,17 @@
         parcels[at + 3 : at + 4, :] = roll(named, -left)[:1]
 
 
-def arrange(flow, parcels, core, inter, wide, strips, to_core, to_inter):
+def arrange(flow, parcels, core, inter, even_edges, odd_edges, wide, strips, to_core, to_inter):
     ln = lanes(8)
-    me = lax.axis_index("lon")
+    here = lax.rem(lax.axis_index("lon"), 2) == 0
     even = lax.axis_index("lat_2") == 0
     wide[:EDGE, :] = jnp.where(even, inter[...], core[...])
     wide[EDGE + ROWS * 2 * LEVELS :, :] = jnp.where(even, core[...], inter[...])
-    from_left = lax.rem(me + LON - 1, LON) * PARCEL + LIST
-    from_right = lax.rem(me + 1, LON) * PARCEL + LIST
     for f in range(2):
         for g in range(2):
             at = (f * 2 + g) * 8
-            left = parcels[pl.ds(pl.multiple_of(from_left + at, 8), 8), :]
-            right = parcels[pl.ds(pl.multiple_of(from_right + at, 8), 8), :]
+            first, second = even_edges[at : at + 8, :], odd_edges[at : at + 8, :]
+            left, right = jnp.where(here, second, first), jnp.where(here, first, second)
             for k in range(8):
                 at = f * LEVELS * ROWS + g * 8 + k
                 low, high = flow[pl.ds(at, 8, stride=ROWS), :], flow[pl.ds(at + 8 * ROWS, 8, stride=ROWS), :]
@@ -450,7 +451,13 @@
 
 
 def in_plane(step):
-    return lax.axis_index("lat_1") * LON + lax.rem(lax.axis_index("lon") + LON + step, LON)
+    size = lax.axis_size(("lat_1", "lon"))
+    at = lax.axis_index("lat_1") * LON + lax.rem(lax.axis_index("lon") + LON + step, LON)
+    return lax.rem(at + size - middle_of_plane(), size)
+
+
+def middle_of_plane():
+    return lax.axis_size("lat_1") // 2 * LON + LON // 2
 
 
 def gathered(parts, mine, sums, message):
@@ -511,31 +518,33 @@
     return lax.ppermute(x, "lon", [(i, (((i + 1) % LON ^ 1) - 1) % LON) for i in range(LON)])
 
 
-def spread_out(x, axes):
-    return lax.all_to_all(x, axes, split_axis=0, concat_axis=0, tiled=True)
+def spread_out(x, axes, first):
+    count = lax.axis_size(axes)
+    group = [(i + first) % count for i in range(count)]
+    return lax.all_to_all(x, axes, split_axis=0, concat_axis=0, tiled=True, axis_index_groups=[group])
 
 
 def shards(courant, obs_matrix, obs_weight, innovation, block_owner, block_row, block_count):
     flow = courant.reshape(-1, LANES)
-    owner, row, count = block_owner.reshape(-1), block_row.reshape(-1), block_count.reshape(-1)
+    owner, row, count = block_owner.reshape(-1), block_row.reshape(-1), block_count
     wholes = (flow, obs_matrix[0], obs_weight[0], innovation[0])
-    parcels, for_core, for_inter = call(
+    parcels, for_core, for_inter, for_even, for_odd = call(
         prepare,
-        [(LON * PARCEL, LANES), (EDGE, LANES), (EDGE, LANES)],
+        [(LON * PARCEL, LANES), (EDGE, LANES), (EDGE, LANES), (2 * OWN, LANES), (2 * OWN, LANES)],
         (owner, row, count, *wholes),
         4_000_000,
-        [pltpu.SMEM((CAP,), jnp.int32), pltpu.SMEM((CAP,), jnp.int32), pltpu.SMEM((1,), jnp.int32)]
+        [pltpu.SMEM((CAP,), jnp.int32), pltpu.SMEM((CAP,), jnp.int32), pltpu.SMEM((1, 1), jnp.int32)]
         + [pltpu.VMEM(x.shape, F32) for x in wholes]
         + [pltpu.VMEM((OWN, LANES), F32), pltpu.SemaphoreType.DMA((7,))],
         [pl.BlockSpec(memory_space=pltpu.HBM)] * 7,
         62,
     )
-    parcels = spread_out(parcels.reshape(LON, PARCEL, LANES), "lon").reshape(LON * PARCEL, LANES)
+    parcels = spread_out(parcels.reshape(LON, PARCEL, LANES), "lon", LON // 2).reshape(LON * PARCEL, LANES)
     core, inter = to_core(for_core), to_inter(for_inter)
     wide, strips, for_core, for_inter = call(
         arrange,
         [(WIDE * 2 * LEVELS, LANES), (2 * STRIP, LANES), (MESSAGE, LANES), (MESSAGE, LANES)],
-        (flow, parcels, core, inter),
+        (flow, parcels, core, inter, to_even(for_even), to_odd(for_odd)),
         2_000_000,
     )
     core, inter = to_core(for_core), to_inter(for_inter)
@@ -560,10 +569,10 @@
     image, mine, parcels = call(
         second_half, [cells, short, (plane * 2, LANES)], (spots, by_lane, *lists, *rates, grams, sums), 4_000_000, work_too
     )
-    parcels = spread_out(parcels.reshape(plane, 2, LANES), ("lat_1", "lon")).reshape(plane * 2, LANES)
+    parcels = spread_out(parcels.reshape(plane, 2, LANES), ("lat_1", "lon"), middle_of_plane()).reshape(plane * 2, LANES)
     sums, mine = call(gathered, [(towers, LANES), short], (parcels, mine), 10_000)
     core, inter = to_core(mine), to_inter(mine)
-    parts = spread_out(sums.reshape(towers, 1, LANES), ("lat_0", "lat_2")).reshape(towers, LANES)
+    parts = spread_out(sums.reshape(towers, 1, LANES), ("lat_0", "lat_2"), towers * 12 // 16 + 1).reshape(towers, LANES)
     (second,) = call(last_rows, [cells], (spots, by_lane, core, mine, inter, *rates), 4_000_000, work)
     increment, residual = call(finish, [cells, cells], (parts, right_side, image, second), 100_000)
     shape = courant.shape[1:]

time: 112 us -> 103 us (0.920)
  blocking collectives: 17.3 us -> 11 us
  waiting for transfers between devices: 14.8 us -> 8.95 us
  starting transfers between devices: 66 us -> 69.1 us
    all_to_all x1, blocking collectives: 17.3 us -> 11 us  [spread_out(): lax.all_to_all(x, axes, split_axis=0, concat_axis=0, tiled=True, axis_ind...]
    ppermute x4, waiting for transfers between devices: 5.89 us -> 0.43 us  [to_inter(): lax.ppermute(x, LAT, [(i, (i + 1 ^ 1) - 1) for i in range(1, lax.axis_siz...]
    all_to_all x2, waiting for transfers between devices: 5.17 us -> 0.01 us  [spread_out(): lax.all_to_all(x, axes, split_axis=0, concat_axis=0, tiled=True, axis_ind...]
    ppermute x1 -> x2, waiting for transfers between devices: 1.43 us -> 4.87 us  [to_odd(): lax.ppermute(x, 'lon', [(i, (((i + 1) % LON ^ 1) - 1) % LON) for i in ran...]
    ppermute x1 -> x2, starting transfers between devices: 1.91 us -> 4.36 us  [to_odd(): lax.ppermute(x, 'lon', [(i, (((i + 1) % LON ^ 1) - 1) % LON) for i in ran...]
    ppermute x1 -> x2, starting transfers between devices: 2.19 us -> 4.11 us  [to_even(): return lax.ppermute(x, 'lon', [(i, i ^ 1) for i in range(LON)])]
    all_to_all x2, starting transfers between devices: 30 us -> 28.4 us  [spread_out(): lax.all_to_all(x, axes, split_axis=0, concat_axis=0, tiled=True, axis_ind...]
    ppermute x4, waiting for transfers between devices: 1.43 us -> 2.6 us  [to_core(): return lax.ppermute(x, LAT, [(i, i ^ 1) for i in range(lax.axis_size(LAT))])]
  transfers between devices with their start and end apart: 12 -> 14, of which waited for: 9 -> 8; matrix products, arithmetic and copies ran while one was open for 0% -> 0% of each run, Pallas kernels for 1% -> 2%
where the time goes in v6:
time: 103 us
  starting transfers between devices  69.1 us (67%)
  Pallas kernels  12.1 us (12%)
  blocking collectives  11 us (11%)
  waiting for transfers between devices  8.95 us (9%)
  between operations  1.5 us (1%)
    all_to_all x2, starting transfers between devices, spread_out(): lax.all_to_all(x, axes, split_axis=0, concat_axis=0, tiled=True, axis_ind...  28.4 us
    ppermute x4, starting transfers between devices, to_core(): return lax.ppermute(x, LAT, [(i, i ^ 1) for i in range(lax.axis_size(LAT))])  19.2 us
    ppermute x4, starting transfers between devices, to_inter(): lax.ppermute(x, LAT, [(i, (i + 1 ^ 1) - 1) for i in range(1, lax.axis_siz...  13 us
    pallas_call x10, Pallas kernels, call(): pl.pallas_call(body, out_shape=[jax.ShapeDtypeStruct(s, F32) for s in out...  12.1 us
    all_to_all x1, blocking collectives, spread_out(): lax.all_to_all(x, axes, split_axis=0, concat_axis=0, tiled=True, axis_ind...  11 us
    ppermute x2, waiting for transfers between devices, to_odd(): lax.ppermute(x, 'lon', [(i, (((i + 1) % LON ^ 1) - 1) % LON) for i in ran...  4.87 us
    ppermute x2, starting transfers between devices, to_odd(): lax.ppermute(x, 'lon', [(i, (((i + 1) % LON ^ 1) - 1) % LON) for i in ran...  4.36 us
    ppermute x2, starting transfers between devices, to_even(): return lax.ppermute(x, 'lon', [(i, i ^ 1) for i in range(LON)])  4.11 us
  transfers between devices with their start and end apart: 14, of which 8 were waited for; matrix products, arithmetic and copies ran while one was open for 0% of the time, Pallas kernels for 2%

profile of v6, /device:TPU:1, one launch (start us, length us, event | category | flops | bytes accessed | tf_op | source)
XLA Modules:
  0.0 102.6 jit_solution(15325104137114811296)
XLA Ops:
  1.3 2.9 %prepare.1 = (f32[1088,128]{1,0:T(8,128)}, f32[256,128]{1,0:T(8,128)}, f32[256,128]{1,0:T(8,128)}, f32[32,128]{1,0:T(8,128)}, f32[32,128]{1,0:T(8,128)}) custom-call(s32[8]{0:T(128)} %bitcast.27, s32[8]{0:T(128)} %bitcast.28, s32[1,1]{1,0:T(1,128)S(6)} %copy.10.count_at, f32[512,128]{1,0:T(8,128)} %bitcast.18, f32[8,128,128]{2,1,0:T(8,128)} %bitcast.24, ...), custom_call_target="tpu_custom_call" | custom-call | flops 4000000 | tf_op jit(solution)/shard_map/prepare/pallas_call | solution.py:53
  4.2 0.0 copy-start.2
  4.2 0.0 copy-start.1
  4.3 0.0 copy-start.4
  4.3 0.0 copy-start.3
  4.3 0.0 copy-start
  4.3 10.0 %all-to-all-start = ((f32[8,136,128]{2,1,0:T(8,128)}), f32[8,136,128]{2,1,0:T(8,128)S(1)}, u32[]{:S(2)}, u32[]{:S(2)}) async-start(f32[8,136,128]{2,1,0:T(8,128)} %bitcast.23), calls=%async_computation | async-start | bytes 1114112 | tf_op jit(solution)/shard_map/all_to_all | solution.py:524
  14.3 0.0 copy-done.2
  14.3 13.4 %collective-permute-start = (f32[256,128]{1,0:T(8,128)S(1)}, f32[256,128]{1,0:T(8,128)S(1)}, u32[]{:S(2)}, u32[]{:S(2)}) collective-permute-start(f32[256,128]{1,0:T(8,128)S(1)} %copy-done.2), channel_id=1, source_target_pairs={{0,8},{8,0},{16,24},{24,16},{32,40},{40,32},{48,56},{56,48},{64,72... | collective-permute-start | bytes 393224 | tf_op jit(solution)/shard_map/ppermute | solution.py:506
  27.7 0.0 copy-done.1
  27.7 1.9 %collective-permute-start.1 = (f32[256,128]{1,0:T(8,128)S(1)}, f32[256,128]{1,0:T(8,128)S(1)}, u32[]{:S(2)}, u32[]{:S(2)}) collective-permute-start(f32[256,128]{1,0:T(8,128)S(1)} %copy-done.1), channel_id=1, source_target_pairs={{8,16},{16,8},{24,32},{32,24},{40,48},{48,40},{56,64},{64,56},{72,... | collective-permute-start | bytes 393224 | tf_op jit(solution)/shard_map/ppermute | solution.py:510
  29.6 0.0 copy-done.4
  29.6 2.2 %collective-permute-start.2 = (f32[32,128]{1,0:T(8,128)S(1)}, f32[32,128]{1,0:T(8,128)S(1)}, u32[]{:S(2)}, u32[]{:S(2)}) collective-permute-start(f32[32,128]{1,0:T(8,128)S(1)} %copy-done.4), channel_id=1, source_target_pairs={{0,1},{1,0},{2,3},{3,2},{4,5},{5,4},{6,7},{7,6},{8,9},{9,8},{10,11... | collective-permute-start | bytes 49160 | tf_op jit(solution)/shard_map/ppermute | solution.py:514
  31.8 0.0 copy-done.3
  31.8 2.2 %collective-permute-start.3 = (f32[32,128]{1,0:T(8,128)S(1)}, f32[32,128]{1,0:T(8,128)S(1)}, u32[]{:S(2)}, u32[]{:S(2)}) collective-permute-start(f32[32,128]{1,0:T(8,128)S(1)} %copy-done.3), channel_id=1, source_target_pairs={{0,7},{1,2},{2,1},{3,4},{4,3},{5,6},{6,5},{7,0},{8,15},{9,10},{10,... | collective-permute-start | bytes 49160 | tf_op jit(solution)/shard_map/ppermute | solution.py:518
  34.0 0.1 collective-permute-done.2.even_edges
  34.1 3.4 %collective-permute-done.3.odd_edges = f32[32,128]{1,0:T(8,128)S(1)} collective-permute-done((f32[32,128]{1,0:T(8,128)S(1)}, f32[32,128]{1,0:T(8,128)S(1)}, u32[]{:S(2)}, u32[]{:S(2)}) %collective-permute-start.3) | collective-permute-done | bytes 16416 | tf_op jit(solution)/shard_map/ppermute | solution.py:518
  37.5 0.0 collective-permute-done.core
  37.5 0.0 collective-permute-done.1.inter
  37.5 0.0 all-to-all-done
  37.5 0.0 copy-done
  37.5 0.4 arrange.1
  37.9 5.1 %collective-permute-start.5 = (f32[184,128]{1,0:T(8,128)S(1)}, f32[184,128]{1,0:T(8,128)S(1)}, u32[]{:S(2)}, u32[]{:S(2)}) collective-permute-start(f32[184,128]{1,0:T(8,128)S(1)} %get-tuple-element.34), channel_id=1, source_target_pairs={{8,16},{16,8},{24,32},{32,24},{40,48},{48,40},{56,64},{64,56},{72,... | collective-permute-start | bytes 282632 | tf_op jit(solution)/shard_map/ppermute | solution.py:510
  43.0 1.9 %collective-permute-start.4 = (f32[184,128]{1,0:T(8,128)S(1)}, f32[184,128]{1,0:T(8,128)S(1)}, u32[]{:S(2)}, u32[]{:S(2)}) collective-permute-start(f32[184,128]{1,0:T(8,128)S(1)} %get-tuple-element.33.own_message), channel_id=1, source_target_pairs={{0,8},{8,0},{16,24},{24,16},{32,40},{40,32},{48,56},{56,48},{64,72... | collective-permute-start | bytes 282632 | tf_op jit(solution)/shard_map/ppermute | solution.py:506
  44.9 0.5 unpack.1.grams
  45.4 0.0 collective-permute-done.5.inter
  45.5 0.7 collective-permute-done.4.core
  46.2 1.9 %first_half.1 = (f32[256,128]{1,0:T(8,128)S(1)}, f32[256,128]{1,0:T(8,128)S(1)}, f32[16,128]{1,0:T(8,128)S(1)}, f32[256,128]{1,0:T(8,128)S(1)}, f32[16,128]{1,0:T(8,128)S(1)}, /*index=5*/f32[8,128]{1,0:T(8,128)S(1)}) custom-call(f32[1024,128]{1,0:T(8,128)S(1)} %get-tuple-element.31.wide, f32[256,128]{1,0:T(8,128)S(1)} %get-tuple-element.32.mine.strips, ...), custom_call_target="tpu_custom_call" | custom-call | flops 4000000 | tf_op jit(solution)/shard_map/first_half/pallas_call | solution.py:53
  48.1 0.9 first_terms.1
  49.0 2.7 %collective-permute-start.7 = (f32[24,128]{1,0:T(8,128)S(1)}, f32[24,128]{1,0:T(8,128)S(1)}, u32[]{:S(2)}, u32[]{:S(2)}) collective-permute-start(f32[24,128]{1,0:T(8,128)S(1)} %get-tuple-element.39.mine), channel_id=1, source_target_pairs={{8,16},{16,8},{24,32},{32,24},{40,48},{48,40},{56,64},{64,56},{72,... | collective-permute-start | bytes 36872 | tf_op jit(solution)/shard_map/ppermute | solution.py:510
  51.7 1.9 %collective-permute-start.6 = (f32[24,128]{1,0:T(8,128)S(1)}, f32[24,128]{1,0:T(8,128)S(1)}, u32[]{:S(2)}, u32[]{:S(2)}) collective-permute-start(f32[24,128]{1,0:T(8,128)S(1)} %get-tuple-element.39.mine), channel_id=1, source_target_pairs={{0,8},{8,0},{16,24},{24,16},{32,40},{40,32},{48,56},{56,48},{64,72... | collective-permute-start | bytes 36872 | tf_op jit(solution)/shard_map/ppermute | solution.py:506
  53.6 0.4 collective-permute-done.7.inter
  54.0 0.8 collective-permute-done.6.core
  54.8 2.2 %collective-permute-start.9 = (f32[8,128]{1,0:T(8,128)S(1)}, f32[8,128]{1,0:T(8,128)S(1)}, u32[]{:S(2)}, u32[]{:S(2)}) collective-permute-start(f32[8,128]{1,0:T(8,128)S(1)} %edges_of.1), channel_id=1, source_target_pairs={{0,7},{1,2},{2,1},{3,4},{4,3},{5,6},{6,5},{7,0},{8,15},{9,10},{10,... | collective-permute-start | bytes 12296 | tf_op jit(solution)/shard_map/ppermute | solution.py:518
  56.9 1.9 %collective-permute-start.8 = (f32[8,128]{1,0:T(8,128)S(1)}, f32[8,128]{1,0:T(8,128)S(1)}, u32[]{:S(2)}, u32[]{:S(2)}) collective-permute-start(f32[8,128]{1,0:T(8,128)S(1)} %edges_of.1), channel_id=1, source_target_pairs={{0,1},{1,0},{2,3},{3,2},{4,5},{5,4},{6,7},{7,6},{8,9},{9,8},{10,11... | collective-permute-start | bytes 12296 | tf_op jit(solution)/shard_map/ppermute | solution.py:514
  58.9 1.4 %collective-permute-done.9.odd = f32[8,128]{1,0:T(8,128)S(1)} collective-permute-done((f32[8,128]{1,0:T(8,128)S(1)}, f32[8,128]{1,0:T(8,128)S(1)}, u32[]{:S(2)}, u32[]{:S(2)}) %collective-permute-start.9) | collective-permute-done | bytes 4128 | tf_op jit(solution)/shard_map/ppermute | solution.py:518
  60.3 1.0 collective-permute-done.8.even
  61.3 2.8 %second_half.1 = (f32[256,128]{1,0:T(8,128)S(1)}, f32[24,128]{1,0:T(8,128)S(1)}, f32[64,128]{1,0:T(8,128)S(1)}) custom-call(f32[256,128]{1,0:T(8,128)S(1)} %get-tuple-element.35.spots, f32[16,128]{1,0:T(8,128)S(1)} %get-tuple-element.36.by_lane, f32[24,128]{1,0:T(8,128)S(1)} %collective-permute-done.6.core, f32[24,128]{1,0:T(8,128)S(1)} %get-tuple-element.39.mine, ...), custom_call_target="tpu_custom_call" | custom-call | flops 4000000 | tf_op jit(solution)/shard_map/second_half/pallas_call | solution.py:53
  64.1 11.0 %all_to_all.15 = f32[32,2,128]{2,1,0:T(2,128)S(1)} all-to-all(f32[32,2,128]{2,1,0:T(2,128)S(1)} %bitcast.22), channel_id=1, replica_groups={{36,37,38,39,48,49,50,51,52,53,54,55,0,1,2,3,4,5,6,7,16,17,18,19,20,21,..., dimensions={0} | all-to-all | bytes 65536 | tf_op jit(solution)/shard_map/all_to_all | solution.py:524
  75.0 0.6 gathered.1
  75.7 18.5 %all-to-all-start.2 = ((f32[32,1,128]{2,1,0:T(1,128)}), f32[32,1,128]{2,1,0:T(1,128)S(1)}, u32[]{:S(2)}, u32[]{:S(2)}) async-start(f32[32,1,128]{2,1,0:T(1,128)} %bitcast.11), calls=%async_computation.2 | async-start | bytes 32768 | tf_op jit(solution)/shard_map/all_to_all | solution.py:524
  94.1 3.3 %collective-permute-start.11 = (f32[24,128]{1,0:T(8,128)S(1)}, f32[24,128]{1,0:T(8,128)S(1)}, u32[]{:S(2)}, u32[]{:S(2)}) collective-permute-start(f32[24,128]{1,0:T(8,128)S(1)} %get-tuple-element.47.mine), channel_id=1, source_target_pairs={{8,16},{16,8},{24,32},{32,24},{40,48},{48,40},{56,64},{64,56},{72,... | collective-permute-start | bytes 36872 | tf_op jit(solution)/shard_map/ppermute | solution.py:510
  97.5 1.9 %collective-permute-start.10 = (f32[24,128]{1,0:T(8,128)S(1)}, f32[24,128]{1,0:T(8,128)S(1)}, u32[]{:S(2)}, u32[]{:S(2)}) collective-permute-start(f32[24,128]{1,0:T(8,128)S(1)} %get-tuple-element.47.mine), channel_id=1, source_target_pairs={{0,8},{8,0},{16,24},{24,16},{32,40},{40,32},{48,56},{56,48},{64,72... | collective-permute-start | bytes 36872 | tf_op jit(solution)/shard_map/ppermute | solution.py:506
  99.4 0.0 collective-permute-done.11.inter
  99.4 1.1 %collective-permute-done.10.core = f32[24,128]{1,0:T(8,128)S(1)} collective-permute-done((f32[24,128]{1,0:T(8,128)S(1)}, f32[24,128]{1,0:T(8,128)S(1)}, u32[]{:S(2)}, u32[]{:S(2)}) %collective-permute-start.10) | collective-permute-done | bytes 12320 | tf_op jit(solution)/shard_map/ppermute | solution.py:506
  100.5 1.1 %last_rows.1.second = f32[256,128]{1,0:T(8,128)S(1)} custom-call(f32[256,128]{1,0:T(8,128)S(1)} %get-tuple-element.35.spots, f32[16,128]{1,0:T(8,128)S(1)} %get-tuple-element.36.by_lane, f32[24,128]{1,0:T(8,128)S(1)} %collective-permute-done.10.core, f32[24,128]{1,0:T(8,128)S(1)} %get-tuple-element.47.mine, f32[24,128]{1,0:T(8,128)S(1)} %collective-permute-done.11.inter, ...), custom_call_target="tpu_custom_call" | custom-call | flops 4000000 | tf_op jit(solution)/shard_map/last_rows/pallas_call | solution.py:53
  101.7 0.0 all-to-all-done.2
  101.7 1.0 finish.1
  (1 shorter events, 0.0 us)
Async XLA Ops:
  4.2 10.0 %copy-start.2 = (f32[256,128]{1,0:T(8,128)S(1)}, f32[256,128]{1,0:T(8,128)}, u32[]{:S(2)}) copy-start(f32[256,128]{1,0:T(8,128)} %get-tuple-element.27) | copy-start | bytes 393220
  4.2 23.4 %copy-start.1 = (f32[256,128]{1,0:T(8,128)S(1)}, f32[256,128]{1,0:T(8,128)}, u32[]{:S(2)}) copy-start(f32[256,128]{1,0:T(8,128)} %get-tuple-element.28) | copy-start | bytes 393220
  4.3 25.3 %copy-start.4 = (f32[32,128]{1,0:T(8,128)S(1)}, f32[32,128]{1,0:T(8,128)}, u32[]{:S(2)}) copy-start(f32[32,128]{1,0:T(8,128)} %get-tuple-element.29) | copy-start | bytes 49156
  4.3 27.5 %copy-start.3 = (f32[32,128]{1,0:T(8,128)S(1)}, f32[32,128]{1,0:T(8,128)}, u32[]{:S(2)}) copy-start(f32[32,128]{1,0:T(8,128)} %get-tuple-element.30) | copy-start | bytes 49156
  4.3 33.3 %copy-start = (f32[2,16,16,128]{3,2,1,0:T(8,128)S(1)}, f32[2,16,16,128]{3,2,1,0:T(8,128)}, u32[]{:S(2)}) copy-start(f32[2,16,16,128]{3,2,1,0:T(8,128)} %param.7) | copy-start | bytes 786436
  4.3 33.2 %all-to-all-start = ((f32[8,136,128]{2,1,0:T(8,128)}), f32[8,136,128]{2,1,0:T(8,128)S(1)}, u32[]{:S(2)}, u32[]{:S(2)}) async-start(f32[8,136,128]{2,1,0:T(8,128)} %bitcast.23), calls=%async_computation | async-start | bytes 1114112 | tf_op jit(solution)/shard_map/all_to_all | solution.py:524
  14.3 23.3 %collective-permute-start = (f32[256,128]{1,0:T(8,128)S(1)}, f32[256,128]{1,0:T(8,128)S(1)}, u32[]{:S(2)}, u32[]{:S(2)}) collective-permute-start(f32[256,128]{1,0:T(8,128)S(1)} %copy-done.2), channel_id=1, source_target_pairs={{0,8},{8,0},{16,24},{24,16},{32,40},{40,32},{48,56},{56,48},{64,72... | collective-permute-start | bytes 393224 | tf_op jit(solution)/shard_map/ppermute | solution.py:506
  27.7 9.8 %collective-permute-start.1 = (f32[256,128]{1,0:T(8,128)S(1)}, f32[256,128]{1,0:T(8,128)S(1)}, u32[]{:S(2)}, u32[]{:S(2)}) collective-permute-start(f32[256,128]{1,0:T(8,128)S(1)} %copy-done.1), channel_id=1, source_target_pairs={{8,16},{16,8},{24,32},{32,24},{40,48},{48,40},{56,64},{64,56},{72,... | collective-permute-start | bytes 393224 | tf_op jit(solution)/shard_map/ppermute | solution.py:510
  29.6 4.5 %collective-permute-start.2 = (f32[32,128]{1,0:T(8,128)S(1)}, f32[32,128]{1,0:T(8,128)S(1)}, u32[]{:S(2)}, u32[]{:S(2)}) collective-permute-start(f32[32,128]{1,0:T(8,128)S(1)} %copy-done.4), channel_id=1, source_target_pairs={{0,1},{1,0},{2,3},{3,2},{4,5},{5,4},{6,7},{7,6},{8,9},{9,8},{10,11... | collective-permute-start | bytes 49160 | tf_op jit(solution)/shard_map/ppermute | solution.py:514
  31.8 5.7 %collective-permute-start.3 = (f32[32,128]{1,0:T(8,128)S(1)}, f32[32,128]{1,0:T(8,128)S(1)}, u32[]{:S(2)}, u32[]{:S(2)}) collective-permute-start(f32[32,128]{1,0:T(8,128)S(1)} %copy-done.3), channel_id=1, source_target_pairs={{0,7},{1,2},{2,1},{3,4},{4,3},{5,6},{6,5},{7,0},{8,15},{9,10},{10,... | collective-permute-start | bytes 49160 | tf_op jit(solution)/shard_map/ppermute | solution.py:518
  37.9 7.5 %collective-permute-start.5 = (f32[184,128]{1,0:T(8,128)S(1)}, f32[184,128]{1,0:T(8,128)S(1)}, u32[]{:S(2)}, u32[]{:S(2)}) collective-permute-start(f32[184,128]{1,0:T(8,128)S(1)} %get-tuple-element.34), channel_id=1, source_target_pairs={{8,16},{16,8},{24,32},{32,24},{40,48},{48,40},{56,64},{64,56},{72,... | collective-permute-start | bytes 282632 | tf_op jit(solution)/shard_map/ppermute | solution.py:510
  43.0 3.2 %collective-permute-start.4 = (f32[184,128]{1,0:T(8,128)S(1)}, f32[184,128]{1,0:T(8,128)S(1)}, u32[]{:S(2)}, u32[]{:S(2)}) collective-permute-start(f32[184,128]{1,0:T(8,128)S(1)} %get-tuple-element.33.own_message), channel_id=1, source_target_pairs={{0,8},{8,0},{16,24},{24,16},{32,40},{40,32},{48,56},{56,48},{64,72... | collective-permute-start | bytes 282632 | tf_op jit(solution)/shard_map/ppermute | solution.py:506
  49.0 5.0 %collective-permute-start.7 = (f32[24,128]{1,0:T(8,128)S(1)}, f32[24,128]{1,0:T(8,128)S(1)}, u32[]{:S(2)}, u32[]{:S(2)}) collective-permute-start(f32[24,128]{1,0:T(8,128)S(1)} %get-tuple-element.39.mine), channel_id=1, source_target_pairs={{8,16},{16,8},{24,32},{32,24},{40,48},{48,40},{56,64},{64,56},{72,... | collective-permute-start | bytes 36872 | tf_op jit(solution)/shard_map/ppermute | solution.py:510
  51.7 3.1 %collective-permute-start.6 = (f32[24,128]{1,0:T(8,128)S(1)}, f32[24,128]{1,0:T(8,128)S(1)}, u32[]{:S(2)}, u32[]{:S(2)}) collective-permute-start(f32[24,128]{1,0:T(8,128)S(1)} %get-tuple-element.39.mine), channel_id=1, source_target_pairs={{0,8},{8,0},{16,24},{24,16},{32,40},{40,32},{48,56},{56,48},{64,72... | collective-permute-start | bytes 36872 | tf_op jit(solution)/shard_map/ppermute | solution.py:506
  54.8 5.6 %collective-permute-start.9 = (f32[8,128]{1,0:T(8,128)S(1)}, f32[8,128]{1,0:T(8,128)S(1)}, u32[]{:S(2)}, u32[]{:S(2)}) collective-permute-start(f32[8,128]{1,0:T(8,128)S(1)} %edges_of.1), channel_id=1, source_target_pairs={{0,7},{1,2},{2,1},{3,4},{4,3},{5,6},{6,5},{7,0},{8,15},{9,10},{10,... | collective-permute-start | bytes 12296 | tf_op jit(solution)/shard_map/ppermute | solution.py:518
  56.9 4.4 %collective-permute-start.8 = (f32[8,128]{1,0:T(8,128)S(1)}, f32[8,128]{1,0:T(8,128)S(1)}, u32[]{:S(2)}, u32[]{:S(2)}) collective-permute-start(f32[8,128]{1,0:T(8,128)S(1)} %edges_of.1), channel_id=1, source_target_pairs={{0,1},{1,0},{2,3},{3,2},{4,5},{5,4},{6,7},{7,6},{8,9},{9,8},{10,11... | collective-permute-start | bytes 12296 | tf_op jit(solution)/shard_map/ppermute | solution.py:514
  75.7 26.0 %all-to-all-start.2 = ((f32[32,1,128]{2,1,0:T(1,128)}), f32[32,1,128]{2,1,0:T(1,128)S(1)}, u32[]{:S(2)}, u32[]{:S(2)}) async-start(f32[32,1,128]{2,1,0:T(1,128)} %bitcast.11), calls=%async_computation.2 | async-start | bytes 32768 | tf_op jit(solution)/shard_map/all_to_all | solution.py:524
  94.1 5.3 %collective-permute-start.11 = (f32[24,128]{1,0:T(8,128)S(1)}, f32[24,128]{1,0:T(8,128)S(1)}, u32[]{:S(2)}, u32[]{:S(2)}) collective-permute-start(f32[24,128]{1,0:T(8,128)S(1)} %get-tuple-element.47.mine), channel_id=1, source_target_pairs={{8,16},{16,8},{24,32},{32,24},{40,48},{48,40},{56,64},{64,56},{72,... | collective-permute-start | bytes 36872 | tf_op jit(solution)/shard_map/ppermute | solution.py:510
  97.5 3.1 %collective-permute-start.10 = (f32[24,128]{1,0:T(8,128)S(1)}, f32[24,128]{1,0:T(8,128)S(1)}, u32[]{:S(2)}, u32[]{:S(2)}) collective-permute-start(f32[24,128]{1,0:T(8,128)S(1)} %get-tuple-element.47.mine), channel_id=1, source_target_pairs={{0,8},{8,0},{16,24},{24,16},{32,40},{40,32},{48,56},{56,48},{64,72... | collective-permute-start | bytes 36872 | tf_op jit(solution)/shard_map/ppermute | solution.py:506

commit v7 on v6

--- a/solution.py
+++ b/solution.py
@@ -5,6 +5,7 @@
 from jax.experimental.pallas import tpu as pltpu
 from jax.sharding import Mesh
 from jax.sharding import PartitionSpec as P
+
 
 LAT = ("lat_0", "lat_1", "lat_2")
 LEVELS = 16
@@ -18,7 +19,6 @@
 LON = 8
 HALF = LANES // 2
 OWN = LON * SLOT
-NEAR = 3 * OWN
 BULK = 2 * HALF + 2
 LIST = BULK + 6
 PARCEL = LIST
@@ -30,6 +30,7 @@
 MESSAGE = SPOTS + 8
 HERALD = OWN + 8
 NOWHERE = -4096.0
+FIRST = 6
 HIGHEST = lax.Precision.HIGHEST
 F32 = jnp.float32
 VMEM = pl.BlockSpec(memory_space=pltpu.VMEM)
@@ -58,7 +59,6 @@
         scratch_shapes=list(scratch),
         compiler_params=pltpu.CompilerParams(vmem_limit_bytes=room << 20),
         cost_estimate=pl.CostEstimate(flops=flops, bytes_accessed=0, transcendentals=0),
-        name=body.__name__,
     )(*args)
 
 
@@ -67,7 +67,7 @@
 
 
 def chunk(owner):
-    return (owner + LON // 2) % LON if isinstance(owner, int) else lax.rem(owner + LON // 2, LON)
+    return (owner + LON - FIRST) % LON if isinstance(owner, int) else lax.rem(owner + LON - FIRST, LON)
 
 
 def packed_edges(pick, shift):
@@ -94,37 +94,16 @@
         parcels[pl.ds(chunk(owners[j]) * PARCEL + 2 * HALF + turns[j], 1), :] = diagonal
 
 
-def prepare(owner_at, row_at, count_at, flow_at, matrix_at, weight_at, innovation_at, parcels, to_core, to_inter, to_even, to_odd, owner, row, count, flow, matrix, weight, innovation, lists, sems):
-    pairs = ((owner_at, owner), (row_at, row), (count_at, count), (flow_at, flow), (weight_at, weight), (innovation_at, innovation), (matrix_at, matrix))
+def prepare(owner_at, row_at, count_at, matrix_at, weight_at, innovation_at, parcels, owner, row, count, matrix, weight, innovation, lists, sems):
+    pairs = ((matrix_at, matrix), (owner_at, owner), (row_at, row), (count_at, count), (weight_at, weight), (innovation_at, innovation))
     copies = [pltpu.make_async_copy(a, b, sems.at[i]) for i, (a, b) in enumerate(pairs)]
     for copy in copies:
         copy.start()
     for d in range(LON):
         parcels[d * PARCEL : d * PARCEL + LIST, :] = jnp.zeros((LIST, LANES), F32)
     lists[...] = jnp.zeros(lists.shape, F32)
-    even = lax.axis_index("lat_2") == 0
-    here = lax.rem(lax.axis_index("lon"), 2) == 0
-    copies[3].wait()
-    for f in range(2):
-        for g in range(2):
-
-            def pick(k, f=f, g=g):
-                at = f * LEVELS * ROWS + g * 8 + k
-                return flow[pl.ds(at, 8, stride=ROWS), :], flow[pl.ds(at + 8 * ROWS, 8, stride=ROWS), :]
-
-            at = (f * 2 + g) * 8
-            to_right, to_left = packed_edges(pick, 8), packed_edges(pick, 0)
-            to_even[at : at + 8, :] = jnp.where(here, to_right, to_left)
-            to_odd[at : at + 8, :] = jnp.where(here, to_left, to_right)
-        for i in range(HALO):
-            for h in range(2):
-                at = f * LEVELS * ROWS + h * 8 * ROWS + i
-                up, down = flow[pl.ds(at + ROWS - HALO, 8, stride=ROWS), :], flow[pl.ds(at, 8, stride=ROWS), :]
-                at = (i * 2 + f) * LEVELS + h * 8
-                to_core[at : at + 8, :] = jnp.where(even, up, down)
-                to_inter[at : at + 8, :] = jnp.where(even, down, up)
-    for i in (0, 1, 2, 4, 5, 6):
-        copies[i].wait()
+    for copy in copies:
+        copy.wait()
     owners = [owner[j] for j in range(CAP)]
     turns = turns_of(owners)
     column = jnp.transpose(weight[...] * innovation[...])
@@ -150,6 +129,29 @@
         edge = jnp.where(line < 16, edge, jnp.where(line < 24, roll(lists[right : right + 1, :], 16), roll(lists[right + 1 : right + 2, :], 24)))
         parcels[at + 2 : at + 3, :] = edge
         parcels[at + 3 : at + 4, :] = roll(named, -left)[:1]
+
+
+def halo(flow, to_core, to_inter, to_even, to_odd):
+    even = lax.axis_index("lat_2") == 0
+    here = lax.rem(lax.axis_index("lon"), 2) == 0
+    for f in range(2):
+        for g in range(2):
+
+            def pick(k, f=f, g=g):
+                at = f * LEVELS * ROWS + g * 8 + k
+                return flow[pl.ds(at, 8, stride=ROWS), :], flow[pl.ds(at + 8 * ROWS, 8, stride=ROWS), :]
+
+            at = (f * 2 + g) * 8
+            to_right, to_left = packed_edges(pick, 8), packed_edges(pick, 0)
+            to_even[at : at + 8, :] = jnp.where(here, to_right, to_left)
+            to_odd[at : at + 8, :] = jnp.where(here, to_left, to_right)
+        for i in range(HALO):
+            for h in range(2):
+                at = f * LEVELS * ROWS + h * 8 * ROWS + i
+                up, down = flow[pl.ds(at + ROWS - HALO, 8, stride=ROWS), :], flow[pl.ds(at, 8, stride=ROWS), :]
+                at = (i * 2 + f) * LEVELS + h * 8
+                to_core[at : at + 8, :] = jnp.where(even, up, down)
+                to_inter[at : at + 8, :] = jnp.where(even, down, up)
 
 
 def arrange(flow, parcels, core, inter, even_edges, odd_edges, wide, strips, to_core, to_inter):
@@ -238,10 +240,6 @@
     return jnp.concatenate([x, jnp.zeros((rows - x.shape[0], LANES), F32)], axis=0)
 
 
-def left_strips(x):
-    return jnp.where(lanes(x.shape[0]) < 8, roll(x, 8), 0.0)
-
-
 def right_strips(x):
     ln = lanes(x.shape[0])
     return jnp.where((ln >= 56) & (ln < 64), roll(x, 56), 0.0)
@@ -468,17 +466,12 @@
         message[OWN + i : OWN + i + 1, :] = parts[pl.ds(in_plane(step) * 2 + 1, 1), :]
 
 
-def last_rows(spots, by_lane, core, mine, inter, wide, strips, beside, kept, field, other, strip, other_strip):
+def finish(spots, by_lane, core, mine, inter, wide, strips, beside, parts, right_side, image, increment, residual, field, other, strip, other_strip):
     lists = (core, mine, inter)
     own = padded(jnp.concatenate([x[:OWN, :] for x in lists], axis=0), LANES)
     sides = side_strips(*([x[OWN + i : OWN + i + 1, :] for x in lists] for i in range(2)))
     lay_out(spots, by_lane, own, sides, field, strip, HALO - STEPS, HALO + ROWS + STEPS)
     fields, narrow = steps_back(rates_of(wide, strips, beside), (field, other), (strip, other_strip), STEPS)
-    for r in range(ROWS):
-        kept[r * LEVELS : r * LEVELS + 8, :], kept[r * LEVELS + 8 : (r + 1) * LEVELS, :] = merged(fields[0], narrow[0], r + HALO)
-
-
-def finish(parts, right_side, image, second, increment, residual):
     total = jnp.sum(parts[...], axis=0, keepdims=True)
     m0, m1, m2, m3 = (jnp.sum(jnp.where(lanes(1) == i, total, 0.0), keepdims=True) for i in range(4))
     step_0 = m0 / (m0 + m1)
@@ -494,12 +487,12 @@
     rest_kk = step_0 * step_1
     on_b, on_k, rest_b, rest_k, rest_kk = (jnp.broadcast_to(v, (8, LANES)) for v in (on_b, on_k, rest_b, rest_k, rest_kk))
     for r in range(ROWS):
-        for h in range(2):
+        for h, second in enumerate(merged(fields[0], narrow[0], r + HALO)):
             at = r * LEVELS + h * 8
-            b, k, kk = right_side[at : at + 8, :], image[at : at + 8, :], second[at : at + 8, :]
+            b, first = right_side[at : at + 8, :], image[at : at + 8, :]
             to = pl.ds(h * 8 * ROWS + r, 8, stride=ROWS)
-            increment[to, :] = on_b * b + on_k * k
-            residual[to, :] = rest_b * b + rest_k * k + rest_kk * kk
+            increment[to, :] = on_b * b + on_k * first
+            residual[to, :] = rest_b * b + rest_k * first + rest_kk * second
 
 
 def to_core(x):
@@ -527,19 +520,21 @@
 def shards(courant, obs_matrix, obs_weight, innovation, block_owner, block_row, block_count):
     flow = courant.reshape(-1, LANES)
     owner, row, count = block_owner.reshape(-1), block_row.reshape(-1), block_count
-    wholes = (flow, obs_matrix[0], obs_weight[0], innovation[0])
-    parcels, for_core, for_inter, for_even, for_odd = call(
+    wholes = (obs_matrix[0], obs_weight[0], innovation[0])
+    (parcels,) = call(
         prepare,
-        [(LON * PARCEL, LANES), (EDGE, LANES), (EDGE, LANES), (2 * OWN, LANES), (2 * OWN, LANES)],
+        [(LON * PARCEL, LANES)],
         (owner, row, count, *wholes),
         4_000_000,
         [pltpu.SMEM((CAP,), jnp.int32), pltpu.SMEM((CAP,), jnp.int32), pltpu.SMEM((1, 1), jnp.int32)]
         + [pltpu.VMEM(x.shape, F32) for x in wholes]
-        + [pltpu.VMEM((OWN, LANES), F32), pltpu.SemaphoreType.DMA((7,))],
-        [pl.BlockSpec(memory_space=pltpu.HBM)] * 7,
+        + [pltpu.VMEM((OWN, LANES), F32), pltpu.SemaphoreType.DMA((6,))],
+        [pl.BlockSpec(memory_space=pltpu.HBM)] * 6,
         62,
     )
-    parcels = spread_out(parcels.reshape(LON, PARCEL, LANES), "lon", LON // 2).reshape(LON * PARCEL, LANES)
+    parcels = spread_out(parcels.reshape(LON, PARCEL, LANES), "lon", FIRST).reshape(LON * PARCEL, LANES)
+    edge = (EDGE, LANES), (2 * OWN, LANES)
+    for_core, for_inter, for_even, for_odd = call(halo, [edge[0], edge[0], edge[1], edge[1]], (flow,), 1_000_000)
     core, inter = to_core(for_core), to_inter(for_inter)
     wide, strips, for_core, for_inter = call(
         arrange,
@@ -573,8 +568,9 @@
     sums, mine = call(gathered, [(towers, LANES), short], (parcels, mine), 10_000)
     core, inter = to_core(mine), to_inter(mine)
     parts = spread_out(sums.reshape(towers, 1, LANES), ("lat_0", "lat_2"), towers * 12 // 16 + 1).reshape(towers, LANES)
-    (second,) = call(last_rows, [cells], (spots, by_lane, core, mine, inter, *rates), 4_000_000, work)
-    increment, residual = call(finish, [cells, cells], (parts, right_side, image, second), 100_000)
+    increment, residual = call(
+        finish, [cells, cells], (spots, by_lane, core, mine, inter, *rates, parts, right_side, image), 2_000_000, work
+    )
     shape = courant.shape[1:]
     return increment.reshape(shape), residual.reshape(shape)
 

time: 103 us -> 103 us (level)
    all_to_all x2, starting transfers between devices: 28.4 us -> 27.1 us  [spread_out(): lax.all_to_all(x, axes, split_axis=0, concat_axis=0, tiled=True, axis_ind...]
    ppermute x2, starting transfers between devices: 4.11 us -> 5.24 us  [to_even(): return lax.ppermute(x, 'lon', [(i, i ^ 1) for i in range(LON)])]
  transfers between devices with their start and end apart: 14 -> 14, of which waited for: 8 -> 9; matrix products, arithmetic and copies ran while one was open for 0% -> 0% of each run, Pallas kernels for 2% -> 1%
where the time goes in v7:
time: 103 us; the launch traced here: 102 us
  starting transfers between devices  68.1 us (66%)
  Pallas kernels  11.8 us (11%)
  blocking collectives  11 us (11%)
  waiting for transfers between devices  9.76 us (9%)
  between operations  1.44 us (1%)
    all_to_all x2, starting transfers between devices, spread_out(): lax.all_to_all(x, axes, split_axis=0, concat_axis=0, tiled=True, axis_ind...  27.1 us
    ppermute x4, starting transfers between devices, to_core(): return lax.ppermute(x, LAT, [(i, i ^ 1) for i in range(lax.axis_size(LAT))])  19 us
    ppermute x4, starting transfers between devices, to_inter(): lax.ppermute(x, LAT, [(i, (i + 1 ^ 1) - 1) for i in range(1, lax.axis_siz...  13 us
    pallas_call x10, Pallas kernels, call(): pl.pallas_call(body, out_shape=[jax.ShapeDtypeStruct(s, F32) for s in out...  11.8 us
    all_to_all x1, blocking collectives, spread_out(): lax.all_to_all(x, axes, split_axis=0, concat_axis=0, tiled=True, axis_ind...  11 us
    ppermute x2, starting transfers between devices, to_even(): return lax.ppermute(x, 'lon', [(i, i ^ 1) for i in range(LON)])  5.24 us
    ppermute x2, waiting for transfers between devices, to_odd(): lax.ppermute(x, 'lon', [(i, (((i + 1) % LON ^ 1) - 1) % LON) for i in ran...  5.13 us
    ppermute x2, starting transfers between devices, to_odd(): lax.ppermute(x, 'lon', [(i, (((i + 1) % LON ^ 1) - 1) % LON) for i in ran...  3.83 us
  transfers between devices with their start and end apart: 14, of which 9 were waited for; matrix products, arithmetic and copies ran while one was open for 0% of the time, Pallas kernels for 1%

profile of v7, /device:TPU:1, one launch (start us, length us, event | category | flops | bytes accessed | tf_op | source)
XLA Modules:
  0.0 102.1 jit_solution(10608608520498322965)
XLA Ops:
  1.3 2.7 %shard_map.86 = f32[1088,128]{1,0:T(8,128)} custom-call(s32[8]{0:T(128)} %bitcast.27, s32[8]{0:T(128)} %bitcast.28, s32[1,1]{1,0:T(1,128)S(6)} %copy.10.count_at, f32[8,128,128]{2,1,0:T(8,128)} %bitcast.24, f32[8,128]{1,0:T(8,128)} %bitcast.25, f32[8,128]{1,0:T(8,128)} %bitcast.26), custom_call_target="tpu_custom_call" | custom-call | flops 4000000 | tf_op jit(solution)/shard_map/pallas_call | solution.py:54
  4.0 0.0 copy-start
  4.0 8.4 %all-to-all-start = ((f32[8,136,128]{2,1,0:T(8,128)}), f32[8,136,128]{2,1,0:T(8,128)S(1)}, u32[]{:S(2)}, u32[]{:S(2)}) async-start(f32[8,136,128]{2,1,0:T(8,128)} %bitcast.23), calls=%async_computation | async-start | bytes 1114112 | tf_op jit(solution)/shard_map/all_to_all | solution.py:517
  12.4 0.0 copy-done
  12.4 0.2 shard_map.87
  12.6 13.2 %collective-permute-start = (f32[256,128]{1,0:T(8,128)S(1)}, f32[256,128]{1,0:T(8,128)S(1)}, u32[]{:S(2)}, u32[]{:S(2)}) collective-permute-start(f32[256,128]{1,0:T(8,128)S(1)} %get-tuple-element.25), channel_id=1, source_target_pairs={{0,8},{8,0},{16,24},{24,16},{32,40},{40,32},{48,56},{56,48},{64,72... | collective-permute-start | bytes 393224 | tf_op jit(solution)/shard_map/ppermute | solution.py:499
  25.8 1.9 %collective-permute-start.1 = (f32[256,128]{1,0:T(8,128)S(1)}, f32[256,128]{1,0:T(8,128)S(1)}, u32[]{:S(2)}, u32[]{:S(2)}) collective-permute-start(f32[256,128]{1,0:T(8,128)S(1)} %get-tuple-element.26), channel_id=1, source_target_pairs={{8,16},{16,8},{24,32},{32,24},{40,48},{48,40},{56,64},{64,56},{72,... | collective-permute-start | bytes 393224 | tf_op jit(solution)/shard_map/ppermute | solution.py:503
  27.8 3.1 %collective-permute-start.2 = (f32[32,128]{1,0:T(8,128)S(1)}, f32[32,128]{1,0:T(8,128)S(1)}, u32[]{:S(2)}, u32[]{:S(2)}) collective-permute-start(f32[32,128]{1,0:T(8,128)S(1)} %get-tuple-element.27), channel_id=1, source_target_pairs={{0,1},{1,0},{2,3},{3,2},{4,5},{5,4},{6,7},{7,6},{8,9},{9,8},{10,11... | collective-permute-start | bytes 49160 | tf_op jit(solution)/shard_map/ppermute | solution.py:507
  30.9 1.9 %collective-permute-start.3 = (f32[32,128]{1,0:T(8,128)S(1)}, f32[32,128]{1,0:T(8,128)S(1)}, u32[]{:S(2)}, u32[]{:S(2)}) collective-permute-start(f32[32,128]{1,0:T(8,128)S(1)} %get-tuple-element.28), channel_id=1, source_target_pairs={{0,7},{1,2},{2,1},{3,4},{4,3},{5,6},{6,5},{7,0},{8,15},{9,10},{10,... | collective-permute-start | bytes 49160 | tf_op jit(solution)/shard_map/ppermute | solution.py:511
  32.8 0.1 collective-permute-done.2.even_edges
  32.9 3.6 %collective-permute-done.3.odd_edges = f32[32,128]{1,0:T(8,128)S(1)} collective-permute-done((f32[32,128]{1,0:T(8,128)S(1)}, f32[32,128]{1,0:T(8,128)S(1)}, u32[]{:S(2)}, u32[]{:S(2)}) %collective-permute-start.3) | collective-permute-done | bytes 16416 | tf_op jit(solution)/shard_map/ppermute | solution.py:511
  36.5 0.0 collective-permute-done.core
  36.6 0.0 collective-permute-done.1.inter
  36.6 0.0 all-to-all-done
  36.6 0.4 shard_map.88
  36.9 5.1 %collective-permute-start.5 = (f32[184,128]{1,0:T(8,128)S(1)}, f32[184,128]{1,0:T(8,128)S(1)}, u32[]{:S(2)}, u32[]{:S(2)}) collective-permute-start(f32[184,128]{1,0:T(8,128)S(1)} %get-tuple-element.32), channel_id=1, source_target_pairs={{8,16},{16,8},{24,32},{32,24},{40,48},{48,40},{56,64},{64,56},{72,... | collective-permute-start | bytes 282632 | tf_op jit(solution)/shard_map/ppermute | solution.py:503
  42.0 1.9 %collective-permute-start.4 = (f32[184,128]{1,0:T(8,128)S(1)}, f32[184,128]{1,0:T(8,128)S(1)}, u32[]{:S(2)}, u32[]{:S(2)}) collective-permute-start(f32[184,128]{1,0:T(8,128)S(1)} %get-tuple-element.31.own_message), channel_id=1, source_target_pairs={{0,8},{8,0},{16,24},{24,16},{32,40},{40,32},{48,56},{56,48},{64,72... | collective-permute-start | bytes 282632 | tf_op jit(solution)/shard_map/ppermute | solution.py:499
  43.9 0.5 shard_map.90.grams
  44.5 0.0 collective-permute-done.5.inter
  44.5 0.7 collective-permute-done.4.core
  45.2 1.9 %shard_map.89 = (f32[256,128]{1,0:T(8,128)S(1)}, f32[256,128]{1,0:T(8,128)S(1)}, f32[16,128]{1,0:T(8,128)S(1)}, f32[256,128]{1,0:T(8,128)S(1)}, f32[16,128]{1,0:T(8,128)S(1)}, /*index=5*/f32[8,128]{1,0:T(8,128)S(1)}) custom-call(f32[1024,128]{1,0:T(8,128)S(1)} %get-tuple-element.29.wide, f32[256,128]{1,0:T(8,128)S(1)} %get-tuple-element.30.mine.strips, ...), custom_call_target="tpu_custom_call" | custom-call | flops 4000000 | tf_op jit(solution)/shard_map/pallas_call | solution.py:54
  47.1 0.9 shard_map.91
  48.0 2.7 %collective-permute-start.7 = (f32[24,128]{1,0:T(8,128)S(1)}, f32[24,128]{1,0:T(8,128)S(1)}, u32[]{:S(2)}, u32[]{:S(2)}) collective-permute-start(f32[24,128]{1,0:T(8,128)S(1)} %get-tuple-element.37.mine), channel_id=1, source_target_pairs={{8,16},{16,8},{24,32},{32,24},{40,48},{48,40},{56,64},{64,56},{72,... | collective-permute-start | bytes 36872 | tf_op jit(solution)/shard_map/ppermute | solution.py:503
  50.7 1.9 %collective-permute-start.6 = (f32[24,128]{1,0:T(8,128)S(1)}, f32[24,128]{1,0:T(8,128)S(1)}, u32[]{:S(2)}, u32[]{:S(2)}) collective-permute-start(f32[24,128]{1,0:T(8,128)S(1)} %get-tuple-element.37.mine), channel_id=1, source_target_pairs={{0,8},{8,0},{16,24},{24,16},{32,40},{40,32},{48,56},{56,48},{64,72... | collective-permute-start | bytes 36872 | tf_op jit(solution)/shard_map/ppermute | solution.py:499
  52.6 0.4 collective-permute-done.7.inter
  53.0 0.8 collective-permute-done.6.core
  53.8 1.9 %collective-permute-start.9 = (f32[8,128]{1,0:T(8,128)S(1)}, f32[8,128]{1,0:T(8,128)S(1)}, u32[]{:S(2)}, u32[]{:S(2)}) collective-permute-start(f32[8,128]{1,0:T(8,128)S(1)} %shard_map.92), channel_id=1, source_target_pairs={{0,7},{1,2},{2,1},{3,4},{4,3},{5,6},{6,5},{7,0},{8,15},{9,10},{10,... | collective-permute-start | bytes 12296 | tf_op jit(solution)/shard_map/ppermute | solution.py:511
  55.7 2.1 %collective-permute-start.8 = (f32[8,128]{1,0:T(8,128)S(1)}, f32[8,128]{1,0:T(8,128)S(1)}, u32[]{:S(2)}, u32[]{:S(2)}) collective-permute-start(f32[8,128]{1,0:T(8,128)S(1)} %shard_map.92), channel_id=1, source_target_pairs={{0,1},{1,0},{2,3},{3,2},{4,5},{5,4},{6,7},{7,6},{8,9},{9,8},{10,11... | collective-permute-start | bytes 12296 | tf_op jit(solution)/shard_map/ppermute | solution.py:507
  57.8 1.5 %collective-permute-done.9.odd = f32[8,128]{1,0:T(8,128)S(1)} collective-permute-done((f32[8,128]{1,0:T(8,128)S(1)}, f32[8,128]{1,0:T(8,128)S(1)}, u32[]{:S(2)}, u32[]{:S(2)}) %collective-permute-start.9) | collective-permute-done | bytes 4128 | tf_op jit(solution)/shard_map/ppermute | solution.py:511
  59.3 0.9 collective-permute-done.8.even
  60.2 2.7 %shard_map.93 = (f32[256,128]{1,0:T(8,128)S(1)}, f32[24,128]{1,0:T(8,128)S(1)}, f32[64,128]{1,0:T(8,128)S(1)}) custom-call(f32[256,128]{1,0:T(8,128)S(1)} %get-tuple-element.33.spots, f32[16,128]{1,0:T(8,128)S(1)} %get-tuple-element.34.by_lane, f32[24,128]{1,0:T(8,128)S(1)} %collective-permute-done.6.core, f32[24,128]{1,0:T(8,128)S(1)} %get-tuple-element.37.mine, ...), custom_call_target="tpu_custom_call" | custom-call | flops 4000000 | tf_op jit(solution)/shard_map/pallas_call | solution.py:54
  63.0 11.0 %all_to_all.15 = f32[32,2,128]{2,1,0:T(2,128)S(1)} all-to-all(f32[32,2,128]{2,1,0:T(2,128)S(1)} %bitcast.22), channel_id=1, replica_groups={{36,37,38,39,48,49,50,51,52,53,54,55,0,1,2,3,4,5,6,7,16,17,18,19,20,21,..., dimensions={0} | all-to-all | bytes 65536 | tf_op jit(solution)/shard_map/all_to_all | solution.py:517
  74.0 0.6 shard_map.94
  74.6 18.7 %all-to-all-start.2 = ((f32[32,1,128]{2,1,0:T(1,128)}), f32[32,1,128]{2,1,0:T(1,128)S(1)}, u32[]{:S(2)}, u32[]{:S(2)}) async-start(f32[32,1,128]{2,1,0:T(1,128)} %bitcast.11), calls=%async_computation.2 | async-start | bytes 32768 | tf_op jit(solution)/shard_map/all_to_all | solution.py:517
  93.3 3.3 %collective-permute-start.11 = (f32[24,128]{1,0:T(8,128)S(1)}, f32[24,128]{1,0:T(8,128)S(1)}, u32[]{:S(2)}, u32[]{:S(2)}) collective-permute-start(f32[24,128]{1,0:T(8,128)S(1)} %get-tuple-element.42.mine), channel_id=1, source_target_pairs={{8,16},{16,8},{24,32},{32,24},{40,48},{48,40},{56,64},{64,56},{72,... | collective-permute-start | bytes 36872 | tf_op jit(solution)/shard_map/ppermute | solution.py:503
  96.7 1.9 %collective-permute-start.10 = (f32[24,128]{1,0:T(8,128)S(1)}, f32[24,128]{1,0:T(8,128)S(1)}, u32[]{:S(2)}, u32[]{:S(2)}) collective-permute-start(f32[24,128]{1,0:T(8,128)S(1)} %get-tuple-element.42.mine), channel_id=1, source_target_pairs={{0,8},{8,0},{16,24},{24,16},{32,40},{40,32},{48,56},{56,48},{64,72... | collective-permute-start | bytes 36872 | tf_op jit(solution)/shard_map/ppermute | solution.py:499
  98.6 0.0 collective-permute-done.11.inter
  98.6 1.1 %collective-permute-done.10.core = f32[24,128]{1,0:T(8,128)S(1)} collective-permute-done((f32[24,128]{1,0:T(8,128)S(1)}, f32[24,128]{1,0:T(8,128)S(1)}, u32[]{:S(2)}, u32[]{:S(2)}) %collective-permute-start.10) | collective-permute-done | bytes 12320 | tf_op jit(solution)/shard_map/ppermute | solution.py:499
  99.7 0.6 all-to-all-done.2
  100.3 1.8 %shard_map.95 = (f32[256,128]{1,0:T(8,128)}, f32[256,128]{1,0:T(8,128)}) custom-call(f32[256,128]{1,0:T(8,128)S(1)} %get-tuple-element.33.spots, f32[16,128]{1,0:T(8,128)S(1)} %get-tuple-element.34.by_lane, f32[24,128]{1,0:T(8,128)S(1)} %collective-permute-done.10.core, f32[24,128]{1,0:T(8,128)S(1)} %get-tuple-element.42.mine, ...), custom_call_target="tpu_custom_call" | custom-call | flops 2000000 | tf_op jit(solution)/shard_map/pallas_call | solution.py:54
  (1 shorter events, 0.0 us)
Async XLA Ops:
  4.0 8.4 %copy-start = (f32[2,16,16,128]{3,2,1,0:T(8,128)S(1)}, f32[2,16,16,128]{3,2,1,0:T(8,128)}, u32[]{:S(2)}) copy-start(f32[2,16,16,128]{3,2,1,0:T(8,128)} %param.7) | copy-start | bytes 786436
  4.0 32.5 %all-to-all-start = ((f32[8,136,128]{2,1,0:T(8,128)}), f32[8,136,128]{2,1,0:T(8,128)S(1)}, u32[]{:S(2)}, u32[]{:S(2)}) async-start(f32[8,136,128]{2,1,0:T(8,128)} %bitcast.23), calls=%async_computation | async-start | bytes 1114112 | tf_op jit(solution)/shard_map/all_to_all | solution.py:517
  12.6 23.9 %collective-permute-start = (f32[256,128]{1,0:T(8,128)S(1)}, f32[256,128]{1,0:T(8,128)S(1)}, u32[]{:S(2)}, u32[]{:S(2)}) collective-permute-start(f32[256,128]{1,0:T(8,128)S(1)} %get-tuple-element.25), channel_id=1, source_target_pairs={{0,8},{8,0},{16,24},{24,16},{32,40},{40,32},{48,56},{56,48},{64,72... | collective-permute-start | bytes 393224 | tf_op jit(solution)/shard_map/ppermute | solution.py:499
  25.8 10.7 %collective-permute-start.1 = (f32[256,128]{1,0:T(8,128)S(1)}, f32[256,128]{1,0:T(8,128)S(1)}, u32[]{:S(2)}, u32[]{:S(2)}) collective-permute-start(f32[256,128]{1,0:T(8,128)S(1)} %get-tuple-element.26), channel_id=1, source_target_pairs={{8,16},{16,8},{24,32},{32,24},{40,48},{48,40},{56,64},{64,56},{72,... | collective-permute-start | bytes 393224 | tf_op jit(solution)/shard_map/ppermute | solution.py:503
  27.8 5.1 %collective-permute-start.2 = (f32[32,128]{1,0:T(8,128)S(1)}, f32[32,128]{1,0:T(8,128)S(1)}, u32[]{:S(2)}, u32[]{:S(2)}) collective-permute-start(f32[32,128]{1,0:T(8,128)S(1)} %get-tuple-element.27), channel_id=1, source_target_pairs={{0,1},{1,0},{2,3},{3,2},{4,5},{5,4},{6,7},{7,6},{8,9},{9,8},{10,11... | collective-permute-start | bytes 49160 | tf_op jit(solution)/shard_map/ppermute | solution.py:507
  30.9 5.7 %collective-permute-start.3 = (f32[32,128]{1,0:T(8,128)S(1)}, f32[32,128]{1,0:T(8,128)S(1)}, u32[]{:S(2)}, u32[]{:S(2)}) collective-permute-start(f32[32,128]{1,0:T(8,128)S(1)} %get-tuple-element.28), channel_id=1, source_target_pairs={{0,7},{1,2},{2,1},{3,4},{4,3},{5,6},{6,5},{7,0},{8,15},{9,10},{10,... | collective-permute-start | bytes 49160 | tf_op jit(solution)/shard_map/ppermute | solution.py:511
  36.9 7.5 %collective-permute-start.5 = (f32[184,128]{1,0:T(8,128)S(1)}, f32[184,128]{1,0:T(8,128)S(1)}, u32[]{:S(2)}, u32[]{:S(2)}) collective-permute-start(f32[184,128]{1,0:T(8,128)S(1)} %get-tuple-element.32), channel_id=1, source_target_pairs={{8,16},{16,8},{24,32},{32,24},{40,48},{48,40},{56,64},{64,56},{72,... | collective-permute-start | bytes 282632 | tf_op jit(solution)/shard_map/ppermute | solution.py:503
  42.0 3.2 %collective-permute-start.4 = (f32[184,128]{1,0:T(8,128)S(1)}, f32[184,128]{1,0:T(8,128)S(1)}, u32[]{:S(2)}, u32[]{:S(2)}) collective-permute-start(f32[184,128]{1,0:T(8,128)S(1)} %get-tuple-element.31.own_message), channel_id=1, source_target_pairs={{0,8},{8,0},{16,24},{24,16},{32,40},{40,32},{48,56},{56,48},{64,72... | collective-permute-start | bytes 282632 | tf_op jit(solution)/shard_map/ppermute | solution.py:499
  48.0 5.0 %collective-permute-start.7 = (f32[24,128]{1,0:T(8,128)S(1)}, f32[24,128]{1,0:T(8,128)S(1)}, u32[]{:S(2)}, u32[]{:S(2)}) collective-permute-start(f32[24,128]{1,0:T(8,128)S(1)} %get-tuple-element.37.mine), channel_id=1, source_target_pairs={{8,16},{16,8},{24,32},{32,24},{40,48},{48,40},{56,64},{64,56},{72,... | collective-permute-start | bytes 36872 | tf_op jit(solution)/shard_map/ppermute | solution.py:503
  50.7 3.1 %collective-permute-start.6 = (f32[24,128]{1,0:T(8,128)S(1)}, f32[24,128]{1,0:T(8,128)S(1)}, u32[]{:S(2)}, u32[]{:S(2)}) collective-permute-start(f32[24,128]{1,0:T(8,128)S(1)} %get-tuple-element.37.mine), channel_id=1, source_target_pairs={{0,8},{8,0},{16,24},{24,16},{32,40},{40,32},{48,56},{56,48},{64,72... | collective-permute-start | bytes 36872 | tf_op jit(solution)/shard_map/ppermute | solution.py:499
  53.8 5.6 %collective-permute-start.9 = (f32[8,128]{1,0:T(8,128)S(1)}, f32[8,128]{1,0:T(8,128)S(1)}, u32[]{:S(2)}, u32[]{:S(2)}) collective-permute-start(f32[8,128]{1,0:T(8,128)S(1)} %shard_map.92), channel_id=1, source_target_pairs={{0,7},{1,2},{2,1},{3,4},{4,3},{5,6},{6,5},{7,0},{8,15},{9,10},{10,... | collective-permute-start | bytes 12296 | tf_op jit(solution)/shard_map/ppermute | solution.py:511
  55.7 4.6 %collective-permute-start.8 = (f32[8,128]{1,0:T(8,128)S(1)}, f32[8,128]{1,0:T(8,128)S(1)}, u32[]{:S(2)}, u32[]{:S(2)}) collective-permute-start(f32[8,128]{1,0:T(8,128)S(1)} %shard_map.92), channel_id=1, source_target_pairs={{0,1},{1,0},{2,3},{3,2},{4,5},{5,4},{6,7},{7,6},{8,9},{9,8},{10,11... | collective-permute-start | bytes 12296 | tf_op jit(solution)/shard_map/ppermute | solution.py:507
  74.6 25.7 %all-to-all-start.2 = ((f32[32,1,128]{2,1,0:T(1,128)}), f32[32,1,128]{2,1,0:T(1,128)S(1)}, u32[]{:S(2)}, u32[]{:S(2)}) async-start(f32[32,1,128]{2,1,0:T(1,128)} %bitcast.11), calls=%async_computation.2 | async-start | bytes 32768 | tf_op jit(solution)/shard_map/all_to_all | solution.py:517
  93.3 5.3 %collective-permute-start.11 = (f32[24,128]{1,0:T(8,128)S(1)}, f32[24,128]{1,0:T(8,128)S(1)}, u32[]{:S(2)}, u32[]{:S(2)}) collective-permute-start(f32[24,128]{1,0:T(8,128)S(1)} %get-tuple-element.42.mine), channel_id=1, source_target_pairs={{8,16},{16,8},{24,32},{32,24},{40,48},{48,40},{56,64},{64,56},{72,... | collective-permute-start | bytes 36872 | tf_op jit(solution)/shard_map/ppermute | solution.py:503
  96.7 3.1 %collective-permute-start.10 = (f32[24,128]{1,0:T(8,128)S(1)}, f32[24,128]{1,0:T(8,128)S(1)}, u32[]{:S(2)}, u32[]{:S(2)}) collective-permute-start(f32[24,128]{1,0:T(8,128)S(1)} %get-tuple-element.42.mine), channel_id=1, source_target_pairs={{0,8},{8,0},{16,24},{24,16},{32,40},{40,32},{48,56},{56,48},{64,72... | collective-permute-start | bytes 36872 | tf_op jit(solution)/shard_map/ppermute | solution.py:499

commit v8 on v7

--- a/solution.py
+++ b/solution.py
@@ -535,11 +535,14 @@
     parcels = spread_out(parcels.reshape(LON, PARCEL, LANES), "lon", FIRST).reshape(LON * PARCEL, LANES)
     edge = (EDGE, LANES), (2 * OWN, LANES)
     for_core, for_inter, for_even, for_odd = call(halo, [edge[0], edge[0], edge[1], edge[1]], (flow,), 1_000_000)
-    core, inter = to_core(for_core), to_inter(for_inter)
+    odd = to_odd(for_odd)
+    even = to_even(for_even)
+    inter = to_inter(for_inter)
+    core = to_core(for_core)
     wide, strips, for_core, for_inter = call(
         arrange,
         [(WIDE * 2 * LEVELS, LANES), (2 * STRIP, LANES), (MESSAGE, LANES), (MESSAGE, LANES)],
-        (flow, parcels, core, inter, to_even(for_even), to_odd(for_odd)),
+        (flow, parcels, core, inter, even, odd),
         2_000_000,
     )
     core, inter = to_core(for_core), to_inter(for_inter)

time: 103 us -> 103 us (level)
  no operation moved by 1% of the time
where the time goes in v8:
time: 103 us; the launch traced here: 102 us
  starting transfers between devices  68.1 us (66%)
  Pallas kernels  11.8 us (11%)
  blocking collectives  11 us (11%)
  waiting for transfers between devices  9.76 us (9%)
  between operations  1.44 us (1%)
    all_to_all x2, starting transfers between devices, spread_out(): lax.all_to_all(x, axes, split_axis=0, concat_axis=0, tiled=True, axis_ind...  27.1 us
    ppermute x4, starting transfers between devices, to_core(): return lax.ppermute(x, LAT, [(i, i ^ 1) for i in range(lax.axis_size(LAT))])  19 us
    ppermute x4, starting transfers between devices, to_inter(): lax.ppermute(x, LAT, [(i, (i + 1 ^ 1) - 1) for i in range(1, lax.axis_siz...  13 us
    pallas_call x10, Pallas kernels, call(): pl.pallas_call(body, out_shape=[jax.ShapeDtypeStruct(s, F32) for s in out...  11.8 us
    all_to_all x1, blocking collectives, spread_out(): lax.all_to_all(x, axes, split_axis=0, concat_axis=0, tiled=True, axis_ind...  11 us
    ppermute x2, starting transfers between devices, to_even(): return lax.ppermute(x, 'lon', [(i, i ^ 1) for i in range(LON)])  5.24 us
    ppermute x2, waiting for transfers between devices, to_odd(): lax.ppermute(x, 'lon', [(i, (((i + 1) % LON ^ 1) - 1) % LON) for i in ran...  5.13 us
    ppermute x2, starting transfers between devices, to_odd(): lax.ppermute(x, 'lon', [(i, (((i + 1) % LON ^ 1) - 1) % LON) for i in ran...  3.83 us
  transfers between devices with their start and end apart: 14, of which 9 were waited for; matrix products, arithmetic and copies ran while one was open for 0% of the time, Pallas kernels for 1%

profile of v8, /device:TPU:1, one launch (start us, length us, event | category | flops | bytes accessed | tf_op | source)
XLA Modules:
  0.0 102.1 jit_solution(10608608520498322965)
XLA Ops:
  1.3 2.7 %shard_map.86 = f32[1088,128]{1,0:T(8,128)} custom-call(s32[8]{0:T(128)} %bitcast.27, s32[8]{0:T(128)} %bitcast.28, s32[1,1]{1,0:T(1,128)S(6)} %copy.10.count_at, f32[8,128,128]{2,1,0:T(8,128)} %bitcast.24, f32[8,128]{1,0:T(8,128)} %bitcast.25, f32[8,128]{1,0:T(8,128)} %bitcast.26), custom_call_target="tpu_custom_call" | custom-call | flops 4000000 | tf_op jit(solution)/shard_map/pallas_call | solution.py:54
  4.0 0.0 copy-start
  4.0 8.4 %all-to-all-start = ((f32[8,136,128]{2,1,0:T(8,128)}), f32[8,136,128]{2,1,0:T(8,128)S(1)}, u32[]{:S(2)}, u32[]{:S(2)}) async-start(f32[8,136,128]{2,1,0:T(8,128)} %bitcast.23), calls=%async_computation | async-start | bytes 1114112 | tf_op jit(solution)/shard_map/all_to_all | solution.py:517
  12.4 0.0 copy-done
  12.4 0.2 shard_map.87
  12.6 13.2 %collective-permute-start = (f32[256,128]{1,0:T(8,128)S(1)}, f32[256,128]{1,0:T(8,128)S(1)}, u32[]{:S(2)}, u32[]{:S(2)}) collective-permute-start(f32[256,128]{1,0:T(8,128)S(1)} %get-tuple-element.25), channel_id=1, source_target_pairs={{0,8},{8,0},{16,24},{24,16},{32,40},{40,32},{48,56},{56,48},{64,72... | collective-permute-start | bytes 393224 | tf_op jit(solution)/shard_map/ppermute | solution.py:499
  25.8 1.9 %collective-permute-start.1 = (f32[256,128]{1,0:T(8,128)S(1)}, f32[256,128]{1,0:T(8,128)S(1)}, u32[]{:S(2)}, u32[]{:S(2)}) collective-permute-start(f32[256,128]{1,0:T(8,128)S(1)} %get-tuple-element.26), channel_id=1, source_target_pairs={{8,16},{16,8},{24,32},{32,24},{40,48},{48,40},{56,64},{64,56},{72,... | collective-permute-start | bytes 393224 | tf_op jit(solution)/shard_map/ppermute | solution.py:503
  27.8 3.1 %collective-permute-start.2 = (f32[32,128]{1,0:T(8,128)S(1)}, f32[32,128]{1,0:T(8,128)S(1)}, u32[]{:S(2)}, u32[]{:S(2)}) collective-permute-start(f32[32,128]{1,0:T(8,128)S(1)} %get-tuple-element.27), channel_id=1, source_target_pairs={{0,1},{1,0},{2,3},{3,2},{4,5},{5,4},{6,7},{7,6},{8,9},{9,8},{10,11... | collective-permute-start | bytes 49160 | tf_op jit(solution)/shard_map/ppermute | solution.py:507
  30.9 1.9 %collective-permute-start.3 = (f32[32,128]{1,0:T(8,128)S(1)}, f32[32,128]{1,0:T(8,128)S(1)}, u32[]{:S(2)}, u32[]{:S(2)}) collective-permute-start(f32[32,128]{1,0:T(8,128)S(1)} %get-tuple-element.28), channel_id=1, source_target_pairs={{0,7},{1,2},{2,1},{3,4},{4,3},{5,6},{6,5},{7,0},{8,15},{9,10},{10,... | collective-permute-start | bytes 49160 | tf_op jit(solution)/shard_map/ppermute | solution.py:511
  32.8 0.1 collective-permute-done.2.even_edges
  32.9 3.6 %collective-permute-done.3.odd_edges = f32[32,128]{1,0:T(8,128)S(1)} collective-permute-done((f32[32,128]{1,0:T(8,128)S(1)}, f32[32,128]{1,0:T(8,128)S(1)}, u32[]{:S(2)}, u32[]{:S(2)}) %collective-permute-start.3) | collective-permute-done | bytes 16416 | tf_op jit(solution)/shard_map/ppermute | solution.py:511
  36.5 0.0 collective-permute-done.core
  36.6 0.0 collective-permute-done.1.inter
  36.6 0.0 all-to-all-done
  36.6 0.4 shard_map.88
  36.9 5.1 %collective-permute-start.5 = (f32[184,128]{1,0:T(8,128)S(1)}, f32[184,128]{1,0:T(8,128)S(1)}, u32[]{:S(2)}, u32[]{:S(2)}) collective-permute-start(f32[184,128]{1,0:T(8,128)S(1)} %get-tuple-element.32), channel_id=1, source_target_pairs={{8,16},{16,8},{24,32},{32,24},{40,48},{48,40},{56,64},{64,56},{72,... | collective-permute-start | bytes 282632 | tf_op jit(solution)/shard_map/ppermute | solution.py:503
  42.0 1.9 %collective-permute-start.4 = (f32[184,128]{1,0:T(8,128)S(1)}, f32[184,128]{1,0:T(8,128)S(1)}, u32[]{:S(2)}, u32[]{:S(2)}) collective-permute-start(f32[184,128]{1,0:T(8,128)S(1)} %get-tuple-element.31.own_message), channel_id=1, source_target_pairs={{0,8},{8,0},{16,24},{24,16},{32,40},{40,32},{48,56},{56,48},{64,72... | collective-permute-start | bytes 282632 | tf_op jit(solution)/shard_map/ppermute | solution.py:499
  43.9 0.5 shard_map.90.grams
  44.5 0.0 collective-permute-done.5.inter
  44.5 0.7 collective-permute-done.4.core
  45.2 1.9 %shard_map.89 = (f32[256,128]{1,0:T(8,128)S(1)}, f32[256,128]{1,0:T(8,128)S(1)}, f32[16,128]{1,0:T(8,128)S(1)}, f32[256,128]{1,0:T(8,128)S(1)}, f32[16,128]{1,0:T(8,128)S(1)}, /*index=5*/f32[8,128]{1,0:T(8,128)S(1)}) custom-call(f32[1024,128]{1,0:T(8,128)S(1)} %get-tuple-element.29.wide, f32[256,128]{1,0:T(8,128)S(1)} %get-tuple-element.30.mine.strips, ...), custom_call_target="tpu_custom_call" | custom-call | flops 4000000 | tf_op jit(solution)/shard_map/pallas_call | solution.py:54
  47.1 0.9 shard_map.91
  48.0 2.7 %collective-permute-start.7 = (f32[24,128]{1,0:T(8,128)S(1)}, f32[24,128]{1,0:T(8,128)S(1)}, u32[]{:S(2)}, u32[]{:S(2)}) collective-permute-start(f32[24,128]{1,0:T(8,128)S(1)} %get-tuple-element.37.mine), channel_id=1, source_target_pairs={{8,16},{16,8},{24,32},{32,24},{40,48},{48,40},{56,64},{64,56},{72,... | collective-permute-start | bytes 36872 | tf_op jit(solution)/shard_map/ppermute | solution.py:503
  50.7 1.9 %collective-permute-start.6 = (f32[24,128]{1,0:T(8,128)S(1)}, f32[24,128]{1,0:T(8,128)S(1)}, u32[]{:S(2)}, u32[]{:S(2)}) collective-permute-start(f32[24,128]{1,0:T(8,128)S(1)} %get-tuple-element.37.mine), channel_id=1, source_target_pairs={{0,8},{8,0},{16,24},{24,16},{32,40},{40,32},{48,56},{56,48},{64,72... | collective-permute-start | bytes 36872 | tf_op jit(solution)/shard_map/ppermute | solution.py:499
  52.6 0.4 collective-permute-done.7.inter
  53.0 0.8 collective-permute-done.6.core
  53.8 1.9 %collective-permute-start.9 = (f32[8,128]{1,0:T(8,128)S(1)}, f32[8,128]{1,0:T(8,128)S(1)}, u32[]{:S(2)}, u32[]{:S(2)}) collective-permute-start(f32[8,128]{1,0:T(8,128)S(1)} %shard_map.92), channel_id=1, source_target_pairs={{0,7},{1,2},{2,1},{3,4},{4,3},{5,6},{6,5},{7,0},{8,15},{9,10},{10,... | collective-permute-start | bytes 12296 | tf_op jit(solution)/shard_map/ppermute | solution.py:511
  55.7 2.1 %collective-permute-start.8 = (f32[8,128]{1,0:T(8,128)S(1)}, f32[8,128]{1,0:T(8,128)S(1)}, u32[]{:S(2)}, u32[]{:S(2)}) collective-permute-start(f32[8,128]{1,0:T(8,128)S(1)} %shard_map.92), channel_id=1, source_target_pairs={{0,1},{1,0},{2,3},{3,2},{4,5},{5,4},{6,7},{7,6},{8,9},{9,8},{10,11... | collective-permute-start | bytes 12296 | tf_op jit(solution)/shard_map/ppermute | solution.py:507
  57.8 1.5 %collective-permute-done.9.odd = f32[8,128]{1,0:T(8,128)S(1)} collective-permute-done((f32[8,128]{1,0:T(8,128)S(1)}, f32[8,128]{1,0:T(8,128)S(1)}, u32[]{:S(2)}, u32[]{:S(2)}) %collective-permute-start.9) | collective-permute-done | bytes 4128 | tf_op jit(solution)/shard_map/ppermute | solution.py:511
  59.3 0.9 collective-permute-done.8.even
  60.2 2.7 %shard_map.93 = (f32[256,128]{1,0:T(8,128)S(1)}, f32[24,128]{1,0:T(8,128)S(1)}, f32[64,128]{1,0:T(8,128)S(1)}) custom-call(f32[256,128]{1,0:T(8,128)S(1)} %get-tuple-element.33.spots, f32[16,128]{1,0:T(8,128)S(1)} %get-tuple-element.34.by_lane, f32[24,128]{1,0:T(8,128)S(1)} %collective-permute-done.6.core, f32[24,128]{1,0:T(8,128)S(1)} %get-tuple-element.37.mine, ...), custom_call_target="tpu_custom_call" | custom-call | flops 4000000 | tf_op jit(solution)/shard_map/pallas_call | solution.py:54
  63.0 11.0 %all_to_all.15 = f32[32,2,128]{2,1,0:T(2,128)S(1)} all-to-all(f32[32,2,128]{2,1,0:T(2,128)S(1)} %bitcast.22), channel_id=1, replica_groups={{36,37,38,39,48,49,50,51,52,53,54,55,0,1,2,3,4,5,6,7,16,17,18,19,20,21,..., dimensions={0} | all-to-all | bytes 65536 | tf_op jit(solution)/shard_map/all_to_all | solution.py:517
  74.0 0.6 shard_map.94
  74.6 18.7 %all-to-all-start.2 = ((f32[32,1,128]{2,1,0:T(1,128)}), f32[32,1,128]{2,1,0:T(1,128)S(1)}, u32[]{:S(2)}, u32[]{:S(2)}) async-start(f32[32,1,128]{2,1,0:T(1,128)} %bitcast.11), calls=%async_computation.2 | async-start | bytes 32768 | tf_op jit(solution)/shard_map/all_to_all | solution.py:517
  93.3 3.3 %collective-permute-start.11 = (f32[24,128]{1,0:T(8,128)S(1)}, f32[24,128]{1,0:T(8,128)S(1)}, u32[]{:S(2)}, u32[]{:S(2)}) collective-permute-start(f32[24,128]{1,0:T(8,128)S(1)} %get-tuple-element.42.mine), channel_id=1, source_target_pairs={{8,16},{16,8},{24,32},{32,24},{40,48},{48,40},{56,64},{64,56},{72,... | collective-permute-start | bytes 36872 | tf_op jit(solution)/shard_map/ppermute | solution.py:503
  96.7 1.9 %collective-permute-start.10 = (f32[24,128]{1,0:T(8,128)S(1)}, f32[24,128]{1,0:T(8,128)S(1)}, u32[]{:S(2)}, u32[]{:S(2)}) collective-permute-start(f32[24,128]{1,0:T(8,128)S(1)} %get-tuple-element.42.mine), channel_id=1, source_target_pairs={{0,8},{8,0},{16,24},{24,16},{32,40},{40,32},{48,56},{56,48},{64,72... | collective-permute-start | bytes 36872 | tf_op jit(solution)/shard_map/ppermute | solution.py:499
  98.6 0.0 collective-permute-done.11.inter
  98.6 1.1 %collective-permute-done.10.core = f32[24,128]{1,0:T(8,128)S(1)} collective-permute-done((f32[24,128]{1,0:T(8,128)S(1)}, f32[24,128]{1,0:T(8,128)S(1)}, u32[]{:S(2)}, u32[]{:S(2)}) %collective-permute-start.10) | collective-permute-done | bytes 12320 | tf_op jit(solution)/shard_map/ppermute | solution.py:499
  99.7 0.6 all-to-all-done.2
  100.3 1.8 %shard_map.95 = (f32[256,128]{1,0:T(8,128)}, f32[256,128]{1,0:T(8,128)}) custom-call(f32[256,128]{1,0:T(8,128)S(1)} %get-tuple-element.33.spots, f32[16,128]{1,0:T(8,128)S(1)} %get-tuple-element.34.by_lane, f32[24,128]{1,0:T(8,128)S(1)} %collective-permute-done.10.core, f32[24,128]{1,0:T(8,128)S(1)} %get-tuple-element.42.mine, ...), custom_call_target="tpu_custom_call" | custom-call | flops 2000000 | tf_op jit(solution)/shard_map/pallas_call | solution.py:54
  (1 shorter events, 0.0 us)
Async XLA Ops:
  4.0 8.4 %copy-start = (f32[2,16,16,128]{3,2,1,0:T(8,128)S(1)}, f32[2,16,16,128]{3,2,1,0:T(8,128)}, u32[]{:S(2)}) copy-start(f32[2,16,16,128]{3,2,1,0:T(8,128)} %param.7) | copy-start | bytes 786436
  4.0 32.5 %all-to-all-start = ((f32[8,136,128]{2,1,0:T(8,128)}), f32[8,136,128]{2,1,0:T(8,128)S(1)}, u32[]{:S(2)}, u32[]{:S(2)}) async-start(f32[8,136,128]{2,1,0:T(8,128)} %bitcast.23), calls=%async_computation | async-start | bytes 1114112 | tf_op jit(solution)/shard_map/all_to_all | solution.py:517
  12.6 23.9 %collective-permute-start = (f32[256,128]{1,0:T(8,128)S(1)}, f32[256,128]{1,0:T(8,128)S(1)}, u32[]{:S(2)}, u32[]{:S(2)}) collective-permute-start(f32[256,128]{1,0:T(8,128)S(1)} %get-tuple-element.25), channel_id=1, source_target_pairs={{0,8},{8,0},{16,24},{24,16},{32,40},{40,32},{48,56},{56,48},{64,72... | collective-permute-start | bytes 393224 | tf_op jit(solution)/shard_map/ppermute | solution.py:499
  25.8 10.7 %collective-permute-start.1 = (f32[256,128]{1,0:T(8,128)S(1)}, f32[256,128]{1,0:T(8,128)S(1)}, u32[]{:S(2)}, u32[]{:S(2)}) collective-permute-start(f32[256,128]{1,0:T(8,128)S(1)} %get-tuple-element.26), channel_id=1, source_target_pairs={{8,16},{16,8},{24,32},{32,24},{40,48},{48,40},{56,64},{64,56},{72,... | collective-permute-start | bytes 393224 | tf_op jit(solution)/shard_map/ppermute | solution.py:503
  27.8 5.1 %collective-permute-start.2 = (f32[32,128]{1,0:T(8,128)S(1)}, f32[32,128]{1,0:T(8,128)S(1)}, u32[]{:S(2)}, u32[]{:S(2)}) collective-permute-start(f32[32,128]{1,0:T(8,128)S(1)} %get-tuple-element.27), channel_id=1, source_target_pairs={{0,1},{1,0},{2,3},{3,2},{4,5},{5,4},{6,7},{7,6},{8,9},{9,8},{10,11... | collective-permute-start | bytes 49160 | tf_op jit(solution)/shard_map/ppermute | solution.py:507
  30.9 5.7 %collective-permute-start.3 = (f32[32,128]{1,0:T(8,128)S(1)}, f32[32,128]{1,0:T(8,128)S(1)}, u32[]{:S(2)}, u32[]{:S(2)}) collective-permute-start(f32[32,128]{1,0:T(8,128)S(1)} %get-tuple-element.28), channel_id=1, source_target_pairs={{0,7},{1,2},{2,1},{3,4},{4,3},{5,6},{6,5},{7,0},{8,15},{9,10},{10,... | collective-permute-start | bytes 49160 | tf_op jit(solution)/shard_map/ppermute | solution.py:511
  36.9 7.5 %collective-permute-start.5 = (f32[184,128]{1,0:T(8,128)S(1)}, f32[184,128]{1,0:T(8,128)S(1)}, u32[]{:S(2)}, u32[]{:S(2)}) collective-permute-start(f32[184,128]{1,0:T(8,128)S(1)} %get-tuple-element.32), channel_id=1, source_target_pairs={{8,16},{16,8},{24,32},{32,24},{40,48},{48,40},{56,64},{64,56},{72,... | collective-permute-start | bytes 282632 | tf_op jit(solution)/shard_map/ppermute | solution.py:503
  42.0 3.2 %collective-permute-start.4 = (f32[184,128]{1,0:T(8,128)S(1)}, f32[184,128]{1,0:T(8,128)S(1)}, u32[]{:S(2)}, u32[]{:S(2)}) collective-permute-start(f32[184,128]{1,0:T(8,128)S(1)} %get-tuple-element.31.own_message), channel_id=1, source_target_pairs={{0,8},{8,0},{16,24},{24,16},{32,40},{40,32},{48,56},{56,48},{64,72... | collective-permute-start | bytes 282632 | tf_op jit(solution)/shard_map/ppermute | solution.py:499
  48.0 5.0 %collective-permute-start.7 = (f32[24,128]{1,0:T(8,128)S(1)}, f32[24,128]{1,0:T(8,128)S(1)}, u32[]{:S(2)}, u32[]{:S(2)}) collective-permute-start(f32[24,128]{1,0:T(8,128)S(1)} %get-tuple-element.37.mine), channel_id=1, source_target_pairs={{8,16},{16,8},{24,32},{32,24},{40,48},{48,40},{56,64},{64,56},{72,... | collective-permute-start | bytes 36872 | tf_op jit(solution)/shard_map/ppermute | solution.py:503
  50.7 3.1 %collective-permute-start.6 = (f32[24,128]{1,0:T(8,128)S(1)}, f32[24,128]{1,0:T(8,128)S(1)}, u32[]{:S(2)}, u32[]{:S(2)}) collective-permute-start(f32[24,128]{1,0:T(8,128)S(1)} %get-tuple-element.37.mine), channel_id=1, source_target_pairs={{0,8},{8,0},{16,24},{24,16},{32,40},{40,32},{48,56},{56,48},{64,72... | collective-permute-start | bytes 36872 | tf_op jit(solution)/shard_map/ppermute | solution.py:499
  53.8 5.6 %collective-permute-start.9 = (f32[8,128]{1,0:T(8,128)S(1)}, f32[8,128]{1,0:T(8,128)S(1)}, u32[]{:S(2)}, u32[]{:S(2)}) collective-permute-start(f32[8,128]{1,0:T(8,128)S(1)} %shard_map.92), channel_id=1, source_target_pairs={{0,7},{1,2},{2,1},{3,4},{4,3},{5,6},{6,5},{7,0},{8,15},{9,10},{10,... | collective-permute-start | bytes 12296 | tf_op jit(solution)/shard_map/ppermute | solution.py:511
  55.7 4.6 %collective-permute-start.8 = (f32[8,128]{1,0:T(8,128)S(1)}, f32[8,128]{1,0:T(8,128)S(1)}, u32[]{:S(2)}, u32[]{:S(2)}) collective-permute-start(f32[8,128]{1,0:T(8,128)S(1)} %shard_map.92), channel_id=1, source_target_pairs={{0,1},{1,0},{2,3},{3,2},{4,5},{5,4},{6,7},{7,6},{8,9},{9,8},{10,11... | collective-permute-start | bytes 12296 | tf_op jit(solution)/shard_map/ppermute | solution.py:507
  74.6 25.7 %all-to-all-start.2 = ((f32[32,1,128]{2,1,0:T(1,128)}), f32[32,1,128]{2,1,0:T(1,128)S(1)}, u32[]{:S(2)}, u32[]{:S(2)}) async-start(f32[32,1,128]{2,1,0:T(1,128)} %bitcast.11), calls=%async_computation.2 | async-start | bytes 32768 | tf_op jit(solution)/shard_map/all_to_all | solution.py:517
  93.3 5.3 %collective-permute-start.11 = (f32[24,128]{1,0:T(8,128)S(1)}, f32[24,128]{1,0:T(8,128)S(1)}, u32[]{:S(2)}, u32[]{:S(2)}) collective-permute-start(f32[24,128]{1,0:T(8,128)S(1)} %get-tuple-element.42.mine), channel_id=1, source_target_pairs={{8,16},{16,8},{24,32},{32,24},{40,48},{48,40},{56,64},{64,56},{72,... | collective-permute-start | bytes 36872 | tf_op jit(solution)/shard_map/ppermute | solution.py:503
  96.7 3.1 %collective-permute-start.10 = (f32[24,128]{1,0:T(8,128)S(1)}, f32[24,128]{1,0:T(8,128)S(1)}, u32[]{:S(2)}, u32[]{:S(2)}) collective-permute-start(f32[24,128]{1,0:T(8,128)S(1)} %get-tuple-element.42.mine), channel_id=1, source_target_pairs={{0,8},{8,0},{16,24},{24,16},{32,40},{40,32},{48,56},{56,48},{64,72... | collective-permute-start | bytes 36872 | tf_op jit(solution)/shard_map/ppermute | solution.py:499

commit v9 on v8

--- a/solution.py
+++ b/solution.py
@@ -154,6 +154,10 @@
                 to_inter[at : at + 8, :] = jnp.where(even, down, up)
 
 
+def backwards(x):
+    return jnp.concatenate([x[i : i + 1] for i in reversed(range(x.shape[0]))], axis=0)
+
+
 def arrange(flow, parcels, core, inter, even_edges, odd_edges, wide, strips, to_core, to_inter):
     ln = lanes(8)
     here = lax.rem(lax.axis_index("lon"), 2) == 0
@@ -179,13 +183,14 @@
     lower, upper = strips[:STRIP, :], strips[STRIP:, :]
     to_core[:STRIP, :] = jnp.where(even, upper, lower)
     to_inter[:STRIP, :] = jnp.where(even, lower, upper)
-    edge = parcels[pl.ds(BULK + 2, LON, stride=PARCEL), :]
+    edge = backwards(parcels[pl.ds(BULK + 2, LON, stride=PARCEL), :])
     named = parcels[pl.ds(BULK + 3, LON, stride=PARCEL), :]
-    turned = jnp.transpose(named)
+    turned, turned_back = jnp.transpose(named), jnp.transpose(backwards(named))
     spot = jnp.full((1, LANES), NOWHERE, F32)
     line = lanes(1)
     for i, k in enumerate((2, 3, 0, 1, 4, 5)):
-        line_k = jnp.concatenate([turned[k : k + 1, :], jnp.zeros((1, LANES - LON), F32)], axis=1)
+        rows = turned if k in (2, 3) else turned_back
+        line_k = jnp.concatenate([rows[k : k + 1, :], jnp.zeros((1, LANES - LON), F32)], axis=1)
         spot = jnp.where((line >= 8 * i) & (line < 8 * i + 8), roll(line_k, 8 * i), spot)
     for o in range(SLOT):
         own = parcels[pl.ds(BULK + o, LON, stride=PARCEL), :]
@@ -238,11 +243,6 @@
 
 def padded(x, rows):
     return jnp.concatenate([x, jnp.zeros((rows - x.shape[0], LANES), F32)], axis=0)
-
-
-def right_strips(x):
-    ln = lanes(x.shape[0])
-    return jnp.where((ln >= 56) & (ln < 64), roll(x, 56), 0.0)
 
 
 def lay_out(spots, by_lane, own, sides, field, strips, low, high):
@@ -396,18 +396,16 @@
     sums[...] = in_lanes(0, [square])
 
 
-def stepped(x, unit):
-    row = places(OWN)
-    for bit in range(4):
-        x = jnp.where((row & (1 << bit)) != 0, roll(x, unit << bit), x)
-    return x
+def fanned(x, shift):
+    return pltpu.roll(x, shift % LANES, axis=1, stride=8, stride_axis=0)
 
 
 def herald(rows, message):
     mine = (lanes(OWN) >> 3) == places(OWN)
     message[:OWN, :] = rows
-    message[OWN : OWN + 1, :] = jnp.sum(jnp.where(mine, stepped(rows, 8), 0.0), axis=0, keepdims=True)
-    message[OWN + 1 : OWN + 2, :] = jnp.sum(jnp.where(mine, stepped(roll(rows, 8), 8), 0.0), axis=0, keepdims=True)
+    for at, shift in ((OWN, 0), (OWN + 1, 8)):
+        spread = jnp.concatenate([fanned(rows[:8], shift), fanned(rows[8:], shift + HALF)], axis=0)
+        message[at : at + 1, :] = jnp.sum(jnp.where(mine, spread, 0.0), axis=0, keepdims=True)
     message[OWN + 2 :, :] = jnp.zeros((HERALD - OWN - 2, LANES), F32)
 
 
@@ -426,10 +424,14 @@
 
 def side_strips(lefts, rights):
     ln = lanes(OWN)
-    rows = [stepped(jnp.broadcast_to(x, (OWN, LANES)), -8) for x in lefts]
-    out = [jnp.where(ln < 8, x, 0.0) for x in rows]
-    rows = [stepped(jnp.broadcast_to(x, (OWN, LANES)), -8) for x in rights]
-    return padded(jnp.concatenate(out + [right_strips(x) for x in rows], axis=0), LANES)
+
+    def rows(x, shift):
+        x = jnp.broadcast_to(x, (8, LANES))
+        return jnp.concatenate([fanned(x, shift - 56), fanned(x, shift - 120)], axis=0)
+
+    out = [jnp.where(ln < 8, rows(x, 0), 0.0) for x in lefts]
+    out += [jnp.where((ln >= 56) & (ln < 64), rows(x, 56), 0.0) for x in rights]
+    return padded(jnp.concatenate(out, axis=0), LANES)
 
 
 def second_half(spots, by_lane, core, mine, inter, even, odd, wide, strips, beside, grams, before, kept, message, out, field, other, strip, other_strip, image):

time: 103 us -> 102 us (level)
  no operation moved by 1% of the time
where the time goes in v9:
time: 102 us; the launch traced here: 101 us
  starting transfers between devices  68.1 us (67%)
  Pallas kernels  11 us (11%)
  blocking collectives  11 us (11%)
  waiting for transfers between devices  9.75 us (10%)
  between operations  1.45 us (1%)
    all_to_all x2, starting transfers between devices, spread_out(): lax.all_to_all(x, axes, split_axis=0, concat_axis=0, tiled=True, axis_ind...  27.1 us
    ppermute x4, starting transfers between devices, to_core(): return lax.ppermute(x, LAT, [(i, i ^ 1) for i in range(lax.axis_size(LAT))])  19 us
    ppermute x4, starting transfers between devices, to_inter(): lax.ppermute(x, LAT, [(i, (i + 1 ^ 1) - 1) for i in range(1, lax.axis_siz...  13 us
    all_to_all x1, blocking collectives, spread_out(): lax.all_to_all(x, axes, split_axis=0, concat_axis=0, tiled=True, axis_ind...  11 us
    pallas_call x10, Pallas kernels, call(): pl.pallas_call(body, out_shape=[jax.ShapeDtypeStruct(s, F32) for s in out...  11 us
    ppermute x2, starting transfers between devices, to_even(): return lax.ppermute(x, 'lon', [(i, i ^ 1) for i in range(LON)])  5.24 us
    ppermute x2, waiting for transfers between devices, to_odd(): lax.ppermute(x, 'lon', [(i, (((i + 1) % LON ^ 1) - 1) % LON) for i in ran...  5.12 us
    ppermute x2, starting transfers between devices, to_odd(): lax.ppermute(x, 'lon', [(i, (((i + 1) % LON ^ 1) - 1) % LON) for i in ran...  3.83 us
  transfers between devices with their start and end apart: 14, of which 9 were waited for; matrix products, arithmetic and copies ran while one was open for 0% of the time, Pallas kernels for 1%

profile of v9, /device:TPU:1, one launch (start us, length us, event | category | flops | bytes accessed | tf_op | source)
XLA Modules:
  0.0 101.4 jit_solution(8315400680928687892)
XLA Ops:
  1.3 2.7 %shard_map.86 = f32[1088,128]{1,0:T(8,128)} custom-call(s32[8]{0:T(128)} %bitcast.27, s32[8]{0:T(128)} %bitcast.28, s32[1,1]{1,0:T(1,128)S(6)} %copy.10.count_at, f32[8,128,128]{2,1,0:T(8,128)} %bitcast.24, f32[8,128]{1,0:T(8,128)} %bitcast.25, f32[8,128]{1,0:T(8,128)} %bitcast.26), custom_call_target="tpu_custom_call" | custom-call | flops 4000000 | tf_op jit(solution)/shard_map/pallas_call | solution.py:54
  4.0 0.0 copy-start
  4.0 8.4 %all-to-all-start = ((f32[8,136,128]{2,1,0:T(8,128)}), f32[8,136,128]{2,1,0:T(8,128)S(1)}, u32[]{:S(2)}, u32[]{:S(2)}) async-start(f32[8,136,128]{2,1,0:T(8,128)} %bitcast.23), calls=%async_computation | async-start | bytes 1114112 | tf_op jit(solution)/shard_map/all_to_all | solution.py:519
  12.4 0.0 copy-done
  12.4 0.2 shard_map.87
  12.6 13.2 %collective-permute-start = (f32[256,128]{1,0:T(8,128)S(1)}, f32[256,128]{1,0:T(8,128)S(1)}, u32[]{:S(2)}, u32[]{:S(2)}) collective-permute-start(f32[256,128]{1,0:T(8,128)S(1)} %get-tuple-element.25), channel_id=1, source_target_pairs={{0,8},{8,0},{16,24},{24,16},{32,40},{40,32},{48,56},{56,48},{64,72... | collective-permute-start | bytes 393224 | tf_op jit(solution)/shard_map/ppermute | solution.py:501
  25.8 1.9 %collective-permute-start.1 = (f32[256,128]{1,0:T(8,128)S(1)}, f32[256,128]{1,0:T(8,128)S(1)}, u32[]{:S(2)}, u32[]{:S(2)}) collective-permute-start(f32[256,128]{1,0:T(8,128)S(1)} %get-tuple-element.26), channel_id=1, source_target_pairs={{8,16},{16,8},{24,32},{32,24},{40,48},{48,40},{56,64},{64,56},{72,... | collective-permute-start | bytes 393224 | tf_op jit(solution)/shard_map/ppermute | solution.py:505
  27.8 3.1 %collective-permute-start.2 = (f32[32,128]{1,0:T(8,128)S(1)}, f32[32,128]{1,0:T(8,128)S(1)}, u32[]{:S(2)}, u32[]{:S(2)}) collective-permute-start(f32[32,128]{1,0:T(8,128)S(1)} %get-tuple-element.27), channel_id=1, source_target_pairs={{0,1},{1,0},{2,3},{3,2},{4,5},{5,4},{6,7},{7,6},{8,9},{9,8},{10,11... | collective-permute-start | bytes 49160 | tf_op jit(solution)/shard_map/ppermute | solution.py:509
  30.9 1.9 %collective-permute-start.3 = (f32[32,128]{1,0:T(8,128)S(1)}, f32[32,128]{1,0:T(8,128)S(1)}, u32[]{:S(2)}, u32[]{:S(2)}) collective-permute-start(f32[32,128]{1,0:T(8,128)S(1)} %get-tuple-element.28), channel_id=1, source_target_pairs={{0,7},{1,2},{2,1},{3,4},{4,3},{5,6},{6,5},{7,0},{8,15},{9,10},{10,... | collective-permute-start | bytes 49160 | tf_op jit(solution)/shard_map/ppermute | solution.py:513
  32.8 0.1 collective-permute-done.2.even_edges
  32.9 3.6 %collective-permute-done.3.odd_edges = f32[32,128]{1,0:T(8,128)S(1)} collective-permute-done((f32[32,128]{1,0:T(8,128)S(1)}, f32[32,128]{1,0:T(8,128)S(1)}, u32[]{:S(2)}, u32[]{:S(2)}) %collective-permute-start.3) | collective-permute-done | bytes 16416 | tf_op jit(solution)/shard_map/ppermute | solution.py:513
  36.5 0.0 collective-permute-done.core
  36.6 0.0 collective-permute-done.1.inter
  36.6 0.0 all-to-all-done
  36.6 0.4 shard_map.88
  36.9 5.1 %collective-permute-start.5 = (f32[184,128]{1,0:T(8,128)S(1)}, f32[184,128]{1,0:T(8,128)S(1)}, u32[]{:S(2)}, u32[]{:S(2)}) collective-permute-start(f32[184,128]{1,0:T(8,128)S(1)} %get-tuple-element.32), channel_id=1, source_target_pairs={{8,16},{16,8},{24,32},{32,24},{40,48},{48,40},{56,64},{64,56},{72,... | collective-permute-start | bytes 282632 | tf_op jit(solution)/shard_map/ppermute | solution.py:505
  42.0 1.9 %collective-permute-start.4 = (f32[184,128]{1,0:T(8,128)S(1)}, f32[184,128]{1,0:T(8,128)S(1)}, u32[]{:S(2)}, u32[]{:S(2)}) collective-permute-start(f32[184,128]{1,0:T(8,128)S(1)} %get-tuple-element.31.own_message), channel_id=1, source_target_pairs={{0,8},{8,0},{16,24},{24,16},{32,40},{40,32},{48,56},{56,48},{64,72... | collective-permute-start | bytes 282632 | tf_op jit(solution)/shard_map/ppermute | solution.py:501
  43.9 0.5 shard_map.90.grams
  44.5 0.0 collective-permute-done.5.inter
  44.5 0.7 collective-permute-done.4.core
  45.2 1.9 %shard_map.89 = (f32[256,128]{1,0:T(8,128)S(1)}, f32[256,128]{1,0:T(8,128)S(1)}, f32[16,128]{1,0:T(8,128)S(1)}, f32[256,128]{1,0:T(8,128)S(1)}, f32[16,128]{1,0:T(8,128)S(1)}, /*index=5*/f32[8,128]{1,0:T(8,128)S(1)}) custom-call(f32[1024,128]{1,0:T(8,128)S(1)} %get-tuple-element.29.wide, f32[256,128]{1,0:T(8,128)S(1)} %get-tuple-element.30.mine.strips, ...), custom_call_target="tpu_custom_call" | custom-call | flops 4000000 | tf_op jit(solution)/shard_map/pallas_call | solution.py:54
  47.1 0.6 shard_map.91
  47.7 2.7 %collective-permute-start.7 = (f32[24,128]{1,0:T(8,128)S(1)}, f32[24,128]{1,0:T(8,128)S(1)}, u32[]{:S(2)}, u32[]{:S(2)}) collective-permute-start(f32[24,128]{1,0:T(8,128)S(1)} %get-tuple-element.37.mine), channel_id=1, source_target_pairs={{8,16},{16,8},{24,32},{32,24},{40,48},{48,40},{56,64},{64,56},{72,... | collective-permute-start | bytes 36872 | tf_op jit(solution)/shard_map/ppermute | solution.py:505
  50.5 1.9 %collective-permute-start.6 = (f32[24,128]{1,0:T(8,128)S(1)}, f32[24,128]{1,0:T(8,128)S(1)}, u32[]{:S(2)}, u32[]{:S(2)}) collective-permute-start(f32[24,128]{1,0:T(8,128)S(1)} %get-tuple-element.37.mine), channel_id=1, source_target_pairs={{0,8},{8,0},{16,24},{24,16},{32,40},{40,32},{48,56},{56,48},{64,72... | collective-permute-start | bytes 36872 | tf_op jit(solution)/shard_map/ppermute | solution.py:501
  52.4 0.4 collective-permute-done.7.inter
  52.8 0.8 collective-permute-done.6.core
  53.5 1.9 %collective-permute-start.9 = (f32[8,128]{1,0:T(8,128)S(1)}, f32[8,128]{1,0:T(8,128)S(1)}, u32[]{:S(2)}, u32[]{:S(2)}) collective-permute-start(f32[8,128]{1,0:T(8,128)S(1)} %shard_map.92), channel_id=1, source_target_pairs={{0,7},{1,2},{2,1},{3,4},{4,3},{5,6},{6,5},{7,0},{8,15},{9,10},{10,... | collective-permute-start | bytes 12296 | tf_op jit(solution)/shard_map/ppermute | solution.py:513
  55.4 2.1 %collective-permute-start.8 = (f32[8,128]{1,0:T(8,128)S(1)}, f32[8,128]{1,0:T(8,128)S(1)}, u32[]{:S(2)}, u32[]{:S(2)}) collective-permute-start(f32[8,128]{1,0:T(8,128)S(1)} %shard_map.92), channel_id=1, source_target_pairs={{0,1},{1,0},{2,3},{3,2},{4,5},{5,4},{6,7},{7,6},{8,9},{9,8},{10,11... | collective-permute-start | bytes 12296 | tf_op jit(solution)/shard_map/ppermute | solution.py:509
  57.6 1.5 %collective-permute-done.9.odd = f32[8,128]{1,0:T(8,128)S(1)} collective-permute-done((f32[8,128]{1,0:T(8,128)S(1)}, f32[8,128]{1,0:T(8,128)S(1)}, u32[]{:S(2)}, u32[]{:S(2)}) %collective-permute-start.9) | collective-permute-done | bytes 4128 | tf_op jit(solution)/shard_map/ppermute | solution.py:513
  59.1 0.9 collective-permute-done.8.even
  60.0 2.4 %shard_map.93 = (f32[256,128]{1,0:T(8,128)S(1)}, f32[24,128]{1,0:T(8,128)S(1)}, f32[64,128]{1,0:T(8,128)S(1)}) custom-call(f32[256,128]{1,0:T(8,128)S(1)} %get-tuple-element.33.spots, f32[16,128]{1,0:T(8,128)S(1)} %get-tuple-element.34.by_lane, f32[24,128]{1,0:T(8,128)S(1)} %collective-permute-done.6.core, f32[24,128]{1,0:T(8,128)S(1)} %get-tuple-element.37.mine, ...), custom_call_target="tpu_custom_call" | custom-call | flops 4000000 | tf_op jit(solution)/shard_map/pallas_call | solution.py:54
  62.5 11.0 %all_to_all.15 = f32[32,2,128]{2,1,0:T(2,128)S(1)} all-to-all(f32[32,2,128]{2,1,0:T(2,128)S(1)} %bitcast.22), channel_id=1, replica_groups={{36,37,38,39,48,49,50,51,52,53,54,55,0,1,2,3,4,5,6,7,16,17,18,19,20,21,..., dimensions={0} | all-to-all | bytes 65536 | tf_op jit(solution)/shard_map/all_to_all | solution.py:519
  73.5 0.6 shard_map.94
  74.1 18.7 %all-to-all-start.2 = ((f32[32,1,128]{2,1,0:T(1,128)}), f32[32,1,128]{2,1,0:T(1,128)S(1)}, u32[]{:S(2)}, u32[]{:S(2)}) async-start(f32[32,1,128]{2,1,0:T(1,128)} %bitcast.11), calls=%async_computation.2 | async-start | bytes 32768 | tf_op jit(solution)/shard_map/all_to_all | solution.py:519
  92.8 3.3 %collective-permute-start.11 = (f32[24,128]{1,0:T(8,128)S(1)}, f32[24,128]{1,0:T(8,128)S(1)}, u32[]{:S(2)}, u32[]{:S(2)}) collective-permute-start(f32[24,128]{1,0:T(8,128)S(1)} %get-tuple-element.42.mine), channel_id=1, source_target_pairs={{8,16},{16,8},{24,32},{32,24},{40,48},{48,40},{56,64},{64,56},{72,... | collective-permute-start | bytes 36872 | tf_op jit(solution)/shard_map/ppermute | solution.py:505
  96.1 1.9 %collective-permute-start.10 = (f32[24,128]{1,0:T(8,128)S(1)}, f32[24,128]{1,0:T(8,128)S(1)}, u32[]{:S(2)}, u32[]{:S(2)}) collective-permute-start(f32[24,128]{1,0:T(8,128)S(1)} %get-tuple-element.42.mine), channel_id=1, source_target_pairs={{0,8},{8,0},{16,24},{24,16},{32,40},{40,32},{48,56},{56,48},{64,72... | collective-permute-start | bytes 36872 | tf_op jit(solution)/shard_map/ppermute | solution.py:501
  98.1 0.0 collective-permute-done.11.inter
  98.1 1.1 %collective-permute-done.10.core = f32[24,128]{1,0:T(8,128)S(1)} collective-permute-done((f32[24,128]{1,0:T(8,128)S(1)}, f32[24,128]{1,0:T(8,128)S(1)}, u32[]{:S(2)}, u32[]{:S(2)}) %collective-permute-start.10) | collective-permute-done | bytes 12320 | tf_op jit(solution)/shard_map/ppermute | solution.py:501
  99.2 0.6 all-to-all-done.2
  99.8 1.6 %shard_map.95 = (f32[256,128]{1,0:T(8,128)}, f32[256,128]{1,0:T(8,128)}) custom-call(f32[256,128]{1,0:T(8,128)S(1)} %get-tuple-element.33.spots, f32[16,128]{1,0:T(8,128)S(1)} %get-tuple-element.34.by_lane, f32[24,128]{1,0:T(8,128)S(1)} %collective-permute-done.10.core, f32[24,128]{1,0:T(8,128)S(1)} %get-tuple-element.42.mine, ...), custom_call_target="tpu_custom_call" | custom-call | flops 2000000 | tf_op jit(solution)/shard_map/pallas_call | solution.py:54
  (1 shorter events, 0.0 us)
Async XLA Ops:
  4.0 8.4 %copy-start = (f32[2,16,16,128]{3,2,1,0:T(8,128)S(1)}, f32[2,16,16,128]{3,2,1,0:T(8,128)}, u32[]{:S(2)}) copy-start(f32[2,16,16,128]{3,2,1,0:T(8,128)} %param.7) | copy-start | bytes 786436
  4.0 32.5 %all-to-all-start = ((f32[8,136,128]{2,1,0:T(8,128)}), f32[8,136,128]{2,1,0:T(8,128)S(1)}, u32[]{:S(2)}, u32[]{:S(2)}) async-start(f32[8,136,128]{2,1,0:T(8,128)} %bitcast.23), calls=%async_computation | async-start | bytes 1114112 | tf_op jit(solution)/shard_map/all_to_all | solution.py:519
  12.6 23.9 %collective-permute-start = (f32[256,128]{1,0:T(8,128)S(1)}, f32[256,128]{1,0:T(8,128)S(1)}, u32[]{:S(2)}, u32[]{:S(2)}) collective-permute-start(f32[256,128]{1,0:T(8,128)S(1)} %get-tuple-element.25), channel_id=1, source_target_pairs={{0,8},{8,0},{16,24},{24,16},{32,40},{40,32},{48,56},{56,48},{64,72... | collective-permute-start | bytes 393224 | tf_op jit(solution)/shard_map/ppermute | solution.py:501
  25.8 10.7 %collective-permute-start.1 = (f32[256,128]{1,0:T(8,128)S(1)}, f32[256,128]{1,0:T(8,128)S(1)}, u32[]{:S(2)}, u32[]{:S(2)}) collective-permute-start(f32[256,128]{1,0:T(8,128)S(1)} %get-tuple-element.26), channel_id=1, source_target_pairs={{8,16},{16,8},{24,32},{32,24},{40,48},{48,40},{56,64},{64,56},{72,... | collective-permute-start | bytes 393224 | tf_op jit(solution)/shard_map/ppermute | solution.py:505
  27.8 5.1 %collective-permute-start.2 = (f32[32,128]{1,0:T(8,128)S(1)}, f32[32,128]{1,0:T(8,128)S(1)}, u32[]{:S(2)}, u32[]{:S(2)}) collective-permute-start(f32[32,128]{1,0:T(8,128)S(1)} %get-tuple-element.27), channel_id=1, source_target_pairs={{0,1},{1,0},{2,3},{3,2},{4,5},{5,4},{6,7},{7,6},{8,9},{9,8},{10,11... | collective-permute-start | bytes 49160 | tf_op jit(solution)/shard_map/ppermute | solution.py:509
  30.9 5.7 %collective-permute-start.3 = (f32[32,128]{1,0:T(8,128)S(1)}, f32[32,128]{1,0:T(8,128)S(1)}, u32[]{:S(2)}, u32[]{:S(2)}) collective-permute-start(f32[32,128]{1,0:T(8,128)S(1)} %get-tuple-element.28), channel_id=1, source_target_pairs={{0,7},{1,2},{2,1},{3,4},{4,3},{5,6},{6,5},{7,0},{8,15},{9,10},{10,... | collective-permute-start | bytes 49160 | tf_op jit(solution)/shard_map/ppermute | solution.py:513
  36.9 7.5 %collective-permute-start.5 = (f32[184,128]{1,0:T(8,128)S(1)}, f32[184,128]{1,0:T(8,128)S(1)}, u32[]{:S(2)}, u32[]{:S(2)}) collective-permute-start(f32[184,128]{1,0:T(8,128)S(1)} %get-tuple-element.32), channel_id=1, source_target_pairs={{8,16},{16,8},{24,32},{32,24},{40,48},{48,40},{56,64},{64,56},{72,... | collective-permute-start | bytes 282632 | tf_op jit(solution)/shard_map/ppermute | solution.py:505
  42.0 3.2 %collective-permute-start.4 = (f32[184,128]{1,0:T(8,128)S(1)}, f32[184,128]{1,0:T(8,128)S(1)}, u32[]{:S(2)}, u32[]{:S(2)}) collective-permute-start(f32[184,128]{1,0:T(8,128)S(1)} %get-tuple-element.31.own_message), channel_id=1, source_target_pairs={{0,8},{8,0},{16,24},{24,16},{32,40},{40,32},{48,56},{56,48},{64,72... | collective-permute-start | bytes 282632 | tf_op jit(solution)/shard_map/ppermute | solution.py:501
  47.7 5.0 %collective-permute-start.7 = (f32[24,128]{1,0:T(8,128)S(1)}, f32[24,128]{1,0:T(8,128)S(1)}, u32[]{:S(2)}, u32[]{:S(2)}) collective-permute-start(f32[24,128]{1,0:T(8,128)S(1)} %get-tuple-element.37.mine), channel_id=1, source_target_pairs={{8,16},{16,8},{24,32},{32,24},{40,48},{48,40},{56,64},{64,56},{72,... | collective-permute-start | bytes 36872 | tf_op jit(solution)/shard_map/ppermute | solution.py:505
  50.5 3.1 %collective-permute-start.6 = (f32[24,128]{1,0:T(8,128)S(1)}, f32[24,128]{1,0:T(8,128)S(1)}, u32[]{:S(2)}, u32[]{:S(2)}) collective-permute-start(f32[24,128]{1,0:T(8,128)S(1)} %get-tuple-element.37.mine), channel_id=1, source_target_pairs={{0,8},{8,0},{16,24},{24,16},{32,40},{40,32},{48,56},{56,48},{64,72... | collective-permute-start | bytes 36872 | tf_op jit(solution)/shard_map/ppermute | solution.py:501
  53.5 5.6 %collective-permute-start.9 = (f32[8,128]{1,0:T(8,128)S(1)}, f32[8,128]{1,0:T(8,128)S(1)}, u32[]{:S(2)}, u32[]{:S(2)}) collective-permute-start(f32[8,128]{1,0:T(8,128)S(1)} %shard_map.92), channel_id=1, source_target_pairs={{0,7},{1,2},{2,1},{3,4},{4,3},{5,6},{6,5},{7,0},{8,15},{9,10},{10,... | collective-permute-start | bytes 12296 | tf_op jit(solution)/shard_map/ppermute | solution.py:513
  55.4 4.6 %collective-permute-start.8 = (f32[8,128]{1,0:T(8,128)S(1)}, f32[8,128]{1,0:T(8,128)S(1)}, u32[]{:S(2)}, u32[]{:S(2)}) collective-permute-start(f32[8,128]{1,0:T(8,128)S(1)} %shard_map.92), channel_id=1, source_target_pairs={{0,1},{1,0},{2,3},{3,2},{4,5},{5,4},{6,7},{7,6},{8,9},{9,8},{10,11... | collective-permute-start | bytes 12296 | tf_op jit(solution)/shard_map/ppermute | solution.py:509
  74.1 25.7 %all-to-all-start.2 = ((f32[32,1,128]{2,1,0:T(1,128)}), f32[32,1,128]{2,1,0:T(1,128)S(1)}, u32[]{:S(2)}, u32[]{:S(2)}) async-start(f32[32,1,128]{2,1,0:T(1,128)} %bitcast.11), calls=%async_computation.2 | async-start | bytes 32768 | tf_op jit(solution)/shard_map/all_to_all | solution.py:519
  92.8 5.3 %collective-permute-start.11 = (f32[24,128]{1,0:T(8,128)S(1)}, f32[24,128]{1,0:T(8,128)S(1)}, u32[]{:S(2)}, u32[]{:S(2)}) collective-permute-start(f32[24,128]{1,0:T(8,128)S(1)} %get-tuple-element.42.mine), channel_id=1, source_target_pairs={{8,16},{16,8},{24,32},{32,24},{40,48},{48,40},{56,64},{64,56},{72,... | collective-permute-start | bytes 36872 | tf_op jit(solution)/shard_map/ppermute | solution.py:505
  96.1 3.1 %collective-permute-start.10 = (f32[24,128]{1,0:T(8,128)S(1)}, f32[24,128]{1,0:T(8,128)S(1)}, u32[]{:S(2)}, u32[]{:S(2)}) collective-permute-start(f32[24,128]{1,0:T(8,128)S(1)} %get-tuple-element.42.mine), channel_id=1, source_target_pairs={{0,8},{8,0},{16,24},{24,16},{32,40},{40,32},{48,56},{56,48},{64,72... | collective-permute-start | bytes 36872 | tf_op jit(solution)/shard_map/ppermute | solution.py:501

commit v10 on v9

--- a/solution.py
+++ b/solution.py
@@ -24,7 +24,8 @@
 PARCEL = LIST
 EDGE = HALO * 2 * LEVELS
 STRIP = HALO * 2 * 8
-LEFTS = STRIP + OWN
+RAW = 2 * 2 * 8
+LEFTS = RAW + OWN
 RIGHTS = LEFTS + OWN
 SPOTS = RIGHTS + OWN
 MESSAGE = SPOTS + 8
@@ -158,31 +159,46 @@
     return jnp.concatenate([x[i : i + 1] for i in reversed(range(x.shape[0]))], axis=0)
 
 
-def arrange(flow, parcels, core, inter, even_edges, odd_edges, wide, strips, to_core, to_inter):
+def strip_of(low, high, left, right, k):
     ln = lanes(8)
-    here = lax.rem(lax.axis_index("lon"), 2) == 0
+    a = jnp.where(ln < 8, roll(left, -16 * k), jnp.where(ln < 32, roll(low, 8), jnp.where(ln < 56, roll(low, 56), roll(right, 56 - 16 * k))))
+    b = jnp.where(ln < 72, roll(left, 56 - 16 * k), jnp.where(ln < 96, roll(high, 72), jnp.where(ln < 120, roll(high, 120), roll(right, 112 - 16 * k))))
+    return jnp.where(ln < HALF, a, b)
+
+
+def widen(flow, core, inter, even_edges, odd_edges, wide, strips):
     even = lax.axis_index("lat_2") == 0
     wide[:EDGE, :] = jnp.where(even, inter[...], core[...])
     wide[EDGE + ROWS * 2 * LEVELS :, :] = jnp.where(even, core[...], inter[...])
     for f in range(2):
         for g in range(2):
-            at = (f * 2 + g) * 8
-            first, second = even_edges[at : at + 8, :], odd_edges[at : at + 8, :]
-            left, right = jnp.where(here, second, first), jnp.where(here, first, second)
+            left, right = left_and_right(even_edges, odd_edges, f, g)
             for k in range(8):
                 at = f * LEVELS * ROWS + g * 8 + k
                 low, high = flow[pl.ds(at, 8, stride=ROWS), :], flow[pl.ds(at + 8 * ROWS, 8, stride=ROWS), :]
                 at = EDGE + ((g * 8 + k) * 2 + f) * LEVELS
                 wide[at : at + 8, :] = low
                 wide[at + 8 : at + 16, :] = high
-                a = jnp.where(ln < 8, roll(left, -16 * k), jnp.where(ln < 32, roll(low, 8), jnp.where(ln < 56, roll(low, 56), roll(right, 56 - 16 * k))))
-                b = jnp.where(ln < 72, roll(left, 56 - 16 * k), jnp.where(ln < 96, roll(high, 72), jnp.where(ln < 120, roll(high, 120), roll(right, 112 - 16 * k))))
-                strip = jnp.where(ln < HALF, a, b)
                 at = ((g * 8 + k) * 2 + f) * 8
-                strips[at : at + 8, :] = strip
-    lower, upper = strips[:STRIP, :], strips[STRIP:, :]
-    to_core[:STRIP, :] = jnp.where(even, upper, lower)
-    to_inter[:STRIP, :] = jnp.where(even, lower, upper)
+                strips[at : at + 8, :] = strip_of(low, high, left, right, k)
+
+
+def left_and_right(even_edges, odd_edges, f, g):
+    here = lax.rem(lax.axis_index("lon"), 2) == 0
+    at = (f * 2 + g) * 8
+    first, second = even_edges[at : at + 8, :], odd_edges[at : at + 8, :]
+    return jnp.where(here, second, first), jnp.where(here, first, second)
+
+
+def arrange(parcels, even_edges, odd_edges, to_core, to_inter):
+    ln = lanes(8)
+    even = lax.axis_index("lat_2") == 0
+    for f in range(2):
+        lower, upper = (left_and_right(even_edges, odd_edges, f, g) for g in range(2))
+        for side in range(2):
+            at = (f * 2 + side) * 8
+            to_core[at : at + 8, :] = jnp.where(even, upper[side], lower[side])
+            to_inter[at : at + 8, :] = jnp.where(even, lower[side], upper[side])
     edge = backwards(parcels[pl.ds(BULK + 2, LON, stride=PARCEL), :])
     named = parcels[pl.ds(BULK + 3, LON, stride=PARCEL), :]
     turned, turned_back = jnp.transpose(named), jnp.transpose(backwards(named))
@@ -197,7 +213,7 @@
         left = jnp.where(ln < 8, roll(edge, -8 * o), 0.0)
         right = jnp.where((ln >= 56) & (ln < 64), roll(edge, 40 - 8 * o), 0.0)
         for out in (to_core, to_inter):
-            out[STRIP + o * LON : STRIP + (o + 1) * LON, :] = own
+            out[RAW + o * LON : RAW + (o + 1) * LON, :] = own
             out[LEFTS + o * LON : LEFTS + (o + 1) * LON, :] = left
             out[RIGHTS + o * LON : RIGHTS + (o + 1) * LON, :] = right
     for out in (to_core, to_inter):
@@ -377,8 +393,15 @@
 def first_half(wide, mine, core, own_message, inter, beside, spots, by_lane, kept, seen, sums, field, other, strip, other_strip, image):
     ln = lanes(8)
     even = lax.axis_index("lat_2") == 0
-    beside[:STRIP, :] = jnp.where(even, inter[:STRIP, :], core[:STRIP, :])
-    beside[STRIP:, :] = jnp.where(even, core[:STRIP, :], inter[:STRIP, :])
+    for n in range(2):
+        edges = jnp.where(even == (n == 0), inter[:RAW, :], core[:RAW, :])
+        for f in range(2):
+            left, right = edges[f * 16 : f * 16 + 8], edges[f * 16 + 8 : f * 16 + 16]
+            for k in range(HALO):
+                at = ((n * (HALO + ROWS) + k) * 2 + f) * LEVELS
+                low, high = wide[at : at + 8, :], wide[at + 8 : at + 16, :]
+                at = n * STRIP + (k * 2 + f) * 8
+                beside[at : at + 8, :] = strip_of(low, high, left, right, k)
     step = jnp.where(even, float(ROWS * LEVELS), -float(ROWS * LEVELS))
     c, o, i = core[SPOTS:, :] + step, own_message[SPOTS:, :], inter[SPOTS:, :] - step
     tables = (((c, 0), (o, 0), (i, 0)), ((c, 16), (o, 16), (i, 16), (c, 32), (o, 32), (i, 32)))
@@ -389,7 +412,7 @@
         by_lane[t * 8 : t * 8 + 8, :] = spot
         spots[t * LANES : (t + 1) * LANES, :] = jnp.transpose(jnp.broadcast_to(spot[:1], (LANES, LANES)))
     parts = (core, own_message, inter)
-    own = padded(jnp.concatenate([x[STRIP:LEFTS, :] for x in parts], axis=0), LANES)
+    own = padded(jnp.concatenate([x[RAW:LEFTS, :] for x in parts], axis=0), LANES)
     sides = padded(jnp.concatenate([x[LEFTS:RIGHTS, :] for x in parts] + [x[RIGHTS:SPOTS, :] for x in parts], axis=0), LANES)
     square, rows = back_and_on(spots, by_lane, own, sides, rates_of(wide, mine, beside), kept, (field, other), (strip, other_strip), image)
     seen[...] = rows
@@ -541,12 +564,10 @@
     even = to_even(for_even)
     inter = to_inter(for_inter)
     core = to_core(for_core)
-    wide, strips, for_core, for_inter = call(
-        arrange,
-        [(WIDE * 2 * LEVELS, LANES), (2 * STRIP, LANES), (MESSAGE, LANES), (MESSAGE, LANES)],
-        (flow, parcels, core, inter, even, odd),
-        2_000_000,
-    )
+    wide, strips = call(
+        widen, [(WIDE * 2 * LEVELS, LANES), (2 * STRIP, LANES)], (flow, core, inter, even, odd), 4_000_000
+    )
+    for_core, for_inter = call(arrange, [(MESSAGE, LANES)] * 2, (parcels, even, odd), 1_000_000)
     core, inter = to_core(for_core), to_inter(for_inter)
     (grams,) = call(unpack, [(OWN * LANES, LANES)], (parcels,), 4_000_000)
     cells, listed = (ROWS * LEVELS, LANES), (OWN, LANES)

time: 102 us -> 102 us (level)
    pallas_call x10 -> x11, Pallas kernels: 11 us -> 11.6 us  [call(): pl.pallas_call(body, out_shape=[jax.ShapeDtypeStruct(s, F32) for s in out...]
where the time goes in v10:
time: 102 us; the launch traced here: 101 us
  starting transfers between devices  67.6 us (66%)
  Pallas kernels  11.6 us (11%)
  blocking collectives  11.1 us (11%)
  waiting for transfers between devices  9.3 us (9%)
  between operations  1.47 us (1%)
    all_to_all x2, starting transfers between devices, spread_out(): lax.all_to_all(x, axes, split_axis=0, concat_axis=0, tiled=True, axis_ind...  27 us
    ppermute x4, starting transfers between devices, to_core(): return lax.ppermute(x, LAT, [(i, i ^ 1) for i in range(lax.axis_size(LAT))])  19 us
    ppermute x4, starting transfers between devices, to_inter(): lax.ppermute(x, LAT, [(i, (i + 1 ^ 1) - 1) for i in range(1, lax.axis_siz...  12.6 us
    pallas_call x11, Pallas kernels, call(): pl.pallas_call(body, out_shape=[jax.ShapeDtypeStruct(s, F32) for s in out...  11.6 us
    all_to_all x1, blocking collectives, spread_out(): lax.all_to_all(x, axes, split_axis=0, concat_axis=0, tiled=True, axis_ind...  11.1 us
    ppermute x2, starting transfers between devices, to_even(): return lax.ppermute(x, 'lon', [(i, i ^ 1) for i in range(LON)])  5.24 us
    ppermute x2, waiting for transfers between devices, to_odd(): lax.ppermute(x, 'lon', [(i, (((i + 1) % LON ^ 1) - 1) % LON) for i in ran...  5.12 us
    ppermute x2, starting transfers between devices, to_odd(): lax.ppermute(x, 'lon', [(i, (((i + 1) % LON ^ 1) - 1) % LON) for i in ran...  3.83 us
  transfers between devices with their start and end apart: 14, of which 9 were waited for; matrix products, arithmetic and copies ran while one was open for 0% of the time, Pallas kernels for 1%

profile of v10, /device:TPU:1, one launch (start us, length us, event | category | flops | bytes accessed | tf_op | source)
XLA Modules:
  0.0 101.1 jit_solution(3082716339089317337)
XLA Ops:
  1.3 2.7 %shard_map.88 = f32[1088,128]{1,0:T(8,128)} custom-call(s32[8]{0:T(128)} %bitcast.27, s32[8]{0:T(128)} %bitcast.28, s32[1,1]{1,0:T(1,128)S(6)} %copy.10.count_at, f32[8,128,128]{2,1,0:T(8,128)} %bitcast.24, f32[8,128]{1,0:T(8,128)} %bitcast.25, f32[8,128]{1,0:T(8,128)} %bitcast.26), custom_call_target="tpu_custom_call" | custom-call | flops 4000000 | tf_op jit(solution)/shard_map/pallas_call | solution.py:55
  4.0 0.0 copy-start
  4.0 8.4 %all-to-all-start = ((f32[8,136,128]{2,1,0:T(8,128)}), f32[8,136,128]{2,1,0:T(8,128)S(1)}, u32[]{:S(2)}, u32[]{:S(2)}) async-start(f32[8,136,128]{2,1,0:T(8,128)} %bitcast.23), calls=%async_computation | async-start | bytes 1114112 | tf_op jit(solution)/shard_map/all_to_all | solution.py:542
  12.4 0.0 copy-done
  12.4 0.2 shard_map.86
  12.6 13.2 %collective-permute-start = (f32[256,128]{1,0:T(8,128)S(1)}, f32[256,128]{1,0:T(8,128)S(1)}, u32[]{:S(2)}, u32[]{:S(2)}) collective-permute-start(f32[256,128]{1,0:T(8,128)S(1)} %get-tuple-element.25), channel_id=1, source_target_pairs={{0,8},{8,0},{16,24},{24,16},{32,40},{40,32},{48,56},{56,48},{64,72... | collective-permute-start | bytes 393224 | tf_op jit(solution)/shard_map/ppermute | solution.py:524
  25.8 1.9 %collective-permute-start.1 = (f32[256,128]{1,0:T(8,128)S(1)}, f32[256,128]{1,0:T(8,128)S(1)}, u32[]{:S(2)}, u32[]{:S(2)}) collective-permute-start(f32[256,128]{1,0:T(8,128)S(1)} %get-tuple-element.26), channel_id=1, source_target_pairs={{8,16},{16,8},{24,32},{32,24},{40,48},{48,40},{56,64},{64,56},{72,... | collective-permute-start | bytes 393224 | tf_op jit(solution)/shard_map/ppermute | solution.py:528
  27.8 3.1 %collective-permute-start.2 = (f32[32,128]{1,0:T(8,128)S(1)}, f32[32,128]{1,0:T(8,128)S(1)}, u32[]{:S(2)}, u32[]{:S(2)}) collective-permute-start(f32[32,128]{1,0:T(8,128)S(1)} %get-tuple-element.27), channel_id=1, source_target_pairs={{0,1},{1,0},{2,3},{3,2},{4,5},{5,4},{6,7},{7,6},{8,9},{9,8},{10,11... | collective-permute-start | bytes 49160 | tf_op jit(solution)/shard_map/ppermute | solution.py:532
  30.9 1.9 %collective-permute-start.3 = (f32[32,128]{1,0:T(8,128)S(1)}, f32[32,128]{1,0:T(8,128)S(1)}, u32[]{:S(2)}, u32[]{:S(2)}) collective-permute-start(f32[32,128]{1,0:T(8,128)S(1)} %get-tuple-element.28), channel_id=1, source_target_pairs={{0,7},{1,2},{2,1},{3,4},{4,3},{5,6},{6,5},{7,0},{8,15},{9,10},{10,... | collective-permute-start | bytes 49160 | tf_op jit(solution)/shard_map/ppermute | solution.py:536
  32.8 0.1 collective-permute-done.2.even_edges
  32.9 3.6 %collective-permute-done.3.odd_edges = f32[32,128]{1,0:T(8,128)S(1)} collective-permute-done((f32[32,128]{1,0:T(8,128)S(1)}, f32[32,128]{1,0:T(8,128)S(1)}, u32[]{:S(2)}, u32[]{:S(2)}) %collective-permute-start.3) | collective-permute-done | bytes 16416 | tf_op jit(solution)/shard_map/ppermute | solution.py:536
  36.5 0.0 all-to-all-done
  36.5 0.1 shard_map.89
  36.7 5.1 %collective-permute-start.5 = (f32[88,128]{1,0:T(8,128)S(1)}, f32[88,128]{1,0:T(8,128)S(1)}, u32[]{:S(2)}, u32[]{:S(2)}) collective-permute-start(f32[88,128]{1,0:T(8,128)S(1)} %get-tuple-element.32), channel_id=1, source_target_pairs={{8,16},{16,8},{24,32},{32,24},{40,48},{48,40},{56,64},{64,56},{72,... | collective-permute-start | bytes 135176 | tf_op jit(solution)/shard_map/ppermute | solution.py:528
  41.8 1.9 %collective-permute-start.4 = (f32[88,128]{1,0:T(8,128)S(1)}, f32[88,128]{1,0:T(8,128)S(1)}, u32[]{:S(2)}, u32[]{:S(2)}) collective-permute-start(f32[88,128]{1,0:T(8,128)S(1)} %get-tuple-element.31.own_message), channel_id=1, source_target_pairs={{0,8},{8,0},{16,24},{24,16},{32,40},{40,32},{48,56},{56,48},{64,72... | collective-permute-start | bytes 135176 | tf_op jit(solution)/shard_map/ppermute | solution.py:524
  43.7 0.0 collective-permute-done.core
  43.7 0.0 collective-permute-done.1.inter
  43.7 0.4 shard_map.87
  44.1 0.5 shard_map.91.grams
  44.6 0.0 collective-permute-done.5.inter
  44.6 0.3 collective-permute-done.4.core
  44.9 2.3 %shard_map.90 = (f32[256,128]{1,0:T(8,128)S(1)}, f32[256,128]{1,0:T(8,128)S(1)}, f32[16,128]{1,0:T(8,128)S(1)}, f32[256,128]{1,0:T(8,128)S(1)}, f32[16,128]{1,0:T(8,128)S(1)}, /*index=5*/f32[8,128]{1,0:T(8,128)S(1)}) custom-call(f32[1024,128]{1,0:T(8,128)S(1)} %get-tuple-element.29.wide, f32[256,128]{1,0:T(8,128)S(1)} %get-tuple-element.30.mine.strips, ...), custom_call_target="tpu_custom_call" | custom-call | flops 4000000 | tf_op jit(solution)/shard_map/pallas_call | solution.py:55
  47.2 0.6 shard_map.92
  47.9 2.2 %collective-permute-start.7 = (f32[24,128]{1,0:T(8,128)S(1)}, f32[24,128]{1,0:T(8,128)S(1)}, u32[]{:S(2)}, u32[]{:S(2)}) collective-permute-start(f32[24,128]{1,0:T(8,128)S(1)} %get-tuple-element.37.mine), channel_id=1, source_target_pairs={{8,16},{16,8},{24,32},{32,24},{40,48},{48,40},{56,64},{64,56},{72,... | collective-permute-start | bytes 36872 | tf_op jit(solution)/shard_map/ppermute | solution.py:528
  50.1 1.9 %collective-permute-start.6 = (f32[24,128]{1,0:T(8,128)S(1)}, f32[24,128]{1,0:T(8,128)S(1)}, u32[]{:S(2)}, u32[]{:S(2)}) collective-permute-start(f32[24,128]{1,0:T(8,128)S(1)} %get-tuple-element.37.mine), channel_id=1, source_target_pairs={{0,8},{8,0},{16,24},{24,16},{32,40},{40,32},{48,56},{56,48},{64,72... | collective-permute-start | bytes 36872 | tf_op jit(solution)/shard_map/ppermute | solution.py:524
  52.0 0.8 collective-permute-done.7.inter
  52.9 0.3 collective-permute-done.6.core
  53.2 1.9 %collective-permute-start.9 = (f32[8,128]{1,0:T(8,128)S(1)}, f32[8,128]{1,0:T(8,128)S(1)}, u32[]{:S(2)}, u32[]{:S(2)}) collective-permute-start(f32[8,128]{1,0:T(8,128)S(1)} %shard_map.93), channel_id=1, source_target_pairs={{0,7},{1,2},{2,1},{3,4},{4,3},{5,6},{6,5},{7,0},{8,15},{9,10},{10,... | collective-permute-start | bytes 12296 | tf_op jit(solution)/shard_map/ppermute | solution.py:536
  55.1 2.2 %collective-permute-start.8 = (f32[8,128]{1,0:T(8,128)S(1)}, f32[8,128]{1,0:T(8,128)S(1)}, u32[]{:S(2)}, u32[]{:S(2)}) collective-permute-start(f32[8,128]{1,0:T(8,128)S(1)} %shard_map.93), channel_id=1, source_target_pairs={{0,1},{1,0},{2,3},{3,2},{4,5},{5,4},{6,7},{7,6},{8,9},{9,8},{10,11... | collective-permute-start | bytes 12296 | tf_op jit(solution)/shard_map/ppermute | solution.py:532
  57.3 1.5 %collective-permute-done.9.odd = f32[8,128]{1,0:T(8,128)S(1)} collective-permute-done((f32[8,128]{1,0:T(8,128)S(1)}, f32[8,128]{1,0:T(8,128)S(1)}, u32[]{:S(2)}, u32[]{:S(2)}) %collective-permute-start.9) | collective-permute-done | bytes 4128 | tf_op jit(solution)/shard_map/ppermute | solution.py:536
  58.7 0.9 collective-permute-done.8.even
  59.7 2.4 %shard_map.94 = (f32[256,128]{1,0:T(8,128)S(1)}, f32[24,128]{1,0:T(8,128)S(1)}, f32[64,128]{1,0:T(8,128)S(1)}) custom-call(f32[256,128]{1,0:T(8,128)S(1)} %get-tuple-element.33.spots, f32[16,128]{1,0:T(8,128)S(1)} %get-tuple-element.34.by_lane, f32[24,128]{1,0:T(8,128)S(1)} %collective-permute-done.6.core, f32[24,128]{1,0:T(8,128)S(1)} %get-tuple-element.37.mine, ...), custom_call_target="tpu_custom_call" | custom-call | flops 4000000 | tf_op jit(solution)/shard_map/pallas_call | solution.py:55
  62.1 11.1 %all_to_all.15 = f32[32,2,128]{2,1,0:T(2,128)S(1)} all-to-all(f32[32,2,128]{2,1,0:T(2,128)S(1)} %bitcast.22), channel_id=1, replica_groups={{36,37,38,39,48,49,50,51,52,53,54,55,0,1,2,3,4,5,6,7,16,17,18,19,20,21,..., dimensions={0} | all-to-all | bytes 65536 | tf_op jit(solution)/shard_map/all_to_all | solution.py:542
  73.2 0.6 shard_map.95
  73.8 18.7 %all-to-all-start.2 = ((f32[32,1,128]{2,1,0:T(1,128)}), f32[32,1,128]{2,1,0:T(1,128)S(1)}, u32[]{:S(2)}, u32[]{:S(2)}) async-start(f32[32,1,128]{2,1,0:T(1,128)} %bitcast.11), calls=%async_computation.2 | async-start | bytes 32768 | tf_op jit(solution)/shard_map/all_to_all | solution.py:542
  92.5 3.3 %collective-permute-start.11 = (f32[24,128]{1,0:T(8,128)S(1)}, f32[24,128]{1,0:T(8,128)S(1)}, u32[]{:S(2)}, u32[]{:S(2)}) collective-permute-start(f32[24,128]{1,0:T(8,128)S(1)} %get-tuple-element.42.mine), channel_id=1, source_target_pairs={{8,16},{16,8},{24,32},{32,24},{40,48},{48,40},{56,64},{64,56},{72,... | collective-permute-start | bytes 36872 | tf_op jit(solution)/shard_map/ppermute | solution.py:528
  95.8 1.9 %collective-permute-start.10 = (f32[24,128]{1,0:T(8,128)S(1)}, f32[24,128]{1,0:T(8,128)S(1)}, u32[]{:S(2)}, u32[]{:S(2)}) collective-permute-start(f32[24,128]{1,0:T(8,128)S(1)} %get-tuple-element.42.mine), channel_id=1, source_target_pairs={{0,8},{8,0},{16,24},{24,16},{32,40},{40,32},{48,56},{56,48},{64,72... | collective-permute-start | bytes 36872 | tf_op jit(solution)/shard_map/ppermute | solution.py:524
  97.7 0.0 collective-permute-done.11.inter
  97.8 1.1 %collective-permute-done.10.core = f32[24,128]{1,0:T(8,128)S(1)} collective-permute-done((f32[24,128]{1,0:T(8,128)S(1)}, f32[24,128]{1,0:T(8,128)S(1)}, u32[]{:S(2)}, u32[]{:S(2)}) %collective-permute-start.10) | collective-permute-done | bytes 12320 | tf_op jit(solution)/shard_map/ppermute | solution.py:524
  98.9 0.6 all-to-all-done.2
  99.4 1.6 %shard_map.96 = (f32[256,128]{1,0:T(8,128)}, f32[256,128]{1,0:T(8,128)}) custom-call(f32[256,128]{1,0:T(8,128)S(1)} %get-tuple-element.33.spots, f32[16,128]{1,0:T(8,128)S(1)} %get-tuple-element.34.by_lane, f32[24,128]{1,0:T(8,128)S(1)} %collective-permute-done.10.core, f32[24,128]{1,0:T(8,128)S(1)} %get-tuple-element.42.mine, ...), custom_call_target="tpu_custom_call" | custom-call | flops 2000000 | tf_op jit(solution)/shard_map/pallas_call | solution.py:55
  (1 shorter events, 0.0 us)
Async XLA Ops:
  4.0 8.4 %copy-start = (f32[2,16,16,128]{3,2,1,0:T(8,128)S(1)}, f32[2,16,16,128]{3,2,1,0:T(8,128)}, u32[]{:S(2)}) copy-start(f32[2,16,16,128]{3,2,1,0:T(8,128)} %param.7) | copy-start | bytes 786436
  4.0 32.5 %all-to-all-start = ((f32[8,136,128]{2,1,0:T(8,128)}), f32[8,136,128]{2,1,0:T(8,128)S(1)}, u32[]{:S(2)}, u32[]{:S(2)}) async-start(f32[8,136,128]{2,1,0:T(8,128)} %bitcast.23), calls=%async_computation | async-start | bytes 1114112 | tf_op jit(solution)/shard_map/all_to_all | solution.py:542
  12.6 31.1 %collective-permute-start = (f32[256,128]{1,0:T(8,128)S(1)}, f32[256,128]{1,0:T(8,128)S(1)}, u32[]{:S(2)}, u32[]{:S(2)}) collective-permute-start(f32[256,128]{1,0:T(8,128)S(1)} %get-tuple-element.25), channel_id=1, source_target_pairs={{0,8},{8,0},{16,24},{24,16},{32,40},{40,32},{48,56},{56,48},{64,72... | collective-permute-start | bytes 393224 | tf_op jit(solution)/shard_map/ppermute | solution.py:524
  25.8 17.9 %collective-permute-start.1 = (f32[256,128]{1,0:T(8,128)S(1)}, f32[256,128]{1,0:T(8,128)S(1)}, u32[]{:S(2)}, u32[]{:S(2)}) collective-permute-start(f32[256,128]{1,0:T(8,128)S(1)} %get-tuple-element.26), channel_id=1, source_target_pairs={{8,16},{16,8},{24,32},{32,24},{40,48},{48,40},{56,64},{64,56},{72,... | collective-permute-start | bytes 393224 | tf_op jit(solution)/shard_map/ppermute | solution.py:528
  27.8 5.1 %collective-permute-start.2 = (f32[32,128]{1,0:T(8,128)S(1)}, f32[32,128]{1,0:T(8,128)S(1)}, u32[]{:S(2)}, u32[]{:S(2)}) collective-permute-start(f32[32,128]{1,0:T(8,128)S(1)} %get-tuple-element.27), channel_id=1, source_target_pairs={{0,1},{1,0},{2,3},{3,2},{4,5},{5,4},{6,7},{7,6},{8,9},{9,8},{10,11... | collective-permute-start | bytes 49160 | tf_op jit(solution)/shard_map/ppermute | solution.py:532
  30.9 5.7 %collective-permute-start.3 = (f32[32,128]{1,0:T(8,128)S(1)}, f32[32,128]{1,0:T(8,128)S(1)}, u32[]{:S(2)}, u32[]{:S(2)}) collective-permute-start(f32[32,128]{1,0:T(8,128)S(1)} %get-tuple-element.28), channel_id=1, source_target_pairs={{0,7},{1,2},{2,1},{3,4},{4,3},{5,6},{6,5},{7,0},{8,15},{9,10},{10,... | collective-permute-start | bytes 49160 | tf_op jit(solution)/shard_map/ppermute | solution.py:536
  36.7 7.9 %collective-permute-start.5 = (f32[88,128]{1,0:T(8,128)S(1)}, f32[88,128]{1,0:T(8,128)S(1)}, u32[]{:S(2)}, u32[]{:S(2)}) collective-permute-start(f32[88,128]{1,0:T(8,128)S(1)} %get-tuple-element.32), channel_id=1, source_target_pairs={{8,16},{16,8},{24,32},{32,24},{40,48},{48,40},{56,64},{64,56},{72,... | collective-permute-start | bytes 135176 | tf_op jit(solution)/shard_map/ppermute | solution.py:528
  41.8 3.1 %collective-permute-start.4 = (f32[88,128]{1,0:T(8,128)S(1)}, f32[88,128]{1,0:T(8,128)S(1)}, u32[]{:S(2)}, u32[]{:S(2)}) collective-permute-start(f32[88,128]{1,0:T(8,128)S(1)} %get-tuple-element.31.own_message), channel_id=1, source_target_pairs={{0,8},{8,0},{16,24},{24,16},{32,40},{40,32},{48,56},{56,48},{64,72... | collective-permute-start | bytes 135176 | tf_op jit(solution)/shard_map/ppermute | solution.py:524
  47.9 5.0 %collective-permute-start.7 = (f32[24,128]{1,0:T(8,128)S(1)}, f32[24,128]{1,0:T(8,128)S(1)}, u32[]{:S(2)}, u32[]{:S(2)}) collective-permute-start(f32[24,128]{1,0:T(8,128)S(1)} %get-tuple-element.37.mine), channel_id=1, source_target_pairs={{8,16},{16,8},{24,32},{32,24},{40,48},{48,40},{56,64},{64,56},{72,... | collective-permute-start | bytes 36872 | tf_op jit(solution)/shard_map/ppermute | solution.py:528
  50.1 3.1 %collective-permute-start.6 = (f32[24,128]{1,0:T(8,128)S(1)}, f32[24,128]{1,0:T(8,128)S(1)}, u32[]{:S(2)}, u32[]{:S(2)}) collective-permute-start(f32[24,128]{1,0:T(8,128)S(1)} %get-tuple-element.37.mine), channel_id=1, source_target_pairs={{0,8},{8,0},{16,24},{24,16},{32,40},{40,32},{48,56},{56,48},{64,72... | collective-permute-start | bytes 36872 | tf_op jit(solution)/shard_map/ppermute | solution.py:524
  53.2 5.6 %collective-permute-start.9 = (f32[8,128]{1,0:T(8,128)S(1)}, f32[8,128]{1,0:T(8,128)S(1)}, u32[]{:S(2)}, u32[]{:S(2)}) collective-permute-start(f32[8,128]{1,0:T(8,128)S(1)} %shard_map.93), channel_id=1, source_target_pairs={{0,7},{1,2},{2,1},{3,4},{4,3},{5,6},{6,5},{7,0},{8,15},{9,10},{10,... | collective-permute-start | bytes 12296 | tf_op jit(solution)/shard_map/ppermute | solution.py:536
  55.1 4.6 %collective-permute-start.8 = (f32[8,128]{1,0:T(8,128)S(1)}, f32[8,128]{1,0:T(8,128)S(1)}, u32[]{:S(2)}, u32[]{:S(2)}) collective-permute-start(f32[8,128]{1,0:T(8,128)S(1)} %shard_map.93), channel_id=1, source_target_pairs={{0,1},{1,0},{2,3},{3,2},{4,5},{5,4},{6,7},{7,6},{8,9},{9,8},{10,11... | collective-permute-start | bytes 12296 | tf_op jit(solution)/shard_map/ppermute | solution.py:532
  73.8 25.6 %all-to-all-start.2 = ((f32[32,1,128]{2,1,0:T(1,128)}), f32[32,1,128]{2,1,0:T(1,128)S(1)}, u32[]{:S(2)}, u32[]{:S(2)}) async-start(f32[32,1,128]{2,1,0:T(1,128)} %bitcast.11), calls=%async_computation.2 | async-start | bytes 32768 | tf_op jit(solution)/shard_map/all_to_all | solution.py:542
  92.5 5.3 %collective-permute-start.11 = (f32[24,128]{1,0:T(8,128)S(1)}, f32[24,128]{1,0:T(8,128)S(1)}, u32[]{:S(2)}, u32[]{:S(2)}) collective-permute-start(f32[24,128]{1,0:T(8,128)S(1)} %get-tuple-element.42.mine), channel_id=1, source_target_pairs={{8,16},{16,8},{24,32},{32,24},{40,48},{48,40},{56,64},{64,56},{72,... | collective-permute-start | bytes 36872 | tf_op jit(solution)/shard_map/ppermute | solution.py:528
  95.8 3.1 %collective-permute-start.10 = (f32[24,128]{1,0:T(8,128)S(1)}, f32[24,128]{1,0:T(8,128)S(1)}, u32[]{:S(2)}, u32[]{:S(2)}) collective-permute-start(f32[24,128]{1,0:T(8,128)S(1)} %get-tuple-element.42.mine), channel_id=1, source_target_pairs={{0,8},{8,0},{16,24},{24,16},{32,40},{40,32},{48,56},{56,48},{64,72... | collective-permute-start | bytes 36872 | tf_op jit(solution)/shard_map/ppermute | solution.py:524

commit v11 on v10

--- a/solution.py
+++ b/solution.py
@@ -19,6 +19,7 @@
 LON = 8
 HALF = LANES // 2
 OWN = LON * SLOT
+NEAR = 3 * OWN
 BULK = 2 * HALF + 2
 LIST = BULK + 6
 PARCEL = LIST
@@ -31,7 +32,7 @@
 MESSAGE = SPOTS + 8
 HERALD = OWN + 8
 NOWHERE = -4096.0
-FIRST = 6
+FIRST = 5
 HIGHEST = lax.Precision.HIGHEST
 F32 = jnp.float32
 VMEM = pl.BlockSpec(memory_space=pltpu.VMEM)
@@ -262,12 +263,18 @@
 
 
 def lay_out(spots, by_lane, own, sides, field, strips, low, high):
-    ln = lanes(LANES)
-    own_strip = jnp.where(ln < 32, jnp.where(ln >= 8, roll(own, 8), 0.0), jnp.where(ln < 56, roll(own, 56), 0.0))
-    pieces = []
-    for i, strip in enumerate((own_strip, sides)):
-        upper = (spots[i * LANES : (i + 1) * LANES, :].astype(jnp.int32) & 8) != 0
-        pieces.append(split(jnp.where(upper, roll(strip, HALF), strip)))
+    ln = lanes(NEAR)
+    first, last = (ln & (HALF - 1)) < 32, (ln & (HALF - 1)) < 56
+    inner = (ln & (HALF - 1)) >= 8
+    rows = own[:NEAR]
+    own_upper = (spots[:NEAR, :].astype(jnp.int32) & 8) != 0
+    near_left = jnp.where(own_upper, roll(rows, 72), roll(rows, 8))
+    near_right = jnp.where(own_upper, roll(rows, 120), roll(rows, 56))
+    own_strip = jnp.where((ln >= HALF) == own_upper, jnp.where(first, jnp.where(inner, near_left, 0.0), jnp.where(last, near_right, 0.0)), 0.0)
+    edge = sides[: 2 * NEAR]
+    side_upper = (spots[LANES : LANES + 2 * NEAR, :].astype(jnp.int32) & 8) != 0
+    side_strip = jnp.where(side_upper, roll(edge, HALF), edge)
+    pieces = [split(padded(own_strip, LANES)), split(padded(side_strip, LANES))]
     own_parts = split(own)
     lane_spots = [by_lane[i * 8 : i * 8 + 1, :].astype(jnp.int32) for i in range(2)]
     p = jnp.broadcast_to(lane_spots[0], (LANES, LANES))

time: 102 us -> 102 us (level)
  transfers between devices with their start and end apart: 14 -> 14, of which waited for: 9 -> 8; matrix products, arithmetic and copies ran while one was open for 0% -> 0% of each run, Pallas kernels for 1% -> 1%
where the time goes in v11:
time: 102 us
  starting transfers between devices  68.2 us (67%)
  Pallas kernels  11.4 us (11%)
  blocking collectives  11.1 us (11%)
  waiting for transfers between devices  9.53 us (9%)
  between operations  1.48 us (1%)
    all_to_all x2, starting transfers between devices, spread_out(): lax.all_to_all(x, axes, split_axis=0, concat_axis=0, tiled=True, axis_ind...  27.7 us
    ppermute x4, starting transfers between devices, to_core(): return lax.ppermute(x, LAT, [(i, i ^ 1) for i in range(lax.axis_size(LAT))])  19.1 us
    ppermute x4, starting transfers between devices, to_inter(): lax.ppermute(x, LAT, [(i, (i + 1 ^ 1) - 1) for i in range(1, lax.axis_siz...  12.6 us
    pallas_call x11, Pallas kernels, call(): pl.pallas_call(body, out_shape=[jax.ShapeDtypeStruct(s, F32) for s in out...  11.4 us
    all_to_all x1, blocking collectives, spread_out(): lax.all_to_all(x, axes, split_axis=0, concat_axis=0, tiled=True, axis_ind...  11.1 us
    ppermute x2, waiting for transfers between devices, to_odd(): lax.ppermute(x, 'lon', [(i, (((i + 1) % LON ^ 1) - 1) % LON) for i in ran...  5.46 us
    ppermute x2, starting transfers between devices, to_even(): return lax.ppermute(x, 'lon', [(i, i ^ 1) for i in range(LON)])  5.01 us
    ppermute x2, starting transfers between devices, to_odd(): lax.ppermute(x, 'lon', [(i, (((i + 1) % LON ^ 1) - 1) % LON) for i in ran...  3.83 us
  transfers between devices with their start and end apart: 14, of which 8 were waited for; matrix products, arithmetic and copies ran while one was open for 0% of the time, Pallas kernels for 1%

profile of v11, /device:TPU:1, one launch (start us, length us, event | category | flops | bytes accessed | tf_op | source)
XLA Modules:
  0.0 101.7 jit_solution(2317789219237744845)
XLA Ops:
  1.3 2.7 %shard_map.88 = f32[1088,128]{1,0:T(8,128)} custom-call(s32[8]{0:T(128)} %bitcast.27, s32[8]{0:T(128)} %bitcast.28, s32[1,1]{1,0:T(1,128)S(6)} %copy.10.count_at, f32[8,128,128]{2,1,0:T(8,128)} %bitcast.24, f32[8,128]{1,0:T(8,128)} %bitcast.25, f32[8,128]{1,0:T(8,128)} %bitcast.26), custom_call_target="tpu_custom_call" | custom-call | flops 4000000 | tf_op jit(solution)/shard_map/pallas_call | solution.py:56
  4.0 0.0 copy-start
  4.0 9.2 %all-to-all-start = ((f32[8,136,128]{2,1,0:T(8,128)}), f32[8,136,128]{2,1,0:T(8,128)S(1)}, u32[]{:S(2)}, u32[]{:S(2)}) async-start(f32[8,136,128]{2,1,0:T(8,128)} %bitcast.23), calls=%async_computation | async-start | bytes 1114112 | tf_op jit(solution)/shard_map/all_to_all | solution.py:549
  13.2 0.0 copy-done
  13.2 0.2 shard_map.86
  13.4 13.3 %collective-permute-start = (f32[256,128]{1,0:T(8,128)S(1)}, f32[256,128]{1,0:T(8,128)S(1)}, u32[]{:S(2)}, u32[]{:S(2)}) collective-permute-start(f32[256,128]{1,0:T(8,128)S(1)} %get-tuple-element.25), channel_id=1, source_target_pairs={{0,8},{8,0},{16,24},{24,16},{32,40},{40,32},{48,56},{56,48},{64,72... | collective-permute-start | bytes 393224 | tf_op jit(solution)/shard_map/ppermute | solution.py:531
  26.7 1.9 %collective-permute-start.1 = (f32[256,128]{1,0:T(8,128)S(1)}, f32[256,128]{1,0:T(8,128)S(1)}, u32[]{:S(2)}, u32[]{:S(2)}) collective-permute-start(f32[256,128]{1,0:T(8,128)S(1)} %get-tuple-element.26), channel_id=1, source_target_pairs={{8,16},{16,8},{24,32},{32,24},{40,48},{48,40},{56,64},{64,56},{72,... | collective-permute-start | bytes 393224 | tf_op jit(solution)/shard_map/ppermute | solution.py:535
  28.7 3.1 %collective-permute-start.2 = (f32[32,128]{1,0:T(8,128)S(1)}, f32[32,128]{1,0:T(8,128)S(1)}, u32[]{:S(2)}, u32[]{:S(2)}) collective-permute-start(f32[32,128]{1,0:T(8,128)S(1)} %get-tuple-element.27), channel_id=1, source_target_pairs={{0,1},{1,0},{2,3},{3,2},{4,5},{5,4},{6,7},{7,6},{8,9},{9,8},{10,11... | collective-permute-start | bytes 49160 | tf_op jit(solution)/shard_map/ppermute | solution.py:539
  31.8 1.9 %collective-permute-start.3 = (f32[32,128]{1,0:T(8,128)S(1)}, f32[32,128]{1,0:T(8,128)S(1)}, u32[]{:S(2)}, u32[]{:S(2)}) collective-permute-start(f32[32,128]{1,0:T(8,128)S(1)} %get-tuple-element.28), channel_id=1, source_target_pairs={{0,7},{1,2},{2,1},{3,4},{4,3},{5,6},{6,5},{7,0},{8,15},{9,10},{10,... | collective-permute-start | bytes 49160 | tf_op jit(solution)/shard_map/ppermute | solution.py:543
  33.7 0.0 collective-permute-done.2.even_edges
  33.7 3.8 %collective-permute-done.3.odd_edges = f32[32,128]{1,0:T(8,128)S(1)} collective-permute-done((f32[32,128]{1,0:T(8,128)S(1)}, f32[32,128]{1,0:T(8,128)S(1)}, u32[]{:S(2)}, u32[]{:S(2)}) %collective-permute-start.3) | collective-permute-done | bytes 16416 | tf_op jit(solution)/shard_map/ppermute | solution.py:543
  37.4 0.0 all-to-all-done
  37.4 0.1 shard_map.89
  37.6 5.1 %collective-permute-start.5 = (f32[88,128]{1,0:T(8,128)S(1)}, f32[88,128]{1,0:T(8,128)S(1)}, u32[]{:S(2)}, u32[]{:S(2)}) collective-permute-start(f32[88,128]{1,0:T(8,128)S(1)} %get-tuple-element.32), channel_id=1, source_target_pairs={{8,16},{16,8},{24,32},{32,24},{40,48},{48,40},{56,64},{64,56},{72,... | collective-permute-start | bytes 135176 | tf_op jit(solution)/shard_map/ppermute | solution.py:535
  42.7 1.9 %collective-permute-start.4 = (f32[88,128]{1,0:T(8,128)S(1)}, f32[88,128]{1,0:T(8,128)S(1)}, u32[]{:S(2)}, u32[]{:S(2)}) collective-permute-start(f32[88,128]{1,0:T(8,128)S(1)} %get-tuple-element.31.own_message), channel_id=1, source_target_pairs={{0,8},{8,0},{16,24},{24,16},{32,40},{40,32},{48,56},{56,48},{64,72... | collective-permute-start | bytes 135176 | tf_op jit(solution)/shard_map/ppermute | solution.py:531
  44.6 0.0 collective-permute-done.core
  44.6 0.0 collective-permute-done.1.inter
  44.6 0.4 shard_map.87
  45.0 0.5 shard_map.91.grams
  45.5 0.0 collective-permute-done.5.inter
  45.5 0.3 collective-permute-done.4.core
  45.8 2.2 %shard_map.90 = (f32[256,128]{1,0:T(8,128)S(1)}, f32[256,128]{1,0:T(8,128)S(1)}, f32[16,128]{1,0:T(8,128)S(1)}, f32[256,128]{1,0:T(8,128)S(1)}, f32[16,128]{1,0:T(8,128)S(1)}, /*index=5*/f32[8,128]{1,0:T(8,128)S(1)}) custom-call(f32[1024,128]{1,0:T(8,128)S(1)} %get-tuple-element.29.wide, f32[256,128]{1,0:T(8,128)S(1)} %get-tuple-element.30.mine.strips, ...), custom_call_target="tpu_custom_call" | custom-call | flops 4000000 | tf_op jit(solution)/shard_map/pallas_call | solution.py:56
  48.0 0.6 shard_map.92
  48.7 2.2 %collective-permute-start.7 = (f32[24,128]{1,0:T(8,128)S(1)}, f32[24,128]{1,0:T(8,128)S(1)}, u32[]{:S(2)}, u32[]{:S(2)}) collective-permute-start(f32[24,128]{1,0:T(8,128)S(1)} %get-tuple-element.37.mine), channel_id=1, source_target_pairs={{8,16},{16,8},{24,32},{32,24},{40,48},{48,40},{56,64},{64,56},{72,... | collective-permute-start | bytes 36872 | tf_op jit(solution)/shard_map/ppermute | solution.py:535
  50.9 1.9 %collective-permute-start.6 = (f32[24,128]{1,0:T(8,128)S(1)}, f32[24,128]{1,0:T(8,128)S(1)}, u32[]{:S(2)}, u32[]{:S(2)}) collective-permute-start(f32[24,128]{1,0:T(8,128)S(1)} %get-tuple-element.37.mine), channel_id=1, source_target_pairs={{0,8},{8,0},{16,24},{24,16},{32,40},{40,32},{48,56},{56,48},{64,72... | collective-permute-start | bytes 36872 | tf_op jit(solution)/shard_map/ppermute | solution.py:531
  52.9 0.8 collective-permute-done.7.inter
  53.7 0.3 collective-permute-done.6.core
  54.0 1.9 %collective-permute-start.9 = (f32[8,128]{1,0:T(8,128)S(1)}, f32[8,128]{1,0:T(8,128)S(1)}, u32[]{:S(2)}, u32[]{:S(2)}) collective-permute-start(f32[8,128]{1,0:T(8,128)S(1)} %shard_map.93), channel_id=1, source_target_pairs={{0,7},{1,2},{2,1},{3,4},{4,3},{5,6},{6,5},{7,0},{8,15},{9,10},{10,... | collective-permute-start | bytes 12296 | tf_op jit(solution)/shard_map/ppermute | solution.py:543
  55.9 1.9 %collective-permute-start.8 = (f32[8,128]{1,0:T(8,128)S(1)}, f32[8,128]{1,0:T(8,128)S(1)}, u32[]{:S(2)}, u32[]{:S(2)}) collective-permute-start(f32[8,128]{1,0:T(8,128)S(1)} %shard_map.93), channel_id=1, source_target_pairs={{0,1},{1,0},{2,3},{3,2},{4,5},{5,4},{6,7},{7,6},{8,9},{9,8},{10,11... | collective-permute-start | bytes 12296 | tf_op jit(solution)/shard_map/ppermute | solution.py:539
  57.8 1.7 %collective-permute-done.9.odd = f32[8,128]{1,0:T(8,128)S(1)} collective-permute-done((f32[8,128]{1,0:T(8,128)S(1)}, f32[8,128]{1,0:T(8,128)S(1)}, u32[]{:S(2)}, u32[]{:S(2)}) %collective-permute-start.9) | collective-permute-done | bytes 4128 | tf_op jit(solution)/shard_map/ppermute | solution.py:543
  59.5 0.9 collective-permute-done.8.even
  60.5 2.4 %shard_map.94 = (f32[256,128]{1,0:T(8,128)S(1)}, f32[24,128]{1,0:T(8,128)S(1)}, f32[64,128]{1,0:T(8,128)S(1)}) custom-call(f32[256,128]{1,0:T(8,128)S(1)} %get-tuple-element.33.spots, f32[16,128]{1,0:T(8,128)S(1)} %get-tuple-element.34.by_lane, f32[24,128]{1,0:T(8,128)S(1)} %collective-permute-done.6.core, f32[24,128]{1,0:T(8,128)S(1)} %get-tuple-element.37.mine, ...), custom_call_target="tpu_custom_call" | custom-call | flops 4000000 | tf_op jit(solution)/shard_map/pallas_call | solution.py:56
  62.9 11.1 %all_to_all.15 = f32[32,2,128]{2,1,0:T(2,128)S(1)} all-to-all(f32[32,2,128]{2,1,0:T(2,128)S(1)} %bitcast.22), channel_id=1, replica_groups={{36,37,38,39,48,49,50,51,52,53,54,55,0,1,2,3,4,5,6,7,16,17,18,19,20,21,..., dimensions={0} | all-to-all | bytes 65536 | tf_op jit(solution)/shard_map/all_to_all | solution.py:549
  74.0 0.6 shard_map.95
  74.6 18.6 %all-to-all-start.2 = ((f32[32,1,128]{2,1,0:T(1,128)}), f32[32,1,128]{2,1,0:T(1,128)S(1)}, u32[]{:S(2)}, u32[]{:S(2)}) async-start(f32[32,1,128]{2,1,0:T(1,128)} %bitcast.11), calls=%async_computation.2 | async-start | bytes 32768 | tf_op jit(solution)/shard_map/all_to_all | solution.py:549
  93.1 3.3 %collective-permute-start.11 = (f32[24,128]{1,0:T(8,128)S(1)}, f32[24,128]{1,0:T(8,128)S(1)}, u32[]{:S(2)}, u32[]{:S(2)}) collective-permute-start(f32[24,128]{1,0:T(8,128)S(1)} %get-tuple-element.42.mine), channel_id=1, source_target_pairs={{8,16},{16,8},{24,32},{32,24},{40,48},{48,40},{56,64},{64,56},{72,... | collective-permute-start | bytes 36872 | tf_op jit(solution)/shard_map/ppermute | solution.py:535
  96.5 1.9 %collective-permute-start.10 = (f32[24,128]{1,0:T(8,128)S(1)}, f32[24,128]{1,0:T(8,128)S(1)}, u32[]{:S(2)}, u32[]{:S(2)}) collective-permute-start(f32[24,128]{1,0:T(8,128)S(1)} %get-tuple-element.42.mine), channel_id=1, source_target_pairs={{0,8},{8,0},{16,24},{24,16},{32,40},{40,32},{48,56},{56,48},{64,72... | collective-permute-start | bytes 36872 | tf_op jit(solution)/shard_map/ppermute | solution.py:531
  98.4 0.0 collective-permute-done.11.inter
  98.4 1.1 %collective-permute-done.10.core = f32[24,128]{1,0:T(8,128)S(1)} collective-permute-done((f32[24,128]{1,0:T(8,128)S(1)}, f32[24,128]{1,0:T(8,128)S(1)}, u32[]{:S(2)}, u32[]{:S(2)}) %collective-permute-start.10) | collective-permute-done | bytes 12320 | tf_op jit(solution)/shard_map/ppermute | solution.py:531
  99.5 0.6 all-to-all-done.2
  100.1 1.6 %shard_map.96 = (f32[256,128]{1,0:T(8,128)}, f32[256,128]{1,0:T(8,128)}) custom-call(f32[256,128]{1,0:T(8,128)S(1)} %get-tuple-element.33.spots, f32[16,128]{1,0:T(8,128)S(1)} %get-tuple-element.34.by_lane, f32[24,128]{1,0:T(8,128)S(1)} %collective-permute-done.10.core, f32[24,128]{1,0:T(8,128)S(1)} %get-tuple-element.42.mine, ...), custom_call_target="tpu_custom_call" | custom-call | flops 2000000 | tf_op jit(solution)/shard_map/pallas_call | solution.py:56
  (1 shorter events, 0.0 us)
Async XLA Ops:
  4.0 9.2 %copy-start = (f32[2,16,16,128]{3,2,1,0:T(8,128)S(1)}, f32[2,16,16,128]{3,2,1,0:T(8,128)}, u32[]{:S(2)}) copy-start(f32[2,16,16,128]{3,2,1,0:T(8,128)} %param.7) | copy-start | bytes 786436
  4.0 33.4 %all-to-all-start = ((f32[8,136,128]{2,1,0:T(8,128)}), f32[8,136,128]{2,1,0:T(8,128)S(1)}, u32[]{:S(2)}, u32[]{:S(2)}) async-start(f32[8,136,128]{2,1,0:T(8,128)} %bitcast.23), calls=%async_computation | async-start | bytes 1114112 | tf_op jit(solution)/shard_map/all_to_all | solution.py:549
  13.4 31.2 %collective-permute-start = (f32[256,128]{1,0:T(8,128)S(1)}, f32[256,128]{1,0:T(8,128)S(1)}, u32[]{:S(2)}, u32[]{:S(2)}) collective-permute-start(f32[256,128]{1,0:T(8,128)S(1)} %get-tuple-element.25), channel_id=1, source_target_pairs={{0,8},{8,0},{16,24},{24,16},{32,40},{40,32},{48,56},{56,48},{64,72... | collective-permute-start | bytes 393224 | tf_op jit(solution)/shard_map/ppermute | solution.py:531
  26.7 17.9 %collective-permute-start.1 = (f32[256,128]{1,0:T(8,128)S(1)}, f32[256,128]{1,0:T(8,128)S(1)}, u32[]{:S(2)}, u32[]{:S(2)}) collective-permute-start(f32[256,128]{1,0:T(8,128)S(1)} %get-tuple-element.26), channel_id=1, source_target_pairs={{8,16},{16,8},{24,32},{32,24},{40,48},{48,40},{56,64},{64,56},{72,... | collective-permute-start | bytes 393224 | tf_op jit(solution)/shard_map/ppermute | solution.py:535
  28.7 5.0 %collective-permute-start.2 = (f32[32,128]{1,0:T(8,128)S(1)}, f32[32,128]{1,0:T(8,128)S(1)}, u32[]{:S(2)}, u32[]{:S(2)}) collective-permute-start(f32[32,128]{1,0:T(8,128)S(1)} %get-tuple-element.27), channel_id=1, source_target_pairs={{0,1},{1,0},{2,3},{3,2},{4,5},{5,4},{6,7},{7,6},{8,9},{9,8},{10,11... | collective-permute-start | bytes 49160 | tf_op jit(solution)/shard_map/ppermute | solution.py:539
  31.8 5.7 %collective-permute-start.3 = (f32[32,128]{1,0:T(8,128)S(1)}, f32[32,128]{1,0:T(8,128)S(1)}, u32[]{:S(2)}, u32[]{:S(2)}) collective-permute-start(f32[32,128]{1,0:T(8,128)S(1)} %get-tuple-element.28), channel_id=1, source_target_pairs={{0,7},{1,2},{2,1},{3,4},{4,3},{5,6},{6,5},{7,0},{8,15},{9,10},{10,... | collective-permute-start | bytes 49160 | tf_op jit(solution)/shard_map/ppermute | solution.py:543
  37.6 7.9 %collective-permute-start.5 = (f32[88,128]{1,0:T(8,128)S(1)}, f32[88,128]{1,0:T(8,128)S(1)}, u32[]{:S(2)}, u32[]{:S(2)}) collective-permute-start(f32[88,128]{1,0:T(8,128)S(1)} %get-tuple-element.32), channel_id=1, source_target_pairs={{8,16},{16,8},{24,32},{32,24},{40,48},{48,40},{56,64},{64,56},{72,... | collective-permute-start | bytes 135176 | tf_op jit(solution)/shard_map/ppermute | solution.py:535
  42.7 3.1 %collective-permute-start.4 = (f32[88,128]{1,0:T(8,128)S(1)}, f32[88,128]{1,0:T(8,128)S(1)}, u32[]{:S(2)}, u32[]{:S(2)}) collective-permute-start(f32[88,128]{1,0:T(8,128)S(1)} %get-tuple-element.31.own_message), channel_id=1, source_target_pairs={{0,8},{8,0},{16,24},{24,16},{32,40},{40,32},{48,56},{56,48},{64,72... | collective-permute-start | bytes 135176 | tf_op jit(solution)/shard_map/ppermute | solution.py:531
  48.7 5.0 %collective-permute-start.7 = (f32[24,128]{1,0:T(8,128)S(1)}, f32[24,128]{1,0:T(8,128)S(1)}, u32[]{:S(2)}, u32[]{:S(2)}) collective-permute-start(f32[24,128]{1,0:T(8,128)S(1)} %get-tuple-element.37.mine), channel_id=1, source_target_pairs={{8,16},{16,8},{24,32},{32,24},{40,48},{48,40},{56,64},{64,56},{72,... | collective-permute-start | bytes 36872 | tf_op jit(solution)/shard_map/ppermute | solution.py:535
  50.9 3.1 %collective-permute-start.6 = (f32[24,128]{1,0:T(8,128)S(1)}, f32[24,128]{1,0:T(8,128)S(1)}, u32[]{:S(2)}, u32[]{:S(2)}) collective-permute-start(f32[24,128]{1,0:T(8,128)S(1)} %get-tuple-element.37.mine), channel_id=1, source_target_pairs={{0,8},{8,0},{16,24},{24,16},{32,40},{40,32},{48,56},{56,48},{64,72... | collective-permute-start | bytes 36872 | tf_op jit(solution)/shard_map/ppermute | solution.py:531
  54.0 5.6 %collective-permute-start.9 = (f32[8,128]{1,0:T(8,128)S(1)}, f32[8,128]{1,0:T(8,128)S(1)}, u32[]{:S(2)}, u32[]{:S(2)}) collective-permute-start(f32[8,128]{1,0:T(8,128)S(1)} %shard_map.93), channel_id=1, source_target_pairs={{0,7},{1,2},{2,1},{3,4},{4,3},{5,6},{6,5},{7,0},{8,15},{9,10},{10,... | collective-permute-start | bytes 12296 | tf_op jit(solution)/shard_map/ppermute | solution.py:543
  55.9 4.6 %collective-permute-start.8 = (f32[8,128]{1,0:T(8,128)S(1)}, f32[8,128]{1,0:T(8,128)S(1)}, u32[]{:S(2)}, u32[]{:S(2)}) collective-permute-start(f32[8,128]{1,0:T(8,128)S(1)} %shard_map.93), channel_id=1, source_target_pairs={{0,1},{1,0},{2,3},{3,2},{4,5},{5,4},{6,7},{7,6},{8,9},{9,8},{10,11... | collective-permute-start | bytes 12296 | tf_op jit(solution)/shard_map/ppermute | solution.py:539
  74.6 25.5 %all-to-all-start.2 = ((f32[32,1,128]{2,1,0:T(1,128)}), f32[32,1,128]{2,1,0:T(1,128)S(1)}, u32[]{:S(2)}, u32[]{:S(2)}) async-start(f32[32,1,128]{2,1,0:T(1,128)} %bitcast.11), calls=%async_computation.2 | async-start | bytes 32768 | tf_op jit(solution)/shard_map/all_to_all | solution.py:549
  93.1 5.3 %collective-permute-start.11 = (f32[24,128]{1,0:T(8,128)S(1)}, f32[24,128]{1,0:T(8,128)S(1)}, u32[]{:S(2)}, u32[]{:S(2)}) collective-permute-start(f32[24,128]{1,0:T(8,128)S(1)} %get-tuple-element.42.mine), channel_id=1, source_target_pairs={{8,16},{16,8},{24,32},{32,24},{40,48},{48,40},{56,64},{64,56},{72,... | collective-permute-start | bytes 36872 | tf_op jit(solution)/shard_map/ppermute | solution.py:535
  96.5 3.1 %collective-permute-start.10 = (f32[24,128]{1,0:T(8,128)S(1)}, f32[24,128]{1,0:T(8,128)S(1)}, u32[]{:S(2)}, u32[]{:S(2)}) collective-permute-start(f32[24,128]{1,0:T(8,128)S(1)} %get-tuple-element.42.mine), channel_id=1, source_target_pairs={{0,8},{8,0},{16,24},{24,16},{32,40},{40,32},{48,56},{56,48},{64,72... | collective-permute-start | bytes 36872 | tf_op jit(solution)/shard_map/ppermute | solution.py:531
